TPU v7x, 128 devices: a whole 4x4x4 slice. The times are simulated.
128 devices in a mesh: dp: 8 (over z, core), seq: 16 (over x, y).
Axes of the slice: x: 4, y: 4, z: 4, core: 2. Of those that a mesh axis runs over, the one named last changes fastest.
Arguments:
- loaded: bfloat16 [32768, 1024], P(('dp', 'seq')), may hold values from -6 to 6
- plan: int32 [128, 128], replicated, may hold values from 1 to 4, as said below
- segment_ids: int32 [16, 2048], P('dp'), may hold values from 0 to 31, never falling along the last dimension, each value on 1 to 1024 neighbouring positions
- in_weight: bfloat16 [1024, 2048], P('dp'), may hold values from -0.1875 to 0.1875
- out_weight: bfloat16 [1024, 1024], P('dp'), may hold values from -0.1875 to 0.1875
- depth_kernel: bfloat16 [1024, 31], P('dp'), may hold values from -2 to 2
- norm_gains: bfloat16 [1024, 2], P('dp'), may hold values from 0.25 to 1.75
- upstream: bfloat16 [16, 2048, 1024], P('dp', 'seq'), may hold values from -6 to 6
Outputs:
- encoded: bfloat16 [16, 2048, 1024], P('dp', 'seq')
- grad_frames: bfloat16 [16, 2048, 1024], P('dp', 'seq')
- grad_in_weight: float32 [1024, 2048], P('dp')
- grad_out_weight: float32 [1024, 1024], P('dp')
- grad_kernel: float32 [1024, 31], P('dp')
- grad_gains: float32 [1024, 2], P('dp')
Inputs may be any that keep to these rules, and one draw needn't show every extreme that they name: Every row and every column of plan sums to 256; every row reaches 4.
All inputs are finite; a program needn't handle non-finite values.
Results may differ from a plain program's by a relative error of at most 0.006.
Values may be sent and summed in bfloat16 or wider, within the bound.
No kernel may reach another device: no remote copies, remote signals or barrier semaphores. Data moves between devices by JAX's collectives and lax.ppermute only.
A program may use at most 128 MiB of HBM per device.

v0:
```python
import math

import jax
import jax.numpy as jnp
from jax import lax
from jax.sharding import PartitionSpec as P


def sent_together(arrays, axis, dim, along):
    both = jnp.concatenate(arrays, axis=along)
    filled, at, finished = (lax.all_gather(both, axis, axis=dim, tiled=True), 0, [])
    for a in arrays:
        finished.append(lax.slice_in_dim(filled, at, at + a.shape[along], axis=along))
        at += a.shape[along]
    return tuple(finished)


def padded(block, sides, width):
    for axis, dim in sides:
        count = lax.axis_size(axis)
        forward = [(i, i + 1) for i in range(count - 1)]
        backward = [(target, source) for source, target in forward]
        low = lax.ppermute(
            lax.slice_in_dim(block, block.shape[dim] - width, None, axis=dim), axis, forward
        )
        high = lax.ppermute(lax.slice_in_dim(block, 0, width, axis=dim), axis, backward)
        block = jnp.concatenate([low, block, high], axis=dim)
    return block


def joined_along(tiles, dim):
    tiles = jnp.moveaxis(tiles, 0, dim)
    lengths = tiles.shape
    return tiles.reshape(*lengths[:dim], lengths[dim] * lengths[dim + 1], *lengths[dim + 2 :])


def from_everyone(shard, axis):
    devices = lax.axis_size(axis)
    return lax.all_to_all(
        jnp.broadcast_to(shard[None], (devices, *shard.shape)), axis, 0, 0, tiled=True
    )


def gather_directly(shard, axis, dim):
    return joined_along(from_everyone(shard, axis), dim)


def in_one_piece(arrays, axis, dim, along):
    widths = [a.shape[along] for a in arrays]
    both = jnp.concatenate(arrays, axis=along)
    filled = lax.psum_scatter(both, axis, scatter_dimension=dim, tiled=True)
    return tuple(jnp.split(filled, [sum(widths[:k]) for k in range(1, len(widths))], axis=along))


def norm_rows(values, gain):
    average = jnp.mean(values, axis=-1, keepdims=True)
    centered = values - average
    spread = jnp.mean(centered * centered, axis=-1, keepdims=True)
    return centered * lax.rsqrt(spread + 1e-05) * gain


def mid_section(values, gain):
    normed = norm_rows(values, gain)
    return normed * jax.nn.sigmoid(normed)


def per_device(
    loaded, plan, segment_ids, in_weight, out_weight, depth_kernel, norm_gains, upstream
):
    rows_dev, width = loaded.shape
    devices = plan.shape[0]
    capacity = 2 * rows_dev // devices
    slabs, slab_len = segment_ids.shape
    frames_dev = slab_len // lax.axis_size("seq")
    kernel_len = depth_kernel.shape[1]
    margin = kernel_len // 2
    sender = lax.axis_index(("dp", "seq"))
    send_plan = lax.dynamic_index_in_dim(plan, sender, 0, keepdims=False)
    send_start = jnp.cumsum(send_plan) - send_plan
    slot_index = jnp.arange(capacity, dtype=jnp.int32)
    source_rows = send_start[:, None] + slot_index[None, :]
    filled = slot_index[None, :] < send_plan[:, None]
    picked = jnp.take(loaded, jnp.clip(source_rows, 0, rows_dev - 1).reshape(-1), axis=0)
    outgoing = jnp.where(filled.reshape(-1, 1), picked, jnp.zeros_like(picked)).reshape(
        devices, capacity, width
    )
    arrived = lax.all_to_all(
        outgoing, ("dp", "seq"), split_axis=0, concat_axis=0, tiled=True
    ).reshape(devices * capacity, width)
    recv_plan = lax.dynamic_index_in_dim(plan, sender, 1, keepdims=False)
    recv_end = jnp.cumsum(recv_plan)
    frame_index = jnp.arange(rows_dev, dtype=jnp.int32)
    before = recv_end[None, :] <= frame_index[:, None]
    source_dev = jnp.sum(before.astype(jnp.int32), axis=1)
    start_of = jnp.sum(jnp.where(before, recv_plan[None, :], 0), axis=1)
    frames = jnp.take(arrived, source_dev * capacity + frame_index - start_of, axis=0)
    kernel_full, gains_full = sent_together((depth_kernel, norm_gains), "dp", 0, 1)
    taps = kernel_full.astype(jnp.float32)
    gain_pre = gains_full[:, 0].astype(jnp.float32)
    gain_mid = gains_full[:, 1].astype(jnp.float32)
    frame_rows = frames.astype(jnp.float32)
    normed_full, pull_pre = jax.vjp(norm_rows, frame_rows, gain_pre)
    normed = normed_full.astype(jnp.bfloat16)
    part_cols = normed
    hidden = jnp.dot(
        part_cols,
        lax.all_gather(in_weight, "dp", axis=0, tiled=True),
        preferred_element_type=jnp.float32,
    )
    gate_lin = hidden[:, :width]
    gate_sig = jax.nn.sigmoid(hidden[:, width:])
    gated = (gate_lin * gate_sig).astype(jnp.bfloat16).reshape(slabs, frames_dev, width)
    gated_pad = padded(gated, (("seq", 1),), margin)
    id_pad = jnp.pad(segment_ids, ((0, 0), (margin, margin)), constant_values=-1)
    window = lax.dynamic_slice_in_dim(
        id_pad, lax.axis_index("seq") * frames_dev, frames_dev + 2 * margin, 1
    )
    center = window[:, margin : margin + frames_dev]
    mixing = jnp.zeros((slabs, frames_dev, width), jnp.float32)
    for tap_index in range(kernel_len):
        same = (window[:, tap_index : tap_index + frames_dev] == center)[..., None]
        mixing = mixing + jnp.where(
            same,
            gated_pad[:, tap_index : tap_index + frames_dev].astype(jnp.float32)
            * taps[:, tap_index],
            0.0,
        )
    activated_full, pull_mid = jax.vjp(mid_section, mixing.reshape(rows_dev, width), gain_mid)
    activated = activated_full.astype(jnp.bfloat16)
    upstream_rows = upstream.reshape(rows_dev, width)
    part_cols = activated
    projected = jnp.dot(
        part_cols, gather_directly(out_weight, "dp", 0), preferred_element_type=jnp.float32
    )
    grad_act = jnp.dot(
        upstream_rows, gather_directly(out_weight, "dp", 0).T, preferred_element_type=jnp.float32
    )
    encoded = (frame_rows + projected).astype(jnp.bfloat16).reshape(slabs, frames_dev, width)
    grad_out_w = jnp.dot(activated.T, upstream_rows, preferred_element_type=jnp.float32)
    grad_mixing, grad_gain_mid = pull_mid(grad_act)
    grad_cells = grad_mixing.reshape(slabs, frames_dev, width)
    grad_pad = padded(grad_cells, (("seq", 1),), margin)
    grad_gated = jnp.zeros((slabs, frames_dev, width), jnp.float32)
    tap_grads = []
    for tap_index in range(kernel_len):
        same = (window[:, tap_index : tap_index + frames_dev] == center)[..., None]
        tap_grads.append(
            jnp.sum(
                jnp.where(
                    same,
                    grad_cells
                    * gated_pad[:, tap_index : tap_index + frames_dev].astype(jnp.float32),
                    0.0,
                ),
                axis=(0, 1),
            )
        )
        mirror = 2 * margin - tap_index
        back_same = (window[:, mirror : mirror + frames_dev] == center)[..., None]
        grad_gated = grad_gated + jnp.where(
            back_same, grad_pad[:, mirror : mirror + frames_dev] * taps[:, tap_index], 0.0
        )
    grad_taps = jnp.stack(tap_grads, axis=1)
    grad_gated = grad_gated.reshape(rows_dev, width)
    grad_hidden = jnp.concatenate(
        [grad_gated * gate_sig, grad_gated * gate_lin * gate_sig * (1.0 - gate_sig)], axis=1
    ).astype(jnp.bfloat16)
    grad_in_w = jnp.dot(normed.T, grad_hidden, preferred_element_type=jnp.float32)
    grad_normed = jnp.dot(
        grad_hidden,
        lax.all_gather(in_weight, "dp", axis=0, tiled=True).T,
        preferred_element_type=jnp.float32,
    )
    grad_rows, grad_gain_pre = pull_pre(grad_normed)
    grad_frames = (
        (upstream_rows.astype(jnp.float32) + grad_rows)
        .astype(jnp.bfloat16)
        .reshape(slabs, frames_dev, width)
    )
    grad_gain = jnp.stack([grad_gain_pre, grad_gain_mid], axis=1)
    shares = in_one_piece((grad_in_w, grad_out_w, grad_taps, grad_gain), "dp", 0, 1)
    totals = lax.psum((shares[0], shares[1], shares[2], shares[3]), "seq")
    scale = 1.0 / math.sqrt(lax.axis_size("dp") * lax.axis_size("seq") * rows_dev)
    return (
        encoded,
        grad_frames,
        totals[0] * scale,
        totals[1] * scale,
        totals[2] * scale,
        totals[3] * scale,
    )


def solution(mesh):
    placed = (
        P(("dp", "seq"), None),
        P(),
        P("dp", None),
        P("dp", None),
        P("dp", None),
        P("dp", None),
        P("dp", None),
        P("dp", "seq", None),
    )
    return jax.shard_map(
        per_device,
        mesh=mesh,
        in_specs=placed,
        out_specs=(
            P("dp", "seq", None),
            P("dp", "seq", None),
            P("dp", None),
            P("dp", None),
            P("dp", None),
            P("dp", None),
        ),
        check_vma=False,
    )
```

profile of v0, /device:TPU:0, one launch (start us, length us, event | category | flops | bytes accessed | tf_op | source)
XLA Modules:
  0.0 370.0 jit_solution(7582916796538782629)
XLA Ops:
  10.0 2.1 gather_fusion
  12.6 1.7 select_select_fusion
  14.3 11.2 %all-to-all-start = ((bf16[128,4,1024]{2,1,0:T(4,128)(2,1)}), bf16[128,4,1024]{2,1,0:T(4,128)(2,1)S(1)}, u32[]{:S(2)}, u32[]{:S(2)}) async-start(bf16[128,4,1024]{2,1,0:T(4,128)(2,1)} %select_select_fusion), calls=%async_computation | async-start | bytes 2097152 | tf_op jit(solution)/shard_map/all_to_all | solution.py:87
  27.7 17.0 %all_gather.7 = bf16[1024,33]{0,1:T(8,128)(2,1)S(1)} all-gather(bf16[128,33]{0,1:T(8,128)(2,1)S(1)} %pad_maximum_fusion.7), channel_id=1, replica_groups=mesh['dp'=8,'seq'=16] {'dp'}, dimensions={0}, use_global_device_ids=true | all-gather | bytes 76032 | tf_op jit(solution)/shard_map/all_gather | solution.py:11
  46.8 4.4 %all-to-all-start.1 = ((bf16[8,128,1024]{2,1,0:T(8,128)(2,1)}), bf16[8,128,1024]{2,1,0:T(8,128)(2,1)}, u32[]{:S(2)}, u32[]{:S(2)}) async-start(bf16[8,128,1024]{2,1,0:T(8,128)(2,1)} %broadcast_in_dim.651), calls=%async_computation.1 | async-start | bytes 4194304 | tf_op jit(solution)/shard_map/all_to_all | solution.py:39
  53.3 3.1 all-gather.2.cloned.1.call-done
  56.4 3.6 fusion.326
  61.7 3.4 collective-permute-start
  67.4 3.9 %collective-permute-done.1 = bf16[2,15,1024]{2,1,0:T(8,128)(2,1)S(1)} collective-permute-done((bf16[2,15,1024]{2,1,0:T(8,128)(2,1)S(1)}, bf16[2,15,1024]{2,1,0:T(8,128)(2,1)S(1)}, u32[]{:S(2)}, u32[]{:S(2)}) %collective-permute-start.1) | collective-permute-done | bytes 61472 | tf_op jit(solution)/shard_map/ppermute | solution.py:26
  71.6 8.0 %fusion.331 = (f32[2,128]{1,0:T(2,128)S(1)}, f32[2,128,1024]{2,1,0:T(8,128)S(1)}) fusion(f32[1024]{0:T(1024)S(1)} %bitcast.198, bf16[2,15,1024]{2,1,0:T(8,128)(2,1)S(1)} %collective-permute-done.1, bf16[2,128,1024]{2,1,0:T(8,128)(2,1)S(1)} %bitcast.158, pred[2,128]{1,0:T(4,128)(4,1)} %get-tuple-element.146, f32[1024]{0:T(1024)S(1)} %bitcast.200, ...), kind=kLoop, calls=%fused_computation.565 | loop fusion | flops 55836416 | bytes 1831424 | tf_op jit(solution)/shard_map/jvp()/reduce_sum | solution.py:56
  80.4 3.5 multiply_reduce_fusion
  84.3 3.2 fusion.239
  89.7 5.2 %collective-permute-start.3 = (f32[2,15,1024]{2,1,0:T(8,128)S(1)}, f32[2,15,1024]{2,1,0:T(8,128)}, u32[]{:S(2)}, u32[]{:S(2)}) collective-permute-start(f32[2,15,1024]{2,1,0:T(8,128)S(1)} %get-tuple-element.82), channel_id=1, source_target_pairs={{0,1},{1,2},{2,3},{3,4},{4,5},{5,6},{6,7},{7,8},{8,9},{9,10},{10,1... | collective-permute-start | bytes 368648 | tf_op jit(solution)/shard_map/ppermute | solution.py:23
  94.9 2.8 fusion.191
  98.7 1.7 copy.74
  100.4 2.8 fusion.236
  104.8 1.7 copy.88
  106.6 3.0 fusion.242
  109.6 1.7 copy.76
  111.3 1.7 copy.90
  113.1 2.0 fusion.188
  142.5 2.8 convolution_bitcast_fusion
  145.7 12.7 %fusion.11 = f32[2,128,1024]{2,1,0:T(8,128)S(1)} fusion(f32[2,128,1024]{2,1,0:T(8,128)S(1)} %bitcast.156, f32[2,15,1024]{2,1,0:T(8,128)} %collective-permute-done.3, f32[2,15,1024]{2,1,0:T(8,128)} %collective-permute-done.2, f32[1024]{0:T(1024)S(1)} %bitcast.199, f32[1024]{0:T(1024)S(1)} %bitcast.201, f32[1024]{0:T(1024)S(1)} %bitcast.203, ...), kind=kLoop, calls=%fused_computation.164 | loop fusion | flops 31719424 | bytes 2477568 | tf_op jit(solution)/shard_map/add | solution.py:160
  159.1 4.7 %fusion.258 = f32[1024,2048]{1,0:T(8,128)} fusion(bf16[256,1024]{1,0:T(8,128)(2,1)S(1)} %get-tuple-element.80, bf16[256,1024]{1,0:T(8,128)(2,1)S(1)} %get-tuple-element.79, f32[1024]{0:T(1024)S(1)} %bitcast.168, f32[256]{0:T(256)S(1)} %copy-done.73, f32[256]{0:T(256)S(1)} %copy-done.71, bf16[256,1024]{1,0:T(8,128)(2,1)S(1)} %gather_fusion.1, ...), kind=kOutput, calls=%fused_computation.426 | convolution fusion | flops 1077411840 | bytes 9967872 | tf_op jit(solution)/shard_map/dot_general | solution.py:168
  166.9 21.8 %concatenate.86 = f32[1024,3105]{1,0:T(8,128)} concatenate(f32[1024,2048]{1,0:T(8,128)} %fusion.258, f32[1024,1024]{1,0:T(8,128)} %convolution_bitcast_fusion, f32[1024,1]{1,0:T(8,128)S(1)} %copy.60, f32[1024,1]{1,0:T(8,128)} %copy.61, f32[1024,1]{1,0:T(8,128)} %copy.62, f32[1024,1]{1,0:T(8,128)} %copy.63, f32[1024,1]{1,0:T(8,128)} %copy.64, f32[1024,1]{1,0:T(8,128)} %copy.65, ...), dimensions={1} | concatenate | bytes 25436160 | tf_op jit(solution)/shard_map/concatenate | solution.py:50
  188.8 78.6 %reduce-scatter.2.cloned.1.call-done = f32[128,3105]{1,0:T(8,128)} async-done(((f32[1024,3105]{1,0:T(8,128)}), f32[128,3105]{1,0:T(8,128)}) %reduce-scatter.2.cloned.1.call-update) | async-done | bytes 1589776 | tf_op jit(solution)/shard_map/reduce_scatter | solution.py:51
  267.4 1.9 split.17
  269.3 2.3 split.16
  271.7 3.2 fusion.4
  276.3 75.3 %all-reduce.1 = (f32[128,31]{1,0:T(8,128)S(1)}, f32[128,2]{1,0:T(8,128)S(1)}) all-reduce(f32[128,31]{1,0:T(8,128)S(1)} %slice-done, f32[128,2]{1,0:T(8,128)S(1)} %split.19), channel_id=1, replica_groups=mesh['dp'=8,'seq'=16] {'seq'}, use_global_device_ids=true, to_apply=%region_48.49 | all-reduce | flops 4224 | bytes 33792 | tf_op jit(solution)/shard_map/psum | solution.py:182
  353.0 7.2 %all-reduce.5.cloned.1.call-done = (f32[128,2048]{1,0:T(8,128)}, f32[128,1024]{1,0:T(8,128)}) async-done(((f32[128,2048]{1,0:T(8,128)}, f32[128,1024]{1,0:T(8,128)}), (f32[128,2048]{1,0:T(8,128)}, f32[128,1024]{1,0:T(8,128)})) %all-reduce.5.cloned.1.call-update) | async-done | bytes 1572880 | tf_op jit(solution)/shard_map/psum | solution.py:182
  360.3 2.4 broadcast_multiply_fusion
  (348 shorter events, 54.0 us)
Async XLA Ops:
  7.2 49.2 %all-gather.2.cloned.1.call-start = ((), (), s32[]{:S(2)}) async-start(), calls=%async_computation.3 | async-start | bytes 4718592 | tf_op jit(solution)/shard_map/all_gather | solution.py:107
  14.3 30.8 %copy-start.11 = (bf16[128,1024]{1,0:T(8,128)(2,1)S(1)}, bf16[128,1024]{1,0:T(8,128)(2,1)}, u32[]{:S(2)}) copy-start(bf16[128,1024]{1,0:T(8,128)(2,1)} %param.12) | copy-start | bytes 786436
  14.3 30.8 %all-to-all-start = ((bf16[128,4,1024]{2,1,0:T(4,128)(2,1)}), bf16[128,4,1024]{2,1,0:T(4,128)(2,1)S(1)}, u32[]{:S(2)}, u32[]{:S(2)}) async-start(bf16[128,4,1024]{2,1,0:T(4,128)(2,1)} %select_select_fusion), calls=%async_computation | async-start | bytes 2097152 | tf_op jit(solution)/shard_map/all_to_all | solution.py:87
  26.8 29.6 %copy-start.74 = (pred[256]{0:T(512)(128)(4,1)}, pred[256]{0:T(512)(128)(4,1)S(1)}, u32[]{:S(2)}) copy-start(pred[256]{0:T(512)(128)(4,1)S(1)} %compare_and_fusion.1) | copy-start | bytes 772
  27.6 43.6 %copy-start.98 = (pred[2,128]{1,0:T(4,128)(4,1)}, pred[2,128]{1,0:T(4,128)(4,1)S(1)}, u32[]{:S(2)}) copy-start(pred[2,128]{1,0:T(4,128)(4,1)S(1)} %get-tuple-element.118) | copy-start | bytes 772
  27.6 43.6 %copy-start.101 = (pred[2,128]{1,0:T(4,128)(4,1)}, pred[2,128]{1,0:T(4,128)(4,1)S(1)}, u32[]{:S(2)}) copy-start(pred[2,128]{1,0:T(4,128)(4,1)S(1)} %get-tuple-element.120) | copy-start | bytes 772
  27.6 43.6 %copy-start.103 = (pred[2,128]{1,0:T(4,128)(4,1)}, pred[2,128]{1,0:T(4,128)(4,1)S(1)}, u32[]{:S(2)}) copy-start(pred[2,128]{1,0:T(4,128)(4,1)S(1)} %get-tuple-element.121) | copy-start | bytes 772
  27.6 43.6 %copy-start.105 = (pred[2,128]{1,0:T(4,128)(4,1)}, pred[2,128]{1,0:T(4,128)(4,1)S(1)}, u32[]{:S(2)}) copy-start(pred[2,128]{1,0:T(4,128)(4,1)S(1)} %get-tuple-element.122) | copy-start | bytes 772
  27.7 43.6 %copy-start.107 = (pred[2,128]{1,0:T(4,128)(4,1)}, pred[2,128]{1,0:T(4,128)(4,1)S(1)}, u32[]{:S(2)}) copy-start(pred[2,128]{1,0:T(4,128)(4,1)S(1)} %get-tuple-element.128) | copy-start | bytes 772
  27.7 43.6 %copy-start.109 = (pred[2,128]{1,0:T(4,128)(4,1)}, pred[2,128]{1,0:T(4,128)(4,1)S(1)}, u32[]{:S(2)}) copy-start(pred[2,128]{1,0:T(4,128)(4,1)S(1)} %get-tuple-element.129) | copy-start | bytes 772
  44.8 26.5 %copy-start.14 = (f32[1024,1]{0,1:T(1,128)}, f32[1024,1]{0,1:T(1,128)S(1)}, u32[]{:S(2)}) copy-start(f32[1024,1]{0,1:T(1,128)S(1)} %get-tuple-element.107) | copy-start | bytes 12292
  44.8 26.5 %copy-start.16 = (f32[1024,1]{0,1:T(1,128)}, f32[1024,1]{0,1:T(1,128)S(1)}, u32[]{:S(2)}) copy-start(f32[1024,1]{0,1:T(1,128)S(1)} %get-tuple-element.108) | copy-start | bytes 12292
  44.8 26.5 %copy-start.18 = (f32[1024,1]{0,1:T(1,128)}, f32[1024,1]{0,1:T(1,128)S(1)}, u32[]{:S(2)}) copy-start(f32[1024,1]{0,1:T(1,128)S(1)} %get-tuple-element.109) | copy-start | bytes 12292
  44.8 26.5 %copy-start.20 = (f32[1024,1]{0,1:T(1,128)}, f32[1024,1]{0,1:T(1,128)S(1)}, u32[]{:S(2)}) copy-start(f32[1024,1]{0,1:T(1,128)S(1)} %get-tuple-element.110) | copy-start | bytes 12292
  44.8 26.5 %copy-start.22 = (f32[1024,1]{0,1:T(1,128)}, f32[1024,1]{0,1:T(1,128)S(1)}, u32[]{:S(2)}) copy-start(f32[1024,1]{0,1:T(1,128)S(1)} %get-tuple-element.111) | copy-start | bytes 12292
  44.9 26.5 %copy-start.24 = (f32[1024,1]{0,1:T(1,128)}, f32[1024,1]{0,1:T(1,128)S(1)}, u32[]{:S(2)}) copy-start(f32[1024,1]{0,1:T(1,128)S(1)} %get-tuple-element.112) | copy-start | bytes 12292
  44.9 26.5 %copy-start.26 = (f32[1024,1]{0,1:T(1,128)}, f32[1024,1]{0,1:T(1,128)S(1)}, u32[]{:S(2)}) copy-start(f32[1024,1]{0,1:T(1,128)S(1)} %get-tuple-element.113) | copy-start | bytes 12292
  44.9 26.5 %copy-start.28 = (f32[1024,1]{0,1:T(1,128)}, f32[1024,1]{0,1:T(1,128)S(1)}, u32[]{:S(2)}) copy-start(f32[1024,1]{0,1:T(1,128)S(1)} %get-tuple-element.114) | copy-start | bytes 12292
  44.9 26.5 %copy-start.30 = (f32[1024,1]{0,1:T(1,128)}, f32[1024,1]{0,1:T(1,128)S(1)}, u32[]{:S(2)}) copy-start(f32[1024,1]{0,1:T(1,128)S(1)} %get-tuple-element.115) | copy-start | bytes 12292
  45.0 26.4 %copy-start.32 = (f32[1024,1]{0,1:T(1,128)}, f32[1024,1]{0,1:T(1,128)S(1)}, u32[]{:S(2)}) copy-start(f32[1024,1]{0,1:T(1,128)S(1)} %get-tuple-element.85) | copy-start | bytes 12292
  45.0 26.4 %copy-start.34 = (f32[1024,1]{0,1:T(1,128)}, f32[1024,1]{0,1:T(1,128)S(1)}, u32[]{:S(2)}) copy-start(f32[1024,1]{0,1:T(1,128)S(1)} %get-tuple-element.86) | copy-start | bytes 12292
  45.0 26.4 %copy-start.36 = (f32[1024,1]{0,1:T(1,128)}, f32[1024,1]{0,1:T(1,128)S(1)}, u32[]{:S(2)}) copy-start(f32[1024,1]{0,1:T(1,128)S(1)} %get-tuple-element.87) | copy-start | bytes 12292
  45.0 26.4 %copy-start.38 = (f32[1024,1]{0,1:T(1,128)}, f32[1024,1]{0,1:T(1,128)S(1)}, u32[]{:S(2)}) copy-start(f32[1024,1]{0,1:T(1,128)S(1)} %get-tuple-element.88) | copy-start | bytes 12292
  45.0 26.4 %copy-start.40 = (f32[1024,1]{0,1:T(1,128)}, f32[1024,1]{0,1:T(1,128)S(1)}, u32[]{:S(2)}) copy-start(f32[1024,1]{0,1:T(1,128)S(1)} %get-tuple-element.89) | copy-start | bytes 12292
  46.8 33.6 %all-to-all-start.1 = ((bf16[8,128,1024]{2,1,0:T(8,128)(2,1)}), bf16[8,128,1024]{2,1,0:T(8,128)(2,1)}, u32[]{:S(2)}, u32[]{:S(2)}) async-start(bf16[8,128,1024]{2,1,0:T(8,128)(2,1)} %broadcast_in_dim.651), calls=%async_computation.1 | async-start | bytes 4194304 | tf_op jit(solution)/shard_map/all_to_all | solution.py:39
  51.2 216.3 %reduce-scatter.2.cloned.1.call-start = ((), (), s32[]{:S(2)}) async-start(), calls=%async_computation.4 | async-start | bytes 14745600 | tf_op jit(solution)/shard_map/reduce_scatter | solution.py:51
  61.7 5.6 %collective-permute-start = (bf16[2,15,1024]{2,1,0:T(8,128)(2,1)S(1)}, bf16[2,15,1024]{2,1,0:T(8,128)(2,1)S(1)}, u32[]{:S(2)}, u32[]{:S(2)}) collective-permute-start(bf16[2,15,1024]{2,1,0:T(8,128)(2,1)S(1)} %get-tuple-element.83), channel_id=1, source_target_pairs={{0,1},{1,2},{2,3},{3,4},{4,5},{5,6},{6,7},{7,8},{8,9},{9,10},{10,1... | collective-permute-start | bytes 184328 | tf_op jit(solution)/shard_map/ppermute | solution.py:23
  65.1 6.2 %collective-permute-start.1 = (bf16[2,15,1024]{2,1,0:T(8,128)(2,1)S(1)}, bf16[2,15,1024]{2,1,0:T(8,128)(2,1)S(1)}, u32[]{:S(2)}, u32[]{:S(2)}) collective-permute-start(bf16[2,15,1024]{2,1,0:T(8,128)(2,1)S(1)} %get-tuple-element.84), channel_id=1, source_target_pairs={{1,0},{2,1},{3,2},{4,3},{5,4},{6,5},{7,6},{8,7},{9,8},{10,9},{11,1... | collective-permute-start | bytes 184328 | tf_op jit(solution)/shard_map/ppermute | solution.py:26
  88.4 56.9 %collective-permute-start.2 = (f32[2,15,1024]{2,1,0:T(8,128)S(1)}, f32[2,15,1024]{2,1,0:T(8,128)}, u32[]{:S(2)}, u32[]{:S(2)}) collective-permute-start(f32[2,15,1024]{2,1,0:T(8,128)S(1)} %get-tuple-element.81), channel_id=1, source_target_pairs={{1,0},{2,1},{3,2},{4,3},{5,4},{6,5},{7,6},{8,7},{9,8},{10,9},{11,1... | collective-permute-start | bytes 368648 | tf_op jit(solution)/shard_map/ppermute | solution.py:26
  89.7 55.6 %collective-permute-start.3 = (f32[2,15,1024]{2,1,0:T(8,128)S(1)}, f32[2,15,1024]{2,1,0:T(8,128)}, u32[]{:S(2)}, u32[]{:S(2)}) collective-permute-start(f32[2,15,1024]{2,1,0:T(8,128)S(1)} %get-tuple-element.82), channel_id=1, source_target_pairs={{0,1},{1,2},{2,3},{3,4},{4,5},{5,6},{6,7},{7,8},{8,9},{9,10},{10,1... | collective-permute-start | bytes 368648 | tf_op jit(solution)/shard_map/ppermute | solution.py:23
  188.8 171.5 %all-reduce.5.cloned.1.call-start = ((), (), s32[]{:S(2)}) async-start(), calls=%async_computation.5 | async-start | bytes 3145728 | tf_op jit(solution)/shard_map/psum | solution.py:182
  274.8 88.6 %copy-start.1 = (bf16[256,1024]{1,0:T(8,128)(2,1)S(1)}, bf16[256,1024]{1,0:T(8,128)(2,1)}, u32[]{:S(2)}) copy-start(bf16[256,1024]{1,0:T(8,128)(2,1)} %param.8) | copy-start | bytes 1572868
  (101 other events, 860.5 us)
Sparse Core Ops, SparseCore 0:
  9.7 46.6 all-gather.1
  188.9 78.4 reduce-scatter.1
  271.8 88.4 all-reduce.4
where the time goes:
time: 372 us; the launch traced here: 370 us
  waiting for transfers between devices  93.6 us (25%)
  blocking collectives  92.4 us (25%)
  local copies, waits for them, and re-layouts  73.9 us (20%)
  other arithmetic  48.5 us (13%)
  starting transfers between devices  27 us (7%)
  matrix products  19.1 us (5%)
  between operations  15.5 us (4%)
    reduce_scatter x1, waiting for transfers between devices, in_one_piece(): filled = lax.psum_scatter(both, axis, scatter_dimension=dim, tiled=True)  78.6 us
    psum x1, blocking collectives, per_device(): totals = lax.psum((shares[0], shares[1], shares[2], shares[3]), 'seq')  75.3 us
    another operation x31, local copies, waits for them, and re-layouts, per_device(): grad_taps = jnp.stack(tap_grads, axis=1)  35.5 us
    concatenate x1, local copies, waits for them, and re-layouts, in_one_piece(): both = jnp.concatenate(arrays, axis=along)  21.8 us
    all_gather x1, blocking collectives, sent_together(): lax.all_gather(both, axis, axis=dim, tiled=True)  17 us
    reduce_sum x6, other arithmetic, per_device(): jnp.sum(jnp.where(same, grad_cells * gated_pad[:, tap_index:tap_index + f...  14.7 us
    add x1, other arithmetic, per_device(): grad_gated + jnp.where(back_same, grad_pad[:, mirror:mirror + frames_dev]...  12.7 us
    all_to_all x1, starting transfers between devices, per_device(): lax.all_to_all(outgoing, ('dp', 'seq'), split_axis=0, concat_axis=0, tile...  11.2 us
  transfers between devices with their start and end apart: 9, of which 4 were waited for; matrix products, arithmetic and copies ran while one was open for 22% of the time, Pallas kernels for 0%

commit v1 on v0

v1 whole, which is shorter than its diff:
```python
import math

import jax
import jax.numpy as jnp
from jax import lax
from jax.experimental import pallas as pl
from jax.experimental.pallas import tpu as pltpu
from jax.sharding import Mesh, PartitionSpec as P

DP = ("z", "core")
SEQ = ("x", "y")
ZXY = ("z", "x", "y")
EDGE = 16
LANES = 128
ROWS_STEP = 32
EPS = 1e-05


def forward_kernel(
    gated_ref, low_ref, high_ref, ids_ref, taps_ref, gain_ref, grad_act_ref,
    act_ref, grad_mix_ref, grad_gain_ref, pad_ref, mix_ref,
):
    slabs, frames, width = gated_ref.shape
    blocks = width // LANES
    taps_count = taps_ref.shape[1] - 1
    shift = EDGE - taps_count // 2

    def one_slab(s, total):
        for b in range(blocks):
            cols = slice(b * LANES, (b + 1) * LANES)
            pad_ref[b, 0:EDGE] = low_ref[s, :, cols].astype(jnp.float32)
            pad_ref[b, EDGE : EDGE + frames] = gated_ref[s, :, cols].astype(jnp.float32)
            pad_ref[b, EDGE + frames :] = high_ref[s, :, cols].astype(jnp.float32)

        def conv_step(i, carry):
            row = pl.multiple_of((i // (blocks // 2)) * ROWS_STEP, ROWS_STEP)
            b = (i % (blocks // 2)) * 2
            center = ids_ref[s, pl.ds(row + EDGE, ROWS_STEP)]
            sums = [jnp.zeros((ROWS_STEP, LANES), jnp.float32) for _ in range(2)]
            for k in range(taps_count):
                same = ids_ref[s, pl.ds(row + k + shift, ROWS_STEP)] == center
                for j in range(2):
                    term = pad_ref[b + j, pl.ds(row + k + shift, ROWS_STEP)]
                    sums[j] = sums[j] + jnp.where(same, term, 0.0) * taps_ref[b + j, k : k + 1, :]
            for j in range(2):
                mix_ref[b + j, pl.ds(row, ROWS_STEP)] = sums[j]
            return carry

        lax.fori_loop(0, (frames // ROWS_STEP) * (blocks // 2), conv_step, 0)

        def row_step(i, total):
            row = pl.multiple_of(i * 16, 16)
            out_row = pl.multiple_of(s * frames + i * 16, 16)
            mixing = jnp.concatenate([mix_ref[b, pl.ds(row, 16)] for b in range(blocks)], axis=1)
            grad_act = grad_act_ref[pl.ds(out_row, 16), :]
            gain = gain_ref[0:1, :]
            centered = mixing - jnp.mean(mixing, axis=-1, keepdims=True)
            scale = lax.rsqrt(jnp.mean(centered * centered, axis=-1, keepdims=True) + EPS)
            normed = centered * scale
            value = normed * gain
            sig = jax.nn.sigmoid(value)
            act_ref[pl.ds(out_row, 16), :] = (value * sig).astype(act_ref.dtype)
            grad_value = grad_act * (sig * (1.0 + value * (1.0 - sig)))
            part = grad_value * normed
            total = total + part[0:8] + part[8:16]
            grad_normed = grad_value * gain
            first = jnp.mean(grad_normed, axis=-1, keepdims=True)
            second = jnp.mean(grad_normed * normed, axis=-1, keepdims=True)
            grad_mix_ref[s, pl.ds(row, 16), :] = (
                scale * (grad_normed - first - normed * second)
            ).astype(grad_mix_ref.dtype)
            return total

        return lax.fori_loop(0, frames // 16, row_step, total)

    grad_gain_ref[...] = lax.fori_loop(
        0, slabs, one_slab, jnp.zeros(grad_gain_ref.shape, jnp.float32)
    )


def backward_kernel(
    grad_mix_ref, low_ref, high_ref, gated_ref, ids_ref, taps_ref, hidden_ref,
    grad_hidden_ref, grad_taps_ref, pad_ref, sum_ref,
):
    slabs, frames, width = gated_ref.shape
    blocks = width // LANES
    taps_count = taps_ref.shape[1] - 1
    half = taps_count // 2
    sum_ref[...] = jnp.zeros(sum_ref.shape, jnp.float32)

    def one_slab(s, carry):
        for b in range(blocks):
            cols = slice(b * LANES, (b + 1) * LANES)
            pad_ref[b, 0:EDGE] = low_ref[s, :, cols].astype(jnp.float32)
            pad_ref[b, EDGE : EDGE + frames] = grad_mix_ref[s, :, cols].astype(jnp.float32)
            pad_ref[b, EDGE + frames :] = high_ref[s, :, cols].astype(jnp.float32)

        def conv_step(i, carry):
            row = pl.multiple_of((i // (blocks // 2)) * ROWS_STEP, ROWS_STEP)
            out_row = pl.multiple_of(s * frames + row, ROWS_STEP)
            b = (i % (blocks // 2)) * 2
            center = ids_ref[s, pl.ds(row + EDGE, ROWS_STEP)]
            sums = [jnp.zeros((ROWS_STEP, LANES), jnp.float32) for _ in range(2)]
            cols = [pl.ds(pl.multiple_of((b + j) * LANES, LANES), LANES) for j in range(2)]
            here = [gated_ref[s, pl.ds(row, ROWS_STEP), cols[j]].astype(jnp.float32) for j in range(2)]
            for k in range(taps_count):
                at = row + EDGE + half - k
                same = ids_ref[s, pl.ds(at, ROWS_STEP)] == center
                for j in range(2):
                    term = jnp.where(same, pad_ref[b + j, pl.ds(at, ROWS_STEP)], 0.0)
                    sums[j] = sums[j] + term * taps_ref[b + j, k : k + 1, :]
                    part = term * here[j]
                    sum_ref[b + j, k] = sum_ref[b + j, k] + (
                        (part[0:8] + part[8:16]) + (part[16:24] + part[24:32])
                    )
            for j in range(2):
                lin = hidden_ref[pl.ds(out_row, ROWS_STEP), cols[j]]
                sig = jax.nn.sigmoid(
                    hidden_ref[
                        pl.ds(out_row, ROWS_STEP),
                        pl.ds(pl.multiple_of(width + (b + j) * LANES, LANES), LANES),
                    ]
                )
                grad_lin = sums[j] * sig
                grad_hidden_ref[pl.ds(out_row, ROWS_STEP), cols[j]] = grad_lin.astype(jnp.bfloat16)
                grad_hidden_ref[
                    pl.ds(out_row, ROWS_STEP),
                    pl.ds(pl.multiple_of(width + (b + j) * LANES, LANES), LANES),
                ] = (grad_lin * lin * (1.0 - sig)).astype(jnp.bfloat16)
            return carry

        return lax.fori_loop(0, (frames // ROWS_STEP) * (blocks // 2), conv_step, carry)

    lax.fori_loop(0, slabs, one_slab, 0)
    for b in range(blocks):
        for k in range(taps_count):
            grad_taps_ref[k : k + 1, b * LANES : (b + 1) * LANES] = jnp.sum(
                sum_ref[b, k], axis=0, keepdims=True
            )
        grad_taps_ref[taps_count:, b * LANES : (b + 1) * LANES] = jnp.zeros(
            (grad_taps_ref.shape[0] - taps_count, LANES), jnp.float32
        )


def kernel_call(body, name, outs, scratch, flops, *args):
    moved = sum(a.size * a.dtype.itemsize for a in args)
    return pl.pallas_call(
        body,
        out_shape=outs,
        scratch_shapes=scratch,
        name=name,
        compiler_params=pltpu.CompilerParams(vmem_limit_bytes=48 * 1024 * 1024),
        cost_estimate=pl.CostEstimate(flops=flops, bytes_accessed=moved, transcendentals=0),
    )(*args)


def spread(shard, axes, count):
    return lax.all_to_all(
        jnp.broadcast_to(shard[None], (count, *shard.shape)), axes, 0, 0, tiled=True
    )


def edges(block, count):
    forward = [(i, i + 1) for i in range(count - 1)]
    backward = [(i + 1, i) for i in range(count - 1)]
    low = lax.ppermute(block[:, -EDGE:].astype(jnp.bfloat16), SEQ, forward)
    high = lax.ppermute(block[:, :EDGE].astype(jnp.bfloat16), SEQ, backward)
    return low, high


def norm_rows(values, gain):
    average = jnp.mean(values, axis=-1, keepdims=True)
    centered = values - average
    spread_ = jnp.mean(centered * centered, axis=-1, keepdims=True)
    return centered * lax.rsqrt(spread_ + EPS) * gain


def per_device(
    loaded, plan, segment_ids, in_weight, out_weight, depth_kernel, norm_gains, upstream
):
    rows_dev, width = loaded.shape
    devices = plan.shape[0]
    capacity = 2 * rows_dev // devices
    slabs, slab_len = segment_ids.shape
    n_seq = lax.axis_size(SEQ)
    n_z = lax.axis_size("z")
    frames_dev = slab_len // n_seq
    kernel_len = depth_kernel.shape[1]
    core = lax.axis_index("core")
    sender = lax.axis_index((*DP, *SEQ))
    swap = [(0, 1), (1, 0)]

    extras = jnp.pad(
        jnp.concatenate([depth_kernel, norm_gains], axis=1), ((0, 0), (0, LANES - kernel_len - 2))
    )
    in_full = lax.all_gather(in_weight, DP, axis=0, tiled=True)
    out_full = lax.all_gather(
        jnp.concatenate([out_weight, extras], axis=1), DP, axis=0, tiled=True
    )
    upstream_rows = upstream.reshape(rows_dev, width)
    upstream_other = lax.ppermute(upstream_rows, "core", swap)

    send_plan = lax.dynamic_index_in_dim(plan, sender, 0, keepdims=False)
    send_start = jnp.cumsum(send_plan) - send_plan
    slot_index = jnp.arange(capacity, dtype=jnp.int32)
    source_rows = send_start[:, None] + slot_index[None, :]
    outgoing = jnp.take(
        loaded, jnp.clip(source_rows, 0, rows_dev - 1).reshape(-1), axis=0
    ).reshape(devices, capacity, width)
    arrived = lax.all_to_all(
        outgoing, (*DP, *SEQ), split_axis=0, concat_axis=0, tiled=True
    ).reshape(devices * capacity, width)
    recv_plan = lax.dynamic_index_in_dim(plan, sender, 1, keepdims=False)
    recv_end = jnp.cumsum(recv_plan)
    frame_index = jnp.arange(rows_dev, dtype=jnp.int32)
    before = recv_end[None, :] <= frame_index[:, None]
    source_dev = jnp.sum(before.astype(jnp.int32), axis=1)
    start_of = jnp.sum(jnp.where(before, recv_plan[None, :], 0), axis=1)
    frames = jnp.take(arrived, source_dev * capacity + frame_index - start_of, axis=0)

    id_pad = jnp.pad(segment_ids, ((0, 0), (EDGE, EDGE)), constant_values=-1)
    window = lax.dynamic_slice_in_dim(
        id_pad, lax.axis_index(SEQ) * frames_dev, frames_dev + 2 * EDGE, 1
    )
    ids = jnp.broadcast_to(window[:, :, None], (*window.shape, LANES))

    side = out_full[:, width : width + kernel_len + 2].astype(jnp.float32).T
    gain_pre, gain_mid = side[kernel_len], side[kernel_len + 1]
    taps = jnp.pad(side[:kernel_len], ((0, 1), (0, 0)))
    taps = taps.reshape(kernel_len + 1, width // LANES, LANES).transpose(1, 0, 2)
    out_full = out_full[:, :width]

    frame_rows = frames.astype(jnp.float32)
    normed_full, pull_pre = jax.vjp(norm_rows, frame_rows, gain_pre)
    normed = normed_full.astype(jnp.bfloat16)
    hidden = jnp.dot(normed, in_full, preferred_element_type=jnp.float32)
    gated = (
        (hidden[:, :width] * jax.nn.sigmoid(hidden[:, width:]))
        .astype(jnp.bfloat16)
        .reshape(slabs, frames_dev, width)
    )
    low, high = edges(gated, n_seq)
    grad_act = jnp.dot(upstream_rows, out_full.T, preferred_element_type=jnp.float32)
    elements = rows_dev * width
    blocked = pltpu.VMEM((width // LANES, frames_dev + 2 * EDGE, LANES), jnp.float32)
    activated, grad_mixing, grad_gain_mid = kernel_call(
        forward_kernel,
        "mixing_forward",
        (
            jax.ShapeDtypeStruct((rows_dev, width), jnp.bfloat16),
            jax.ShapeDtypeStruct((slabs, frames_dev, width), jnp.float32),
            jax.ShapeDtypeStruct((8, width), jnp.float32),
        ),
        [blocked, pltpu.VMEM((width // LANES, frames_dev, LANES), jnp.float32)],
        elements * 3 * kernel_len,
        gated, low, high, ids, taps, gain_mid[None], grad_act,
    )
    grad_low, grad_high = edges(grad_mixing, n_seq)

    def for_core(rows, which):
        parts = rows.reshape(rows.shape[0], n_z, 2, LANES)
        return lax.dynamic_index_in_dim(parts, which, 2, keepdims=False).reshape(
            rows.shape[0], n_z * LANES
        )

    normed_other = lax.ppermute(for_core(normed, 1 - core), "core", swap)
    act_other = lax.ppermute(for_core(activated, 1 - core), "core", swap)
    projected = jnp.dot(activated, out_full, preferred_element_type=jnp.float32)
    encoded = (frame_rows + projected).astype(jnp.bfloat16).reshape(slabs, frames_dev, width)

    def weight_part(mine, other, right, right_other):
        left = jnp.concatenate([mine, other], axis=0)
        both = jnp.concatenate([right, right_other], axis=0)
        return lax.dot_general(
            left, both, (((0,), (0,)), ((), ())), preferred_element_type=jnp.float32
        ).astype(jnp.bfloat16)

    def summed(part):
        arrived_parts = lax.all_to_all(
            part.reshape(n_z * n_seq, LANES // n_seq, part.shape[1]), ZXY, 0, 0, tiled=True
        )
        return jnp.sum(arrived_parts.astype(jnp.float32), axis=0)

    scale = 1.0 / math.sqrt(devices * rows_dev)
    out_part = weight_part(for_core(activated, core), act_other, upstream_rows, upstream_other)
    out_sum = summed(out_part)

    grad_hidden, grad_taps = kernel_call(
        backward_kernel,
        "mixing_backward",
        (
            jax.ShapeDtypeStruct((rows_dev, 2 * width), jnp.bfloat16),
            jax.ShapeDtypeStruct((kernel_len + 1, width), jnp.float32),
        ),
        [blocked, pltpu.VMEM((width // LANES, kernel_len, 8, LANES), jnp.float32)],
        elements * 5 * kernel_len,
        grad_mixing, grad_low, grad_high, gated, ids, taps, hidden,
    )
    hidden_other = lax.ppermute(grad_hidden, "core", swap)
    grad_normed = lax.dot_general(
        grad_hidden, in_full, (((1,), (1,)), ((), ())), preferred_element_type=jnp.float32
    )
    grad_rows, grad_gain_pre = pull_pre(grad_normed)
    grad_frames = (
        (upstream_rows.astype(jnp.float32) + grad_rows)
        .astype(jnp.bfloat16)
        .reshape(slabs, frames_dev, width)
    )
    small = jnp.concatenate(
        [grad_taps[:kernel_len], grad_gain_pre[None], jnp.sum(grad_gain_mid, axis=0)[None]], axis=0
    )
    small_other = lax.ppermute(for_core(small, 1 - core), "core", swap)
    small_part = (for_core(small, core) + small_other).T.astype(jnp.bfloat16)
    small_part = jnp.pad(small_part, ((0, 0), (0, LANES - small_part.shape[1])))
    in_part = weight_part(for_core(normed, core), normed_other, grad_hidden, hidden_other)
    in_sum = summed(jnp.concatenate([in_part, small_part], axis=1))
    total = (jnp.concatenate([in_sum, out_sum], axis=1) * scale).astype(jnp.bfloat16)
    final = spread(total, SEQ, n_seq).reshape(LANES, total.shape[1]).astype(jnp.float32)
    return (
        encoded,
        grad_frames,
        final[:, : 2 * width],
        final[:, 2 * width + LANES :],
        final[:, 2 * width : 2 * width + kernel_len],
        final[:, 2 * width + kernel_len : 2 * width + kernel_len + 2],
    )


def solution(mesh):
    n_dp, n_seq = mesh.devices.shape
    side = math.isqrt(n_seq)
    split = Mesh(mesh.devices.reshape(n_dp // 2, 2, side, side), ("z", "core", "x", "y"))
    placed = (
        P((*DP, *SEQ), None),
        P(),
        P(DP, None),
        P(DP, None),
        P(DP, None),
        P(DP, None),
        P(DP, None),
        P(DP, SEQ, None),
    )
    return jax.shard_map(
        per_device,
        mesh=split,
        in_specs=placed,
        out_specs=(
            P(DP, SEQ, None),
            P(DP, SEQ, None),
            P(DP, None),
            P(DP, None),
            P(DP, None),
            P(DP, None),
        ),
        check_vma=False,
    )
```

time: 372 us -> 244 us (0.66)
  blocking collectives: 92.4 us -> 0 us
  local copies, waits for them, and re-layouts: 73.9 us -> 26.6 us
  other arithmetic: 48.5 us -> 15.9 us
  Pallas kernels: 0 us -> 20.5 us
  starting transfers between devices: 27 us -> 43.1 us
  waiting for transfers between devices: 93.6 us -> 102 us
    reduce_scatter x1 -> x0, waiting for transfers between devices: 78.6 us -> none  [in_one_piece(): filled = lax.psum_scatter(both, axis, scatter_dimension=dim, tiled=True)]
    psum x1 -> x0, blocking collectives: 75.3 us -> none  [per_device(): totals = lax.psum((shares[0], shares[1], shares[2], shares[3]), 'seq')]
    all_to_all x2 -> x4, waiting for transfers between devices: 0.01 us -> 63.9 us  [the longest x2 38.8 us: summed(): lax.all_to_all(part.reshape(n_z * n_seq, LANES // n_seq, part.shape[1]),...]
    another operation x35 -> x2, local copies, waits for them, and re-layouts: 38.4 us -> 0.81 us  [the longest x31 35.5 us: per_device(): grad_taps = jnp.stack(tap_grads, axis=1)]
    all_gather x1 -> x2, waiting for transfers between devices: 3.09 us -> 31.6 us  [the longest x1 30 us: per_device(): in_full = lax.all_gather(in_weight, DP, axis=0, tiled=True)]
    concatenate x1, local copies, waits for them, and re-layouts: 21.8 us -> 1.01 us  [per_device(): jnp.concatenate([grad_taps[:kernel_len], grad_gain_pre[None], jnp.sum(gra...]
    pallas_call x0 -> x2, Pallas kernels: none -> 20.5 us  [kernel_call(): pl.pallas_call(body, out_shape=outs, scratch_shapes=scratch, name=name, c...]
    all_gather x1 -> x0, blocking collectives: 17 us -> none  [sent_together(): lax.all_gather(both, axis, axis=dim, tiled=True)]
  transfers between devices with their start and end apart: 9 -> 15, of which waited for: 4 -> 9; matrix products, arithmetic and copies ran while one was open for 22% -> 21% of each run, Pallas kernels for 0% -> 8%
where the time goes in v1:
time: 244 us; the launch traced here: 243 us
  waiting for transfers between devices  102 us (42%)
  starting transfers between devices  43.1 us (18%)
  local copies, waits for them, and re-layouts  26.6 us (11%)
  Pallas kernels  20.5 us (8%)
  matrix products  19.9 us (8%)
  other arithmetic  15.9 us (7%)
  between operations  14.6 us (6%)
    all_to_all x2, waiting for transfers between devices, summed(): lax.all_to_all(part.reshape(n_z * n_seq, LANES // n_seq, part.shape[1]),...  38.8 us
    all_gather x1, waiting for transfers between devices, per_device(): in_full = lax.all_gather(in_weight, DP, axis=0, tiled=True)  30 us
    pallas_call x2, Pallas kernels, kernel_call(): pl.pallas_call(body, out_shape=outs, scratch_shapes=scratch, name=name, c...  20.5 us
    all_to_all x1, waiting for transfers between devices, per_device(): lax.all_to_all(outgoing, (*DP, *SEQ), split_axis=0, concat_axis=0, tiled=...  18.3 us
    all_to_all x2, starting transfers between devices, summed(): lax.all_to_all(part.reshape(n_z * n_seq, LANES // n_seq, part.shape[1]),...  17.4 us
    all_to_all x1, starting transfers between devices, per_device(): lax.all_to_all(outgoing, (*DP, *SEQ), split_axis=0, concat_axis=0, tiled=...  11.2 us
    unnamed x43, local copies, waits for them, and re-layouts  9.21 us
    all_to_all x1, waiting for transfers between devices, spread(): lax.all_to_all(jnp.broadcast_to(shard[None], (count, *shard.shape)), axes...  6.81 us
  transfers between devices with their start and end apart: 15, of which 9 were waited for; matrix products, arithmetic and copies ran while one was open for 21% of the time, Pallas kernels for 8%

profile of v1, /device:TPU:0, one launch (start us, length us, event | category | flops | bytes accessed | tf_op | source)
XLA Modules:
  0.0 242.6 jit_solution(13997890934513038181)
XLA Ops:
  12.0 2.1 gather_fusion
  14.6 1.6 broadcast_select_fusion
  16.2 11.2 %all-to-all-start = ((bf16[128,4,1024]{2,1,0:T(4,128)(2,1)}), bf16[128,4,1024]{2,1,0:T(4,128)(2,1)S(1)}, u32[]{:S(2)}, u32[]{:S(2)}) async-start(bf16[128,4,1024]{2,1,0:T(4,128)(2,1)} %broadcast_select_fusion), calls=%async_computation | async-start | bytes 2097152 | tf_op jit(solution)/shard_map/all_to_all | solution.py:210
  28.3 18.3 %all-to-all-done = bf16[128,4,1024]{2,1,0:T(4,128)(2,1)S(1)} async-done(((bf16[128,4,1024]{2,1,0:T(4,128)(2,1)}), bf16[128,4,1024]{2,1,0:T(4,128)(2,1)S(1)}, u32[]{:S(2)}, u32[]{:S(2)}) %all-to-all-start) | async-done | bytes 1048608 | tf_op jit(solution)/shard_map/all_to_all | solution.py:210
  49.5 1.6 all-gather.3.cloned.1.call-done
  53.0 3.4 %fusion.14.grad_act_ref = f32[256,1024]{1,0:T(8,128)} fusion(bf16[256,1024]{1,0:T(8,128)(2,1)} %bitcast.10, bf16[1024,1152]{0,1:T(8,128)(2,1)} %all-gather.3.cloned.1.call-done), kind=kOutput, calls=%fused_computation.25 | convolution fusion | flops 536870912 | bytes 3670016 | tf_op jit(solution)/shard_map/dot_general | solution.py:243
  56.5 30.0 %all-gather.5.cloned.1.call-done = bf16[1024,2048]{1,0:T(8,128)(2,1)} async-done(((bf16[128,2048]{1,0:T(8,128)(2,1)}), bf16[1024,2048]{1,0:T(8,128)(2,1)}) %all-gather.5.cloned.1.call-update) | async-done | bytes 4194320 | tf_op jit(solution)/shard_map/all_gather | solution.py:196
  86.5 3.6 %fusion.37.hidden_ref = f32[256,2048]{1,0:T(8,128)S(1)} fusion(bf16[1024,2048]{1,0:T(8,128)(2,1)} %all-gather.5.cloned.1.call-done, f32[1024]{0:T(1024)S(1)} %bitcast.62, f32[256]{0:T(256)S(1)} %fusion.54, f32[256]{0:T(256)S(1)} %broadcast_multiply_fusion, bf16[256,1024]{1,0:T(8,128)(2,1)S(1)} %gather_fusion.1, pred[256]{0:T(512)(128)(4,1)S(1)} %compare_and_fusion.1), kind=kOutput, calls=%fused_computation.47 | convolution fusion | flops 1075314688 | bytes 6822144 | tf_op jit(solution)/shard_map/dot_general | solution.py:236
  90.4 3.4 %collective-permute-start = (bf16[2,16,1024]{2,1,0:T(8,128)(2,1)S(1)}, bf16[2,16,1024]{2,1,0:T(8,128)(2,1)S(1)}, u32[]{:S(2)}, u32[]{:S(2)}) collective-permute-start(bf16[2,16,1024]{2,1,0:T(8,128)(2,1)S(1)} %get-tuple-element.47), channel_id=1, source_target_pairs={{0,1},{1,2},{2,3},{3,4},{4,5},{5,6},{6,7},{7,8},{8,9},{9,10},{10,1... | collective-permute-start | bytes 196616 | tf_op jit(solution)/shard_map/ppermute | solution.py:166
  93.8 1.3 collective-permute-start.1
  95.7 4.3 %collective-permute-done.1.high_ref = bf16[2,16,1024]{2,1,0:T(8,128)(2,1)S(1)} collective-permute-done((bf16[2,16,1024]{2,1,0:T(8,128)(2,1)S(1)}, bf16[2,16,1024]{2,1,0:T(8,128)(2,1)S(1)}, u32[]{:S(2)}, u32[]{:S(2)}) %collective-permute-start.1) | collective-permute-done | bytes 65568 | tf_op jit(solution)/shard_map/ppermute | solution.py:167
  100.1 9.8 %mixing_forward.1 = (bf16[256,1024]{1,0:T(8,128)(2,1)S(1)}, f32[2,128,1024]{2,1,0:T(8,128)S(1)}, f32[8,1024]{1,0:T(8,128)S(1)}) custom-call(bf16[2,128,1024]{2,1,0:T(8,128)(2,1)S(1)} %bitcast.52, bf16[2,16,1024]{2,1,0:T(8,128)(2,1)S(1)} %collective-permute-done.low_ref, bf16[2,16,1024]{2,1,0:T(8,128)(2,1)S(1)} %collective-permute-done.1.high_ref, ...), custom_call_target="tpu_custom_call" | custom-call | flops 24379392 | bytes 2002944 | tf_op jit(solution)/shard_map/mixing_forward/pallas_call | solution.py:147
  112.3 3.4 %collective-permute-start.2 = (bf16[2,16,1024]{2,1,0:T(8,128)(2,1)}, bf16[2,16,1024]{2,1,0:T(8,128)(2,1)S(1)}, u32[]{:S(2)}, u32[]{:S(2)}) collective-permute-start(bf16[2,16,1024]{2,1,0:T(8,128)(2,1)} %get-tuple-element.45), channel_id=1, source_target_pairs={{0,1},{1,2},{2,3},{3,4},{4,5},{5,6},{6,7},{7,8},{8,9},{9,10},{10,1... | collective-permute-start | bytes 196616 | tf_op jit(solution)/shard_map/ppermute | solution.py:166
  117.0 2.2 reshape.297
  119.2 3.3 %constant_dynamic-slice_fusion.1 = (bf16[256,4,1,128]{3,2,1,0:T(2,128)(2,1)}, bf16[256,4,1,128]{3,2,1,0:T(2,128)(2,1)}) fusion(bf16[256,4,2,128]{3,2,1,0:T(2,128)(2,1)} %reshape.297, s32[]{:T(128)S(6)} %select_n.80, s32[]{:T(128)S(6)} %select_n.81), kind=kLoop, calls=%fused_computation.85 | loop fusion | bytes 1048584 | tf_op jit(solution)/shard_map/jit(dynamic_index_in_dim)/dynamic_slice | solution.py:262
  122.5 1.9 copy.47
  124.3 1.9 copy.46
  127.5 10.7 %mixing_backward.1 = (bf16[256,2048]{1,0:T(8,128)(2,1)}, f32[32,1024]{1,0:T(8,128)S(1)}) custom-call(f32[2,128,1024]{2,1,0:T(8,128)S(1)} %copy-done.2, bf16[2,16,1024]{2,1,0:T(8,128)(2,1)S(1)} %collective-permute-done.2.low_ref, bf16[2,16,1024]{2,1,0:T(8,128)(2,1)} %collective-permute-done.3.high_ref, bf16[2,128,1024]{2,1,0:T(8,128)(2,1)S(1)} %bitcast.53, ...), custom_call_target="tpu_custom_call" | custom-call | flops 40632320 | bytes 4096000 | tf_op jit(solution)/shard_map/mixing_backward/pallas_call | solution.py:147
  139.0 3.9 %fusion.28 = (f32[256]{0:T(256)S(1)}, f32[256,1024]{1,0:T(8,128)S(1)}) fusion(f32[1024]{0:T(1024)S(1)} %bitcast.63, f32[256]{0:T(256)S(1)} %broadcast_multiply_fusion, bf16[256,1024]{1,0:T(8,128)(2,1)S(1)} %copy-done.8, pred[256]{0:T(512)(128)(4,1)S(1)} %compare_and_fusion.1, bf16[256,2048]{1,0:T(8,128)(2,1)} %get-tuple-element.13, ...), kind=kOutput, calls=%fused_computation.33 | convolution fusion | flops 1075314432 | bytes 6822144 | tf_op jit(solution)/shard_map/dot_general | solution.py:300
  144.7 3.0 %fusion.17 = bf16[64,8,1024]{2,1,0:T(8,128)(2,1)} fusion(bf16[256,1024]{1,0:T(8,128)(2,1)} %collective-permute-done.8, bf16[256,1024]{1,0:T(8,128)(2,1)} %bitcast.10, bf16[256,512]{0,1:T(8,128)(2,1)} %collective-permute-done.7, bf16[256,512]{0,1:T(8,128)(2,1)S(1)} %bitcast.58), kind=kOutput, calls=%fused_computation.26 | convolution fusion | flops 540540928 | bytes 2621440 | tf_op jit(solution)/shard_map/dot_general | solution.py:274
  147.6 11.8 %all-to-all-start.2 = ((bf16[64,8,1024]{2,1,0:T(8,128)(2,1)}), bf16[64,8,1024]{2,1,0:T(8,128)(2,1)}, u32[]{:S(2)}, u32[]{:S(2)}) async-start(bf16[64,8,1024]{2,1,0:T(8,128)(2,1)} %fusion.17), calls=%async_computation.2 | async-start | bytes 2097152 | tf_op jit(solution)/shard_map/all_to_all | solution.py:279
  163.3 2.8 %convolution_convert_fusion = bf16[512,2048]{1,0:T(8,128)(2,1)S(1)} fusion(bf16[256,2048]{1,0:T(8,128)(2,1)} %collective-permute-done.5, bf16[256,2048]{1,0:T(8,128)(2,1)} %get-tuple-element.13, bf16[256,512]{0,1:T(8,128)(2,1)S(1)} %collective-permute-done.4, bf16[256,512]{0,1:T(8,128)(2,1)S(1)} %bitcast.59), kind=kOutput, calls=%fused_computation.5 | convolution fusion | flops 1080033280 | bytes 4718592 | tf_op jit(solution)/shard_map/dot_general | solution.py:274
  166.2 1.6 fusion.2
  167.7 10.5 %all-to-all-done.2 = bf16[64,8,1024]{2,1,0:T(8,128)(2,1)} async-done(((bf16[64,8,1024]{2,1,0:T(8,128)(2,1)}), bf16[64,8,1024]{2,1,0:T(8,128)(2,1)}, u32[]{:S(2)}, u32[]{:S(2)}) %all-to-all-start.2) | async-done | bytes 1048608 | tf_op jit(solution)/shard_map/all_to_all | solution.py:279
  178.2 5.5 %all-to-all-start.1 = ((bf16[64,8,2176]{2,1,0:T(8,128)(2,1)}), bf16[64,8,2176]{2,1,0:T(8,128)(2,1)}, u32[]{:S(2)}, u32[]{:S(2)}) async-start(bf16[64,8,2176]{2,1,0:T(8,128)(2,1)} %fusion.2), calls=%async_computation.1 | async-start | bytes 4456448 | tf_op jit(solution)/shard_map/all_to_all | solution.py:279
  183.8 1.4 convert_reduce_fusion.1
  185.2 28.3 %all-to-all-done.1 = bf16[64,8,2176]{2,1,0:T(8,128)(2,1)} async-done(((bf16[64,8,2176]{2,1,0:T(8,128)(2,1)}), bf16[64,8,2176]{2,1,0:T(8,128)(2,1)}, u32[]{:S(2)}, u32[]{:S(2)}) %all-to-all-start.1) | async-done | bytes 2228256 | tf_op jit(solution)/shard_map/all_to_all | solution.py:279
  213.5 2.0 convert_reduce_fusion
  216.5 3.6 %all-to-all-start.3 = ((bf16[16,8,3200]{2,1,0:T(8,128)(2,1)}), bf16[16,8,3200]{2,1,0:T(8,128)(2,1)S(1)}, u32[]{:S(2)}, u32[]{:S(2)}) async-start(bf16[16,8,3200]{2,1,0:T(8,128)(2,1)} %broadcast_in_dim.77), calls=%async_computation.3 | async-start | bytes 1638400 | tf_op jit(solution)/shard_map/all_to_all | solution.py:158
  220.1 3.1 %fusion.20 = bf16[256,1024]{1,0:T(8,128)(2,1)} fusion(bf16[256,1024]{1,0:T(8,128)(2,1)S(1)} %copy-done.5, bf16[1024,1152]{0,1:T(8,128)(2,1)} %all-gather.3.cloned.1.call-done, bf16[256,1024]{1,0:T(8,128)(2,1)S(1)} %copy-done.9, pred[256]{0:T(512)(128)(4,1)S(1)} %compare_and_fusion.1), kind=kOutput, calls=%fused_computation.27 | convolution fusion | flops 537919488 | bytes 3670272 | tf_op jit(solution)/shard_map/dot_general | solution.py:268
  223.2 2.3 add_convert_fusion
  225.5 6.8 %all-to-all-done.3 = bf16[16,8,3200]{2,1,0:T(8,128)(2,1)S(1)} async-done(((bf16[16,8,3200]{2,1,0:T(8,128)(2,1)}), bf16[16,8,3200]{2,1,0:T(8,128)(2,1)S(1)}, u32[]{:S(2)}, u32[]{:S(2)}) %all-to-all-start.3) | async-done | bytes 819232 | tf_op jit(solution)/shard_map/all_to_all | solution.py:158
  (117 shorter events, 27.5 us)
Async XLA Ops:
  7.2 4.8 %copy-start = (bf16[256,1024]{1,0:T(8,128)(2,1)S(1)}, bf16[256,1024]{1,0:T(8,128)(2,1)}, u32[]{:S(2)}) copy-start(bf16[256,1024]{1,0:T(8,128)(2,1)} %param.8) | copy-start | bytes 1572868
  7.2 4.6 %copy-start.12 = (s32[128,128]{1,0:T(8,128)S(1)}, s32[128,128]{1,0:T(8,128)}, u32[]{:S(2)}) copy-start(s32[128,128]{1,0:T(8,128)} %param.9) | copy-start | bytes 196612
  7.2 43.9 %all-gather.3.cloned.1.call-start = ((), (), s32[]{:S(2)}) async-start(), calls=%async_computation.4 | async-start | bytes 2654208 | tf_op jit(solution)/shard_map/all_gather | solution.py:197
  9.9 76.6 %all-gather.5.cloned.1.call-start = ((), (), s32[]{:S(2)}) async-start(), calls=%async_computation.5 | async-start | bytes 4718592 | tf_op jit(solution)/shard_map/all_gather | solution.py:196
  14.6 13.3 %copy-start.13 = (s32[2,2048]{1,0:T(2,128)S(1)}, s32[2,2048]{1,0:T(2,128)}, u32[]{:S(2)}) copy-start(s32[2,2048]{1,0:T(2,128)} %param.10) | copy-start | bytes 49156
  16.2 30.3 %all-to-all-start = ((bf16[128,4,1024]{2,1,0:T(4,128)(2,1)}), bf16[128,4,1024]{2,1,0:T(4,128)(2,1)S(1)}, u32[]{:S(2)}, u32[]{:S(2)}) async-start(bf16[128,4,1024]{2,1,0:T(4,128)(2,1)} %broadcast_select_fusion), calls=%async_computation | async-start | bytes 2097152 | tf_op jit(solution)/shard_map/all_to_all | solution.py:210
  27.4 117.2 %collective-permute-start.8 = (bf16[256,1024]{1,0:T(8,128)(2,1)}, bf16[256,1024]{1,0:T(8,128)(2,1)}, u32[]{:S(2)}, u32[]{:S(2)}) collective-permute-start(bf16[256,1024]{1,0:T(8,128)(2,1)} %bitcast.10), channel_id=1, source_target_pairs={{0,16},{16,0},{1,17},{17,1},{2,18},{18,2},{3,19},{19,3},{4,20},{20... | collective-permute-start | bytes 1572872 | tf_op jit(solution)/shard_map/ppermute | solution.py:201
  48.0 38.5 %copy-start.7 = (bf16[256,1024]{1,0:T(8,128)(2,1)}, bf16[256,1024]{1,0:T(8,128)(2,1)S(1)}, u32[]{:S(2)}) copy-start(bf16[256,1024]{1,0:T(8,128)(2,1)S(1)} %gather_fusion.1) | copy-start | bytes 1572868
  49.5 7.0 %copy-start.16 = (f32[256]{0:T(256)}, f32[256]{0:T(256)S(1)}, u32[]{:S(2)}) copy-start(f32[256]{0:T(256)S(1)} %fusion.27) | copy-start | bytes 3076
  49.5 37.0 %copy-start.14 = (f32[256]{0:T(256)}, f32[256]{0:T(256)S(1)}, u32[]{:S(2)}) copy-start(f32[256]{0:T(256)S(1)} %fusion.54) | copy-start | bytes 3076
  90.1 5.0 %copy-start.18 = (pred[32]{0:T(512)(128)(4,1)S(1)}, pred[32]{0:T(512)(128)(4,1)}, u32[]{:S(2)}) copy-start(pred[32]{0:T(512)(128)(4,1)} %constant.110.clone.1) | copy-start | bytes 100
  90.1 10.0 %copy-start.3 = (f32[256,1024]{1,0:T(8,128)S(1)}, f32[256,1024]{1,0:T(8,128)}, u32[]{:S(2)}) copy-start(f32[256,1024]{1,0:T(8,128)} %fusion.14.grad_act_ref) | copy-start | bytes 3145732
  90.4 5.3 %collective-permute-start = (bf16[2,16,1024]{2,1,0:T(8,128)(2,1)S(1)}, bf16[2,16,1024]{2,1,0:T(8,128)(2,1)S(1)}, u32[]{:S(2)}, u32[]{:S(2)}) collective-permute-start(bf16[2,16,1024]{2,1,0:T(8,128)(2,1)S(1)} %get-tuple-element.47), channel_id=1, source_target_pairs={{0,1},{1,2},{2,3},{3,4},{4,5},{5,6},{6,7},{7,8},{8,9},{9,10},{10,1... | collective-permute-start | bytes 196616 | tf_op jit(solution)/shard_map/ppermute | solution.py:166
  93.8 6.2 %collective-permute-start.1 = (bf16[2,16,1024]{2,1,0:T(8,128)(2,1)S(1)}, bf16[2,16,1024]{2,1,0:T(8,128)(2,1)S(1)}, u32[]{:S(2)}, u32[]{:S(2)}) collective-permute-start(bf16[2,16,1024]{2,1,0:T(8,128)(2,1)S(1)} %get-tuple-element.46), channel_id=1, source_target_pairs={{1,0},{2,1},{3,2},{4,3},{5,4},{6,5},{7,6},{8,7},{9,8},{10,9},{11,1... | collective-permute-start | bytes 196616 | tf_op jit(solution)/shard_map/ppermute | solution.py:167
  112.3 13.9 %collective-permute-start.2 = (bf16[2,16,1024]{2,1,0:T(8,128)(2,1)}, bf16[2,16,1024]{2,1,0:T(8,128)(2,1)S(1)}, u32[]{:S(2)}, u32[]{:S(2)}) collective-permute-start(bf16[2,16,1024]{2,1,0:T(8,128)(2,1)} %get-tuple-element.45), channel_id=1, source_target_pairs={{0,1},{1,2},{2,3},{3,4},{4,5},{5,6},{6,7},{7,8},{8,9},{9,10},{10,1... | collective-permute-start | bytes 196616 | tf_op jit(solution)/shard_map/ppermute | solution.py:166
  115.7 10.6 %collective-permute-start.3 = (bf16[2,16,1024]{2,1,0:T(8,128)(2,1)}, bf16[2,16,1024]{2,1,0:T(8,128)(2,1)}, u32[]{:S(2)}, u32[]{:S(2)}) collective-permute-start(bf16[2,16,1024]{2,1,0:T(8,128)(2,1)} %get-tuple-element.44), channel_id=1, source_target_pairs={{1,0},{2,1},{3,2},{4,3},{5,4},{6,5},{7,6},{8,7},{9,8},{10,9},{11,1... | collective-permute-start | bytes 196616 | tf_op jit(solution)/shard_map/ppermute | solution.py:167
  124.3 20.3 %collective-permute-start.7 = (bf16[256,512]{0,1:T(8,128)(2,1)}, bf16[256,512]{0,1:T(8,128)(2,1)}, u32[]{:S(2)}, u32[]{:S(2)}) collective-permute-start(bf16[256,512]{0,1:T(8,128)(2,1)} %bitcast.57), channel_id=1, source_target_pairs={{0,16},{16,0},{1,17},{17,1},{2,18},{18,2},{3,19},{19,3},{4,20},{20... | collective-permute-start | bytes 786440 | tf_op jit(solution)/shard_map/ppermute | solution.py:267
  126.2 1.2 copy-start.2
  127.5 11.5 %copy-start.8 = (bf16[256,1024]{1,0:T(8,128)(2,1)S(1)}, bf16[256,1024]{1,0:T(8,128)(2,1)}, u32[]{:S(2)}) copy-start(bf16[256,1024]{1,0:T(8,128)(2,1)} %copy-done.7) | copy-start | bytes 1572868
  138.2 4.7 %copy-start.6 = (f32[32,1024]{1,0:T(8,128)}, f32[32,1024]{1,0:T(8,128)S(1)}, u32[]{:S(2)}) copy-start(f32[32,1024]{1,0:T(8,128)S(1)} %get-tuple-element.14) | copy-start | bytes 393220
  138.2 4.7 %copy-start.17 = (f32[256]{0:T(256)S(1)}, f32[256]{0:T(256)}, u32[]{:S(2)}) copy-start(f32[256]{0:T(256)} %copy-done.16) | copy-start | bytes 3076
  138.2 5.8 %copy-start.9 = (bf16[256,1024]{1,0:T(8,128)(2,1)S(1)}, bf16[256,1024]{1,0:T(8,128)(2,1)}, u32[]{:S(2)}) copy-start(bf16[256,1024]{1,0:T(8,128)(2,1)} %copy-done.7) | copy-start | bytes 1572868
  138.2 5.8 %copy-start.15 = (f32[256]{0:T(256)S(1)}, f32[256]{0:T(256)}, u32[]{:S(2)}) copy-start(f32[256]{0:T(256)} %copy-done.14) | copy-start | bytes 3076
  138.2 6.5 %copy-start.11 = (bf16[256,4,1,128]{0,3,1,2:T(8,128)(2,1)S(1)}, bf16[256,4,1,128]{0,3,1,2:T(8,128)(2,1)}, u32[]{:S(2)}) copy-start(bf16[256,4,1,128]{0,3,1,2:T(8,128)(2,1)} %copy.46) | copy-start | bytes 786436
  138.2 25.1 %collective-permute-start.5 = (bf16[256,2048]{1,0:T(8,128)(2,1)}, bf16[256,2048]{1,0:T(8,128)(2,1)}, u32[]{:S(2)}, u32[]{:S(2)}) collective-permute-start(bf16[256,2048]{1,0:T(8,128)(2,1)} %get-tuple-element.13), channel_id=1, source_target_pairs={{0,16},{16,0},{1,17},{17,1},{2,18},{18,2},{3,19},{19,3},{4,20},{20... | collective-permute-start | bytes 3145736 | tf_op jit(solution)/shard_map/ppermute | solution.py:299
  147.6 12.8 %copy-start.10 = (bf16[256,4,2,128]{0,3,1,2:T(8,128)(2,1)S(1)}, bf16[256,4,2,128]{0,3,1,2:T(8,128)(2,1)}, u32[]{:S(2)}) copy-start(bf16[256,4,2,128]{0,3,1,2:T(8,128)(2,1)} %multiply_convert_fusion) | copy-start | bytes 1572868
  147.6 30.6 %all-to-all-start.2 = ((bf16[64,8,1024]{2,1,0:T(8,128)(2,1)}), bf16[64,8,1024]{2,1,0:T(8,128)(2,1)}, u32[]{:S(2)}, u32[]{:S(2)}) async-start(bf16[64,8,1024]{2,1,0:T(8,128)(2,1)} %fusion.17), calls=%async_computation.2 | async-start | bytes 2097152 | tf_op jit(solution)/shard_map/all_to_all | solution.py:279
  160.5 1.9 collective-permute-start.6
  160.5 2.8 %collective-permute-start.4 = (bf16[256,512]{0,1:T(8,128)(2,1)S(1)}, bf16[256,512]{0,1:T(8,128)(2,1)S(1)}, u32[]{:S(2)}, u32[]{:S(2)}) collective-permute-start(bf16[256,512]{0,1:T(8,128)(2,1)S(1)} %bitcast.60), channel_id=1, source_target_pairs={{0,16},{16,0},{1,17},{17,1},{2,18},{18,2},{3,19},{19,3},{4,20},{20... | collective-permute-start | bytes 786440 | tf_op jit(solution)/shard_map/ppermute | solution.py:266
  178.2 35.3 %all-to-all-start.1 = ((bf16[64,8,2176]{2,1,0:T(8,128)(2,1)}), bf16[64,8,2176]{2,1,0:T(8,128)(2,1)}, u32[]{:S(2)}, u32[]{:S(2)}) async-start(bf16[64,8,2176]{2,1,0:T(8,128)(2,1)} %fusion.2), calls=%async_computation.1 | async-start | bytes 4456448 | tf_op jit(solution)/shard_map/all_to_all | solution.py:279
  185.2 34.9 %copy-start.5 = (bf16[256,1024]{1,0:T(8,128)(2,1)S(1)}, bf16[256,1024]{1,0:T(8,128)(2,1)}, u32[]{:S(2)}) copy-start(bf16[256,1024]{1,0:T(8,128)(2,1)} %copy-done.4) | copy-start | bytes 1572868
  216.5 15.9 %all-to-all-start.3 = ((bf16[16,8,3200]{2,1,0:T(8,128)(2,1)}), bf16[16,8,3200]{2,1,0:T(8,128)(2,1)S(1)}, u32[]{:S(2)}, u32[]{:S(2)}) async-start(bf16[16,8,3200]{2,1,0:T(8,128)(2,1)} %broadcast_in_dim.77), calls=%async_computation.3 | async-start | bytes 1638400 | tf_op jit(solution)/shard_map/all_to_all | solution.py:158
  (2 other events, 1.8 us)
Sparse Core Ops, SparseCore 0:
  10.3 40.7 all-gather.2
  52.8 33.6 all-gather.4

commit v2 on v1

--- a/solution.py
+++ b/solution.py
@@ -6,6 +6,7 @@
 from jax.experimental import pallas as pl
 from jax.experimental.pallas import tpu as pltpu
 from jax.sharding import Mesh, PartitionSpec as P
+
 
 DP = ("z", "core")
 SEQ = ("x", "y")
@@ -17,15 +18,15 @@
 
 
 def forward_kernel(
-    gated_ref, low_ref, high_ref, ids_ref, taps_ref, gain_ref, grad_act_ref,
-    act_ref, grad_mix_ref, grad_gain_ref, pad_ref, mix_ref,
+    gated_ref, low_ref, high_ref, ids_ref, taps_ref, gain_ref,
+    act_ref, normed_ref, scale_ref, pad_ref, mix_ref,
 ):
     slabs, frames, width = gated_ref.shape
     blocks = width // LANES
     taps_count = taps_ref.shape[1] - 1
     shift = EDGE - taps_count // 2
 
-    def one_slab(s, total):
+    def one_slab(s, carry):
         for b in range(blocks):
             cols = slice(b * LANES, (b + 1) * LANES)
             pad_ref[b, 0:EDGE] = low_ref[s, :, cols].astype(jnp.float32)
@@ -48,33 +49,48 @@
 
         lax.fori_loop(0, (frames // ROWS_STEP) * (blocks // 2), conv_step, 0)
 
-        def row_step(i, total):
+        def row_step(i, carry):
             row = pl.multiple_of(i * 16, 16)
             out_row = pl.multiple_of(s * frames + i * 16, 16)
             mixing = jnp.concatenate([mix_ref[b, pl.ds(row, 16)] for b in range(blocks)], axis=1)
-            grad_act = grad_act_ref[pl.ds(out_row, 16), :]
-            gain = gain_ref[0:1, :]
             centered = mixing - jnp.mean(mixing, axis=-1, keepdims=True)
             scale = lax.rsqrt(jnp.mean(centered * centered, axis=-1, keepdims=True) + EPS)
             normed = centered * scale
-            value = normed * gain
-            sig = jax.nn.sigmoid(value)
-            act_ref[pl.ds(out_row, 16), :] = (value * sig).astype(act_ref.dtype)
-            grad_value = grad_act * (sig * (1.0 + value * (1.0 - sig)))
-            part = grad_value * normed
-            total = total + part[0:8] + part[8:16]
-            grad_normed = grad_value * gain
-            first = jnp.mean(grad_normed, axis=-1, keepdims=True)
-            second = jnp.mean(grad_normed * normed, axis=-1, keepdims=True)
-            grad_mix_ref[s, pl.ds(row, 16), :] = (
-                scale * (grad_normed - first - normed * second)
-            ).astype(grad_mix_ref.dtype)
-            return total
-
-        return lax.fori_loop(0, frames // 16, row_step, total)
+            value = normed * gain_ref[0:1, :]
+            act_ref[pl.ds(out_row, 16), :] = (value * jax.nn.sigmoid(value)).astype(act_ref.dtype)
+            normed_ref[pl.ds(out_row, 16), :] = normed
+            scale_ref[pl.ds(out_row, 16), :] = jnp.broadcast_to(scale, (16, LANES))
+            return carry
+
+        return lax.fori_loop(0, frames // 16, row_step, carry)
+
+    lax.fori_loop(0, slabs, one_slab, 0)
+
+
+def middle_kernel(normed_ref, scale_ref, grad_act_ref, gain_ref, grad_mix_ref, grad_gain_ref):
+    slabs, frames, _ = grad_mix_ref.shape
+    steps = frames // 16
+
+    def row_step(i, total):
+        row = pl.multiple_of(i * 16, 16)
+        normed = normed_ref[pl.ds(row, 16), :]
+        scale = scale_ref[pl.ds(row, 16), 0:1]
+        gain = gain_ref[0:1, :]
+        value = normed * gain
+        sig = jax.nn.sigmoid(value)
+        grad_value = grad_act_ref[pl.ds(row, 16), :] * (sig * (1.0 + value * (1.0 - sig)))
+        part = grad_value * normed
+        total = total + (part[0:8] + part[8:16])
+        grad_normed = grad_value * gain
+        first = jnp.mean(grad_normed, axis=-1, keepdims=True)
+        second = jnp.mean(grad_normed * normed, axis=-1, keepdims=True)
+        grad_mix_ref[i // steps, pl.ds(pl.multiple_of((i % steps) * 16, 16), 16), :] = scale * (
+            grad_normed - first - normed * second
+        )
+        return total
 
     grad_gain_ref[...] = lax.fori_loop(
-        0, slabs, one_slab, jnp.zeros(grad_gain_ref.shape, jnp.float32)
+        0, slabs * steps, row_step, jnp.zeros(grad_gain_ref.shape, jnp.float32)
     )
 
 
@@ -142,13 +158,65 @@
         )
 
 
-def kernel_call(body, name, outs, scratch, flops, *args):
+def product_kernel(core_ref, left_ref, left_other_ref, right_ref, right_other_ref, *rest):
+    out_ref = rest[-1]
+    width = right_ref.shape[1]
+    step = 512
+    left, left_other = left_ref[...], left_other_ref[...]
+    over_rows = (((0,), (0,)), ((), ()))
+    for at in range(0, width, step):
+        out_ref[:, at : at + step] = (
+            lax.dot_general(
+                left, right_ref[:, at : at + step], over_rows, preferred_element_type=jnp.float32
+            )
+            + lax.dot_general(
+                left_other,
+                right_other_ref[:, at : at + step],
+                over_rows,
+                preferred_element_type=jnp.float32,
+            )
+        ).astype(out_ref.dtype)
+    if len(rest) > 1:
+        small = rest[0][...] + rest[1][...]
+        filled = jnp.concatenate(
+            [small, jnp.zeros((LANES - small.shape[0], LANES), jnp.float32)], axis=0
+        )
+        out_ref[:, width:] = filled.T.astype(out_ref.dtype)
+
+
+def weight_part(core, left, left_other, right, right_other, *small):
+    rows, channels = left.shape
+    mine = channels // LANES // 2
+    width = right.shape[1]
+    out_width = width + (LANES if small else 0)
+    picked = lambda height: pl.BlockSpec((height, LANES), lambda z, c: (0, 2 * z + c[0]))
+    whole = lambda a: pl.BlockSpec(a.shape, lambda z, c: (0, 0))
+    return pl.pallas_call(
+        product_kernel,
+        out_shape=jax.ShapeDtypeStruct((mine * LANES, out_width), jnp.bfloat16),
+        grid_spec=pltpu.PrefetchScalarGridSpec(
+            num_scalar_prefetch=1,
+            grid=(mine,),
+            in_specs=[picked(rows), picked(rows), whole(right), whole(right_other)]
+            + [picked(a.shape[0]) for a in small],
+            out_specs=pl.BlockSpec((LANES, out_width), lambda z, c: (z, 0)),
+        ),
+        name="weight_part",
+        compiler_params=pltpu.CompilerParams(vmem_limit_bytes=48 * 1024 * 1024),
+        cost_estimate=pl.CostEstimate(
+            flops=4 * rows * mine * LANES * width,
+            bytes_accessed=4 * rows * (channels + width),
+            transcendentals=0,
+        ),
+    )(core, left, left_other, right, right_other, *small)
+
+
+def kernel_call(body, outs, scratch, flops, *args):
     moved = sum(a.size * a.dtype.itemsize for a in args)
     return pl.pallas_call(
         body,
         out_shape=outs,
         scratch_shapes=scratch,
-        name=name,
         compiler_params=pltpu.CompilerParams(vmem_limit_bytes=48 * 1024 * 1024),
         cost_estimate=pl.CostEstimate(flops=flops, bytes_accessed=moved, transcendentals=0),
     )(*args)
@@ -193,20 +261,19 @@
     extras = jnp.pad(
         jnp.concatenate([depth_kernel, norm_gains], axis=1), ((0, 0), (0, LANES - kernel_len - 2))
     )
-    in_full = lax.all_gather(in_weight, DP, axis=0, tiled=True)
-    out_full = lax.all_gather(
-        jnp.concatenate([out_weight, extras], axis=1), DP, axis=0, tiled=True
-    )
-    upstream_rows = upstream.reshape(rows_dev, width)
-    upstream_other = lax.ppermute(upstream_rows, "core", swap)
+    in_all = lax.all_gather(jnp.concatenate([in_weight, extras], axis=1), DP, axis=0, tiled=True)
+    out_full = lax.all_gather(out_weight, DP, axis=0, tiled=True)
+    in_full = in_all[:, : 2 * width]
 
     send_plan = lax.dynamic_index_in_dim(plan, sender, 0, keepdims=False)
     send_start = jnp.cumsum(send_plan) - send_plan
     slot_index = jnp.arange(capacity, dtype=jnp.int32)
-    source_rows = send_start[:, None] + slot_index[None, :]
-    outgoing = jnp.take(
-        loaded, jnp.clip(source_rows, 0, rows_dev - 1).reshape(-1), axis=0
-    ).reshape(devices, capacity, width)
+    source_rows = jnp.minimum(send_start[:, None] + slot_index[None, :], rows_dev - 1)
+    outgoing = (
+        loaded.at[source_rows.reshape(-1)]
+        .get(mode="promise_in_bounds")
+        .reshape(devices, capacity, width)
+    )
     arrived = lax.all_to_all(
         outgoing, (*DP, *SEQ), split_axis=0, concat_axis=0, tiled=True
     ).reshape(devices * capacity, width)
@@ -216,7 +283,11 @@
     before = recv_end[None, :] <= frame_index[:, None]
     source_dev = jnp.sum(before.astype(jnp.int32), axis=1)
     start_of = jnp.sum(jnp.where(before, recv_plan[None, :], 0), axis=1)
-    frames = jnp.take(arrived, source_dev * capacity + frame_index - start_of, axis=0)
+    frames = arrived.at[source_dev * capacity + frame_index - start_of].get(
+        mode="promise_in_bounds"
+    )
+    upstream_rows = upstream.reshape(rows_dev, width)
+    upstream_other = lax.ppermute(upstream_rows, "core", swap)
 
     id_pad = jnp.pad(segment_ids, ((0, 0), (EDGE, EDGE)), constant_values=-1)
     window = lax.dynamic_slice_in_dim(
@@ -224,11 +295,10 @@
     )
     ids = jnp.broadcast_to(window[:, :, None], (*window.shape, LANES))
 
-    side = out_full[:, width : width + kernel_len + 2].astype(jnp.float32).T
+    side = in_all[:, 2 * width : 2 * width + kernel_len + 2].astype(jnp.float32).T
     gain_pre, gain_mid = side[kernel_len], side[kernel_len + 1]
     taps = jnp.pad(side[:kernel_len], ((0, 1), (0, 0)))
     taps = taps.reshape(kernel_len + 1, width // LANES, LANES).transpose(1, 0, 2)
-    out_full = out_full[:, :width]
 
     frame_rows = frames.astype(jnp.float32)
     normed_full, pull_pre = jax.vjp(norm_rows, frame_rows, gain_pre)
@@ -240,40 +310,33 @@
         .reshape(slabs, frames_dev, width)
     )
     low, high = edges(gated, n_seq)
-    grad_act = jnp.dot(upstream_rows, out_full.T, preferred_element_type=jnp.float32)
     elements = rows_dev * width
     blocked = pltpu.VMEM((width // LANES, frames_dev + 2 * EDGE, LANES), jnp.float32)
-    activated, grad_mixing, grad_gain_mid = kernel_call(
+    activated, normed_mid, scale_mid = kernel_call(
         forward_kernel,
-        "mixing_forward",
         (
             jax.ShapeDtypeStruct((rows_dev, width), jnp.bfloat16),
+            jax.ShapeDtypeStruct((rows_dev, width), jnp.float32),
+            jax.ShapeDtypeStruct((rows_dev, LANES), jnp.float32),
+        ),
+        [blocked, pltpu.VMEM((width // LANES, frames_dev, LANES), jnp.float32)],
+        elements * 3 * kernel_len,
+        gated, low, high, ids, taps, gain_mid[None],
+    )
+    act_other = lax.ppermute(activated, "core", swap)
+    normed_other = lax.ppermute(normed, "core", swap)
+    grad_act = jnp.dot(upstream_rows, out_full.T, preferred_element_type=jnp.float32)
+    grad_mixing, grad_gain_mid = kernel_call(
+        middle_kernel,
+        (
             jax.ShapeDtypeStruct((slabs, frames_dev, width), jnp.float32),
             jax.ShapeDtypeStruct((8, width), jnp.float32),
         ),
-        [blocked, pltpu.VMEM((width // LANES, frames_dev, LANES), jnp.float32)],
-        elements * 3 * kernel_len,
-        gated, low, high, ids, taps, gain_mid[None], grad_act,
+        [],
+        elements * 30,
+        normed_mid, scale_mid, grad_act, gain_mid[None],
     )
     grad_low, grad_high = edges(grad_mixing, n_seq)
-
-    def for_core(rows, which):
-        parts = rows.reshape(rows.shape[0], n_z, 2, LANES)
-        return lax.dynamic_index_in_dim(parts, which, 2, keepdims=False).reshape(
-            rows.shape[0], n_z * LANES
-        )
-
-    normed_other = lax.ppermute(for_core(normed, 1 - core), "core", swap)
-    act_other = lax.ppermute(for_core(activated, 1 - core), "core", swap)
-    projected = jnp.dot(activated, out_full, preferred_element_type=jnp.float32)
-    encoded = (frame_rows + projected).astype(jnp.bfloat16).reshape(slabs, frames_dev, width)
-
-    def weight_part(mine, other, right, right_other):
-        left = jnp.concatenate([mine, other], axis=0)
-        both = jnp.concatenate([right, right_other], axis=0)
-        return lax.dot_general(
-            left, both, (((0,), (0,)), ((), ())), preferred_element_type=jnp.float32
-        ).astype(jnp.bfloat16)
 
     def summed(part):
         arrived_parts = lax.all_to_all(
@@ -281,13 +344,14 @@
         )
         return jnp.sum(arrived_parts.astype(jnp.float32), axis=0)
 
-    scale = 1.0 / math.sqrt(devices * rows_dev)
-    out_part = weight_part(for_core(activated, core), act_other, upstream_rows, upstream_other)
+    core_ref = core[None].astype(jnp.int32)
+    out_part = weight_part(core_ref, activated, act_other, upstream_rows, upstream_other)
     out_sum = summed(out_part)
+    projected = jnp.dot(activated, out_full, preferred_element_type=jnp.float32)
+    encoded = (frame_rows + projected).astype(jnp.bfloat16).reshape(slabs, frames_dev, width)
 
     grad_hidden, grad_taps = kernel_call(
         backward_kernel,
-        "mixing_backward",
         (
             jax.ShapeDtypeStruct((rows_dev, 2 * width), jnp.bfloat16),
             jax.ShapeDtypeStruct((kernel_len + 1, width), jnp.float32),
@@ -297,24 +361,41 @@
         grad_mixing, grad_low, grad_high, gated, ids, taps, hidden,
     )
     hidden_other = lax.ppermute(grad_hidden, "core", swap)
+    small = jnp.concatenate(
+        [
+            grad_taps,
+            jnp.sum(grad_gain_mid, axis=0)[None],
+            jnp.zeros((7, width), jnp.float32),
+        ],
+        axis=0,
+    )
+    small_other = lax.ppermute(small, "core", swap)
+    in_part = weight_part(
+        core_ref, normed, normed_other, grad_hidden, hidden_other, small, small_other
+    )
+    in_sum = summed(in_part)
     grad_normed = lax.dot_general(
         grad_hidden, in_full, (((1,), (1,)), ((), ())), preferred_element_type=jnp.float32
     )
-    grad_rows, grad_gain_pre = pull_pre(grad_normed)
+    grad_rows, _ = pull_pre(grad_normed)
     grad_frames = (
         (upstream_rows.astype(jnp.float32) + grad_rows)
         .astype(jnp.bfloat16)
         .reshape(slabs, frames_dev, width)
     )
-    small = jnp.concatenate(
-        [grad_taps[:kernel_len], grad_gain_pre[None], jnp.sum(grad_gain_mid, axis=0)[None]], axis=0
-    )
-    small_other = lax.ppermute(for_core(small, 1 - core), "core", swap)
-    small_part = (for_core(small, core) + small_other).T.astype(jnp.bfloat16)
-    small_part = jnp.pad(small_part, ((0, 0), (0, LANES - small_part.shape[1])))
-    in_part = weight_part(for_core(normed, core), normed_other, grad_hidden, hidden_other)
-    in_sum = summed(jnp.concatenate([in_part, small_part], axis=1))
-    total = (jnp.concatenate([in_sum, out_sum], axis=1) * scale).astype(jnp.bfloat16)
+    share = LANES // n_seq
+    first = lax.axis_index(SEQ) * share
+    own_weight = lax.dynamic_slice_in_dim(in_weight, first, share, 0).astype(jnp.float32)
+    own_gain = lax.dynamic_slice_in_dim(norm_gains, first, share, 0)[:, :1].astype(jnp.float32)
+    grad_gain_pre = (
+        jnp.sum(own_weight * in_sum[:, : 2 * width], axis=1, keepdims=True) / own_gain
+    )
+    place = jnp.arange(LANES) == kernel_len
+    small_sum = jnp.where(place[None], grad_gain_pre, in_sum[:, 2 * width :])
+    scale = 1.0 / math.sqrt(devices * rows_dev)
+    total = (
+        jnp.concatenate([in_sum[:, : 2 * width], small_sum, out_sum], axis=1) * scale
+    ).astype(jnp.bfloat16)
     final = spread(total, SEQ, n_seq).reshape(LANES, total.shape[1]).astype(jnp.float32)
     return (
         encoded,

time: 244 us -> 215 us (0.88)
  local copies, waits for them, and re-layouts: 26.6 us -> 13.5 us
  waiting for transfers between devices: 102 us -> 90 us
  Pallas kernels: 20.5 us -> 30.4 us
  other arithmetic: 15.9 us -> 10.1 us
  matrix products: 19.9 us -> 14.3 us
    all_gather x2, waiting for transfers between devices: 31.6 us -> 15.9 us  [the longest x1 12.9 us: per_device(): lax.all_gather(jnp.concatenate([in_weight, extras], axis=1), DP, axis=0,...]
    pallas_call x2 -> x5, Pallas kernels: 20.5 us -> 30.4 us  [the longest x3 21.5 us: kernel_call(): pl.pallas_call(body, out_shape=outs, scratch_shapes=scratch, compiler_par...]
    dot_general x2 -> x0, matrix products: 5.77 us -> none  [weight_part(): lax.dot_general(left, both, (((0,), (0,)), ((), ())), preferred_element_t...]
    all_to_all x2, waiting for transfers between devices: 38.8 us -> 33.3 us  [summed(): lax.all_to_all(part.reshape(n_z * n_seq, LANES // n_seq, part.shape[1]),...]
    dynamic_slice x5 -> x1, local copies, waits for them, and re-layouts: 4.45 us -> 0.08 us  [per_device(): lax.dynamic_slice_in_dim(norm_gains, first, share, 0)[:, :1]]
    ppermute x2, waiting for transfers between devices: 4.28 us -> 8.55 us  [edges(): high = lax.ppermute(block[:, :EDGE].astype(jnp.bfloat16), SEQ, backward)]
    unnamed x43 -> x35, local copies, waits for them, and re-layouts: 9.21 us -> 5.04 us
    all_to_all x1, waiting for transfers between devices: 6.81 us -> 10.8 us  [spread(): lax.all_to_all(jnp.broadcast_to(shard[None], (count, *shard.shape)), axes...]
  transfers between devices with their start and end apart: 15 -> 15, of which waited for: 9 -> 11; matrix products, arithmetic and copies ran while one was open for 21% -> 13% of each run, Pallas kernels for 8% -> 14%
where the time goes in v2:
time: 215 us; the launch traced here: 214 us
  waiting for transfers between devices  90 us (42%)
  starting transfers between devices  41.4 us (19%)
  Pallas kernels  30.4 us (14%)
  between operations  14.5 us (7%)
  matrix products  14.3 us (7%)
  local copies, waits for them, and re-layouts  13.5 us (6%)
  other arithmetic  10.1 us (5%)
    all_to_all x2, waiting for transfers between devices, summed(): lax.all_to_all(part.reshape(n_z * n_seq, LANES // n_seq, part.shape[1]),...  33.3 us
    pallas_call x3, Pallas kernels, kernel_call(): pl.pallas_call(body, out_shape=outs, scratch_shapes=scratch, compiler_par...  21.5 us
    all_to_all x1, waiting for transfers between devices, per_device(): lax.all_to_all(outgoing, (*DP, *SEQ), split_axis=0, concat_axis=0, tiled=...  18.3 us
    all_to_all x2, starting transfers between devices, summed(): lax.all_to_all(part.reshape(n_z * n_seq, LANES // n_seq, part.shape[1]),...  16 us
    all_gather x1, waiting for transfers between devices, per_device(): lax.all_gather(jnp.concatenate([in_weight, extras], axis=1), DP, axis=0,...  12.9 us
    all_to_all x1, starting transfers between devices, per_device(): lax.all_to_all(outgoing, (*DP, *SEQ), split_axis=0, concat_axis=0, tiled=...  11.2 us
    all_to_all x1, waiting for transfers between devices, spread(): lax.all_to_all(jnp.broadcast_to(shard[None], (count, *shard.shape)), axes...  10.8 us
    pallas_call x2, Pallas kernels, weight_part(): pl.pallas_call(product_kernel, out_shape=jax.ShapeDtypeStruct((mine * LAN...  8.85 us
  transfers between devices with their start and end apart: 15, of which 11 were waited for; matrix products, arithmetic and copies ran while one was open for 13% of the time, Pallas kernels for 14%

profile of v2, /device:TPU:0, one launch (start us, length us, event | category | flops | bytes accessed | tf_op | source)
XLA Modules:
  0.0 214.2 jit_solution(7399027056634500935)
XLA Ops:
  7.2 1.4 copy.25
  11.7 2.1 gather_fusion
  13.7 1.2 reshape.217
  14.9 11.2 %all-to-all-start = ((bf16[128,4,1024]{2,1,0:T(4,128)(2,1)}), bf16[128,4,1024]{2,1,0:T(4,128)(2,1)S(1)}, u32[]{:S(2)}, u32[]{:S(2)}) async-start(bf16[128,4,1024]{2,1,0:T(4,128)(2,1)} %reshape.217), calls=%async_computation | async-start | bytes 2097152 | tf_op jit(solution)/shard_map/all_to_all | solution.py:277
  27.0 18.3 %all-to-all-done = bf16[128,4,1024]{2,1,0:T(4,128)(2,1)S(1)} async-done(((bf16[128,4,1024]{2,1,0:T(4,128)(2,1)}), bf16[128,4,1024]{2,1,0:T(4,128)(2,1)S(1)}, u32[]{:S(2)}, u32[]{:S(2)}) %all-to-all-start) | async-done | bytes 1048608 | tf_op jit(solution)/shard_map/all_to_all | solution.py:277
  45.5 1.2 gather_fusion.1
  47.2 12.9 %all-gather.3.cloned.1.call-done = bf16[1024,2176]{0,1:T(8,128)(2,1)} async-done(((bf16[128,2176]{0,1:T(8,128)(2,1)}), bf16[1024,2176]{0,1:T(8,128)(2,1)}) %all-gather.3.cloned.1.call-update) | async-done | bytes 4456464 | tf_op jit(solution)/shard_map/all_gather | solution.py:264
  61.3 3.7 %fusion.2.hidden_ref = f32[256,2048]{1,0:T(8,128)S(1)} fusion(bf16[256,1024]{1,0:T(8,128)(2,1)S(1)} %fusion.14.left_ref, bf16[1024,2176]{0,1:T(8,128)(2,1)} %all-gather.3.cloned.1.call-done), kind=kOutput, calls=%fused_computation.5 | convolution fusion | flops 1073741824 | bytes 6815744 | tf_op jit(solution)/shard_map/dot_general | solution.py:306
  65.4 3.9 %collective-permute-start = (bf16[2,16,1024]{2,1,0:T(8,128)(2,1)S(1)}, bf16[2,16,1024]{2,1,0:T(8,128)(2,1)S(1)}, u32[]{:S(2)}, u32[]{:S(2)}) collective-permute-start(bf16[2,16,1024]{2,1,0:T(8,128)(2,1)S(1)} %get-tuple-element.45), channel_id=1, source_target_pairs={{0,1},{1,2},{2,3},{3,4},{4,5},{5,6},{6,7},{7,8},{8,9},{9,10},{10,1... | collective-permute-start | bytes 196616 | tf_op jit(solution)/shard_map/ppermute | solution.py:234
  69.3 1.3 collective-permute-start.1
  71.2 4.3 %collective-permute-done.1.high_ref = bf16[2,16,1024]{2,1,0:T(8,128)(2,1)S(1)} collective-permute-done((bf16[2,16,1024]{2,1,0:T(8,128)(2,1)S(1)}, bf16[2,16,1024]{2,1,0:T(8,128)(2,1)S(1)}, u32[]{:S(2)}, u32[]{:S(2)}) %collective-permute-start.1) | collective-permute-done | bytes 65568 | tf_op jit(solution)/shard_map/ppermute | solution.py:235
  75.5 9.1 %shard_map.127 = (bf16[256,1024]{1,0:T(8,128)(2,1)}, f32[256,1024]{1,0:T(8,128)S(1)}, f32[256,128]{1,0:T(8,128)S(1)}) custom-call(bf16[2,128,1024]{2,1,0:T(8,128)(2,1)S(1)} %bitcast.43, bf16[2,16,1024]{2,1,0:T(8,128)(2,1)S(1)} %collective-permute-done.low_ref, bf16[2,16,1024]{2,1,0:T(8,128)(2,1)S(1)} %collective-permute-done.1.high_ref, ...), custom_call_target="tpu_custom_call" | custom-call | flops 24379392 | bytes 954368 | tf_op jit(solution)/shard_map/pallas_call | solution.py:216
  86.3 3.0 %all-gather.5.cloned.1.call-done = bf16[1024,1024]{1,0:T(8,128)(2,1)} async-done(((bf16[128,1024]{1,0:T(8,128)(2,1)}), bf16[1024,1024]{1,0:T(8,128)(2,1)}) %all-gather.5.cloned.1.call-update) | async-done | bytes 2097168 | tf_op jit(solution)/shard_map/all_gather | solution.py:265
  89.2 2.6 %fusion.35.grad_act_ref = f32[256,1024]{1,0:T(8,128)S(1)} fusion(bf16[256,1024]{1,0:T(8,128)(2,1)} %bitcast.11.right_ref, bf16[1024,1024]{1,0:T(8,128)(2,1)} %all-gather.5.cloned.1.call-done), kind=kOutput, calls=%fused_computation.73 | convolution fusion | flops 536870912 | bytes 3670016 | tf_op jit(solution)/shard_map/dot_general | solution.py:328
  91.9 2.0 shard_map.128
  94.0 3.3 %collective-permute-start.2 = (bf16[2,16,1024]{2,1,0:T(8,128)(2,1)S(1)}, bf16[2,16,1024]{2,1,0:T(8,128)(2,1)S(1)}, u32[]{:S(2)}, u32[]{:S(2)}) collective-permute-start(bf16[2,16,1024]{2,1,0:T(8,128)(2,1)S(1)} %get-tuple-element.43), channel_id=1, source_target_pairs={{0,1},{1,2},{2,3},{3,4},{4,5},{5,6},{6,7},{7,8},{8,9},{9,10},{10,1... | collective-permute-start | bytes 196616 | tf_op jit(solution)/shard_map/ppermute | solution.py:234
  97.3 1.3 collective-permute-start.3
  99.2 4.3 %collective-permute-done.3.high_ref = bf16[2,16,1024]{2,1,0:T(8,128)(2,1)S(1)} collective-permute-done((bf16[2,16,1024]{2,1,0:T(8,128)(2,1)S(1)}, bf16[2,16,1024]{2,1,0:T(8,128)(2,1)S(1)}, u32[]{:S(2)}, u32[]{:S(2)}) %collective-permute-start.3) | collective-permute-done | bytes 65568 | tf_op jit(solution)/shard_map/ppermute | solution.py:235
  103.4 10.4 %shard_map.129 = (bf16[256,2048]{1,0:T(8,128)(2,1)}, f32[32,1024]{1,0:T(8,128)S(1)}) custom-call(f32[2,128,1024]{2,1,0:T(8,128)S(1)} %get-tuple-element.16.grad_mix_ref, bf16[2,16,1024]{2,1,0:T(8,128)(2,1)S(1)} %collective-permute-done.2.low_ref, bf16[2,16,1024]{2,1,0:T(8,128)(2,1)S(1)} %collective-permute-done.3.high_ref, ...), custom_call_target="tpu_custom_call" | custom-call | flops 40632320 | bytes 4096000 | tf_op jit(solution)/shard_map/pallas_call | solution.py:216
  114.5 4.4 %weight_part.3 = bf16[512,1024]{1,0:T(8,128)(2,1)} custom-call(s32[1]{0:T(128)} %bitcast.13.core_ref, bf16[256,1024]{1,0:T(8,128)(2,1)} %get-tuple-element.13.left_ref, bf16[256,1024]{1,0:T(8,128)(2,1)} %collective-permute-done.7.left_other_ref, bf16[256,1024]{1,0:T(8,128)(2,1)} %bitcast.11.right_ref, bf16[256,1024]{1,0:T(8,128)(2,1)} %collective-permute-done.8.right_other_ref), custom_call_target="tpu_custom_call" | custom-call | flops 536870912 | bytes 2097152 | tf_op jit(solution)/shard_map/weight_part/pallas_call | solution.py:194
  118.9 10.9 %all-to-all-start.2 = ((bf16[64,8,1024]{2,1,0:T(8,128)(2,1)}), bf16[64,8,1024]{2,1,0:T(8,128)(2,1)}, u32[]{:S(2)}, u32[]{:S(2)}) async-start(bf16[64,8,1024]{2,1,0:T(8,128)(2,1)} %bitcast.18), calls=%async_computation.2 | async-start | bytes 2097152 | tf_op jit(solution)/shard_map/all_to_all | solution.py:342
  130.7 1.4 collective-permute-done.6.rest_1_
  132.0 4.5 %weight_part.2 = bf16[512,2176]{1,0:T(8,128)(2,1)} custom-call(s32[1]{0:T(128)} %bitcast.13.core_ref, bf16[256,1024]{1,0:T(8,128)(2,1)S(1)} %copy-done.2, bf16[256,1024]{1,0:T(8,128)(2,1)S(1)} %collective-permute-done.4.left_other_ref, bf16[256,2048]{1,0:T(8,128)(2,1)} %get-tuple-element.17.right_ref, ...), custom_call_target="tpu_custom_call" | custom-call | flops 1073741824 | bytes 3145728 | tf_op jit(solution)/shard_map/weight_part/pallas_call | solution.py:194
  136.5 12.5 %all-to-all-done.2 = bf16[64,8,1024]{2,1,0:T(8,128)(2,1)} async-done(((bf16[64,8,1024]{2,1,0:T(8,128)(2,1)}), bf16[64,8,1024]{2,1,0:T(8,128)(2,1)}, u32[]{:S(2)}, u32[]{:S(2)}) %all-to-all-start.2) | async-done | bytes 1048608 | tf_op jit(solution)/shard_map/all_to_all | solution.py:342
  149.0 5.1 %all-to-all-start.1 = ((bf16[64,8,2176]{2,1,0:T(8,128)(2,1)}), bf16[64,8,2176]{2,1,0:T(8,128)(2,1)S(1)}, u32[]{:S(2)}, u32[]{:S(2)}) async-start(bf16[64,8,2176]{2,1,0:T(8,128)(2,1)} %bitcast.15), calls=%async_computation.1 | async-start | bytes 4456448 | tf_op jit(solution)/shard_map/all_to_all | solution.py:342
  154.2 3.3 %fusion.11 = bf16[256,1024]{1,0:T(8,128)(2,1)} fusion(bf16[256,1024]{1,0:T(8,128)(2,1)} %get-tuple-element.13.left_ref, bf16[1024,1024]{1,0:T(8,128)(2,1)} %all-gather.5.cloned.1.call-done, bf16[256,1024]{1,0:T(8,128)(2,1)S(1)} %copy-done.10), kind=kOutput, calls=%fused_computation.17 | convolution fusion | flops 537657344 | bytes 3670016 | tf_op jit(solution)/shard_map/dot_general | solution.py:350
  157.5 4.7 %fusion.15 = (f32[256]{0:T(256)S(1)}, f32[256,1024]{1,0:T(8,128)}) fusion(bf16[256,1024]{1,0:T(8,128)(2,1)S(1)} %copy-done.10, f32[256]{0:T(256)S(1)} %broadcast_multiply_fusion, f32[1024]{0:T(1024)S(1)} %bitcast.48, bf16[256,2048]{1,0:T(8,128)(2,1)} %get-tuple-element.17.right_ref, bf16[1024,2176]{0,1:T(8,128)(2,1)} %all-gather.3.cloned.1.call-done), kind=kOutput, calls=%fused_computation.21 | convolution fusion | flops 1075052288 | bytes 6821888 | tf_op jit(solution)/shard_map/dot_general | solution.py:377
  162.2 1.4 convert_reduce_fusion.1
  163.7 20.8 %all-to-all-done.1 = bf16[64,8,2176]{2,1,0:T(8,128)(2,1)S(1)} async-done(((bf16[64,8,2176]{2,1,0:T(8,128)(2,1)}), bf16[64,8,2176]{2,1,0:T(8,128)(2,1)S(1)}, u32[]{:S(2)}, u32[]{:S(2)}) %all-to-all-start.1) | async-done | bytes 2228256 | tf_op jit(solution)/shard_map/all_to_all | solution.py:342
  186.9 3.6 %all-to-all-start.3 = ((bf16[16,8,3200]{2,1,0:T(8,128)(2,1)}), bf16[16,8,3200]{2,1,0:T(8,128)(2,1)S(1)}, u32[]{:S(2)}, u32[]{:S(2)}) async-start(bf16[16,8,3200]{2,1,0:T(8,128)(2,1)} %broadcast_in_dim.85), calls=%async_computation.3 | async-start | bytes 1638400 | tf_op jit(solution)/shard_map/all_to_all | solution.py:226
  190.9 2.2 %add_convert_fusion = bf16[256,1024]{1,0:T(8,128)(2,1)} fusion(f32[256]{0:T(256)S(1)} %negate_multiply_fusion, bf16[2,128,1024]{2,1,0:T(8,128)(2,1)} %param.15, f32[256]{0:T(256)S(1)} %multiply_multiply_fusion, f32[256]{0:T(256)S(1)} %broadcast_multiply_fusion, bf16[256,1024]{1,0:T(8,128)(2,1)S(1)} %copy-done.10, f32[256,1024]{1,0:T(8,128)S(1)} %copy-done.11, ...), kind=kLoop, calls=%fused_computation.27 | loop fusion | flops 2621440 | bytes 2625536 | tf_op jit(solution)/shard_map/convert_element_type | solution.py:383
  193.1 10.8 %all-to-all-done.3 = bf16[16,8,3200]{2,1,0:T(8,128)(2,1)S(1)} async-done(((bf16[16,8,3200]{2,1,0:T(8,128)(2,1)}), bf16[16,8,3200]{2,1,0:T(8,128)(2,1)S(1)}, u32[]{:S(2)}, u32[]{:S(2)}) %all-to-all-start.3) | async-done | bytes 819232 | tf_op jit(solution)/shard_map/all_to_all | solution.py:226
  (102 shorter events, 16.8 us)
Async XLA Ops:
  7.2 4.5 %copy-start = (bf16[256,1024]{1,0:T(8,128)(2,1)S(1)}, bf16[256,1024]{1,0:T(8,128)(2,1)}, u32[]{:S(2)}) copy-start(bf16[256,1024]{1,0:T(8,128)(2,1)} %param.8) | copy-start | bytes 1572868
  7.2 3.8 %copy-start.12 = (s32[128,128]{1,0:T(8,128)S(1)}, s32[128,128]{1,0:T(8,128)}, u32[]{:S(2)}) copy-start(s32[128,128]{1,0:T(8,128)} %param.9) | copy-start | bytes 196612
  7.2 52.9 %all-gather.3.cloned.1.call-start = ((), (), s32[]{:S(2)}) async-start(), calls=%async_computation.4 | async-start | bytes 5013504 | tf_op jit(solution)/shard_map/all_gather | solution.py:264
  10.2 79.0 %all-gather.5.cloned.1.call-start = ((), (), s32[]{:S(2)}) async-start(), calls=%async_computation.5 | async-start | bytes 2359296 | tf_op jit(solution)/shard_map/all_gather | solution.py:265
  13.7 13.0 %copy-start.13 = (s32[2,2048]{1,0:T(2,128)S(1)}, s32[2,2048]{1,0:T(2,128)}, u32[]{:S(2)}) copy-start(s32[2,2048]{1,0:T(2,128)} %param.10) | copy-start | bytes 49156
  14.9 30.3 %all-to-all-start = ((bf16[128,4,1024]{2,1,0:T(4,128)(2,1)}), bf16[128,4,1024]{2,1,0:T(4,128)(2,1)S(1)}, u32[]{:S(2)}, u32[]{:S(2)}) async-start(bf16[128,4,1024]{2,1,0:T(4,128)(2,1)} %reshape.217), calls=%async_computation | async-start | bytes 2097152 | tf_op jit(solution)/shard_map/all_to_all | solution.py:277
  26.1 88.4 %collective-permute-start.8 = (bf16[256,1024]{1,0:T(8,128)(2,1)}, bf16[256,1024]{1,0:T(8,128)(2,1)}, u32[]{:S(2)}, u32[]{:S(2)}) collective-permute-start(bf16[256,1024]{1,0:T(8,128)(2,1)} %bitcast.11.right_ref), channel_id=1, source_target_pairs={{0,16},{16,0},{1,17},{17,1},{2,18},{18,2},{3,19},{19,3},{4,20},{20... | collective-permute-start | bytes 1572872 | tf_op jit(solution)/shard_map/ppermute | solution.py:290
  46.7 14.3 %copy-start.9 = (bf16[256,1024]{1,0:T(8,128)(2,1)}, bf16[256,1024]{1,0:T(8,128)(2,1)S(1)}, u32[]{:S(2)}) copy-start(bf16[256,1024]{1,0:T(8,128)(2,1)S(1)} %gather_fusion.1) | copy-start | bytes 1572868
  61.3 3.7 %copy-start.1 = (bf16[256,1024]{1,0:T(8,128)(2,1)}, bf16[256,1024]{1,0:T(8,128)(2,1)S(1)}, u32[]{:S(2)}) copy-start(bf16[256,1024]{1,0:T(8,128)(2,1)S(1)} %fusion.14.left_ref) | copy-start | bytes 1572868
  65.1 5.5 %copy-start.14 = (pred[32]{0:T(512)(128)(4,1)S(1)}, pred[32]{0:T(512)(128)(4,1)}, u32[]{:S(2)}) copy-start(pred[32]{0:T(512)(128)(4,1)} %constant.73.clone.1) | copy-start | bytes 100
  65.4 5.8 %collective-permute-start = (bf16[2,16,1024]{2,1,0:T(8,128)(2,1)S(1)}, bf16[2,16,1024]{2,1,0:T(8,128)(2,1)S(1)}, u32[]{:S(2)}, u32[]{:S(2)}) collective-permute-start(bf16[2,16,1024]{2,1,0:T(8,128)(2,1)S(1)} %get-tuple-element.45), channel_id=1, source_target_pairs={{0,1},{1,2},{2,3},{3,4},{4,5},{5,6},{6,7},{7,8},{8,9},{9,10},{10,1... | collective-permute-start | bytes 196616 | tf_op jit(solution)/shard_map/ppermute | solution.py:234
  69.3 6.2 %collective-permute-start.1 = (bf16[2,16,1024]{2,1,0:T(8,128)(2,1)S(1)}, bf16[2,16,1024]{2,1,0:T(8,128)(2,1)S(1)}, u32[]{:S(2)}, u32[]{:S(2)}) collective-permute-start(bf16[2,16,1024]{2,1,0:T(8,128)(2,1)S(1)} %get-tuple-element.44), channel_id=1, source_target_pairs={{1,0},{2,1},{3,2},{4,3},{5,4},{6,5},{7,6},{8,7},{9,8},{10,9},{11,1... | collective-permute-start | bytes 196616 | tf_op jit(solution)/shard_map/ppermute | solution.py:235
  84.6 1.0 copy-start.3
  85.6 0.7 copy-start.5
  86.3 28.2 %collective-permute-start.7 = (bf16[256,1024]{1,0:T(8,128)(2,1)}, bf16[256,1024]{1,0:T(8,128)(2,1)}, u32[]{:S(2)}, u32[]{:S(2)}) collective-permute-start(bf16[256,1024]{1,0:T(8,128)(2,1)} %get-tuple-element.13.left_ref), channel_id=1, source_target_pairs={{0,16},{16,0},{1,17},{17,1},{2,18},{18,2},{3,19},{19,3},{4,20},{20... | collective-permute-start | bytes 1572872 | tf_op jit(solution)/shard_map/ppermute | solution.py:326
  89.2 2.6 %copy-start.4 = (f32[256,1024]{1,0:T(8,128)S(1)}, f32[256,1024]{1,0:T(8,128)}, u32[]{:S(2)}) copy-start(f32[256,1024]{1,0:T(8,128)} %copy-done.3) | copy-start | bytes 3145732
  89.2 2.6 %copy-start.6 = (f32[256,128]{1,0:T(8,128)S(1)}, f32[256,128]{1,0:T(8,128)}, u32[]{:S(2)}) copy-start(f32[256,128]{1,0:T(8,128)} %copy-done.5) | copy-start | bytes 393220
  94.0 5.2 %collective-permute-start.2 = (bf16[2,16,1024]{2,1,0:T(8,128)(2,1)S(1)}, bf16[2,16,1024]{2,1,0:T(8,128)(2,1)S(1)}, u32[]{:S(2)}, u32[]{:S(2)}) collective-permute-start(bf16[2,16,1024]{2,1,0:T(8,128)(2,1)S(1)} %get-tuple-element.43), channel_id=1, source_target_pairs={{0,1},{1,2},{2,3},{3,4},{4,5},{5,6},{6,7},{7,8},{8,9},{9,10},{10,1... | collective-permute-start | bytes 196616 | tf_op jit(solution)/shard_map/ppermute | solution.py:234
  97.3 6.2 %collective-permute-start.3 = (bf16[2,16,1024]{2,1,0:T(8,128)(2,1)S(1)}, bf16[2,16,1024]{2,1,0:T(8,128)(2,1)S(1)}, u32[]{:S(2)}, u32[]{:S(2)}) collective-permute-start(bf16[2,16,1024]{2,1,0:T(8,128)(2,1)S(1)} %get-tuple-element.42), channel_id=1, source_target_pairs={{1,0},{2,1},{3,2},{4,3},{5,4},{6,5},{7,6},{8,7},{9,8},{10,9},{11,1... | collective-permute-start | bytes 196616 | tf_op jit(solution)/shard_map/ppermute | solution.py:235
  113.8 0.7 copy-start.7
  114.5 17.5 %collective-permute-start.5 = (bf16[256,2048]{1,0:T(8,128)(2,1)}, bf16[256,2048]{1,0:T(8,128)(2,1)S(1)}, u32[]{:S(2)}, u32[]{:S(2)}) collective-permute-start(bf16[256,2048]{1,0:T(8,128)(2,1)} %get-tuple-element.17.right_ref), channel_id=1, source_target_pairs={{0,16},{16,0},{1,17},{17,1},{2,18},{18,2},{3,19},{19,3},{4,20},{20... | collective-permute-start | bytes 3145736 | tf_op jit(solution)/shard_map/ppermute | solution.py:363
  114.5 15.3 %copy-start.2 = (bf16[256,1024]{1,0:T(8,128)(2,1)S(1)}, bf16[256,1024]{1,0:T(8,128)(2,1)}, u32[]{:S(2)}) copy-start(bf16[256,1024]{1,0:T(8,128)(2,1)} %copy-done.1) | copy-start | bytes 1572868
  114.5 15.7 %copy-start.8 = (f32[32,1024]{1,0:T(8,128)S(1)}, f32[32,1024]{1,0:T(8,128)}, u32[]{:S(2)}) copy-start(f32[32,1024]{1,0:T(8,128)} %copy-done.7) | copy-start | bytes 393220
  118.9 30.1 %all-to-all-start.2 = ((bf16[64,8,1024]{2,1,0:T(8,128)(2,1)}), bf16[64,8,1024]{2,1,0:T(8,128)(2,1)}, u32[]{:S(2)}, u32[]{:S(2)}) async-start(bf16[64,8,1024]{2,1,0:T(8,128)(2,1)} %bitcast.18), calls=%async_computation.2 | async-start | bytes 2097152 | tf_op jit(solution)/shard_map/all_to_all | solution.py:342
  129.8 2.2 %collective-permute-start.4 = (bf16[256,1024]{1,0:T(8,128)(2,1)S(1)}, bf16[256,1024]{1,0:T(8,128)(2,1)S(1)}, u32[]{:S(2)}, u32[]{:S(2)}) collective-permute-start(bf16[256,1024]{1,0:T(8,128)(2,1)S(1)} %copy-done.2), channel_id=1, source_target_pairs={{0,16},{16,0},{1,17},{17,1},{2,18},{18,2},{3,19},{19,3},{4,20},{20... | collective-permute-start | bytes 1572872 | tf_op jit(solution)/shard_map/ppermute | solution.py:327
  130.3 1.7 collective-permute-start.6
  149.0 5.1 %copy-start.15 = (bf16[128,2]{0,1:T(2,128)(2,1)S(1)}, bf16[128,2]{0,1:T(2,128)(2,1)}, u32[]{:S(2)}) copy-start(bf16[128,2]{0,1:T(2,128)(2,1)} %param.14) | copy-start | bytes 1540
  149.0 5.2 %copy-start.10 = (bf16[256,1024]{1,0:T(8,128)(2,1)S(1)}, bf16[256,1024]{1,0:T(8,128)(2,1)}, u32[]{:S(2)}) copy-start(bf16[256,1024]{1,0:T(8,128)(2,1)} %copy-done.9) | copy-start | bytes 1572868
  149.0 35.5 %all-to-all-start.1 = ((bf16[64,8,2176]{2,1,0:T(8,128)(2,1)}), bf16[64,8,2176]{2,1,0:T(8,128)(2,1)S(1)}, u32[]{:S(2)}, u32[]{:S(2)}) async-start(bf16[64,8,2176]{2,1,0:T(8,128)(2,1)} %bitcast.15), calls=%async_computation.1 | async-start | bytes 4456448 | tf_op jit(solution)/shard_map/all_to_all | solution.py:342
  184.8 5.7 %copy-start.11 = (f32[256,1024]{1,0:T(8,128)S(1)}, f32[256,1024]{1,0:T(8,128)}, u32[]{:S(2)}) copy-start(f32[256,1024]{1,0:T(8,128)} %get-tuple-element.51) | copy-start | bytes 3145732
  186.9 17.1 %all-to-all-start.3 = ((bf16[16,8,3200]{2,1,0:T(8,128)(2,1)}), bf16[16,8,3200]{2,1,0:T(8,128)(2,1)S(1)}, u32[]{:S(2)}, u32[]{:S(2)}) async-start(bf16[16,8,3200]{2,1,0:T(8,128)(2,1)} %broadcast_in_dim.85), calls=%async_computation.3 | async-start | bytes 1638400 | tf_op jit(solution)/shard_map/all_to_all | solution.py:226
Sparse Core Ops, SparseCore 0:
  10.3 49.7 all-gather.2
  61.8 27.3 all-gather.4

commit v3 on v2

--- a/solution.py
+++ b/solution.py
@@ -18,20 +18,18 @@
 
 
 def forward_kernel(
-    gated_ref, low_ref, high_ref, ids_ref, taps_ref, gain_ref,
+    gated_ref, ids_ref, taps_ref, gain_ref,
     act_ref, normed_ref, scale_ref, pad_ref, mix_ref,
 ):
-    slabs, frames, width = gated_ref.shape
+    slabs, padded, width = gated_ref.shape
     blocks = width // LANES
     taps_count = taps_ref.shape[1] - 1
+    wide = padded - 2 * EDGE
     shift = EDGE - taps_count // 2
 
     def one_slab(s, carry):
         for b in range(blocks):
-            cols = slice(b * LANES, (b + 1) * LANES)
-            pad_ref[b, 0:EDGE] = low_ref[s, :, cols].astype(jnp.float32)
-            pad_ref[b, EDGE : EDGE + frames] = gated_ref[s, :, cols].astype(jnp.float32)
-            pad_ref[b, EDGE + frames :] = high_ref[s, :, cols].astype(jnp.float32)
+            pad_ref[b] = gated_ref[s, :, b * LANES : (b + 1) * LANES].astype(jnp.float32)
 
         def conv_step(i, carry):
             row = pl.multiple_of((i // (blocks // 2)) * ROWS_STEP, ROWS_STEP)
@@ -47,11 +45,11 @@
                 mix_ref[b + j, pl.ds(row, ROWS_STEP)] = sums[j]
             return carry
 
-        lax.fori_loop(0, (frames // ROWS_STEP) * (blocks // 2), conv_step, 0)
+        lax.fori_loop(0, (wide // ROWS_STEP) * (blocks // 2), conv_step, 0)
 
         def row_step(i, carry):
             row = pl.multiple_of(i * 16, 16)
-            out_row = pl.multiple_of(s * frames + i * 16, 16)
+            out_row = pl.multiple_of(s * wide + i * 16, 16)
             mixing = jnp.concatenate([mix_ref[b, pl.ds(row, 16)] for b in range(blocks)], axis=1)
             centered = mixing - jnp.mean(mixing, axis=-1, keepdims=True)
             scale = lax.rsqrt(jnp.mean(centered * centered, axis=-1, keepdims=True) + EPS)
@@ -62,7 +60,7 @@
             scale_ref[pl.ds(out_row, 16), :] = jnp.broadcast_to(scale, (16, LANES))
             return carry
 
-        return lax.fori_loop(0, frames // 16, row_step, carry)
+        return lax.fori_loop(0, wide // 16, row_step, carry)
 
     lax.fori_loop(0, slabs, one_slab, 0)
 
@@ -80,7 +78,9 @@
         sig = jax.nn.sigmoid(value)
         grad_value = grad_act_ref[pl.ds(row, 16), :] * (sig * (1.0 + value * (1.0 - sig)))
         part = grad_value * normed
-        total = total + (part[0:8] + part[8:16])
+        at = i % steps
+        own = jnp.logical_and(at > 0, at < steps - 1)
+        total = total + jnp.where(own, part[0:8] + part[8:16], 0.0)
         grad_normed = grad_value * gain
         first = jnp.mean(grad_normed, axis=-1, keepdims=True)
         second = jnp.mean(grad_normed * normed, axis=-1, keepdims=True)
@@ -95,10 +95,11 @@
 
 
 def backward_kernel(
-    grad_mix_ref, low_ref, high_ref, gated_ref, ids_ref, taps_ref, hidden_ref,
+    grad_mix_ref, gated_ref, ids_ref, taps_ref, hidden_ref,
     grad_hidden_ref, grad_taps_ref, pad_ref, sum_ref,
 ):
-    slabs, frames, width = gated_ref.shape
+    slabs, padded, width = gated_ref.shape
+    frames = padded - 4 * EDGE
     blocks = width // LANES
     taps_count = taps_ref.shape[1] - 1
     half = taps_count // 2
@@ -106,22 +107,20 @@
 
     def one_slab(s, carry):
         for b in range(blocks):
-            cols = slice(b * LANES, (b + 1) * LANES)
-            pad_ref[b, 0:EDGE] = low_ref[s, :, cols].astype(jnp.float32)
-            pad_ref[b, EDGE : EDGE + frames] = grad_mix_ref[s, :, cols].astype(jnp.float32)
-            pad_ref[b, EDGE + frames :] = high_ref[s, :, cols].astype(jnp.float32)
+            pad_ref[b] = grad_mix_ref[s, :, b * LANES : (b + 1) * LANES]
 
         def conv_step(i, carry):
             row = pl.multiple_of((i // (blocks // 2)) * ROWS_STEP, ROWS_STEP)
             out_row = pl.multiple_of(s * frames + row, ROWS_STEP)
             b = (i % (blocks // 2)) * 2
-            center = ids_ref[s, pl.ds(row + EDGE, ROWS_STEP)]
+            hid_row = pl.multiple_of(s * padded + 2 * EDGE + row, ROWS_STEP)
+            center = ids_ref[s, pl.ds(row + 2 * EDGE, ROWS_STEP)]
             sums = [jnp.zeros((ROWS_STEP, LANES), jnp.float32) for _ in range(2)]
             cols = [pl.ds(pl.multiple_of((b + j) * LANES, LANES), LANES) for j in range(2)]
-            here = [gated_ref[s, pl.ds(row, ROWS_STEP), cols[j]].astype(jnp.float32) for j in range(2)]
+            here = [gated_ref[s, pl.ds(row + 2 * EDGE, ROWS_STEP), cols[j]].astype(jnp.float32) for j in range(2)]
             for k in range(taps_count):
                 at = row + EDGE + half - k
-                same = ids_ref[s, pl.ds(at, ROWS_STEP)] == center
+                same = ids_ref[s, pl.ds(at + EDGE, ROWS_STEP)] == center
                 for j in range(2):
                     term = jnp.where(same, pad_ref[b + j, pl.ds(at, ROWS_STEP)], 0.0)
                     sums[j] = sums[j] + term * taps_ref[b + j, k : k + 1, :]
@@ -130,10 +129,10 @@
                         (part[0:8] + part[8:16]) + (part[16:24] + part[24:32])
                     )
             for j in range(2):
-                lin = hidden_ref[pl.ds(out_row, ROWS_STEP), cols[j]]
+                lin = hidden_ref[pl.ds(hid_row, ROWS_STEP), cols[j]]
                 sig = jax.nn.sigmoid(
                     hidden_ref[
-                        pl.ds(out_row, ROWS_STEP),
+                        pl.ds(hid_row, ROWS_STEP),
                         pl.ds(pl.multiple_of(width + (b + j) * LANES, LANES), LANES),
                     ]
                 )
@@ -156,6 +155,41 @@
         grad_taps_ref[taps_count:, b * LANES : (b + 1) * LANES] = jnp.zeros(
             (grad_taps_ref.shape[0] - taps_count, LANES), jnp.float32
         )
+
+
+def send_kernel(index_ref, rows_ref, out_ref):
+    rows, width = rows_ref.shape
+    pick = (lax.broadcasted_iota(jnp.int32, (index_ref.shape[0], rows), 1) == index_ref[...])
+    pick = pick.astype(jnp.float32).astype(jnp.bfloat16)
+    for h in range(2):
+        part = jnp.dot(
+            pick,
+            rows_ref[:, h * (width // 2) : (h + 1) * (width // 2)],
+            preferred_element_type=jnp.float32,
+        )
+        slots = part.shape[0] // out_ref.shape[0]
+        out_ref[:, h * slots : (h + 1) * slots, :] = part.astype(jnp.bfloat16).reshape(
+            out_ref.shape[0], slots, width // 2
+        )
+
+
+def receive_kernel(index_ref, arrived_ref, out_ref):
+    slots, half = arrived_ref.shape
+    columns = lax.broadcasted_iota(jnp.int32, (index_ref.shape[0], slots), 1)
+    for h in range(2):
+        pick = (columns == index_ref[:, h : h + 1]).astype(jnp.float32).astype(jnp.bfloat16)
+        out_ref[:, h * half : (h + 1) * half] = jnp.dot(
+            pick, arrived_ref[...], preferred_element_type=jnp.float32
+        ).astype(jnp.bfloat16)
+
+
+def finish_kernel(final_ref, grad_in_ref, grad_out_ref, grad_taps_ref, grad_gains_ref):
+    in_width, taps_count = grad_in_ref.shape[1], grad_taps_ref.shape[0]
+    grad_in_ref[...] = final_ref[:, :in_width].astype(jnp.float32)
+    grad_out_ref[...] = final_ref[:, in_width + LANES :].astype(jnp.float32)
+    small = final_ref[:, in_width : in_width + LANES].astype(jnp.float32).T
+    grad_taps_ref[...] = small[:taps_count]
+    grad_gains_ref[...] = small[taps_count : taps_count + 2]
 
 
 def product_kernel(core_ref, left_ref, left_other_ref, right_ref, right_other_ref, *rest):
@@ -228,11 +262,11 @@
     )
 
 
-def edges(block, count):
+def edges(block, count, reach):
     forward = [(i, i + 1) for i in range(count - 1)]
     backward = [(i + 1, i) for i in range(count - 1)]
-    low = lax.ppermute(block[:, -EDGE:].astype(jnp.bfloat16), SEQ, forward)
-    high = lax.ppermute(block[:, :EDGE].astype(jnp.bfloat16), SEQ, backward)
+    low = lax.ppermute(block[:, -reach:], SEQ, forward)
+    high = lax.ppermute(block[:, :reach], SEQ, backward)
     return low, high
 
 
@@ -258,85 +292,106 @@
     sender = lax.axis_index((*DP, *SEQ))
     swap = [(0, 1), (1, 0)]
 
-    extras = jnp.pad(
-        jnp.concatenate([depth_kernel, norm_gains], axis=1), ((0, 0), (0, LANES - kernel_len - 2))
-    )
-    in_all = lax.all_gather(jnp.concatenate([in_weight, extras], axis=1), DP, axis=0, tiled=True)
+    in_full = lax.all_gather(in_weight, DP, axis=0, tiled=True)
     out_full = lax.all_gather(out_weight, DP, axis=0, tiled=True)
-    in_full = in_all[:, : 2 * width]
 
     send_plan = lax.dynamic_index_in_dim(plan, sender, 0, keepdims=False)
     send_start = jnp.cumsum(send_plan) - send_plan
     slot_index = jnp.arange(capacity, dtype=jnp.int32)
     source_rows = jnp.minimum(send_start[:, None] + slot_index[None, :], rows_dev - 1)
-    outgoing = (
-        loaded.at[source_rows.reshape(-1)]
-        .get(mode="promise_in_bounds")
-        .reshape(devices, capacity, width)
+    outgoing = kernel_call(
+        send_kernel,
+        jax.ShapeDtypeStruct((devices, 2 * capacity, width // 2), jnp.bfloat16),
+        [],
+        4 * devices * capacity * rows_dev * width,
+        source_rows.reshape(-1, 1), loaded,
     )
     arrived = lax.all_to_all(
         outgoing, (*DP, *SEQ), split_axis=0, concat_axis=0, tiled=True
-    ).reshape(devices * capacity, width)
+    ).reshape(devices * 2 * capacity, width // 2)
     recv_plan = lax.dynamic_index_in_dim(plan, sender, 1, keepdims=False)
     recv_end = jnp.cumsum(recv_plan)
     frame_index = jnp.arange(rows_dev, dtype=jnp.int32)
     before = recv_end[None, :] <= frame_index[:, None]
     source_dev = jnp.sum(before.astype(jnp.int32), axis=1)
     start_of = jnp.sum(jnp.where(before, recv_plan[None, :], 0), axis=1)
-    frames = arrived.at[source_dev * capacity + frame_index - start_of].get(
-        mode="promise_in_bounds"
-    )
-    upstream_rows = upstream.reshape(rows_dev, width)
-    upstream_other = lax.ppermute(upstream_rows, "core", swap)
-
-    id_pad = jnp.pad(segment_ids, ((0, 0), (EDGE, EDGE)), constant_values=-1)
-    window = lax.dynamic_slice_in_dim(
-        id_pad, lax.axis_index(SEQ) * frames_dev, frames_dev + 2 * EDGE, 1
-    )
-    ids = jnp.broadcast_to(window[:, :, None], (*window.shape, LANES))
-
-    side = in_all[:, 2 * width : 2 * width + kernel_len + 2].astype(jnp.float32).T
+    place = source_dev * 2 * capacity + frame_index - start_of
+    frames = kernel_call(
+        receive_kernel,
+        jax.ShapeDtypeStruct((rows_dev, width), jnp.bfloat16),
+        [],
+        4 * devices * capacity * rows_dev * width,
+        jnp.stack([place, place + capacity], axis=1), arrived,
+    )
+    extras = jnp.pad(
+        jnp.concatenate([depth_kernel, norm_gains], axis=1), ((0, 0), (0, LANES - kernel_len - 2))
+    )
+    extras, frames = lax.optimization_barrier((extras, frames))
+    low, high = edges(frames.reshape(slabs, frames_dev, width), n_seq, 2 * EDGE)
+    side_all = spread(extras, DP, n_z * 2)
+    side = side_all.reshape(width, LANES)[:, : kernel_len + 2].astype(jnp.float32).T
     gain_pre, gain_mid = side[kernel_len], side[kernel_len + 1]
     taps = jnp.pad(side[:kernel_len], ((0, 1), (0, 0)))
     taps = taps.reshape(kernel_len + 1, width // LANES, LANES).transpose(1, 0, 2)
 
+    upstream_rows = upstream.reshape(rows_dev, width)
+    upstream_other = lax.ppermute(upstream_rows, "core", swap)
+    up_low, up_high = edges(upstream, n_seq, EDGE)
+    upstream_wide = jnp.concatenate([up_low, upstream, up_high], axis=1).reshape(-1, width)
+
+    id_pad = jnp.pad(segment_ids, ((0, 0), (2 * EDGE, 2 * EDGE)), constant_values=-1)
+    window = lax.dynamic_slice_in_dim(
+        id_pad, lax.axis_index(SEQ) * frames_dev, frames_dev + 4 * EDGE, 1
+    )
+    ids = jnp.broadcast_to(window[:, :, None], (*window.shape, LANES))
+
     frame_rows = frames.astype(jnp.float32)
-    normed_full, pull_pre = jax.vjp(norm_rows, frame_rows, gain_pre)
-    normed = normed_full.astype(jnp.bfloat16)
-    hidden = jnp.dot(normed, in_full, preferred_element_type=jnp.float32)
+    _, pull_pre = jax.vjp(norm_rows, frame_rows, gain_pre)
+    padded = frames_dev + 4 * EDGE
+    frames_wide = jnp.concatenate(
+        [low, frames.reshape(slabs, frames_dev, width), high], axis=1
+    ).reshape(-1, width)
+    normed_wide = norm_rows(frames_wide.astype(jnp.float32), gain_pre).astype(jnp.bfloat16)
+    hidden = jnp.dot(normed_wide, in_full, preferred_element_type=jnp.float32)
     gated = (
         (hidden[:, :width] * jax.nn.sigmoid(hidden[:, width:]))
         .astype(jnp.bfloat16)
-        .reshape(slabs, frames_dev, width)
-    )
-    low, high = edges(gated, n_seq)
+        .reshape(slabs, padded, width)
+    )
+    normed = normed_wide.reshape(slabs, padded, width)[:, 2 * EDGE : 2 * EDGE + frames_dev]
+    normed = normed.reshape(rows_dev, width)
     elements = rows_dev * width
-    blocked = pltpu.VMEM((width // LANES, frames_dev + 2 * EDGE, LANES), jnp.float32)
-    activated, normed_mid, scale_mid = kernel_call(
+    wide = frames_dev + 2 * EDGE
+    blocks = width // LANES
+    act_wide, normed_mid, scale_mid = kernel_call(
         forward_kernel,
         (
-            jax.ShapeDtypeStruct((rows_dev, width), jnp.bfloat16),
-            jax.ShapeDtypeStruct((rows_dev, width), jnp.float32),
-            jax.ShapeDtypeStruct((rows_dev, LANES), jnp.float32),
-        ),
-        [blocked, pltpu.VMEM((width // LANES, frames_dev, LANES), jnp.float32)],
+            jax.ShapeDtypeStruct((slabs * wide, width), jnp.bfloat16),
+            jax.ShapeDtypeStruct((slabs * wide, width), jnp.float32),
+            jax.ShapeDtypeStruct((slabs * wide, LANES), jnp.float32),
+        ),
+        [
+            pltpu.VMEM((blocks, padded, LANES), jnp.float32),
+            pltpu.VMEM((blocks, wide, LANES), jnp.float32),
+        ],
         elements * 3 * kernel_len,
-        gated, low, high, ids, taps, gain_mid[None],
-    )
+        gated, ids, taps, gain_mid[None],
+    )
+    activated = act_wide.reshape(slabs, wide, width)[:, EDGE : EDGE + frames_dev]
+    activated = activated.reshape(rows_dev, width)
     act_other = lax.ppermute(activated, "core", swap)
     normed_other = lax.ppermute(normed, "core", swap)
-    grad_act = jnp.dot(upstream_rows, out_full.T, preferred_element_type=jnp.float32)
+    grad_act = jnp.dot(upstream_wide, out_full.T, preferred_element_type=jnp.float32)
     grad_mixing, grad_gain_mid = kernel_call(
         middle_kernel,
         (
-            jax.ShapeDtypeStruct((slabs, frames_dev, width), jnp.float32),
+            jax.ShapeDtypeStruct((slabs, wide, width), jnp.float32),
             jax.ShapeDtypeStruct((8, width), jnp.float32),
         ),
         [],
         elements * 30,
         normed_mid, scale_mid, grad_act, gain_mid[None],
     )
-    grad_low, grad_high = edges(grad_mixing, n_seq)
 
     def summed(part):
         arrived_parts = lax.all_to_all(
@@ -356,9 +411,12 @@
             jax.ShapeDtypeStruct((rows_dev, 2 * width), jnp.bfloat16),
             jax.ShapeDtypeStruct((kernel_len + 1, width), jnp.float32),
         ),
-        [blocked, pltpu.VMEM((width // LANES, kernel_len, 8, LANES), jnp.float32)],
+        [
+            pltpu.VMEM((blocks, wide, LANES), jnp.float32),
+            pltpu.VMEM((blocks, kernel_len, 8, LANES), jnp.float32),
+        ],
         elements * 5 * kernel_len,
-        grad_mixing, grad_low, grad_high, gated, ids, taps, hidden,
+        grad_mixing, gated, ids, taps, hidden,
     )
     hidden_other = lax.ppermute(grad_hidden, "core", swap)
     small = jnp.concatenate(
@@ -396,15 +454,20 @@
     total = (
         jnp.concatenate([in_sum[:, : 2 * width], small_sum, out_sum], axis=1) * scale
     ).astype(jnp.bfloat16)
-    final = spread(total, SEQ, n_seq).reshape(LANES, total.shape[1]).astype(jnp.float32)
-    return (
-        encoded,
-        grad_frames,
-        final[:, : 2 * width],
-        final[:, 2 * width + LANES :],
-        final[:, 2 * width : 2 * width + kernel_len],
-        final[:, 2 * width + kernel_len : 2 * width + kernel_len + 2],
-    )
+    final = spread(total, SEQ, n_seq).reshape(LANES, total.shape[1])
+    grad_in, grad_out, grad_kernel, grad_gains = kernel_call(
+        finish_kernel,
+        (
+            jax.ShapeDtypeStruct((LANES, 2 * width), jnp.float32),
+            jax.ShapeDtypeStruct((LANES, width), jnp.float32),
+            jax.ShapeDtypeStruct((kernel_len, LANES), jnp.float32),
+            jax.ShapeDtypeStruct((2, LANES), jnp.float32),
+        ),
+        [],
+        LANES * width,
+        final,
+    )
+    return encoded, grad_frames, grad_in, grad_out, grad_kernel.T, grad_gains.T
 
 
 def solution(mesh):

time: 215 us -> 200 us (0.930)
  waiting for transfers between devices: 90 us -> 67.5 us
  Pallas kernels: 30.4 us -> 35.5 us
  local copies, waits for them, and re-layouts: 13.5 us -> 8.72 us
  other arithmetic: 10.1 us -> 14.8 us
  starting transfers between devices: 41.4 us -> 45.5 us
    all_gather x1, waiting for transfers between devices: 12.9 us -> 0.01 us  [per_device(): in_full = lax.all_gather(in_weight, DP, axis=0, tiled=True)]
    ppermute x4, waiting for transfers between devices: 9.62 us -> 0.01 us  [the longest x2 0.01 us: edges(): low = lax.ppermute(block[:, -reach:], SEQ, forward)]
    pallas_call x3 -> x6, Pallas kernels: 21.5 us -> 26.7 us  [kernel_call(): pl.pallas_call(body, out_shape=outs, scratch_shapes=scratch, compiler_par...]
    all_to_all x1 -> x2, starting transfers between devices: 3.62 us -> 7.03 us  [spread(): lax.all_to_all(jnp.broadcast_to(shard[None], (count, *shard.shape)), axes...]
    gather x2 -> x0, local copies, waits for them, and re-layouts: 3.23 us -> none  [the longest x1 2.06 us: per_device(): outgoing = loaded.at[source_rows.reshape(-1)].get(mode='promise_in_bounds...]
    convert_element_type x2 -> x3, other arithmetic: 0.4 us -> 3.38 us  [the longest x2 3.22 us: per_device(): norm_rows(frames_wide.astype(jnp.float32), gain_pre).astype(jnp.bfloat16)]
    all_gather x1, waiting for transfers between devices: 2.98 us -> 0.01 us  [per_device(): out_full = lax.all_gather(out_weight, DP, axis=0, tiled=True)]
    all_to_all x1 -> x2, waiting for transfers between devices: 10.8 us -> 13.2 us  [spread(): lax.all_to_all(jnp.broadcast_to(shard[None], (count, *shard.shape)), axes...]
  transfers between devices with their start and end apart: 15 -> 16, of which waited for: 11 -> 7; matrix products, arithmetic and copies ran while one was open for 13% -> 14% of each run, Pallas kernels for 14% -> 17%
where the time goes in v3:
time: 200 us; the launch traced here: 199 us
  waiting for transfers between devices  67.5 us (34%)
  starting transfers between devices  45.5 us (23%)
  Pallas kernels  35.5 us (18%)
  other arithmetic  14.8 us (7%)
  between operations  14.5 us (7%)
  matrix products  12.4 us (6%)
  local copies, waits for them, and re-layouts  8.72 us (4%)
    all_to_all x2, waiting for transfers between devices, summed(): lax.all_to_all(part.reshape(n_z * n_seq, LANES // n_seq, part.shape[1]),...  34 us
    pallas_call x6, Pallas kernels, kernel_call(): pl.pallas_call(body, out_shape=outs, scratch_shapes=scratch, compiler_par...  26.7 us
    all_to_all x1, waiting for transfers between devices, per_device(): lax.all_to_all(outgoing, (*DP, *SEQ), split_axis=0, concat_axis=0, tiled=...  17.5 us
    all_to_all x2, starting transfers between devices, summed(): lax.all_to_all(part.reshape(n_z * n_seq, LANES // n_seq, part.shape[1]),...  16.1 us
    all_to_all x2, waiting for transfers between devices, spread(): lax.all_to_all(jnp.broadcast_to(shard[None], (count, *shard.shape)), axes...  13.2 us
    all_to_all x1, starting transfers between devices, per_device(): lax.all_to_all(outgoing, (*DP, *SEQ), split_axis=0, concat_axis=0, tiled=...  11.2 us
    pallas_call x2, Pallas kernels, weight_part(): pl.pallas_call(product_kernel, out_shape=jax.ShapeDtypeStruct((mine * LAN...  8.82 us
    ppermute x2, starting transfers between devices, edges(): low = lax.ppermute(block[:, -reach:], SEQ, forward)  7.18 us
  transfers between devices with their start and end apart: 16, of which 7 were waited for; matrix products, arithmetic and copies ran while one was open for 14% of the time, Pallas kernels for 17%

profile of v3, /device:TPU:0, one launch (start us, length us, event | category | flops | bytes accessed | tf_op | source)
XLA Modules:
  0.0 198.9 jit_solution(14977195045352625765)
XLA Ops:
  11.0 1.5 shard_map.127
  12.4 11.2 %all-to-all-start = ((bf16[128,8,512]{2,1,0:T(8,128)(2,1)}), bf16[128,8,512]{2,1,0:T(8,128)(2,1)S(1)}, u32[]{:S(2)}, u32[]{:S(2)}) async-start(bf16[128,8,512]{2,1,0:T(8,128)(2,1)} %shard_map.127), calls=%async_computation | async-start | bytes 2097152 | tf_op jit(solution)/shard_map/all_to_all | solution.py:309
  25.2 17.5 %all-to-all-done = bf16[128,8,512]{2,1,0:T(8,128)(2,1)S(1)} async-done(((bf16[128,8,512]{2,1,0:T(8,128)(2,1)}), bf16[128,8,512]{2,1,0:T(8,128)(2,1)S(1)}, u32[]{:S(2)}, u32[]{:S(2)}) %all-to-all-start) | async-done | bytes 1048608 | tf_op jit(solution)/shard_map/all_to_all | solution.py:309
  43.6 2.6 %collective-permute-start = (bf16[2,32,1024]{2,1,0:T(8,128)(2,1)S(1)}, bf16[2,32,1024]{2,1,0:T(8,128)(2,1)S(1)}, u32[]{:S(2)}, u32[]{:S(2)}) collective-permute-start(bf16[2,32,1024]{2,1,0:T(8,128)(2,1)S(1)} %get-tuple-element.44), channel_id=1, source_target_pairs={{0,1},{1,2},{2,3},{3,4},{4,5},{5,6},{6,7},{7,8},{8,9},{9,10},{10,1... | collective-permute-start | bytes 393224 | tf_op jit(solution)/shard_map/ppermute | solution.py:268
  46.2 1.3 collective-permute-start.1
  47.5 4.5 %collective-permute-start.2 = (bf16[2,16,1024]{2,1,0:T(8,128)(2,1)S(1)}, bf16[2,16,1024]{2,1,0:T(8,128)(2,1)S(1)}, u32[]{:S(2)}, u32[]{:S(2)}) collective-permute-start(bf16[2,16,1024]{2,1,0:T(8,128)(2,1)S(1)} %get-tuple-element.42), channel_id=1, source_target_pairs={{0,1},{1,2},{2,3},{3,4},{4,5},{5,6},{6,7},{7,8},{8,9},{9,10},{10,1... | collective-permute-start | bytes 196616 | tf_op jit(solution)/shard_map/ppermute | solution.py:268
  52.1 1.3 collective-permute-start.3
  54.3 3.4 %all-to-all-start.1 = ((bf16[8,128,128]{1,2,0:T(8,128)(2,1)}), bf16[8,128,128]{1,2,0:T(8,128)(2,1)S(1)}, u32[]{:S(2)}, u32[]{:S(2)}) async-start(bf16[8,128,128]{1,2,0:T(8,128)(2,1)} %broadcast_in_dim.81), calls=%async_computation.1 | async-start | bytes 524288 | tf_op jit(solution)/shard_map/all_to_all | solution.py:260
  58.0 1.4 broadcast_subtract_fusion
  60.9 4.3 %all-to-all-done.1 = bf16[8,128,128]{1,2,0:T(8,128)(2,1)S(1)} async-done(((bf16[8,128,128]{1,2,0:T(8,128)(2,1)}), bf16[8,128,128]{1,2,0:T(8,128)(2,1)S(1)}, u32[]{:S(2)}, u32[]{:S(2)}) %all-to-all-start.1) | async-done | bytes 262176 | tf_op jit(solution)/shard_map/all_to_all | solution.py:260
  66.0 1.8 fusion.6
  67.8 4.2 %fusion.31.hidden_ref = f32[384,2048]{1,0:T(8,128)S(1)} fusion(bf16[384,1024]{1,0:T(8,128)(2,1)} %fusion.6, bf16[1024,2048]{1,0:T(8,128)(2,1)} %all-gather.3.cloned.1.call-done), kind=kOutput, calls=%fused_computation.76 | convolution fusion | flops 1610612736 | bytes 8126464 | tf_op jit(solution)/shard_map/dot_general | solution.py:355
  72.5 1.2 copy-done.4
  73.8 10.0 %shard_map.129 = (bf16[320,1024]{1,0:T(8,128)(2,1)S(1)}, f32[320,1024]{1,0:T(8,128)S(1)}, f32[320,128]{1,0:T(8,128)S(1)}) custom-call(bf16[2,192,1024]{2,1,0:T(8,128)(2,1)S(1)} %bitcast.65, s32[2,192,128]{2,1,0:T(8,128)S(1)} %broadcast_in_dim.82.ids_ref, f32[8,32,128]{2,1,0:T(8,128)S(1)} %bitcast_bitcast_fusion.taps_ref, ...), custom_call_target="tpu_custom_call" | custom-call | flops 24379392 | bytes 1118208 | tf_op jit(solution)/shard_map/pallas_call | solution.py:250
  86.0 2.8 %fusion.32.grad_act_ref = f32[320,1024]{1,0:T(8,128)S(1)} fusion(bf16[320,1024]{1,0:T(8,128)(2,1)} %bitcast.77, bf16[1024,1024]{1,0:T(8,128)(2,1)} %all-gather.5.cloned.1.call-done), kind=kOutput, calls=%fused_computation.77 | convolution fusion | flops 671088640 | bytes 4063232 | tf_op jit(solution)/shard_map/dot_general | solution.py:384
  88.8 2.5 %shard_map.130 = (f32[2,160,1024]{2,1,0:T(8,128)S(1)}, f32[8,1024]{1,0:T(8,128)S(1)}) custom-call(f32[320,1024]{1,0:T(8,128)S(1)} %copy-done.2, f32[320,128]{1,0:T(8,128)S(1)} %get-tuple-element.23.scale_ref, f32[320,1024]{1,0:T(8,128)S(1)} %fusion.32.grad_act_ref, f32[1,1024]{1,0:T(1,128)S(1)} %get-tuple-element.46.gain_ref), custom_call_target="tpu_custom_call" | custom-call | flops 7864320 | bytes 2789376 | tf_op jit(solution)/shard_map/pallas_call | solution.py:250
  91.4 10.7 %shard_map.131 = (bf16[256,2048]{1,0:T(8,128)(2,1)}, f32[32,1024]{1,0:T(8,128)S(1)}) custom-call(f32[2,160,1024]{2,1,0:T(8,128)S(1)} %get-tuple-element.24.grad_mix_ref, bf16[2,192,1024]{2,1,0:T(8,128)(2,1)S(1)} %bitcast.66, s32[2,192,128]{2,1,0:T(8,128)S(1)} %broadcast_in_dim.82.ids_ref, f32[8,32,128]{2,1,0:T(8,128)S(1)} %bitcast_bitcast_fusion.taps_ref, ...), custom_call_target="tpu_custom_call" | custom-call | flops 40632320 | bytes 5570560 | tf_op jit(solution)/shard_map/pallas_call | solution.py:250
  102.5 4.1 %weight_part.3 = bf16[512,1024]{1,0:T(8,128)(2,1)} custom-call(s32[1]{0:T(128)} %bitcast.17.core_ref, bf16[256,1024]{1,0:T(8,128)(2,1)S(1)} %bitcast.73, bf16[256,1024]{1,0:T(8,128)(2,1)} %collective-permute-done.7.left_other_ref, bf16[256,1024]{1,0:T(8,128)(2,1)S(1)} %bitcast.68, bf16[256,1024]{1,0:T(8,128)(2,1)} %collective-permute-done.8.right_other_ref), custom_call_target="tpu_custom_call" | custom-call | flops 536870912 | bytes 2097152 | tf_op jit(solution)/shard_map/weight_part/pallas_call | solution.py:228
  106.6 10.3 %all-to-all-start.3 = ((bf16[64,8,1024]{2,1,0:T(8,128)(2,1)}), bf16[64,8,1024]{2,1,0:T(8,128)(2,1)}, u32[]{:S(2)}, u32[]{:S(2)}) async-start(bf16[64,8,1024]{2,1,0:T(8,128)(2,1)} %bitcast.23), calls=%async_computation.3 | async-start | bytes 2097152 | tf_op jit(solution)/shard_map/all_to_all | solution.py:397
  116.9 1.4 fusion.15
  120.5 4.8 %weight_part.2 = bf16[512,2176]{1,0:T(8,128)(2,1)} custom-call(s32[1]{0:T(128)} %bitcast.17.core_ref, bf16[256,1024]{1,0:T(8,128)(2,1)S(1)} %bitcast.71, bf16[256,1024]{1,0:T(8,128)(2,1)S(1)} %collective-permute-done.4.left_other_ref, bf16[256,2048]{1,0:T(8,128)(2,1)} %get-tuple-element.25.right_ref, ...), custom_call_target="tpu_custom_call" | custom-call | flops 1073741824 | bytes 3145728 | tf_op jit(solution)/shard_map/weight_part/pallas_call | solution.py:228
  125.3 10.3 %all-to-all-done.3 = bf16[64,8,1024]{2,1,0:T(8,128)(2,1)} async-done(((bf16[64,8,1024]{2,1,0:T(8,128)(2,1)}), bf16[64,8,1024]{2,1,0:T(8,128)(2,1)}, u32[]{:S(2)}, u32[]{:S(2)}) %all-to-all-start.3) | async-done | bytes 1048608 | tf_op jit(solution)/shard_map/all_to_all | solution.py:397
  135.6 5.8 %all-to-all-start.2 = ((bf16[64,8,2176]{2,1,0:T(8,128)(2,1)}), bf16[64,8,2176]{2,1,0:T(8,128)(2,1)}, u32[]{:S(2)}, u32[]{:S(2)}) async-start(bf16[64,8,2176]{2,1,0:T(8,128)(2,1)} %bitcast.20), calls=%async_computation.2 | async-start | bytes 4456448 | tf_op jit(solution)/shard_map/all_to_all | solution.py:397
  141.7 3.9 %fusion.12 = (f32[256]{0:T(256)S(1)}, f32[256]{0:T(256)S(1)}, f32[256,1024]{1,0:T(8,128)S(1)}) fusion(bf16[256,1024]{1,0:T(8,128)(2,1)S(1)} %shard_map.128, f32[256]{0:T(256)S(1)} %broadcast_multiply_fusion.1, f32[1024]{0:T(1024)S(1)} %bitcast.81, bf16[256,2048]{1,0:T(8,128)(2,1)} %get-tuple-element.25.right_ref, ...), kind=kOutput, calls=%fused_computation.22 | convolution fusion | flops 1075576320 | bytes 6822912 | tf_op jit(solution)/shard_map/dot_general | solution.py:435
  146.0 1.4 convert_reduce_fusion.1
  147.4 23.7 %all-to-all-done.2 = bf16[64,8,2176]{2,1,0:T(8,128)(2,1)} async-done(((bf16[64,8,2176]{2,1,0:T(8,128)(2,1)}), bf16[64,8,2176]{2,1,0:T(8,128)(2,1)}, u32[]{:S(2)}, u32[]{:S(2)}) %all-to-all-start.2) | async-done | bytes 2228256 | tf_op jit(solution)/shard_map/all_to_all | solution.py:397
  171.1 2.0 convert_reduce_fusion
  175.0 3.6 %all-to-all-start.4 = ((bf16[16,8,3200]{2,1,0:T(8,128)(2,1)}), bf16[16,8,3200]{2,1,0:T(8,128)(2,1)S(1)}, u32[]{:S(2)}, u32[]{:S(2)}) async-start(bf16[16,8,3200]{2,1,0:T(8,128)(2,1)} %broadcast_in_dim.92), calls=%async_computation.4 | async-start | bytes 1638400 | tf_op jit(solution)/shard_map/all_to_all | solution.py:260
  178.7 1.2 add_convert_fusion
  180.4 1.5 fusion.11
  181.9 8.9 %all-to-all-done.4 = bf16[16,8,3200]{2,1,0:T(8,128)(2,1)S(1)} async-done(((bf16[16,8,3200]{2,1,0:T(8,128)(2,1)}), bf16[16,8,3200]{2,1,0:T(8,128)(2,1)S(1)}, u32[]{:S(2)}, u32[]{:S(2)}) %all-to-all-start.4) | async-done | bytes 819232 | tf_op jit(solution)/shard_map/all_to_all | solution.py:260
  190.9 1.2 shard_map.132
  (93 shorter events, 18.0 us)
Async XLA Ops:
  7.2 60.7 %all-gather.3.cloned.1.call-start = ((), (), s32[]{:S(2)}) async-start(), calls=%async_computation.5 | async-start | bytes 4718592 | tf_op jit(solution)/shard_map/all_gather | solution.py:295
  9.9 1.0 copy-start.3
  12.4 11.9 %copy-start.5 = (s32[128,128]{1,0:T(8,128)S(1)}, s32[128,128]{1,0:T(8,128)}, u32[]{:S(2)}) copy-start(s32[128,128]{1,0:T(8,128)} %param.9) | copy-start | bytes 196612
  12.4 12.8 %copy-start.7 = (bf16[128,31]{0,1:T(8,128)(2,1)S(1)}, bf16[128,31]{0,1:T(8,128)(2,1)}, u32[]{:S(2)}) copy-start(bf16[128,31]{0,1:T(8,128)(2,1)} %param.13) | copy-start | bytes 23812
  12.4 12.8 %copy-start.8 = (bf16[128,2]{0,1:T(2,128)(2,1)S(1)}, bf16[128,2]{0,1:T(2,128)(2,1)}, u32[]{:S(2)}) copy-start(bf16[128,2]{0,1:T(2,128)(2,1)} %param.14) | copy-start | bytes 1540
  12.4 30.3 %all-to-all-start = ((bf16[128,8,512]{2,1,0:T(8,128)(2,1)}), bf16[128,8,512]{2,1,0:T(8,128)(2,1)S(1)}, u32[]{:S(2)}, u32[]{:S(2)}) async-start(bf16[128,8,512]{2,1,0:T(8,128)(2,1)} %shard_map.127), calls=%async_computation | async-start | bytes 2097152 | tf_op jit(solution)/shard_map/all_to_all | solution.py:309
  23.6 62.4 %all-gather.5.cloned.1.call-start = ((), (), s32[]{:S(2)}) async-start(), calls=%async_computation.6 | async-start | bytes 2359296 | tf_op jit(solution)/shard_map/all_gather | solution.py:296
  24.4 23.1 %copy-start = (bf16[2,128,1024]{2,1,0:T(8,128)(2,1)S(1)}, bf16[2,128,1024]{2,1,0:T(8,128)(2,1)}, u32[]{:S(2)}) copy-start(bf16[2,128,1024]{2,1,0:T(8,128)(2,1)} %param.15) | copy-start | bytes 1572868
  24.6 28.9 %copy-start.6 = (s32[2,2048]{1,0:T(2,128)S(1)}, s32[2,2048]{1,0:T(2,128)}, u32[]{:S(2)}) copy-start(s32[2,2048]{1,0:T(2,128)} %param.10) | copy-start | bytes 49156
  43.6 14.2 %collective-permute-start = (bf16[2,32,1024]{2,1,0:T(8,128)(2,1)S(1)}, bf16[2,32,1024]{2,1,0:T(8,128)(2,1)S(1)}, u32[]{:S(2)}, u32[]{:S(2)}) collective-permute-start(bf16[2,32,1024]{2,1,0:T(8,128)(2,1)S(1)} %get-tuple-element.44), channel_id=1, source_target_pairs={{0,1},{1,2},{2,3},{3,4},{4,5},{5,6},{6,7},{7,8},{8,9},{9,10},{10,1... | collective-permute-start | bytes 393224 | tf_op jit(solution)/shard_map/ppermute | solution.py:268
  46.2 11.6 %collective-permute-start.1 = (bf16[2,32,1024]{2,1,0:T(8,128)(2,1)S(1)}, bf16[2,32,1024]{2,1,0:T(8,128)(2,1)S(1)}, u32[]{:S(2)}, u32[]{:S(2)}) collective-permute-start(bf16[2,32,1024]{2,1,0:T(8,128)(2,1)S(1)} %get-tuple-element.45), channel_id=1, source_target_pairs={{1,0},{2,1},{3,2},{4,3},{5,4},{6,5},{7,6},{8,7},{9,8},{10,9},{11,1... | collective-permute-start | bytes 393224 | tf_op jit(solution)/shard_map/ppermute | solution.py:269
  47.5 37.6 %collective-permute-start.2 = (bf16[2,16,1024]{2,1,0:T(8,128)(2,1)S(1)}, bf16[2,16,1024]{2,1,0:T(8,128)(2,1)S(1)}, u32[]{:S(2)}, u32[]{:S(2)}) collective-permute-start(bf16[2,16,1024]{2,1,0:T(8,128)(2,1)S(1)} %get-tuple-element.42), channel_id=1, source_target_pairs={{0,1},{1,2},{2,3},{3,4},{4,5},{5,6},{6,7},{7,8},{8,9},{9,10},{10,1... | collective-permute-start | bytes 196616 | tf_op jit(solution)/shard_map/ppermute | solution.py:268
  52.1 33.1 %collective-permute-start.3 = (bf16[2,16,1024]{2,1,0:T(8,128)(2,1)S(1)}, bf16[2,16,1024]{2,1,0:T(8,128)(2,1)S(1)}, u32[]{:S(2)}, u32[]{:S(2)}) collective-permute-start(bf16[2,16,1024]{2,1,0:T(8,128)(2,1)S(1)} %get-tuple-element.43), channel_id=1, source_target_pairs={{1,0},{2,1},{3,2},{4,3},{5,4},{6,5},{7,6},{8,7},{9,8},{10,9},{11,1... | collective-permute-start | bytes 196616 | tf_op jit(solution)/shard_map/ppermute | solution.py:269
  53.4 49.1 %collective-permute-start.8 = (bf16[256,1024]{1,0:T(8,128)(2,1)S(1)}, bf16[256,1024]{1,0:T(8,128)(2,1)}, u32[]{:S(2)}, u32[]{:S(2)}) collective-permute-start(bf16[256,1024]{1,0:T(8,128)(2,1)S(1)} %bitcast.67), channel_id=1, source_target_pairs={{0,16},{16,0},{1,17},{17,1},{2,18},{18,2},{3,19},{19,3},{4,20},{20... | collective-permute-start | bytes 1572872 | tf_op jit(solution)/shard_map/ppermute | solution.py:338
  54.3 10.9 %all-to-all-start.1 = ((bf16[8,128,128]{1,2,0:T(8,128)(2,1)}), bf16[8,128,128]{1,2,0:T(8,128)(2,1)S(1)}, u32[]{:S(2)}, u32[]{:S(2)}) async-start(bf16[8,128,128]{1,2,0:T(8,128)(2,1)} %broadcast_in_dim.81), calls=%async_computation.1 | async-start | bytes 524288 | tf_op jit(solution)/shard_map/all_to_all | solution.py:260
  72.1 1.7 copy-start.4
  83.9 1.1 copy-start.1
  85.0 17.5 %collective-permute-start.7 = (bf16[256,1024]{1,0:T(8,128)(2,1)S(1)}, bf16[256,1024]{1,0:T(8,128)(2,1)}, u32[]{:S(2)}, u32[]{:S(2)}) collective-permute-start(bf16[256,1024]{1,0:T(8,128)(2,1)S(1)} %bitcast.72), channel_id=1, source_target_pairs={{0,16},{16,0},{1,17},{17,1},{2,18},{18,2},{3,19},{19,3},{4,20},{20... | collective-permute-start | bytes 1572872 | tf_op jit(solution)/shard_map/ppermute | solution.py:382
  86.0 2.8 %copy-start.2 = (f32[320,1024]{1,0:T(8,128)S(1)}, f32[320,1024]{1,0:T(8,128)}, u32[]{:S(2)}) copy-start(f32[320,1024]{1,0:T(8,128)} %copy-done.1) | copy-start | bytes 3932164
  102.0 18.5 %collective-permute-start.5 = (bf16[256,2048]{1,0:T(8,128)(2,1)}, bf16[256,2048]{1,0:T(8,128)(2,1)}, u32[]{:S(2)}, u32[]{:S(2)}) collective-permute-start(bf16[256,2048]{1,0:T(8,128)(2,1)} %get-tuple-element.25.right_ref), channel_id=1, source_target_pairs={{0,16},{16,0},{1,17},{17,1},{2,18},{18,2},{3,19},{19,3},{4,20},{20... | collective-permute-start | bytes 3145736 | tf_op jit(solution)/shard_map/ppermute | solution.py:421
  106.6 29.0 %all-to-all-start.3 = ((bf16[64,8,1024]{2,1,0:T(8,128)(2,1)}), bf16[64,8,1024]{2,1,0:T(8,128)(2,1)}, u32[]{:S(2)}, u32[]{:S(2)}) async-start(bf16[64,8,1024]{2,1,0:T(8,128)(2,1)} %bitcast.23), calls=%async_computation.3 | async-start | bytes 2097152 | tf_op jit(solution)/shard_map/all_to_all | solution.py:397
  118.3 2.0 %collective-permute-start.4 = (bf16[256,1024]{1,0:T(8,128)(2,1)S(1)}, bf16[256,1024]{1,0:T(8,128)(2,1)S(1)}, u32[]{:S(2)}, u32[]{:S(2)}) collective-permute-start(bf16[256,1024]{1,0:T(8,128)(2,1)S(1)} %bitcast.70), channel_id=1, source_target_pairs={{0,16},{16,0},{1,17},{17,1},{2,18},{18,2},{3,19},{19,3},{4,20},{20... | collective-permute-start | bytes 1572872 | tf_op jit(solution)/shard_map/ppermute | solution.py:383
  118.6 1.9 collective-permute-start.6
  135.6 5.9 %copy-start.9 = (bf16[128,2]{0,1:T(2,128)(2,1)S(1)}, bf16[128,2]{0,1:T(2,128)(2,1)}, u32[]{:S(2)}) copy-start(bf16[128,2]{0,1:T(2,128)(2,1)} %param.14) | copy-start | bytes 1540
  135.6 35.5 %all-to-all-start.2 = ((bf16[64,8,2176]{2,1,0:T(8,128)(2,1)}), bf16[64,8,2176]{2,1,0:T(8,128)(2,1)}, u32[]{:S(2)}, u32[]{:S(2)}) async-start(bf16[64,8,2176]{2,1,0:T(8,128)(2,1)} %bitcast.20), calls=%async_computation.2 | async-start | bytes 4456448 | tf_op jit(solution)/shard_map/all_to_all | solution.py:397
  175.0 15.9 %all-to-all-start.4 = ((bf16[16,8,3200]{2,1,0:T(8,128)(2,1)}), bf16[16,8,3200]{2,1,0:T(8,128)(2,1)S(1)}, u32[]{:S(2)}, u32[]{:S(2)}) async-start(bf16[16,8,3200]{2,1,0:T(8,128)(2,1)} %broadcast_in_dim.92), calls=%async_computation.4 | async-start | bytes 1638400 | tf_op jit(solution)/shard_map/all_to_all | solution.py:260
  178.7 1.8 copy-start.10
Sparse Core Ops, SparseCore 0:
  9.7 45.9 all-gather.2
  57.4 25.3 all-gather.4

commit v4 on v3

--- a/solution.py
+++ b/solution.py
@@ -95,7 +95,7 @@
 
 
 def backward_kernel(
-    grad_mix_ref, gated_ref, ids_ref, taps_ref, hidden_ref,
+    grad_mix_ref, gated_ref, ids_ref, taps_ref, lin_ref, sig_ref,
     grad_hidden_ref, grad_taps_ref, pad_ref, sum_ref,
 ):
     slabs, padded, width = gated_ref.shape
@@ -129,13 +129,8 @@
                         (part[0:8] + part[8:16]) + (part[16:24] + part[24:32])
                     )
             for j in range(2):
-                lin = hidden_ref[pl.ds(hid_row, ROWS_STEP), cols[j]]
-                sig = jax.nn.sigmoid(
-                    hidden_ref[
-                        pl.ds(hid_row, ROWS_STEP),
-                        pl.ds(pl.multiple_of(width + (b + j) * LANES, LANES), LANES),
-                    ]
-                )
+                lin = lin_ref[pl.ds(hid_row, ROWS_STEP), cols[j]]
+                sig = sig_ref[pl.ds(hid_row, ROWS_STEP), cols[j]]
                 grad_lin = sums[j] * sig
                 grad_hidden_ref[pl.ds(out_row, ROWS_STEP), cols[j]] = grad_lin.astype(jnp.bfloat16)
                 grad_hidden_ref[
@@ -193,29 +188,32 @@
 
 
 def product_kernel(core_ref, left_ref, left_other_ref, right_ref, right_other_ref, *rest):
-    out_ref = rest[-1]
+    small_refs, out_ref, turned_ref = rest[:-2], rest[-2], rest[-1]
+    rows, channels = left_ref.shape
     width = right_ref.shape[1]
     step = 512
-    left, left_other = left_ref[...], left_other_ref[...]
-    over_rows = (((0,), (0,)), ((), ()))
+    picks = [
+        pl.ds(pl.multiple_of((2 * z + core_ref[0]) * LANES, LANES), LANES)
+        for z in range(channels // LANES // 2)
+    ]
+    for z, pick in enumerate(picks):
+        for h, ref in enumerate((left_ref, left_other_ref)):
+            turned_ref[z * LANES : (z + 1) * LANES, h * rows : (h + 1) * rows] = ref[:, pick].T
     for at in range(0, width, step):
-        out_ref[:, at : at + step] = (
-            lax.dot_general(
-                left, right_ref[:, at : at + step], over_rows, preferred_element_type=jnp.float32
+        right = jnp.concatenate(
+            [right_ref[:, at : at + step], right_other_ref[:, at : at + step]], axis=0
+        )
+        out_ref[:, at : at + step] = jnp.dot(
+            turned_ref[...], right, preferred_element_type=jnp.float32
+        ).astype(out_ref.dtype)
+    if small_refs:
+        for z, pick in enumerate(picks):
+            small = small_refs[0][:, pick] + small_refs[1][:, pick]
+            filled = jnp.concatenate(
+                [small, jnp.zeros((LANES - small.shape[0], LANES), jnp.float32)], axis=0
             )
-            + lax.dot_general(
-                left_other,
-                right_other_ref[:, at : at + step],
-                over_rows,
-                preferred_element_type=jnp.float32,
-            )
-        ).astype(out_ref.dtype)
-    if len(rest) > 1:
-        small = rest[0][...] + rest[1][...]
-        filled = jnp.concatenate(
-            [small, jnp.zeros((LANES - small.shape[0], LANES), jnp.float32)], axis=0
-        )
-        out_ref[:, width:] = filled.T.astype(out_ref.dtype)
+            block = slice(z * LANES, (z + 1) * LANES)
+            out_ref[block, width : width + LANES] = filled.T.astype(out_ref.dtype)
 
 
 def weight_part(core, left, left_other, right, right_other, *small):
@@ -223,18 +221,13 @@
     mine = channels // LANES // 2
     width = right.shape[1]
     out_width = width + (LANES if small else 0)
-    picked = lambda height: pl.BlockSpec((height, LANES), lambda z, c: (0, 2 * z + c[0]))
-    whole = lambda a: pl.BlockSpec(a.shape, lambda z, c: (0, 0))
+    vmem = pl.BlockSpec(memory_space=pltpu.VMEM)
     return pl.pallas_call(
         product_kernel,
         out_shape=jax.ShapeDtypeStruct((mine * LANES, out_width), jnp.bfloat16),
-        grid_spec=pltpu.PrefetchScalarGridSpec(
-            num_scalar_prefetch=1,
-            grid=(mine,),
-            in_specs=[picked(rows), picked(rows), whole(right), whole(right_other)]
-            + [picked(a.shape[0]) for a in small],
-            out_specs=pl.BlockSpec((LANES, out_width), lambda z, c: (z, 0)),
-        ),
+        in_specs=[pl.BlockSpec(memory_space=pltpu.SMEM)] + [vmem] * (4 + len(small)),
+        out_specs=vmem,
+        scratch_shapes=[pltpu.VMEM((mine * LANES, 2 * rows), jnp.bfloat16)],
         name="weight_part",
         compiler_params=pltpu.CompilerParams(vmem_limit_bytes=48 * 1024 * 1024),
         cost_estimate=pl.CostEstimate(
@@ -243,6 +236,72 @@
             transcendentals=0,
         ),
     )(core, left, left_other, right, right_other, *small)
+
+
+def norm_kernel(frames_ref, low_ref, high_ref, gain_ref, wide_ref, own_ref):
+    slabs, padded, _ = wide_ref.shape
+    reach = low_ref.shape[1]
+    own = padded - 2 * reach
+
+    def normed_rows(rows):
+        values = rows.astype(jnp.float32)
+        centered = values - jnp.mean(values, axis=-1, keepdims=True)
+        spread_ = jnp.mean(centered * centered, axis=-1, keepdims=True)
+        return (centered * lax.rsqrt(spread_ + EPS) * gain_ref[0:1, :]).astype(jnp.bfloat16)
+
+    for s in range(slabs):
+        for at in range(0, reach, 16):
+            wide_ref[s, at : at + 16, :] = normed_rows(low_ref[s, at : at + 16, :])
+            high_at = reach + own + at
+            wide_ref[s, high_at : high_at + 16, :] = normed_rows(high_ref[s, at : at + 16, :])
+
+    def step(i, carry):
+        row = pl.multiple_of(i * 16, 16)
+        rows = normed_rows(frames_ref[pl.ds(row, 16), :])
+        own_ref[pl.ds(row, 16), :] = rows
+        steps = own // 16
+        wide_ref[i // steps, pl.ds(pl.multiple_of(reach + (i % steps) * 16, 16), 16), :] = rows
+        return carry
+
+    lax.fori_loop(0, slabs * own // 16, step, 0, unroll=2)
+
+
+def project_kernel(normed_ref, lin_w_ref, gate_w_ref, lin_ref, sig_ref, gated_ref):
+    lin = jnp.dot(normed_ref[...], lin_w_ref[...], preferred_element_type=jnp.float32)
+    gate = jnp.dot(normed_ref[...], gate_w_ref[...], preferred_element_type=jnp.float32)
+    sig = jax.nn.sigmoid(gate)
+    lin_ref[...] = lin
+    sig_ref[...] = sig
+    gated_ref[...] = (lin * sig).astype(jnp.bfloat16)
+
+
+def project(normed, weight):
+    rows, width = normed.shape
+    cols = 256
+    steps = width // cols
+    out = pl.BlockSpec((rows, cols), lambda j: (0, j))
+    return pl.pallas_call(
+        project_kernel,
+        out_shape=(
+            jax.ShapeDtypeStruct((rows, width), jnp.float32),
+            jax.ShapeDtypeStruct((rows, width), jnp.float32),
+            jax.ShapeDtypeStruct((rows, width), jnp.bfloat16),
+        ),
+        grid=(steps,),
+        in_specs=[
+            pl.BlockSpec((rows, width), lambda j: (0, 0)),
+            pl.BlockSpec((width, cols), lambda j: (0, j)),
+            pl.BlockSpec((width, cols), lambda j: (0, j + steps)),
+        ],
+        out_specs=(out, out, out),
+        name="project",
+        compiler_params=pltpu.CompilerParams(vmem_limit_bytes=48 * 1024 * 1024),
+        cost_estimate=pl.CostEstimate(
+            flops=4 * rows * width * width,
+            bytes_accessed=4 * width * width,
+            transcendentals=rows * width,
+        ),
+    )(normed, weight, weight)
 
 
 def kernel_call(body, outs, scratch, flops, *args):
@@ -309,6 +368,26 @@
     arrived = lax.all_to_all(
         outgoing, (*DP, *SEQ), split_axis=0, concat_axis=0, tiled=True
     ).reshape(devices * 2 * capacity, width // 2)
+    extras = jnp.pad(
+        jnp.concatenate([depth_kernel, norm_gains], axis=1), ((0, 0), (0, LANES - kernel_len - 2))
+    )
+    upstream_rows = upstream.reshape(rows_dev, width)
+    up_low, up_high = edges(upstream, n_seq, EDGE)
+    extras_other = lax.ppermute(extras, "core", swap)
+    pair = jnp.where(
+        core == 0, jnp.stack([extras, extras_other]), jnp.stack([extras_other, extras])
+    )
+    from_z = [
+        lax.ppermute(pair, "z", [(i, (i + d) % n_z) for i in range(n_z)]) for d in range(1, n_z)
+    ]
+    upstream_other = lax.ppermute(upstream_rows, "core", swap)
+    arrived, up_low, up_high, upstream_other, pair, *from_z = lax.optimization_barrier(
+        (arrived, up_low, up_high, upstream_other, pair, *from_z)
+    )
+    by_z = jnp.stack([*from_z[::-1], pair])
+    side_all = lax.dynamic_slice_in_dim(
+        jnp.concatenate([by_z, by_z]), n_z - 1 - lax.axis_index("z"), n_z, 0
+    )
     recv_plan = lax.dynamic_index_in_dim(plan, sender, 1, keepdims=False)
     recv_end = jnp.cumsum(recv_plan)
     frame_index = jnp.arange(rows_dev, dtype=jnp.int32)
@@ -323,20 +402,12 @@
         4 * devices * capacity * rows_dev * width,
         jnp.stack([place, place + capacity], axis=1), arrived,
     )
-    extras = jnp.pad(
-        jnp.concatenate([depth_kernel, norm_gains], axis=1), ((0, 0), (0, LANES - kernel_len - 2))
-    )
-    extras, frames = lax.optimization_barrier((extras, frames))
     low, high = edges(frames.reshape(slabs, frames_dev, width), n_seq, 2 * EDGE)
-    side_all = spread(extras, DP, n_z * 2)
     side = side_all.reshape(width, LANES)[:, : kernel_len + 2].astype(jnp.float32).T
     gain_pre, gain_mid = side[kernel_len], side[kernel_len + 1]
     taps = jnp.pad(side[:kernel_len], ((0, 1), (0, 0)))
     taps = taps.reshape(kernel_len + 1, width // LANES, LANES).transpose(1, 0, 2)
 
-    upstream_rows = upstream.reshape(rows_dev, width)
-    upstream_other = lax.ppermute(upstream_rows, "core", swap)
-    up_low, up_high = edges(upstream, n_seq, EDGE)
     upstream_wide = jnp.concatenate([up_low, upstream, up_high], axis=1).reshape(-1, width)
 
     id_pad = jnp.pad(segment_ids, ((0, 0), (2 * EDGE, 2 * EDGE)), constant_values=-1)
@@ -348,18 +419,20 @@
     frame_rows = frames.astype(jnp.float32)
     _, pull_pre = jax.vjp(norm_rows, frame_rows, gain_pre)
     padded = frames_dev + 4 * EDGE
-    frames_wide = jnp.concatenate(
-        [low, frames.reshape(slabs, frames_dev, width), high], axis=1
-    ).reshape(-1, width)
-    normed_wide = norm_rows(frames_wide.astype(jnp.float32), gain_pre).astype(jnp.bfloat16)
-    hidden = jnp.dot(normed_wide, in_full, preferred_element_type=jnp.float32)
-    gated = (
-        (hidden[:, :width] * jax.nn.sigmoid(hidden[:, width:]))
-        .astype(jnp.bfloat16)
-        .reshape(slabs, padded, width)
-    )
-    normed = normed_wide.reshape(slabs, padded, width)[:, 2 * EDGE : 2 * EDGE + frames_dev]
-    normed = normed.reshape(rows_dev, width)
+    normed_wide, normed = kernel_call(
+        norm_kernel,
+        (
+            jax.ShapeDtypeStruct((slabs, padded, width), jnp.bfloat16),
+            jax.ShapeDtypeStruct((rows_dev, width), jnp.bfloat16),
+        ),
+        [],
+        rows_dev * width * 10,
+        frames, low, high, gain_pre[None],
+    )
+    normed_other = lax.ppermute(normed, "core", swap)
+    in_full, normed_other = lax.optimization_barrier((in_full, normed_other))
+    lin, sig, gated = project(normed_wide.reshape(-1, width), in_full)
+    gated = gated.reshape(slabs, padded, width)
     elements = rows_dev * width
     wide = frames_dev + 2 * EDGE
     blocks = width // LANES
@@ -380,7 +453,6 @@
     activated = act_wide.reshape(slabs, wide, width)[:, EDGE : EDGE + frames_dev]
     activated = activated.reshape(rows_dev, width)
     act_other = lax.ppermute(activated, "core", swap)
-    normed_other = lax.ppermute(normed, "core", swap)
     grad_act = jnp.dot(upstream_wide, out_full.T, preferred_element_type=jnp.float32)
     grad_mixing, grad_gain_mid = kernel_call(
         middle_kernel,
@@ -416,7 +488,7 @@
             pltpu.VMEM((blocks, kernel_len, 8, LANES), jnp.float32),
         ],
         elements * 5 * kernel_len,
-        grad_mixing, gated, ids, taps, hidden,
+        grad_mixing, gated, ids, taps, lin, sig,
     )
     hidden_other = lax.ppermute(grad_hidden, "core", swap)
     small = jnp.concatenate(

time: 200 us -> 200 us (level)
  Pallas kernels: 35.5 us -> 41.3 us
  other arithmetic: 14.8 us -> 9.47 us
  matrix products: 12.4 us -> 8.01 us
  local copies, waits for them, and re-layouts: 8.72 us -> 11.8 us
  starting transfers between devices: 45.5 us -> 47.7 us
    all_to_all x1, waiting for transfers between devices: 17.5 us -> 0.01 us  [per_device(): lax.all_to_all(outgoing, (*DP, *SEQ), split_axis=0, concat_axis=0, tiled=...]
    ppermute x0 -> x4, waiting for transfers between devices: none -> 6.46 us  [the longest x3 6.46 us: per_device(): lax.ppermute(pair, 'z', [(i, (i + d) % n_z) for i in range(n_z)])]
    all_gather x1, waiting for transfers between devices: 0.01 us -> 5.18 us  [per_device(): out_full = lax.all_gather(out_weight, DP, axis=0, tiled=True)]
    ppermute x0 -> x4, starting transfers between devices: none -> 4.9 us  [the longest x3 4.81 us: per_device(): lax.ppermute(pair, 'z', [(i, (i + d) % n_z) for i in range(n_z)])]
    unnamed x22 -> x51, local copies, waits for them, and re-layouts: 3.97 us -> 8.69 us
    pallas_call x0 -> x1, Pallas kernels: none -> 4.52 us  [project(): pl.pallas_call(project_kernel, out_shape=(jax.ShapeDtypeStruct((rows, wid...]
    dot_general x1 -> x0, matrix products: 4.23 us -> none  [per_device(): hidden = jnp.dot(normed_wide, in_full, preferred_element_type=jnp.float32)]
    convert_element_type x4 -> x0, other arithmetic: 3.81 us -> none  [the longest x2 3.22 us: per_device(): norm_rows(frames_wide.astype(jnp.float32), gain_pre).astype(jnp.bfloat16)]
  transfers between devices with their start and end apart: 16 -> 19, of which waited for: 7 -> 12; matrix products, arithmetic and copies ran while one was open for 14% -> 8% of each run, Pallas kernels for 17% -> 20%
where the time goes in v4:
time: 200 us; the launch traced here: 199 us
  waiting for transfers between devices  65.8 us (33%)
  starting transfers between devices  47.7 us (24%)
  Pallas kernels  41.3 us (21%)
  between operations  14.6 us (7%)
  local copies, waits for them, and re-layouts  11.8 us (6%)
  other arithmetic  9.47 us (5%)
  matrix products  8.01 us (4%)
    all_to_all x2, waiting for transfers between devices, summed(): lax.all_to_all(part.reshape(n_z * n_seq, LANES // n_seq, part.shape[1]),...  36.3 us
    pallas_call x7, Pallas kernels, kernel_call(): pl.pallas_call(body, out_shape=outs, scratch_shapes=scratch, compiler_par...  30.1 us
    all_to_all x2, starting transfers between devices, summed(): lax.all_to_all(part.reshape(n_z * n_seq, LANES // n_seq, part.shape[1]),...  15.3 us
    all_to_all x1, starting transfers between devices, per_device(): lax.all_to_all(outgoing, (*DP, *SEQ), split_axis=0, concat_axis=0, tiled=...  11.3 us
    all_to_all x1, waiting for transfers between devices, spread(): lax.all_to_all(jnp.broadcast_to(shard[None], (count, *shard.shape)), axes...  9.51 us
    ppermute x2, starting transfers between devices, edges(): low = lax.ppermute(block[:, -reach:], SEQ, forward)  9.1 us
    unnamed x51, local copies, waits for them, and re-layouts  8.69 us
    pallas_call x2, Pallas kernels, weight_part(): pl.pallas_call(product_kernel, out_shape=jax.ShapeDtypeStruct((mine * LAN...  6.74 us
  transfers between devices with their start and end apart: 19, of which 12 were waited for; matrix products, arithmetic and copies ran while one was open for 8% of the time, Pallas kernels for 20%

profile of v4, /device:TPU:0, one launch (start us, length us, event | category | flops | bytes accessed | tf_op | source)
XLA Modules:
  0.0 198.7 jit_solution(10501885926278544848)
XLA Ops:
  11.8 1.5 shard_map.127
  13.2 11.3 %all-to-all-start = ((bf16[128,8,512]{2,1,0:T(8,128)(2,1)}), bf16[128,8,512]{2,1,0:T(8,128)(2,1)S(1)}, u32[]{:S(2)}, u32[]{:S(2)}) async-start(bf16[128,8,512]{2,1,0:T(8,128)(2,1)} %shard_map.127), calls=%async_computation | async-start | bytes 2097152 | tf_op jit(solution)/shard_map/all_to_all | solution.py:368
  25.9 4.6 %collective-permute-start = (bf16[2,16,1024]{2,1,0:T(8,128)(2,1)S(1)}, bf16[2,16,1024]{2,1,0:T(8,128)(2,1)S(1)}, u32[]{:S(2)}, u32[]{:S(2)}) collective-permute-start(bf16[2,16,1024]{2,1,0:T(8,128)(2,1)S(1)} %get-tuple-element.69), channel_id=1, source_target_pairs={{0,1},{1,2},{2,3},{3,4},{4,5},{5,6},{6,7},{7,8},{8,9},{9,10},{10,1... | collective-permute-start | bytes 196616 | tf_op jit(solution)/shard_map/ppermute | solution.py:327
  31.3 2.9 %collective-permute-start.6 = (bf16[2,128,128]{1,2,0:T(8,128)(2,1)S(1)}, bf16[2,128,128]{1,2,0:T(8,128)(2,1)S(1)}, u32[]{:S(2)}, u32[]{:S(2)}) collective-permute-start(bf16[2,128,128]{1,2,0:T(8,128)(2,1)S(1)} %maximum_select_fusion), channel_id=1, source_target_pairs={{0,96},{32,0},{64,32},{96,64},{1,97},{33,1},{65,33},{97,65},{2,98}... | collective-permute-start | bytes 196616 | tf_op jit(solution)/shard_map/ppermute | solution.py:381
  34.5 3.5 %collective-permute-done.1 = bf16[2,16,1024]{2,1,0:T(8,128)(2,1)} collective-permute-done((bf16[2,16,1024]{2,1,0:T(8,128)(2,1)S(1)}, bf16[2,16,1024]{2,1,0:T(8,128)(2,1)}, u32[]{:S(2)}, u32[]{:S(2)}) %collective-permute-start.1) | collective-permute-done | bytes 65568 | tf_op jit(solution)/shard_map/ppermute | solution.py:328
  37.9 1.6 collective-permute-start.4
  39.7 2.5 %collective-permute-done.6 = bf16[2,128,128]{1,2,0:T(8,128)(2,1)S(1)} collective-permute-done((bf16[2,128,128]{1,2,0:T(8,128)(2,1)S(1)}, bf16[2,128,128]{1,2,0:T(8,128)(2,1)S(1)}, u32[]{:S(2)}, u32[]{:S(2)}) %collective-permute-start.6) | collective-permute-done | bytes 65568 | tf_op jit(solution)/shard_map/ppermute | solution.py:381
  42.2 2.0 %collective-permute-done.5 = bf16[2,128,128]{1,2,0:T(8,128)(2,1)S(1)} collective-permute-done((bf16[2,128,128]{1,2,0:T(8,128)(2,1)S(1)}, bf16[2,128,128]{1,2,0:T(8,128)(2,1)S(1)}, u32[]{:S(2)}, u32[]{:S(2)}) %collective-permute-start.5) | collective-permute-done | bytes 65568 | tf_op jit(solution)/shard_map/ppermute | solution.py:381
  44.2 1.9 collective-permute-done.4
  47.8 1.3 collective-permute-start.8
  49.1 4.6 %collective-permute-start.7 = (bf16[2,32,1024]{2,1,0:T(8,128)(2,1)S(1)}, bf16[2,32,1024]{2,1,0:T(8,128)(2,1)S(1)}, u32[]{:S(2)}, u32[]{:S(2)}) collective-permute-start(bf16[2,32,1024]{2,1,0:T(8,128)(2,1)S(1)} %get-tuple-element.67), channel_id=1, source_target_pairs={{0,1},{1,2},{2,3},{3,4},{4,5},{5,6},{6,7},{7,8},{8,9},{9,10},{10,1... | collective-permute-start | bytes 393224 | tf_op jit(solution)/shard_map/ppermute | solution.py:327
  54.7 1.5 collective-permute-done.7.low_ref
  56.2 1.8 shard_map.129
  60.8 4.5 %project.1 = (f32[384,1024]{1,0:T(8,128)S(1)}, f32[384,1024]{1,0:T(8,128)S(1)}, bf16[384,1024]{1,0:T(8,128)(2,1)S(1)}) custom-call(bf16[384,1024]{1,0:T(8,128)(2,1)S(1)} %bitcast.73, bf16[1024,2048]{1,0:T(8,128)(2,1)} %all-gather.3.cloned.1.call-done.lin_w_ref.gate_w_ref, bf16[1024,2048]{1,0:T(8,128)(2,1)} %all-gather.3.cloned.1.call-done.lin_w_ref.gate_w_ref), custom_call_target="tpu_custom_call" | custom-call | flops 1610612736 | bytes 4194304 | tf_op jit(solution)/shard_map/project/pallas_call | solution.py:283
  67.8 10.4 %shard_map.130 = (bf16[320,1024]{1,0:T(8,128)(2,1)S(1)}, f32[320,1024]{1,0:T(8,128)S(1)}, f32[320,128]{1,0:T(8,128)S(1)}) custom-call(bf16[2,192,1024]{2,1,0:T(8,128)(2,1)S(1)} %bitcast.67, s32[2,192,128]{2,1,0:T(8,128)S(1)} %broadcast_in_dim.73.ids_ref, f32[8,32,128]{2,1,0:T(8,128)S(1)} %bitcast_bitcast_fusion.taps_ref, ...), custom_call_target="tpu_custom_call" | custom-call | flops 24379392 | bytes 1118208 | tf_op jit(solution)/shard_map/pallas_call | solution.py:309
  80.5 5.2 %all-gather.5.cloned.1.call-done = bf16[1024,1024]{1,0:T(8,128)(2,1)} async-done(((bf16[128,1024]{1,0:T(8,128)(2,1)}), bf16[1024,1024]{1,0:T(8,128)(2,1)}) %all-gather.5.cloned.1.call-update) | async-done | bytes 2097168 | tf_op jit(solution)/shard_map/all_gather | solution.py:355
  85.7 2.6 %fusion.21.grad_act_ref = f32[320,1024]{1,0:T(8,128)S(1)} fusion(bf16[320,1024]{1,0:T(8,128)(2,1)S(1)} %bitcast.76, bf16[1024,1024]{1,0:T(8,128)(2,1)} %all-gather.5.cloned.1.call-done), kind=kOutput, calls=%fused_computation.67 | convolution fusion | flops 671088640 | bytes 4063232 | tf_op jit(solution)/shard_map/dot_general | solution.py:456
  88.3 2.5 %shard_map.131 = (f32[2,160,1024]{2,1,0:T(8,128)S(1)}, f32[8,1024]{1,0:T(8,128)S(1)}) custom-call(f32[320,1024]{1,0:T(8,128)S(1)} %copy-done.5, f32[320,128]{1,0:T(8,128)S(1)} %get-tuple-element.43.scale_ref, f32[320,1024]{1,0:T(8,128)S(1)} %fusion.21.grad_act_ref, f32[1,1024]{1,0:T(1,128)S(1)} %get-tuple-element.70.gain_ref), custom_call_target="tpu_custom_call" | custom-call | flops 7864320 | bytes 2789376 | tf_op jit(solution)/shard_map/pallas_call | solution.py:309
  90.9 11.9 %shard_map.132 = (bf16[256,2048]{1,0:T(8,128)(2,1)}, f32[32,1024]{1,0:T(8,128)S(1)}) custom-call(f32[2,160,1024]{2,1,0:T(8,128)S(1)} %get-tuple-element.46.grad_mix_ref, bf16[2,192,1024]{2,1,0:T(8,128)(2,1)S(1)} %bitcast.68, s32[2,192,128]{2,1,0:T(8,128)S(1)} %broadcast_in_dim.73.ids_ref, f32[8,32,128]{2,1,0:T(8,128)S(1)} %bitcast_bitcast_fusion.taps_ref, ...), custom_call_target="tpu_custom_call" | custom-call | flops 40632320 | bytes 5570560 | tf_op jit(solution)/shard_map/pallas_call | solution.py:309
  103.0 2.8 %weight_part.3 = bf16[512,1024]{1,0:T(8,128)(2,1)} custom-call(s32[1]{0:T(128)} %bitcast.23.core_ref, bf16[256,1024]{1,0:T(8,128)(2,1)S(1)} %bitcast.70, bf16[256,1024]{1,0:T(8,128)(2,1)} %collective-permute-done.12.left_other_ref, bf16[256,1024]{1,0:T(8,128)(2,1)S(1)} %bitcast.65, bf16[256,1024]{1,0:T(8,128)(2,1)S(1)} %copy-done.11), custom_call_target="tpu_custom_call" | custom-call | flops 536870912 | bytes 2097152 | tf_op jit(solution)/shard_map/weight_part/pallas_call | solution.py:225
  105.9 9.6 %all-to-all-start.2 = ((bf16[64,8,1024]{2,1,0:T(8,128)(2,1)}), bf16[64,8,1024]{2,1,0:T(8,128)(2,1)}, u32[]{:S(2)}, u32[]{:S(2)}) async-start(bf16[64,8,1024]{2,1,0:T(8,128)(2,1)} %bitcast.28), calls=%async_computation.2 | async-start | bytes 2097152 | tf_op jit(solution)/shard_map/all_to_all | solution.py:469
  116.0 1.4 collective-permute-done.11.rest_1_
  118.4 3.9 %weight_part.2 = bf16[512,2176]{1,0:T(8,128)(2,1)} custom-call(s32[1]{0:T(128)} %bitcast.23.core_ref, bf16[256,1024]{1,0:T(8,128)(2,1)S(1)} %copy-done.7, bf16[256,1024]{1,0:T(8,128)(2,1)S(1)} %copy-done.9, bf16[256,2048]{1,0:T(8,128)(2,1)} %get-tuple-element.49.right_ref, bf16[256,2048]{1,0:T(8,128)(2,1)S(1)} %collective-permute-done.10.right_other_ref, ...), custom_call_target="tpu_custom_call" | custom-call | flops 1073741824 | bytes 3145728 | tf_op jit(solution)/shard_map/weight_part/pallas_call | solution.py:225
  122.3 12.2 %all-to-all-done.2 = bf16[64,8,1024]{2,1,0:T(8,128)(2,1)} async-done(((bf16[64,8,1024]{2,1,0:T(8,128)(2,1)}), bf16[64,8,1024]{2,1,0:T(8,128)(2,1)}, u32[]{:S(2)}, u32[]{:S(2)}) %all-to-all-start.2) | async-done | bytes 1048608 | tf_op jit(solution)/shard_map/all_to_all | solution.py:469
  134.5 5.7 %all-to-all-start.1 = ((bf16[64,8,2176]{2,1,0:T(8,128)(2,1)}), bf16[64,8,2176]{2,1,0:T(8,128)(2,1)}, u32[]{:S(2)}, u32[]{:S(2)}) async-start(bf16[64,8,2176]{2,1,0:T(8,128)(2,1)} %bitcast.25), calls=%async_computation.1 | async-start | bytes 4456448 | tf_op jit(solution)/shard_map/all_to_all | solution.py:469
  140.4 3.9 %fusion.4 = (f32[256]{0:T(256)S(1)}, f32[256]{0:T(256)S(1)}, f32[256,1024]{1,0:T(8,128)S(1)}) fusion(bf16[256,1024]{1,0:T(8,128)(2,1)S(1)} %shard_map.128.frames_ref, f32[256]{0:T(256)S(1)} %broadcast_multiply_fusion, f32[1024]{0:T(1024)S(1)} %bitcast.75, bf16[256,2048]{1,0:T(8,128)(2,1)} %get-tuple-element.49.right_ref, ...), kind=kOutput, calls=%fused_computation.11 | convolution fusion | flops 1075576320 | bytes 6822912 | tf_op jit(solution)/shard_map/dot_general | solution.py:507
  144.8 1.4 convert_reduce_fusion.1
  146.2 24.2 %all-to-all-done.1 = bf16[64,8,2176]{2,1,0:T(8,128)(2,1)} async-done(((bf16[64,8,2176]{2,1,0:T(8,128)(2,1)}), bf16[64,8,2176]{2,1,0:T(8,128)(2,1)}, u32[]{:S(2)}, u32[]{:S(2)}) %all-to-all-start.1) | async-done | bytes 2228256 | tf_op jit(solution)/shard_map/all_to_all | solution.py:469
  170.3 2.0 convert_reduce_fusion
  174.2 3.6 %all-to-all-start.3 = ((bf16[16,8,3200]{2,1,0:T(8,128)(2,1)}), bf16[16,8,3200]{2,1,0:T(8,128)(2,1)S(1)}, u32[]{:S(2)}, u32[]{:S(2)}) async-start(bf16[16,8,3200]{2,1,0:T(8,128)(2,1)} %broadcast_in_dim.83), calls=%async_computation.3 | async-start | bytes 1638400 | tf_op jit(solution)/shard_map/all_to_all | solution.py:319
  179.6 1.5 fusion.3
  181.2 9.5 %all-to-all-done.3 = bf16[16,8,3200]{2,1,0:T(8,128)(2,1)S(1)} async-done(((bf16[16,8,3200]{2,1,0:T(8,128)(2,1)}), bf16[16,8,3200]{2,1,0:T(8,128)(2,1)S(1)}, u32[]{:S(2)}, u32[]{:S(2)}) %all-to-all-start.3) | async-done | bytes 819232 | tf_op jit(solution)/shard_map/all_to_all | solution.py:319
  (121 shorter events, 24.5 us)
Async XLA Ops:
  7.2 53.6 %all-gather.3.cloned.1.call-start = ((), (), s32[]{:S(2)}) async-start(), calls=%async_computation.4 | async-start | bytes 4718592 | tf_op jit(solution)/shard_map/all_gather | solution.py:354
  8.6 22.6 %collective-permute-start.3 = (bf16[128,128]{0,1:T(8,128)(2,1)S(1)}, bf16[128,128]{0,1:T(8,128)(2,1)S(1)}, u32[]{:S(2)}, u32[]{:S(2)}) collective-permute-start(bf16[128,128]{0,1:T(8,128)(2,1)S(1)} %get-tuple-element.75), channel_id=1, source_target_pairs={{0,16},{16,0},{1,17},{17,1},{2,18},{18,2},{3,19},{19,3},{4,20},{20... | collective-permute-start | bytes 98312 | tf_op jit(solution)/shard_map/ppermute | solution.py:376
  11.8 12.8 %copy-start = (bf16[2,128,1024]{2,1,0:T(8,128)(2,1)S(1)}, bf16[2,128,1024]{2,1,0:T(8,128)(2,1)}, u32[]{:S(2)}) copy-start(bf16[2,128,1024]{2,1,0:T(8,128)(2,1)} %param.15) | copy-start | bytes 1572868
  11.8 18.8 %copy-start.15 = (s32[128,128]{1,0:T(8,128)S(1)}, s32[128,128]{1,0:T(8,128)}, u32[]{:S(2)}) copy-start(s32[128,128]{1,0:T(8,128)} %param.9) | copy-start | bytes 196612
  13.2 33.7 %all-to-all-start = ((bf16[128,8,512]{2,1,0:T(8,128)(2,1)}), bf16[128,8,512]{2,1,0:T(8,128)(2,1)S(1)}, u32[]{:S(2)}, u32[]{:S(2)}) async-start(bf16[128,8,512]{2,1,0:T(8,128)(2,1)} %shard_map.127), calls=%async_computation | async-start | bytes 2097152 | tf_op jit(solution)/shard_map/all_to_all | solution.py:368
  24.5 61.2 %all-gather.5.cloned.1.call-start = ((), (), s32[]{:S(2)}) async-start(), calls=%async_computation.5 | async-start | bytes 2359296 | tf_op jit(solution)/shard_map/all_gather | solution.py:355
  24.6 13.4 %collective-permute-start.1 = (bf16[2,16,1024]{2,1,0:T(8,128)(2,1)S(1)}, bf16[2,16,1024]{2,1,0:T(8,128)(2,1)}, u32[]{:S(2)}, u32[]{:S(2)}) collective-permute-start(bf16[2,16,1024]{2,1,0:T(8,128)(2,1)S(1)} %get-tuple-element.68), channel_id=1, source_target_pairs={{1,0},{2,1},{3,2},{4,3},{5,4},{6,5},{7,6},{8,7},{9,8},{10,9},{11,1... | collective-permute-start | bytes 196616 | tf_op jit(solution)/shard_map/ppermute | solution.py:328
  25.9 13.8 %collective-permute-start = (bf16[2,16,1024]{2,1,0:T(8,128)(2,1)S(1)}, bf16[2,16,1024]{2,1,0:T(8,128)(2,1)S(1)}, u32[]{:S(2)}, u32[]{:S(2)}) collective-permute-start(bf16[2,16,1024]{2,1,0:T(8,128)(2,1)S(1)} %get-tuple-element.69), channel_id=1, source_target_pairs={{0,1},{1,2},{2,3},{3,4},{4,5},{5,6},{6,7},{7,8},{8,9},{9,10},{10,1... | collective-permute-start | bytes 196616 | tf_op jit(solution)/shard_map/ppermute | solution.py:327
  30.4 15.7 %collective-permute-start.2 = (bf16[256,1024]{1,0:T(8,128)(2,1)S(1)}, bf16[256,1024]{1,0:T(8,128)(2,1)S(1)}, u32[]{:S(2)}, u32[]{:S(2)}) collective-permute-start(bf16[256,1024]{1,0:T(8,128)(2,1)S(1)} %bitcast.64), channel_id=1, source_target_pairs={{0,16},{16,0},{1,17},{17,1},{2,18},{18,2},{3,19},{19,3},{4,20},{20... | collective-permute-start | bytes 1572872 | tf_op jit(solution)/shard_map/ppermute | solution.py:383
  31.3 10.9 %collective-permute-start.6 = (bf16[2,128,128]{1,2,0:T(8,128)(2,1)S(1)}, bf16[2,128,128]{1,2,0:T(8,128)(2,1)S(1)}, u32[]{:S(2)}, u32[]{:S(2)}) collective-permute-start(bf16[2,128,128]{1,2,0:T(8,128)(2,1)S(1)} %maximum_select_fusion), channel_id=1, source_target_pairs={{0,96},{32,0},{64,32},{96,64},{1,97},{33,1},{65,33},{97,65},{2,98}... | collective-permute-start | bytes 196616 | tf_op jit(solution)/shard_map/ppermute | solution.py:381
  34.2 10.1 %collective-permute-start.5 = (bf16[2,128,128]{1,2,0:T(8,128)(2,1)S(1)}, bf16[2,128,128]{1,2,0:T(8,128)(2,1)S(1)}, u32[]{:S(2)}, u32[]{:S(2)}) collective-permute-start(bf16[2,128,128]{1,2,0:T(8,128)(2,1)S(1)} %maximum_select_fusion), channel_id=1, source_target_pairs={{0,64},{32,96},{64,0},{96,32},{1,65},{33,97},{65,1},{97,33},{2,66}... | collective-permute-start | bytes 196616 | tf_op jit(solution)/shard_map/ppermute | solution.py:381
  37.9 8.2 %collective-permute-start.4 = (bf16[2,128,128]{1,2,0:T(8,128)(2,1)S(1)}, bf16[2,128,128]{1,2,0:T(8,128)(2,1)S(1)}, u32[]{:S(2)}, u32[]{:S(2)}) collective-permute-start(bf16[2,128,128]{1,2,0:T(8,128)(2,1)S(1)} %maximum_select_fusion), channel_id=1, source_target_pairs={{0,32},{32,64},{64,96},{96,0},{1,33},{33,65},{65,97},{97,1},{2,34}... | collective-permute-start | bytes 196616 | tf_op jit(solution)/shard_map/ppermute | solution.py:381
  39.7 16.5 %copy-start.16 = (bf16[2,16,1024]{2,1,0:T(8,128)(2,1)}, bf16[2,16,1024]{2,1,0:T(8,128)(2,1)S(1)}, u32[]{:S(2)}) copy-start(bf16[2,16,1024]{2,1,0:T(8,128)(2,1)S(1)} %collective-permute-done) | copy-start | bytes 196612
  47.8 11.1 %copy-start.18 = (s32[2,2048]{1,0:T(2,128)S(1)}, s32[2,2048]{1,0:T(2,128)}, u32[]{:S(2)}) copy-start(s32[2,2048]{1,0:T(2,128)} %param.10) | copy-start | bytes 49156
  47.8 11.2 %copy-start.20 = (pred[32]{0:T(512)(128)(4,1)S(1)}, pred[32]{0:T(512)(128)(4,1)}, u32[]{:S(2)}) copy-start(pred[32]{0:T(512)(128)(4,1)} %constant.69.clone.1) | copy-start | bytes 100
  47.8 6.9 %collective-permute-start.8 = (bf16[2,32,1024]{2,1,0:T(8,128)(2,1)S(1)}, bf16[2,32,1024]{2,1,0:T(8,128)(2,1)S(1)}, u32[]{:S(2)}, u32[]{:S(2)}) collective-permute-start(bf16[2,32,1024]{2,1,0:T(8,128)(2,1)S(1)} %get-tuple-element.66), channel_id=1, source_target_pairs={{1,0},{2,1},{3,2},{4,3},{5,4},{6,5},{7,6},{8,7},{9,8},{10,9},{11,1... | collective-permute-start | bytes 393224 | tf_op jit(solution)/shard_map/ppermute | solution.py:328
  49.1 7.1 %collective-permute-start.7 = (bf16[2,32,1024]{2,1,0:T(8,128)(2,1)S(1)}, bf16[2,32,1024]{2,1,0:T(8,128)(2,1)S(1)}, u32[]{:S(2)}, u32[]{:S(2)}) collective-permute-start(bf16[2,32,1024]{2,1,0:T(8,128)(2,1)S(1)} %get-tuple-element.67), channel_id=1, source_target_pairs={{0,1},{1,2},{2,3},{3,4},{4,5},{5,6},{6,7},{7,8},{8,9},{9,10},{10,1... | collective-permute-start | bytes 393224 | tf_op jit(solution)/shard_map/ppermute | solution.py:327
  58.0 2.0 %collective-permute-start.9 = (bf16[256,1024]{1,0:T(8,128)(2,1)S(1)}, bf16[256,1024]{1,0:T(8,128)(2,1)S(1)}, u32[]{:S(2)}, u32[]{:S(2)}) collective-permute-start(bf16[256,1024]{1,0:T(8,128)(2,1)S(1)} %get-tuple-element.38.left_ref), channel_id=1, source_target_pairs={{0,16},{16,0},{1,17},{17,1},{2,18},{18,2},{3,19},{19,3},{4,20},{20... | collective-permute-start | bytes 1572872 | tf_op jit(solution)/shard_map/ppermute | solution.py:432
  67.7 11.9 %copy-start.17 = (bf16[2,16,1024]{2,1,0:T(8,128)(2,1)S(1)}, bf16[2,16,1024]{2,1,0:T(8,128)(2,1)}, u32[]{:S(2)}) copy-start(bf16[2,16,1024]{2,1,0:T(8,128)(2,1)} %copy-done.16) | copy-start | bytes 196612
  79.4 23.6 %collective-permute-start.12 = (bf16[256,1024]{1,0:T(8,128)(2,1)S(1)}, bf16[256,1024]{1,0:T(8,128)(2,1)}, u32[]{:S(2)}, u32[]{:S(2)}) collective-permute-start(bf16[256,1024]{1,0:T(8,128)(2,1)S(1)} %bitcast.69), channel_id=1, source_target_pairs={{0,16},{16,0},{1,17},{17,1},{2,18},{18,2},{3,19},{19,3},{4,20},{20... | collective-permute-start | bytes 1572872 | tf_op jit(solution)/shard_map/ppermute | solution.py:455
  85.7 2.6 %copy-start.5 = (f32[320,1024]{1,0:T(8,128)S(1)}, f32[320,1024]{1,0:T(8,128)}, u32[]{:S(2)}) copy-start(f32[320,1024]{1,0:T(8,128)} %copy-done.4) | copy-start | bytes 3932164
  88.3 2.6 %copy-start.2 = (f32[384,1024]{1,0:T(8,128)S(1)}, f32[384,1024]{1,0:T(8,128)}, u32[]{:S(2)}) copy-start(f32[384,1024]{1,0:T(8,128)} %copy-done.1) | copy-start | bytes 4718596
  90.9 12.2 %copy-start.11 = (bf16[256,1024]{1,0:T(8,128)(2,1)S(1)}, bf16[256,1024]{1,0:T(8,128)(2,1)}, u32[]{:S(2)}) copy-start(bf16[256,1024]{1,0:T(8,128)(2,1)} %copy-done.10) | copy-start | bytes 1572868
  102.8 3.1 %copy-start.12 = (f32[32,1024]{1,0:T(8,128)}, f32[32,1024]{1,0:T(8,128)S(1)}, u32[]{:S(2)}) copy-start(f32[32,1024]{1,0:T(8,128)S(1)} %get-tuple-element.51) | copy-start | bytes 393220
  102.8 14.6 %collective-permute-start.10 = (bf16[256,2048]{1,0:T(8,128)(2,1)}, bf16[256,2048]{1,0:T(8,128)(2,1)S(1)}, u32[]{:S(2)}, u32[]{:S(2)}) collective-permute-start(bf16[256,2048]{1,0:T(8,128)(2,1)} %get-tuple-element.49.right_ref), channel_id=1, source_target_pairs={{0,16},{16,0},{1,17},{17,1},{2,18},{18,2},{3,19},{19,3},{4,20},{20... | collective-permute-start | bytes 3145736 | tf_op jit(solution)/shard_map/ppermute | solution.py:493
  103.0 14.3 %copy-start.7 = (bf16[256,1024]{1,0:T(8,128)(2,1)S(1)}, bf16[256,1024]{1,0:T(8,128)(2,1)}, u32[]{:S(2)}) copy-start(bf16[256,1024]{1,0:T(8,128)(2,1)} %copy-done.6) | copy-start | bytes 1572868
  105.9 9.7 %copy-start.13 = (f32[32,1024]{1,0:T(8,128)S(1)}, f32[32,1024]{1,0:T(8,128)}, u32[]{:S(2)}) copy-start(f32[32,1024]{1,0:T(8,128)} %copy-done.12) | copy-start | bytes 393220
  105.9 28.6 %all-to-all-start.2 = ((bf16[64,8,1024]{2,1,0:T(8,128)(2,1)}), bf16[64,8,1024]{2,1,0:T(8,128)(2,1)}, u32[]{:S(2)}, u32[]{:S(2)}) async-start(bf16[64,8,1024]{2,1,0:T(8,128)(2,1)} %bitcast.28), calls=%async_computation.2 | async-start | bytes 2097152 | tf_op jit(solution)/shard_map/all_to_all | solution.py:469
  115.7 1.7 collective-permute-start.11
  134.5 5.7 %copy-start.19 = (bf16[128,2]{0,1:T(2,128)(2,1)S(1)}, bf16[128,2]{0,1:T(2,128)(2,1)}, u32[]{:S(2)}) copy-start(bf16[128,2]{0,1:T(2,128)(2,1)} %param.14) | copy-start | bytes 1540
  134.5 35.8 %all-to-all-start.1 = ((bf16[64,8,2176]{2,1,0:T(8,128)(2,1)}), bf16[64,8,2176]{2,1,0:T(8,128)(2,1)}, u32[]{:S(2)}, u32[]{:S(2)}) async-start(bf16[64,8,2176]{2,1,0:T(8,128)(2,1)} %bitcast.25), calls=%async_computation.1 | async-start | bytes 4456448 | tf_op jit(solution)/shard_map/all_to_all | solution.py:469
  174.2 16.4 %all-to-all-start.3 = ((bf16[16,8,3200]{2,1,0:T(8,128)(2,1)}), bf16[16,8,3200]{2,1,0:T(8,128)(2,1)S(1)}, u32[]{:S(2)}, u32[]{:S(2)}) async-start(bf16[16,8,3200]{2,1,0:T(8,128)(2,1)} %broadcast_in_dim.83), calls=%async_computation.3 | async-start | bytes 1638400 | tf_op jit(solution)/shard_map/all_to_all | solution.py:319
  (9 other events, 9.8 us)
Sparse Core Ops, SparseCore 0:
  9.7 48.8 all-gather.2
  60.3 25.3 all-gather.4

commit v5 on v4

--- a/solution.py
+++ b/solution.py
@@ -1,3 +1,4 @@
+import functools
 import math
 
 import jax
@@ -15,6 +16,8 @@
 LANES = 128
 ROWS_STEP = 32
 EPS = 1e-05
+SMALL = 2 * LANES
+VMEM_GRANT = 16 * 1024 * 1024
 
 
 def forward_kernel(
@@ -95,7 +98,7 @@
 
 
 def backward_kernel(
-    grad_mix_ref, gated_ref, ids_ref, taps_ref, lin_ref, sig_ref,
+    grad_mix_ref, gated_ref, ids_ref, taps_ref, lin_ref, sig_ref, grad_gain_ref,
     grad_hidden_ref, grad_taps_ref, pad_ref, sum_ref,
 ):
     slabs, padded, width = gated_ref.shape
@@ -147,9 +150,12 @@
             grad_taps_ref[k : k + 1, b * LANES : (b + 1) * LANES] = jnp.sum(
                 sum_ref[b, k], axis=0, keepdims=True
             )
-        grad_taps_ref[taps_count:, b * LANES : (b + 1) * LANES] = jnp.zeros(
-            (grad_taps_ref.shape[0] - taps_count, LANES), jnp.float32
-        )
+    grad_taps_ref[taps_count:, :] = jnp.zeros(
+        (grad_taps_ref.shape[0] - taps_count, width), jnp.float32
+    )
+    grad_taps_ref[taps_count + 1 : taps_count + 2, :] = jnp.sum(
+        grad_gain_ref[...], axis=0, keepdims=True
+    )
 
 
 def send_kernel(index_ref, rows_ref, out_ref):
@@ -168,20 +174,49 @@
         )
 
 
-def receive_kernel(index_ref, arrived_ref, out_ref):
+def receive_kernel(index_ref, arrived_ref, upstream_ref, out_ref, last_ref, first_ref):
     slots, half = arrived_ref.shape
+    slabs, frames, _ = upstream_ref.shape
+    reach = 2 * EDGE
     columns = lax.broadcasted_iota(jnp.int32, (index_ref.shape[0], slots), 1)
     for h in range(2):
         pick = (columns == index_ref[:, h : h + 1]).astype(jnp.float32).astype(jnp.bfloat16)
-        out_ref[:, h * half : (h + 1) * half] = jnp.dot(
-            pick, arrived_ref[...], preferred_element_type=jnp.float32
-        ).astype(jnp.bfloat16)
+        rows = jnp.dot(pick, arrived_ref[...], preferred_element_type=jnp.float32)
+        rows = rows.astype(jnp.bfloat16)
+        cols = slice(h * half, (h + 1) * half)
+        out_ref[:, cols] = rows
+        for s in range(slabs):
+            last_ref[s, :reach, cols] = rows[(s + 1) * frames - reach : (s + 1) * frames]
+            first_ref[s, :reach, cols] = rows[s * frames : s * frames + reach]
+    for s in range(slabs):
+        last_ref[s, reach:, :] = upstream_ref[s, frames - EDGE :, :]
+        first_ref[s, reach:, :] = upstream_ref[s, :EDGE, :]
+
+
+def total_kernel(parts_ref, out_sum_ref, weight_ref, gain_ref, total_ref, sum_ref, *, tap, scale):
+    count, share, width = parts_ref.shape
+    in_width = weight_ref.shape[1]
+    grad_gain = jnp.zeros((share, 1), jnp.float32)
+    for at in range(0, width, SMALL):
+        cols = slice(at, at + SMALL)
+        part = jnp.zeros((share, SMALL), jnp.float32)
+        for j in range(0, count, 16):
+            part = part + jnp.sum(parts_ref[j : j + 16, :, cols].astype(jnp.float32), axis=0)
+        sum_ref[:, cols] = part
+        if at < in_width:
+            grad_gain = grad_gain + jnp.sum(part * weight_ref[:, cols], axis=1, keepdims=True)
+    small = sum_ref[:, in_width:]
+    column = lax.broadcasted_iota(jnp.int32, small.shape, 1)
+    sum_ref[:, in_width:] = jnp.where(column == tap, grad_gain / gain_ref[...], small)
+    for i in range(total_ref.shape[0]):
+        total_ref[i, :, :width] = (sum_ref[...] * scale).astype(jnp.bfloat16)
+        total_ref[i, :, width:] = (out_sum_ref[...] * scale).astype(jnp.bfloat16)
 
 
 def finish_kernel(final_ref, grad_in_ref, grad_out_ref, grad_taps_ref, grad_gains_ref):
     in_width, taps_count = grad_in_ref.shape[1], grad_taps_ref.shape[0]
     grad_in_ref[...] = final_ref[:, :in_width].astype(jnp.float32)
-    grad_out_ref[...] = final_ref[:, in_width + LANES :].astype(jnp.float32)
+    grad_out_ref[...] = final_ref[:, in_width + SMALL :].astype(jnp.float32)
     small = final_ref[:, in_width : in_width + LANES].astype(jnp.float32).T
     grad_taps_ref[...] = small[:taps_count]
     grad_gains_ref[...] = small[taps_count : taps_count + 2]
@@ -214,13 +249,14 @@
             )
             block = slice(z * LANES, (z + 1) * LANES)
             out_ref[block, width : width + LANES] = filled.T.astype(out_ref.dtype)
+            out_ref[block, width + LANES :] = jnp.zeros((LANES, SMALL - LANES), out_ref.dtype)
 
 
 def weight_part(core, left, left_other, right, right_other, *small):
     rows, channels = left.shape
     mine = channels // LANES // 2
     width = right.shape[1]
-    out_width = width + (LANES if small else 0)
+    out_width = width + (SMALL if small else 0)
     vmem = pl.BlockSpec(memory_space=pltpu.VMEM)
     return pl.pallas_call(
         product_kernel,
@@ -229,7 +265,7 @@
         out_specs=vmem,
         scratch_shapes=[pltpu.VMEM((mine * LANES, 2 * rows), jnp.bfloat16)],
         name="weight_part",
-        compiler_params=pltpu.CompilerParams(vmem_limit_bytes=48 * 1024 * 1024),
+        compiler_params=pltpu.CompilerParams(vmem_limit_bytes=VMEM_GRANT),
         cost_estimate=pl.CostEstimate(
             flops=4 * rows * mine * LANES * width,
             bytes_accessed=4 * rows * (channels + width),
@@ -240,7 +276,7 @@
 
 def norm_kernel(frames_ref, low_ref, high_ref, gain_ref, wide_ref, own_ref):
     slabs, padded, _ = wide_ref.shape
-    reach = low_ref.shape[1]
+    reach = 2 * EDGE
     own = padded - 2 * reach
 
     def normed_rows(rows):
@@ -295,7 +331,7 @@
         ],
         out_specs=(out, out, out),
         name="project",
-        compiler_params=pltpu.CompilerParams(vmem_limit_bytes=48 * 1024 * 1024),
+        compiler_params=pltpu.CompilerParams(vmem_limit_bytes=VMEM_GRANT),
         cost_estimate=pl.CostEstimate(
             flops=4 * rows * width * width,
             bytes_accessed=4 * width * width,
@@ -310,23 +346,15 @@
         body,
         out_shape=outs,
         scratch_shapes=scratch,
-        compiler_params=pltpu.CompilerParams(vmem_limit_bytes=48 * 1024 * 1024),
+        compiler_params=pltpu.CompilerParams(vmem_limit_bytes=VMEM_GRANT),
         cost_estimate=pl.CostEstimate(flops=flops, bytes_accessed=moved, transcendentals=0),
     )(*args)
 
 
-def spread(shard, axes, count):
-    return lax.all_to_all(
-        jnp.broadcast_to(shard[None], (count, *shard.shape)), axes, 0, 0, tiled=True
-    )
-
-
-def edges(block, count, reach):
+def to_neighbours(last, first, count):
     forward = [(i, i + 1) for i in range(count - 1)]
     backward = [(i + 1, i) for i in range(count - 1)]
-    low = lax.ppermute(block[:, -reach:], SEQ, forward)
-    high = lax.ppermute(block[:, :reach], SEQ, backward)
-    return low, high
+    return lax.ppermute(last, SEQ, forward), lax.ppermute(first, SEQ, backward)
 
 
 def norm_rows(values, gain):
@@ -372,7 +400,6 @@
         jnp.concatenate([depth_kernel, norm_gains], axis=1), ((0, 0), (0, LANES - kernel_len - 2))
     )
     upstream_rows = upstream.reshape(rows_dev, width)
-    up_low, up_high = edges(upstream, n_seq, EDGE)
     extras_other = lax.ppermute(extras, "core", swap)
     pair = jnp.where(
         core == 0, jnp.stack([extras, extras_other]), jnp.stack([extras_other, extras])
@@ -381,8 +408,8 @@
         lax.ppermute(pair, "z", [(i, (i + d) % n_z) for i in range(n_z)]) for d in range(1, n_z)
     ]
     upstream_other = lax.ppermute(upstream_rows, "core", swap)
-    arrived, up_low, up_high, upstream_other, pair, *from_z = lax.optimization_barrier(
-        (arrived, up_low, up_high, upstream_other, pair, *from_z)
+    arrived, upstream_other, pair, *from_z = lax.optimization_barrier(
+        (arrived, upstream_other, pair, *from_z)
     )
     by_z = jnp.stack([*from_z[::-1], pair])
     side_all = lax.dynamic_slice_in_dim(
@@ -395,20 +422,26 @@
     source_dev = jnp.sum(before.astype(jnp.int32), axis=1)
     start_of = jnp.sum(jnp.where(before, recv_plan[None, :], 0), axis=1)
     place = source_dev * 2 * capacity + frame_index - start_of
-    frames = kernel_call(
+    frames, last, first = kernel_call(
         receive_kernel,
-        jax.ShapeDtypeStruct((rows_dev, width), jnp.bfloat16),
+        (
+            jax.ShapeDtypeStruct((rows_dev, width), jnp.bfloat16),
+            jax.ShapeDtypeStruct((slabs, 3 * EDGE, width), jnp.bfloat16),
+            jax.ShapeDtypeStruct((slabs, 3 * EDGE, width), jnp.bfloat16),
+        ),
         [],
         4 * devices * capacity * rows_dev * width,
-        jnp.stack([place, place + capacity], axis=1), arrived,
-    )
-    low, high = edges(frames.reshape(slabs, frames_dev, width), n_seq, 2 * EDGE)
+        jnp.stack([place, place + capacity], axis=1), arrived, upstream,
+    )
+    low, high = to_neighbours(last, first, n_seq)
     side = side_all.reshape(width, LANES)[:, : kernel_len + 2].astype(jnp.float32).T
     gain_pre, gain_mid = side[kernel_len], side[kernel_len + 1]
     taps = jnp.pad(side[:kernel_len], ((0, 1), (0, 0)))
     taps = taps.reshape(kernel_len + 1, width // LANES, LANES).transpose(1, 0, 2)
 
-    upstream_wide = jnp.concatenate([up_low, upstream, up_high], axis=1).reshape(-1, width)
+    upstream_wide = jnp.concatenate(
+        [low[:, 2 * EDGE :], upstream, high[:, 2 * EDGE :]], axis=1
+    ).reshape(-1, width)
 
     id_pad = jnp.pad(segment_ids, ((0, 0), (2 * EDGE, 2 * EDGE)), constant_values=-1)
     window = lax.dynamic_slice_in_dim(
@@ -465,15 +498,15 @@
         normed_mid, scale_mid, grad_act, gain_mid[None],
     )
 
-    def summed(part):
-        arrived_parts = lax.all_to_all(
+    def exchanged(part):
+        return lax.all_to_all(
             part.reshape(n_z * n_seq, LANES // n_seq, part.shape[1]), ZXY, 0, 0, tiled=True
         )
-        return jnp.sum(arrived_parts.astype(jnp.float32), axis=0)
 
     core_ref = core[None].astype(jnp.int32)
     out_part = weight_part(core_ref, activated, act_other, upstream_rows, upstream_other)
-    out_sum = summed(out_part)
+    out_parts = exchanged(out_part)
+    out_sum = jnp.sum(out_parts.astype(jnp.float32), axis=0)
     projected = jnp.dot(activated, out_full, preferred_element_type=jnp.float32)
     encoded = (frame_rows + projected).astype(jnp.bfloat16).reshape(slabs, frames_dev, width)
 
@@ -481,29 +514,21 @@
         backward_kernel,
         (
             jax.ShapeDtypeStruct((rows_dev, 2 * width), jnp.bfloat16),
-            jax.ShapeDtypeStruct((kernel_len + 1, width), jnp.float32),
+            jax.ShapeDtypeStruct((kernel_len + 9, width), jnp.float32),
         ),
         [
             pltpu.VMEM((blocks, wide, LANES), jnp.float32),
             pltpu.VMEM((blocks, kernel_len, 8, LANES), jnp.float32),
         ],
         elements * 5 * kernel_len,
-        grad_mixing, gated, ids, taps, lin, sig,
+        grad_mixing, gated, ids, taps, lin, sig, grad_gain_mid,
     )
     hidden_other = lax.ppermute(grad_hidden, "core", swap)
-    small = jnp.concatenate(
-        [
-            grad_taps,
-            jnp.sum(grad_gain_mid, axis=0)[None],
-            jnp.zeros((7, width), jnp.float32),
-        ],
-        axis=0,
-    )
-    small_other = lax.ppermute(small, "core", swap)
+    small_other = lax.ppermute(grad_taps, "core", swap)
     in_part = weight_part(
-        core_ref, normed, normed_other, grad_hidden, hidden_other, small, small_other
-    )
-    in_sum = summed(in_part)
+        core_ref, normed, normed_other, grad_hidden, hidden_other, grad_taps, small_other
+    )
+    in_parts = exchanged(in_part)
     grad_normed = lax.dot_general(
         grad_hidden, in_full, (((1,), (1,)), ((), ())), preferred_element_type=jnp.float32
     )
@@ -514,19 +539,19 @@
         .reshape(slabs, frames_dev, width)
     )
     share = LANES // n_seq
-    first = lax.axis_index(SEQ) * share
-    own_weight = lax.dynamic_slice_in_dim(in_weight, first, share, 0).astype(jnp.float32)
-    own_gain = lax.dynamic_slice_in_dim(norm_gains, first, share, 0)[:, :1].astype(jnp.float32)
-    grad_gain_pre = (
-        jnp.sum(own_weight * in_sum[:, : 2 * width], axis=1, keepdims=True) / own_gain
-    )
-    place = jnp.arange(LANES) == kernel_len
-    small_sum = jnp.where(place[None], grad_gain_pre, in_sum[:, 2 * width :])
-    scale = 1.0 / math.sqrt(devices * rows_dev)
-    total = (
-        jnp.concatenate([in_sum[:, : 2 * width], small_sum, out_sum], axis=1) * scale
-    ).astype(jnp.bfloat16)
-    final = spread(total, SEQ, n_seq).reshape(LANES, total.shape[1])
+    start = lax.axis_index(SEQ) * share
+    own_weight = lax.dynamic_slice_in_dim(in_weight, start, share, 0).astype(jnp.float32)
+    own_gain = lax.dynamic_slice_in_dim(norm_gains, start, share, 0)[:, :1].astype(jnp.float32)
+    total = kernel_call(
+        functools.partial(
+            total_kernel, tap=kernel_len, scale=1.0 / math.sqrt(devices * rows_dev)
+        ),
+        jax.ShapeDtypeStruct((n_seq, share, 3 * width + SMALL), jnp.bfloat16),
+        [pltpu.VMEM((share, 2 * width + SMALL), jnp.float32)],
+        in_parts.size,
+        in_parts, out_sum, own_weight, own_gain,
+    )
+    final = lax.all_to_all(total, SEQ, 0, 0, tiled=True).reshape(LANES, -1)
     grad_in, grad_out, grad_kernel, grad_gains = kernel_call(
         finish_kernel,
         (

time: 200 us -> 195 us (0.975)
  waiting for transfers between devices: 65.8 us -> 75.8 us
  starting transfers between devices: 47.7 us -> 39.6 us
  Pallas kernels: 41.3 us -> 37.3 us
  other arithmetic: 9.47 us -> 7.34 us
    ppermute x5 -> x3, starting transfers between devices: 12 us -> 4.16 us  [the longest x1 2.79 us: to_neighbours(): lax.ppermute(last, SEQ, forward)]
    ppermute x3, waiting for transfers between devices: 6.46 us -> 14.2 us  [per_device(): lax.ppermute(pair, 'z', [(i, (i + d) % n_z) for i in range(n_z)])]
    pallas_call x7 -> x8, Pallas kernels: 30.1 us -> 27.1 us  [kernel_call(): pl.pallas_call(body, out_shape=outs, scratch_shapes=scratch, compiler_par...]
    ppermute x5 -> x3, waiting for transfers between devices: 6.66 us -> 8.02 us  [the longest x1 4.12 us: to_neighbours(): lax.ppermute(first, SEQ, backward)]
    unnamed x51 -> x70, local copies, waits for them, and re-layouts: 8.69 us -> 9.35 us
  transfers between devices with their start and end apart: 19 -> 17, of which waited for: 12 -> 11; matrix products, arithmetic and copies ran while one was open for 8% -> 9% of each run, Pallas kernels for 20% -> 18%
where the time goes in v5:
time: 195 us; the launch traced here: 194 us
  waiting for transfers between devices  75.8 us (39%)
  starting transfers between devices  39.6 us (20%)
  Pallas kernels  37.3 us (19%)
  between operations  14.6 us (7%)
  local copies, waits for them, and re-layouts  11.4 us (6%)
  matrix products  8.26 us (4%)
  other arithmetic  7.34 us (4%)
    all_to_all x2, waiting for transfers between devices, exchanged(): lax.all_to_all(part.reshape(n_z * n_seq, LANES // n_seq, part.shape[1]),...  37.5 us
    pallas_call x8, Pallas kernels, kernel_call(): pl.pallas_call(body, out_shape=outs, scratch_shapes=scratch, compiler_par...  27.1 us
    all_to_all x2, starting transfers between devices, exchanged(): lax.all_to_all(part.reshape(n_z * n_seq, LANES // n_seq, part.shape[1]),...  14.8 us
    ppermute x3, waiting for transfers between devices, per_device(): lax.ppermute(pair, 'z', [(i, (i + d) % n_z) for i in range(n_z)])  14.2 us
    all_to_all x1, starting transfers between devices, per_device(): lax.all_to_all(outgoing, (*DP, *SEQ), split_axis=0, concat_axis=0, tiled=...  11.2 us
    unnamed x70, local copies, waits for them, and re-layouts  9.35 us
    all_to_all x1, waiting for transfers between devices, per_device(): final = lax.all_to_all(total, SEQ, 0, 0, tiled=True).reshape(LANES, -1)  9.33 us
    pallas_call x2, Pallas kernels, weight_part(): pl.pallas_call(product_kernel, out_shape=jax.ShapeDtypeStruct((mine * LAN...  6.92 us
  transfers between devices with their start and end apart: 17, of which 11 were waited for; matrix products, arithmetic and copies ran while one was open for 9% of the time, Pallas kernels for 18%

profile of v5, /device:TPU:0, one launch (start us, length us, event | category | flops | bytes accessed | tf_op | source)
XLA Modules:
  0.0 194.4 jit_solution(3537658791459106555)
XLA Ops:
  11.0 1.5 shard_map.127
  12.4 11.2 %all-to-all-start = ((bf16[128,8,512]{2,1,0:T(8,128)(2,1)}), bf16[128,8,512]{2,1,0:T(8,128)(2,1)S(1)}, u32[]{:S(2)}, u32[]{:S(2)}) async-start(bf16[128,8,512]{2,1,0:T(8,128)(2,1)} %shard_map.127), calls=%async_computation | async-start | bytes 2097152 | tf_op jit(solution)/shard_map/all_to_all | solution.py:396
  25.1 2.9 %collective-permute-start.4 = (bf16[2,128,128]{1,2,0:T(8,128)(2,1)S(1)}, bf16[2,128,128]{1,2,0:T(8,128)(2,1)S(1)}, u32[]{:S(2)}, u32[]{:S(2)}) collective-permute-start(bf16[2,128,128]{1,2,0:T(8,128)(2,1)S(1)} %maximum_select_fusion), channel_id=1, source_target_pairs={{0,96},{32,0},{64,32},{96,64},{1,97},{33,1},{65,33},{97,65},{2,98}... | collective-permute-start | bytes 196616 | tf_op jit(solution)/shard_map/ppermute | solution.py:408
  29.6 10.8 %collective-permute-done.4 = bf16[2,128,128]{1,2,0:T(8,128)(2,1)S(1)} collective-permute-done((bf16[2,128,128]{1,2,0:T(8,128)(2,1)S(1)}, bf16[2,128,128]{1,2,0:T(8,128)(2,1)S(1)}, u32[]{:S(2)}, u32[]{:S(2)}) %collective-permute-start.4) | collective-permute-done | bytes 65568 | tf_op jit(solution)/shard_map/ppermute | solution.py:408
  40.3 1.9 collective-permute-done.3
  42.3 1.5 collective-permute-done.2
  45.4 2.8 %collective-permute-start.5 = (bf16[2,48,1024]{2,1,0:T(8,128)(2,1)S(1)}, bf16[2,48,1024]{2,1,0:T(8,128)(2,1)S(1)}, u32[]{:S(2)}, u32[]{:S(2)}) collective-permute-start(bf16[2,48,1024]{2,1,0:T(8,128)(2,1)S(1)} %get-tuple-element.35), channel_id=1, source_target_pairs={{0,1},{1,2},{2,3},{3,4},{4,5},{5,6},{6,7},{7,8},{8,9},{9,10},{10,1... | collective-permute-start | bytes 589832 | tf_op jit(solution)/shard_map/ppermute | solution.py:357
  48.2 1.3 collective-permute-start.6
  50.2 2.5 %collective-permute-done.5.low_ref = bf16[2,48,1024]{2,1,0:T(8,128)(2,1)S(1)} collective-permute-done((bf16[2,48,1024]{2,1,0:T(8,128)(2,1)S(1)}, bf16[2,48,1024]{2,1,0:T(8,128)(2,1)S(1)}, u32[]{:S(2)}, u32[]{:S(2)}) %collective-permute-start.5) | collective-permute-done | bytes 196640 | tf_op jit(solution)/shard_map/ppermute | solution.py:357
  52.7 4.1 %collective-permute-done.6.high_ref = bf16[2,48,1024]{2,1,0:T(8,128)(2,1)S(1)} collective-permute-done((bf16[2,48,1024]{2,1,0:T(8,128)(2,1)S(1)}, bf16[2,48,1024]{2,1,0:T(8,128)(2,1)S(1)}, u32[]{:S(2)}, u32[]{:S(2)}) %collective-permute-start.6) | collective-permute-done | bytes 196640 | tf_op jit(solution)/shard_map/ppermute | solution.py:357
  56.8 1.8 shard_map.129
  61.5 2.2 %copy-done = bf16[1024,2048]{1,0:T(8,128)(2,1)S(1)} copy-done((bf16[1024,2048]{1,0:T(8,128)(2,1)S(1)}, bf16[1024,2048]{1,0:T(8,128)(2,1)}, u32[]{:S(2)}) %copy-start) | copy-done | bytes 4194328
  63.6 3.3 %project.1 = (f32[384,1024]{1,0:T(8,128)S(1)}, f32[384,1024]{1,0:T(8,128)S(1)}, bf16[384,1024]{1,0:T(8,128)(2,1)S(1)}) custom-call(bf16[384,1024]{1,0:T(8,128)(2,1)S(1)} %bitcast.65, bf16[1024,2048]{1,0:T(8,128)(2,1)S(1)} %copy-done, bf16[1024,2048]{1,0:T(8,128)(2,1)S(1)} %copy-done), custom_call_target="tpu_custom_call" | custom-call | flops 1610612736 | bytes 4194304 | tf_op jit(solution)/shard_map/project/pallas_call | solution.py:319
  68.2 10.0 %shard_map.130 = (bf16[320,1024]{1,0:T(8,128)(2,1)S(1)}, f32[320,1024]{1,0:T(8,128)S(1)}, f32[320,128]{1,0:T(8,128)S(1)}) custom-call(bf16[2,192,1024]{2,1,0:T(8,128)(2,1)S(1)} %bitcast.59, s32[2,192,128]{2,1,0:T(8,128)S(1)} %broadcast_in_dim.39.ids_ref, f32[8,32,128]{2,1,0:T(8,128)S(1)} %bitcast_bitcast_fusion.taps_ref, ...), custom_call_target="tpu_custom_call" | custom-call | flops 24379392 | bytes 1118208 | tf_op jit(solution)/shard_map/pallas_call | solution.py:345
  80.5 5.2 %all-gather.5.cloned.1.call-done = bf16[1024,1024]{1,0:T(8,128)(2,1)} async-done(((bf16[128,1024]{1,0:T(8,128)(2,1)}), bf16[1024,1024]{1,0:T(8,128)(2,1)}) %all-gather.5.cloned.1.call-update) | async-done | bytes 2097168 | tf_op jit(solution)/shard_map/all_gather | solution.py:383
  85.7 2.8 %fusion.16.grad_act_ref = f32[320,1024]{1,0:T(8,128)S(1)} fusion(bf16[320,1024]{1,0:T(8,128)(2,1)} %bitcast.68, bf16[1024,1024]{1,0:T(8,128)(2,1)} %all-gather.5.cloned.1.call-done), kind=kOutput, calls=%fused_computation.56 | convolution fusion | flops 671088640 | bytes 4063232 | tf_op jit(solution)/shard_map/dot_general | solution.py:489
  88.5 2.5 %shard_map.131 = (f32[2,160,1024]{2,1,0:T(8,128)S(1)}, f32[8,1024]{1,0:T(8,128)S(1)}) custom-call(f32[320,1024]{1,0:T(8,128)S(1)} %copy-done.10, f32[320,128]{1,0:T(8,128)S(1)} %get-tuple-element.47.scale_ref, f32[320,1024]{1,0:T(8,128)S(1)} %fusion.16.grad_act_ref, f32[1,1024]{1,0:T(1,128)S(1)} %get-tuple-element.68.gain_ref), custom_call_target="tpu_custom_call" | custom-call | flops 7864320 | bytes 2789376 | tf_op jit(solution)/shard_map/pallas_call | solution.py:345
  91.1 8.9 %shard_map.132 = (bf16[256,2048]{1,0:T(8,128)(2,1)}, f32[40,1024]{1,0:T(8,128)S(1)}) custom-call(f32[2,160,1024]{2,1,0:T(8,128)S(1)} %get-tuple-element.48.grad_mix_ref, bf16[2,192,1024]{2,1,0:T(8,128)(2,1)S(1)} %bitcast.60, s32[2,192,128]{2,1,0:T(8,128)S(1)} %broadcast_in_dim.39.ids_ref, f32[8,32,128]{2,1,0:T(8,128)S(1)} %bitcast_bitcast_fusion.taps_ref, ...), custom_call_target="tpu_custom_call" | custom-call | flops 40632320 | bytes 5603328 | tf_op jit(solution)/shard_map/pallas_call | solution.py:345
  100.2 2.9 %weight_part.3 = bf16[512,1024]{1,0:T(8,128)(2,1)} custom-call(s32[1]{0:T(128)} %bitcast.22.core_ref, bf16[256,1024]{1,0:T(8,128)(2,1)S(1)} %bitcast.62, bf16[256,1024]{1,0:T(8,128)(2,1)} %collective-permute-done.10.left_other_ref, bf16[256,1024]{1,0:T(8,128)(2,1)S(1)} %bitcast.57, bf16[256,1024]{1,0:T(8,128)(2,1)S(1)} %copy-done.16), custom_call_target="tpu_custom_call" | custom-call | flops 536870912 | bytes 2097152 | tf_op jit(solution)/shard_map/weight_part/pallas_call | solution.py:261
  103.2 9.7 %all-to-all-start.2 = ((bf16[64,8,1024]{2,1,0:T(8,128)(2,1)}), bf16[64,8,1024]{2,1,0:T(8,128)(2,1)}, u32[]{:S(2)}, u32[]{:S(2)}) async-start(bf16[64,8,1024]{2,1,0:T(8,128)(2,1)} %bitcast.24), calls=%async_computation.2 | async-start | bytes 2097152 | tf_op jit(solution)/shard_map/all_to_all | solution.py:502
  112.9 1.4 collective-permute-done.9.rest_1_
  114.3 4.0 %weight_part.2 = bf16[512,2304]{1,0:T(8,128)(2,1)} custom-call(s32[1]{0:T(128)} %bitcast.22.core_ref, bf16[256,1024]{1,0:T(8,128)(2,1)S(1)} %copy-done.12, bf16[256,1024]{1,0:T(8,128)(2,1)S(1)} %copy-done.14, bf16[256,2048]{1,0:T(8,128)(2,1)} %get-tuple-element.52.right_ref, bf16[256,2048]{1,0:T(8,128)(2,1)S(1)} %collective-permute-done.8.right_other_ref, ...), custom_call_target="tpu_custom_call" | custom-call | flops 1073741824 | bytes 3145728 | tf_op jit(solution)/shard_map/weight_part/pallas_call | solution.py:261
  118.3 13.5 %all-to-all-done.2 = bf16[64,8,1024]{2,1,0:T(8,128)(2,1)} async-done(((bf16[64,8,1024]{2,1,0:T(8,128)(2,1)}), bf16[64,8,1024]{2,1,0:T(8,128)(2,1)}, u32[]{:S(2)}, u32[]{:S(2)}) %all-to-all-start.2) | async-done | bytes 1048608 | tf_op jit(solution)/shard_map/all_to_all | solution.py:502
  131.8 5.2 %all-to-all-start.1 = ((bf16[64,8,2304]{2,1,0:T(8,128)(2,1)}), bf16[64,8,2304]{2,1,0:T(8,128)(2,1)S(1)}, u32[]{:S(2)}, u32[]{:S(2)}) async-start(bf16[64,8,2304]{2,1,0:T(8,128)(2,1)} %bitcast.23), calls=%async_computation.1 | async-start | bytes 4718592 | tf_op jit(solution)/shard_map/all_to_all | solution.py:502
  138.1 3.9 %fusion.4 = (f32[256]{0:T(256)S(1)}, f32[256]{0:T(256)S(1)}, f32[256,1024]{1,0:T(8,128)S(1)}) fusion(bf16[256,1024]{1,0:T(8,128)(2,1)S(1)} %get-tuple-element.34.frames_ref, f32[256]{0:T(256)S(1)} %broadcast_multiply_fusion, f32[1024]{0:T(1024)S(1)} %bitcast.67, bf16[256,2048]{1,0:T(8,128)(2,1)} %get-tuple-element.52.right_ref, ...), kind=kOutput, calls=%fused_computation.10 | convolution fusion | flops 1075576320 | bytes 6822912 | tf_op jit(solution)/shard_map/dot_general | solution.py:532
  143.0 1.4 convert_reduce_fusion.out_sum_ref
  144.4 24.0 %all-to-all-done.1.parts_ref = bf16[64,8,2304]{2,1,0:T(8,128)(2,1)S(1)} async-done(((bf16[64,8,2304]{2,1,0:T(8,128)(2,1)}), bf16[64,8,2304]{2,1,0:T(8,128)(2,1)S(1)}, u32[]{:S(2)}, u32[]{:S(2)}) %all-to-all-start.1) | async-done | bytes 2359328 | tf_op jit(solution)/shard_map/all_to_all | solution.py:502
  169.8 3.9 %all-to-all-start.3 = ((bf16[16,8,3328]{2,1,0:T(8,128)(2,1)}), bf16[16,8,3328]{2,1,0:T(8,128)(2,1)S(1)}, u32[]{:S(2)}, u32[]{:S(2)}) async-start(bf16[16,8,3328]{2,1,0:T(8,128)(2,1)} %copy-done.2), calls=%async_computation.3 | async-start | bytes 1703936 | tf_op jit(solution)/shard_map/all_to_all | solution.py:554
  173.7 1.2 add_convert_fusion
  175.5 1.5 fusion.3
  177.0 9.3 %all-to-all-done.3 = bf16[16,8,3328]{2,1,0:T(8,128)(2,1)S(1)} async-done(((bf16[16,8,3328]{2,1,0:T(8,128)(2,1)}), bf16[16,8,3328]{2,1,0:T(8,128)(2,1)S(1)}, u32[]{:S(2)}, u32[]{:S(2)}) %all-to-all-start.3) | async-done | bytes 852000 | tf_op jit(solution)/shard_map/all_to_all | solution.py:554
  186.3 1.2 shard_map.134
  (130 shorter events, 19.5 us)
Async XLA Ops:
  7.2 54.3 %all-gather.3.cloned.1.call-start = ((), (), s32[]{:S(2)}) async-start(), calls=%async_computation.4 | async-start | bytes 4718592 | tf_op jit(solution)/shard_map/all_gather | solution.py:382
  11.0 12.7 %copy-start.27 = (bf16[128,31]{0,1:T(8,128)(2,1)S(1)}, bf16[128,31]{0,1:T(8,128)(2,1)}, u32[]{:S(2)}) copy-start(bf16[128,31]{0,1:T(8,128)(2,1)} %param.13) | copy-start | bytes 23812
  11.0 12.7 %copy-start.28 = (bf16[128,2]{0,1:T(2,128)(2,1)S(1)}, bf16[128,2]{0,1:T(2,128)(2,1)}, u32[]{:S(2)}) copy-start(bf16[128,2]{0,1:T(2,128)(2,1)} %param.14) | copy-start | bytes 1540
  11.0 12.8 %copy-start.1 = (bf16[2,128,1024]{2,1,0:T(8,128)(2,1)S(1)}, bf16[2,128,1024]{2,1,0:T(8,128)(2,1)}, u32[]{:S(2)}) copy-start(bf16[2,128,1024]{2,1,0:T(8,128)(2,1)} %upstream_ref.1) | copy-start | bytes 1572868
  11.0 13.4 %copy-start.25 = (s32[128,128]{1,0:T(8,128)S(1)}, s32[128,128]{1,0:T(8,128)}, u32[]{:S(2)}) copy-start(s32[128,128]{1,0:T(8,128)} %param.9) | copy-start | bytes 196612
  12.4 32.1 %all-to-all-start = ((bf16[128,8,512]{2,1,0:T(8,128)(2,1)}), bf16[128,8,512]{2,1,0:T(8,128)(2,1)S(1)}, u32[]{:S(2)}, u32[]{:S(2)}) async-start(bf16[128,8,512]{2,1,0:T(8,128)(2,1)} %shard_map.127), calls=%async_computation | async-start | bytes 2097152 | tf_op jit(solution)/shard_map/all_to_all | solution.py:396
  23.6 62.1 %all-gather.5.cloned.1.call-start = ((), (), s32[]{:S(2)}) async-start(), calls=%async_computation.5 | async-start | bytes 2359296 | tf_op jit(solution)/shard_map/all_gather | solution.py:383
  23.7 1.3 collective-permute-start.1
  23.8 19.9 %collective-permute-start = (bf16[256,1024]{1,0:T(8,128)(2,1)S(1)}, bf16[256,1024]{1,0:T(8,128)(2,1)S(1)}, u32[]{:S(2)}, u32[]{:S(2)}) collective-permute-start(bf16[256,1024]{1,0:T(8,128)(2,1)S(1)} %bitcast.56), channel_id=1, source_target_pairs={{0,16},{16,0},{1,17},{17,1},{2,18},{18,2},{3,19},{19,3},{4,20},{20... | collective-permute-start | bytes 1572872 | tf_op jit(solution)/shard_map/ppermute | solution.py:410
  25.1 15.3 %collective-permute-start.4 = (bf16[2,128,128]{1,2,0:T(8,128)(2,1)S(1)}, bf16[2,128,128]{1,2,0:T(8,128)(2,1)S(1)}, u32[]{:S(2)}, u32[]{:S(2)}) collective-permute-start(bf16[2,128,128]{1,2,0:T(8,128)(2,1)S(1)} %maximum_select_fusion), channel_id=1, source_target_pairs={{0,96},{32,0},{64,32},{96,64},{1,97},{33,1},{65,33},{97,65},{2,98}... | collective-permute-start | bytes 196616 | tf_op jit(solution)/shard_map/ppermute | solution.py:408
  28.0 14.3 %collective-permute-start.3 = (bf16[2,128,128]{1,2,0:T(8,128)(2,1)S(1)}, bf16[2,128,128]{1,2,0:T(8,128)(2,1)S(1)}, u32[]{:S(2)}, u32[]{:S(2)}) collective-permute-start(bf16[2,128,128]{1,2,0:T(8,128)(2,1)S(1)} %maximum_select_fusion), channel_id=1, source_target_pairs={{0,64},{32,96},{64,0},{96,32},{1,65},{33,97},{65,1},{97,33},{2,66}... | collective-permute-start | bytes 196616 | tf_op jit(solution)/shard_map/ppermute | solution.py:408
  28.3 15.4 %collective-permute-start.2 = (bf16[2,128,128]{1,2,0:T(8,128)(2,1)S(1)}, bf16[2,128,128]{1,2,0:T(8,128)(2,1)S(1)}, u32[]{:S(2)}, u32[]{:S(2)}) collective-permute-start(bf16[2,128,128]{1,2,0:T(8,128)(2,1)S(1)} %maximum_select_fusion), channel_id=1, source_target_pairs={{0,32},{32,64},{64,96},{96,0},{1,33},{33,65},{65,97},{97,1},{2,34}... | collective-permute-start | bytes 196616 | tf_op jit(solution)/shard_map/ppermute | solution.py:408
  45.4 13.4 %copy-start.26 = (s32[2,2048]{1,0:T(2,128)S(1)}, s32[2,2048]{1,0:T(2,128)}, u32[]{:S(2)}) copy-start(s32[2,2048]{1,0:T(2,128)} %param.10) | copy-start | bytes 49156
  45.4 13.5 %copy-start.29 = (pred[32]{0:T(512)(128)(4,1)S(1)}, pred[32]{0:T(512)(128)(4,1)}, u32[]{:S(2)}) copy-start(pred[32]{0:T(512)(128)(4,1)} %constant.66.clone.1) | copy-start | bytes 100
  45.4 7.3 %collective-permute-start.5 = (bf16[2,48,1024]{2,1,0:T(8,128)(2,1)S(1)}, bf16[2,48,1024]{2,1,0:T(8,128)(2,1)S(1)}, u32[]{:S(2)}, u32[]{:S(2)}) collective-permute-start(bf16[2,48,1024]{2,1,0:T(8,128)(2,1)S(1)} %get-tuple-element.35), channel_id=1, source_target_pairs={{0,1},{1,2},{2,3},{3,4},{4,5},{5,6},{6,7},{7,8},{8,9},{9,10},{10,1... | collective-permute-start | bytes 589832 | tf_op jit(solution)/shard_map/ppermute | solution.py:357
  48.2 8.6 %collective-permute-start.6 = (bf16[2,48,1024]{2,1,0:T(8,128)(2,1)S(1)}, bf16[2,48,1024]{2,1,0:T(8,128)(2,1)S(1)}, u32[]{:S(2)}, u32[]{:S(2)}) collective-permute-start(bf16[2,48,1024]{2,1,0:T(8,128)(2,1)S(1)} %get-tuple-element.36), channel_id=1, source_target_pairs={{1,0},{2,1},{3,2},{4,3},{5,4},{6,5},{7,6},{8,7},{9,8},{10,9},{11,1... | collective-permute-start | bytes 589832 | tf_op jit(solution)/shard_map/ppermute | solution.py:357
  52.7 14.2 %copy-start.17 = (bf16[2,48,1024]{2,1,0:T(8,128)(2,1)}, bf16[2,48,1024]{2,1,0:T(8,128)(2,1)S(1)}, u32[]{:S(2)}) copy-start(bf16[2,48,1024]{2,1,0:T(8,128)(2,1)S(1)} %collective-permute-done.5.low_ref) | copy-start | bytes 589828
  58.7 2.0 %collective-permute-start.7 = (bf16[256,1024]{1,0:T(8,128)(2,1)S(1)}, bf16[256,1024]{1,0:T(8,128)(2,1)S(1)}, u32[]{:S(2)}, u32[]{:S(2)}) collective-permute-start(bf16[256,1024]{1,0:T(8,128)(2,1)S(1)} %get-tuple-element.42.left_ref), channel_id=1, source_target_pairs={{0,16},{16,0},{1,17},{17,1},{2,18},{18,2},{3,19},{19,3},{4,20},{20... | collective-permute-start | bytes 1572872 | tf_op jit(solution)/shard_map/ppermute | solution.py:465
  68.1 11.3 %copy-start.5 = (f32[384,1024]{1,0:T(8,128)}, f32[384,1024]{1,0:T(8,128)S(1)}, u32[]{:S(2)}) copy-start(f32[384,1024]{1,0:T(8,128)S(1)} %get-tuple-element.49.lin_ref) | copy-start | bytes 4718596
  68.1 11.5 %slice-start.1 = ((bf16[2,48,1024]{2,1,0:T(8,128)(2,1)}), bf16[2,16,1024]{2,1,0:T(8,128)(2,1)S(1)}, s32[]{:S(2)}) async-start(bf16[2,48,1024]{2,1,0:T(8,128)(2,1)} %copy-done.18), calls=%async_computation.7 | async-start | bytes 131072 | tf_op jit(solution)/shard_map/slice | solution.py:443
  68.2 11.4 %slice-start = ((bf16[2,48,1024]{2,1,0:T(8,128)(2,1)}), bf16[2,16,1024]{2,1,0:T(8,128)(2,1)S(1)}, s32[]{:S(2)}) async-start(bf16[2,48,1024]{2,1,0:T(8,128)(2,1)} %copy-done.17), calls=%async_computation.6 | async-start | bytes 131072 | tf_op jit(solution)/shard_map/slice | solution.py:443
  79.4 20.8 %copy-start.3 = (bf16[2,128,1024]{2,1,0:T(8,128)(2,1)}, bf16[2,128,1024]{2,1,0:T(8,128)(2,1)S(1)}, u32[]{:S(2)}) copy-start(bf16[2,128,1024]{2,1,0:T(8,128)(2,1)S(1)} %slice.37) | copy-start | bytes 1572868
  79.4 20.8 %collective-permute-start.10 = (bf16[256,1024]{1,0:T(8,128)(2,1)S(1)}, bf16[256,1024]{1,0:T(8,128)(2,1)}, u32[]{:S(2)}, u32[]{:S(2)}) collective-permute-start(bf16[256,1024]{1,0:T(8,128)(2,1)S(1)} %bitcast.61), channel_id=1, source_target_pairs={{0,16},{16,0},{1,17},{17,1},{2,18},{18,2},{3,19},{19,3},{4,20},{20... | collective-permute-start | bytes 1572872 | tf_op jit(solution)/shard_map/ppermute | solution.py:488
  91.1 9.1 %copy-start.16 = (bf16[256,1024]{1,0:T(8,128)(2,1)S(1)}, bf16[256,1024]{1,0:T(8,128)(2,1)}, u32[]{:S(2)}) copy-start(bf16[256,1024]{1,0:T(8,128)(2,1)} %copy-done.15) | copy-start | bytes 1572868
  100.0 14.3 %collective-permute-start.8 = (bf16[256,2048]{1,0:T(8,128)(2,1)}, bf16[256,2048]{1,0:T(8,128)(2,1)S(1)}, u32[]{:S(2)}, u32[]{:S(2)}) collective-permute-start(bf16[256,2048]{1,0:T(8,128)(2,1)} %get-tuple-element.52.right_ref), channel_id=1, source_target_pairs={{0,16},{16,0},{1,17},{17,1},{2,18},{18,2},{3,19},{19,3},{4,20},{20... | collective-permute-start | bytes 3145736 | tf_op jit(solution)/shard_map/ppermute | solution.py:526
  100.2 14.1 %copy-start.12 = (bf16[256,1024]{1,0:T(8,128)(2,1)S(1)}, bf16[256,1024]{1,0:T(8,128)(2,1)}, u32[]{:S(2)}) copy-start(bf16[256,1024]{1,0:T(8,128)(2,1)} %copy-done.11) | copy-start | bytes 1572868
  103.2 11.2 %copy-start.14 = (bf16[256,1024]{1,0:T(8,128)(2,1)S(1)}, bf16[256,1024]{1,0:T(8,128)(2,1)}, u32[]{:S(2)}) copy-start(bf16[256,1024]{1,0:T(8,128)(2,1)} %copy-done.13) | copy-start | bytes 1572868
  103.2 9.7 %copy-start.20 = (f32[40,1024]{1,0:T(8,128)S(1)}, f32[40,1024]{1,0:T(8,128)}, u32[]{:S(2)}) copy-start(f32[40,1024]{1,0:T(8,128)} %copy-done.19) | copy-start | bytes 491524
  103.2 28.7 %all-to-all-start.2 = ((bf16[64,8,1024]{2,1,0:T(8,128)(2,1)}), bf16[64,8,1024]{2,1,0:T(8,128)(2,1)}, u32[]{:S(2)}, u32[]{:S(2)}) async-start(bf16[64,8,1024]{2,1,0:T(8,128)(2,1)} %bitcast.24), calls=%async_computation.2 | async-start | bytes 2097152 | tf_op jit(solution)/shard_map/all_to_all | solution.py:502
  112.8 1.5 collective-permute-start.9
  131.8 36.6 %all-to-all-start.1 = ((bf16[64,8,2304]{2,1,0:T(8,128)(2,1)}), bf16[64,8,2304]{2,1,0:T(8,128)(2,1)S(1)}, u32[]{:S(2)}, u32[]{:S(2)}) async-start(bf16[64,8,2304]{2,1,0:T(8,128)(2,1)} %bitcast.23), calls=%async_computation.1 | async-start | bytes 4718592 | tf_op jit(solution)/shard_map/all_to_all | solution.py:502
  169.8 16.6 %all-to-all-start.3 = ((bf16[16,8,3328]{2,1,0:T(8,128)(2,1)}), bf16[16,8,3328]{2,1,0:T(8,128)(2,1)S(1)}, u32[]{:S(2)}, u32[]{:S(2)}) async-start(bf16[16,8,3328]{2,1,0:T(8,128)(2,1)} %copy-done.2), calls=%async_computation.3 | async-start | bytes 1703936 | tf_op jit(solution)/shard_map/all_to_all | solution.py:554
  (18 other events, 47.9 us)
Sparse Core Ops, SparseCore 0:
  9.7 48.8 all-gather.2
  60.3 25.3 all-gather.4

commit v6 on v5

--- a/solution.py
+++ b/solution.py
@@ -28,6 +28,7 @@
     blocks = width // LANES
     taps_count = taps_ref.shape[1] - 1
     wide = padded - 2 * EDGE
+    own = wide - 2 * EDGE
     shift = EDGE - taps_count // 2
 
     def one_slab(s, carry):
@@ -50,27 +51,47 @@
 
         lax.fori_loop(0, (wide // ROWS_STEP) * (blocks // 2), conv_step, 0)
 
-        def row_step(i, carry):
+        def row_step(i, own_rows):
             row = pl.multiple_of(i * 16, 16)
             out_row = pl.multiple_of(s * wide + i * 16, 16)
             mixing = jnp.concatenate([mix_ref[b, pl.ds(row, 16)] for b in range(blocks)], axis=1)
             centered = mixing - jnp.mean(mixing, axis=-1, keepdims=True)
             scale = lax.rsqrt(jnp.mean(centered * centered, axis=-1, keepdims=True) + EPS)
             normed = centered * scale
-            value = normed * gain_ref[0:1, :]
-            act_ref[pl.ds(out_row, 16), :] = (value * jax.nn.sigmoid(value)).astype(act_ref.dtype)
+            if own_rows:
+                act_row = pl.multiple_of(s * own + i * 16 - EDGE, 16)
+                value = normed * gain_ref[0:1, :]
+                act_ref[pl.ds(act_row, 16), :] = (value * jax.nn.sigmoid(value)).astype(
+                    act_ref.dtype
+                )
             normed_ref[pl.ds(out_row, 16), :] = normed
             scale_ref[pl.ds(out_row, 16), :] = jnp.broadcast_to(scale, (16, LANES))
+
+        steps = wide // 16
+        row_step(0, False)
+        row_step(steps - 1, False)
+
+        def own_step(i, carry):
+            row_step(i + 1, True)
             return carry
 
-        return lax.fori_loop(0, wide // 16, row_step, carry)
+        return lax.fori_loop(0, steps - 2, own_step, carry, unroll=4)
 
     lax.fori_loop(0, slabs, one_slab, 0)
 
 
-def middle_kernel(normed_ref, scale_ref, grad_act_ref, gain_ref, grad_mix_ref, grad_gain_ref):
+def middle_kernel(
+    normed_ref, scale_ref, upstream_ref, weight_ref, gain_ref,
+    grad_mix_ref, grad_gain_ref, grad_act_ref,
+):
     slabs, frames, _ = grad_mix_ref.shape
     steps = frames // 16
+    grad_act_ref[...] = lax.dot_general(
+        upstream_ref[...],
+        weight_ref[...],
+        (((1,), (1,)), ((), ())),
+        preferred_element_type=jnp.float32,
+    )
 
     def row_step(i, total):
         row = pl.multiple_of(i * 16, 16)
@@ -93,7 +114,7 @@
         return total
 
     grad_gain_ref[...] = lax.fori_loop(
-        0, slabs * steps, row_step, jnp.zeros(grad_gain_ref.shape, jnp.float32)
+        0, slabs * steps, row_step, jnp.zeros(grad_gain_ref.shape, jnp.float32), unroll=4
     )
 
 
@@ -274,7 +295,9 @@
     )(core, left, left_other, right, right_other, *small)
 
 
-def norm_kernel(frames_ref, low_ref, high_ref, gain_ref, wide_ref, own_ref):
+def norm_kernel(
+    frames_ref, low_ref, high_ref, upstream_ref, gain_ref, wide_ref, own_ref, up_wide_ref
+):
     slabs, padded, _ = wide_ref.shape
     reach = 2 * EDGE
     own = padded - 2 * reach
@@ -299,7 +322,12 @@
         wide_ref[i // steps, pl.ds(pl.multiple_of(reach + (i % steps) * 16, 16), 16), :] = rows
         return carry
 
-    lax.fori_loop(0, slabs * own // 16, step, 0, unroll=2)
+    lax.fori_loop(0, slabs * own // 16, step, 0, unroll=4)
+    for s in range(slabs):
+        base = s * (own + 2 * EDGE)
+        up_wide_ref[base : base + EDGE, :] = low_ref[s, reach:, :]
+        up_wide_ref[base + EDGE : base + EDGE + own, :] = upstream_ref[s]
+        up_wide_ref[base + EDGE + own : base + 2 * EDGE + own, :] = high_ref[s, reach:, :]
 
 
 def project_kernel(normed_ref, lin_w_ref, gate_w_ref, lin_ref, sig_ref, gated_ref):
@@ -331,7 +359,7 @@
         ],
         out_specs=(out, out, out),
         name="project",
-        compiler_params=pltpu.CompilerParams(vmem_limit_bytes=VMEM_GRANT),
+        compiler_params=pltpu.CompilerParams(vmem_limit_bytes=50 * 1024 * 1024),
         cost_estimate=pl.CostEstimate(
             flops=4 * rows * width * width,
             bytes_accessed=4 * width * width,
@@ -439,10 +467,6 @@
     taps = jnp.pad(side[:kernel_len], ((0, 1), (0, 0)))
     taps = taps.reshape(kernel_len + 1, width // LANES, LANES).transpose(1, 0, 2)
 
-    upstream_wide = jnp.concatenate(
-        [low[:, 2 * EDGE :], upstream, high[:, 2 * EDGE :]], axis=1
-    ).reshape(-1, width)
-
     id_pad = jnp.pad(segment_ids, ((0, 0), (2 * EDGE, 2 * EDGE)), constant_values=-1)
     window = lax.dynamic_slice_in_dim(
         id_pad, lax.axis_index(SEQ) * frames_dev, frames_dev + 4 * EDGE, 1
@@ -452,27 +476,28 @@
     frame_rows = frames.astype(jnp.float32)
     _, pull_pre = jax.vjp(norm_rows, frame_rows, gain_pre)
     padded = frames_dev + 4 * EDGE
-    normed_wide, normed = kernel_call(
+    normed_wide, normed, upstream_wide = kernel_call(
         norm_kernel,
         (
             jax.ShapeDtypeStruct((slabs, padded, width), jnp.bfloat16),
             jax.ShapeDtypeStruct((rows_dev, width), jnp.bfloat16),
+            jax.ShapeDtypeStruct((slabs * (frames_dev + 2 * EDGE), width), jnp.bfloat16),
         ),
         [],
         rows_dev * width * 10,
-        frames, low, high, gain_pre[None],
+        frames, low, high, upstream, gain_pre[None],
     )
     normed_other = lax.ppermute(normed, "core", swap)
-    in_full, normed_other = lax.optimization_barrier((in_full, normed_other))
     lin, sig, gated = project(normed_wide.reshape(-1, width), in_full)
+    gated, normed_other = lax.optimization_barrier((gated, normed_other))
     gated = gated.reshape(slabs, padded, width)
     elements = rows_dev * width
     wide = frames_dev + 2 * EDGE
     blocks = width // LANES
-    act_wide, normed_mid, scale_mid = kernel_call(
+    activated, normed_mid, scale_mid = kernel_call(
         forward_kernel,
         (
-            jax.ShapeDtypeStruct((slabs * wide, width), jnp.bfloat16),
+            jax.ShapeDtypeStruct((rows_dev, width), jnp.bfloat16),
             jax.ShapeDtypeStruct((slabs * wide, width), jnp.float32),
             jax.ShapeDtypeStruct((slabs * wide, LANES), jnp.float32),
         ),
@@ -483,19 +508,16 @@
         elements * 3 * kernel_len,
         gated, ids, taps, gain_mid[None],
     )
-    activated = act_wide.reshape(slabs, wide, width)[:, EDGE : EDGE + frames_dev]
-    activated = activated.reshape(rows_dev, width)
     act_other = lax.ppermute(activated, "core", swap)
-    grad_act = jnp.dot(upstream_wide, out_full.T, preferred_element_type=jnp.float32)
     grad_mixing, grad_gain_mid = kernel_call(
         middle_kernel,
         (
             jax.ShapeDtypeStruct((slabs, wide, width), jnp.float32),
             jax.ShapeDtypeStruct((8, width), jnp.float32),
         ),
-        [],
-        elements * 30,
-        normed_mid, scale_mid, grad_act, gain_mid[None],
+        [pltpu.VMEM((slabs * wide, width), jnp.float32)],
+        2 * slabs * wide * width * width,
+        normed_mid, scale_mid, upstream_wide, out_full, gain_mid[None],
     )
 
     def exchanged(part):

time: 195 us -> 195 us (level)
    all_gather x1, waiting for transfers between devices: 5.19 us -> 9.59 us  [per_device(): out_full = lax.all_gather(out_weight, DP, axis=0, tiled=True)]
    pallas_call x8, Pallas kernels: 27.1 us -> 23.3 us  [kernel_call(): pl.pallas_call(body, out_shape=outs, scratch_shapes=scratch, compiler_par...]
    dot_general x1 -> x0, matrix products: 2.81 us -> none  [per_device(): jnp.dot(upstream_wide, out_full.T, preferred_element_type=jnp.float32)]
    pallas_call x1, Pallas kernels: 3.28 us -> 5.29 us  [project(): pl.pallas_call(project_kernel, out_shape=(jax.ShapeDtypeStruct((rows, wid...]
    unnamed x70 -> x56, local copies, waits for them, and re-layouts: 9.35 us -> 10.9 us
  transfers between devices with their start and end apart: 17 -> 17, of which waited for: 11 -> 9; matrix products, arithmetic and copies ran while one was open for 9% -> 7% of each run, Pallas kernels for 18% -> 17%
where the time goes in v6:
time: 195 us; the launch traced here: 194 us
  waiting for transfers between devices  77.7 us (40%)
  starting transfers between devices  41.1 us (21%)
  Pallas kernels  35.4 us (18%)
  between operations  14.5 us (7%)
  local copies, waits for them, and re-layouts  12.9 us (7%)
  matrix products  6.48 us (3%)
  other arithmetic  5.56 us (3%)
    all_to_all x2, waiting for transfers between devices, exchanged(): lax.all_to_all(part.reshape(n_z * n_seq, LANES // n_seq, part.shape[1]),...  36.4 us
    pallas_call x8, Pallas kernels, kernel_call(): pl.pallas_call(body, out_shape=outs, scratch_shapes=scratch, compiler_par...  23.3 us
    all_to_all x2, starting transfers between devices, exchanged(): lax.all_to_all(part.reshape(n_z * n_seq, LANES // n_seq, part.shape[1]),...  14.6 us
    ppermute x3, waiting for transfers between devices, per_device(): lax.ppermute(pair, 'z', [(i, (i + d) % n_z) for i in range(n_z)])  14.4 us
    all_to_all x1, starting transfers between devices, per_device(): lax.all_to_all(outgoing, (*DP, *SEQ), split_axis=0, concat_axis=0, tiled=...  11.2 us
    unnamed x56, local copies, waits for them, and re-layouts  10.9 us
    all_gather x1, waiting for transfers between devices, per_device(): out_full = lax.all_gather(out_weight, DP, axis=0, tiled=True)  9.59 us
    all_to_all x1, waiting for transfers between devices, per_device(): final = lax.all_to_all(total, SEQ, 0, 0, tiled=True).reshape(LANES, -1)  8.36 us
  transfers between devices with their start and end apart: 17, of which 9 were waited for; matrix products, arithmetic and copies ran while one was open for 7% of the time, Pallas kernels for 17%

profile of v6, /device:TPU:0, one launch (start us, length us, event | category | flops | bytes accessed | tf_op | source)
XLA Modules:
  0.0 193.5 jit_solution(12929130291605874401)
XLA Ops:
  11.0 1.5 shard_map.127
  12.4 11.2 %all-to-all-start = ((bf16[128,8,512]{2,1,0:T(8,128)(2,1)}), bf16[128,8,512]{2,1,0:T(8,128)(2,1)S(1)}, u32[]{:S(2)}, u32[]{:S(2)}) async-start(bf16[128,8,512]{2,1,0:T(8,128)(2,1)} %shard_map.127), calls=%async_computation | async-start | bytes 2097152 | tf_op jit(solution)/shard_map/all_to_all | solution.py:424
  25.1 1.1 collective-permute-start.2
  26.2 3.2 %collective-permute-start.3 = (bf16[2,128,128]{1,2,0:T(8,128)(2,1)S(1)}, bf16[2,128,128]{1,2,0:T(8,128)(2,1)S(1)}, u32[]{:S(2)}, u32[]{:S(2)}) collective-permute-start(bf16[2,128,128]{1,2,0:T(8,128)(2,1)S(1)} %maximum_select_fusion), channel_id=1, source_target_pairs={{0,64},{32,96},{64,0},{96,32},{1,65},{33,97},{65,1},{97,33},{2,66}... | collective-permute-start | bytes 196616 | tf_op jit(solution)/shard_map/ppermute | solution.py:436
  29.4 1.2 collective-permute-start.4
  30.8 11.3 %collective-permute-done.2 = bf16[2,128,128]{1,2,0:T(8,128)(2,1)S(1)} collective-permute-done((bf16[2,128,128]{1,2,0:T(8,128)(2,1)S(1)}, bf16[2,128,128]{1,2,0:T(8,128)(2,1)S(1)}, u32[]{:S(2)}, u32[]{:S(2)}) %collective-permute-start.2) | collective-permute-done | bytes 65568 | tf_op jit(solution)/shard_map/ppermute | solution.py:436
  42.1 3.1 %collective-permute-done.3 = bf16[2,128,128]{1,2,0:T(8,128)(2,1)S(1)} collective-permute-done((bf16[2,128,128]{1,2,0:T(8,128)(2,1)S(1)}, bf16[2,128,128]{1,2,0:T(8,128)(2,1)S(1)}, u32[]{:S(2)}, u32[]{:S(2)}) %collective-permute-start.3) | collective-permute-done | bytes 65568 | tf_op jit(solution)/shard_map/ppermute | solution.py:436
  46.9 2.8 %collective-permute-start.5 = (bf16[2,48,1024]{2,1,0:T(8,128)(2,1)S(1)}, bf16[2,48,1024]{2,1,0:T(8,128)(2,1)S(1)}, u32[]{:S(2)}, u32[]{:S(2)}) collective-permute-start(bf16[2,48,1024]{2,1,0:T(8,128)(2,1)S(1)} %get-tuple-element.36), channel_id=1, source_target_pairs={{0,1},{1,2},{2,3},{3,4},{4,5},{5,6},{6,7},{7,8},{8,9},{9,10},{10,1... | collective-permute-start | bytes 589832 | tf_op jit(solution)/shard_map/ppermute | solution.py:385
  49.7 1.3 collective-permute-start.6
  51.1 2.7 %collective-permute-done.5.low_ref = bf16[2,48,1024]{2,1,0:T(8,128)(2,1)S(1)} collective-permute-done((bf16[2,48,1024]{2,1,0:T(8,128)(2,1)S(1)}, bf16[2,48,1024]{2,1,0:T(8,128)(2,1)S(1)}, u32[]{:S(2)}, u32[]{:S(2)}) %collective-permute-start.5) | collective-permute-done | bytes 196640 | tf_op jit(solution)/shard_map/ppermute | solution.py:385
  53.8 4.1 %collective-permute-done.6.high_ref = bf16[2,48,1024]{2,1,0:T(8,128)(2,1)S(1)} collective-permute-done((bf16[2,48,1024]{2,1,0:T(8,128)(2,1)S(1)}, bf16[2,48,1024]{2,1,0:T(8,128)(2,1)S(1)}, u32[]{:S(2)}, u32[]{:S(2)}) %collective-permute-start.6) | collective-permute-done | bytes 196640 | tf_op jit(solution)/shard_map/ppermute | solution.py:385
  60.1 5.3 %project.1 = (f32[384,1024]{1,0:T(8,128)S(1)}, f32[384,1024]{1,0:T(8,128)}, bf16[384,1024]{1,0:T(8,128)(2,1)S(1)}) custom-call(bf16[384,1024]{1,0:T(8,128)(2,1)S(1)} %bitcast.57, bf16[1024,2048]{1,0:T(8,128)(2,1)} %all-gather.3.cloned.1.call-done.lin_w_ref.gate_w_ref, bf16[1024,2048]{1,0:T(8,128)(2,1)} %all-gather.3.cloned.1.call-done.lin_w_ref.gate_w_ref), custom_call_target="tpu_custom_call" | custom-call | flops 1610612736 | bytes 4194304 | tf_op jit(solution)/shard_map/project/pallas_call | solution.py:347
  65.4 1.1 copy-done.4
  66.6 8.2 %shard_map.130 = (bf16[256,1024]{1,0:T(8,128)(2,1)}, f32[320,1024]{1,0:T(8,128)S(1)}, f32[320,128]{1,0:T(8,128)S(1)}) custom-call(bf16[2,192,1024]{2,1,0:T(8,128)(2,1)S(1)} %bitcast.54, s32[2,192,128]{2,1,0:T(8,128)S(1)} %broadcast_in_dim.39.ids_ref, f32[8,32,128]{2,1,0:T(8,128)S(1)} %bitcast_bitcast_fusion.taps_ref, f32[1,1024]{1,0:T(1,128)S(1)} %get-tuple-element.70.gain_ref), custom_call_target="tpu_custom_call" | custom-call | flops 24379392 | bytes 1118208 | tf_op jit(solution)/shard_map/pallas_call | solution.py:373
  76.0 9.6 %all-gather.5.cloned.1.call-done.weight_ref = bf16[1024,1024]{1,0:T(8,128)(2,1)} async-done(((bf16[128,1024]{1,0:T(8,128)(2,1)}), bf16[1024,1024]{1,0:T(8,128)(2,1)}) %all-gather.5.cloned.1.call-update) | async-done | bytes 2097168 | tf_op jit(solution)/shard_map/all_gather | solution.py:411
  85.6 1.6 copy-done.2
  89.2 2.1 %shard_map.131 = (f32[2,160,1024]{2,1,0:T(8,128)S(1)}, f32[8,1024]{1,0:T(8,128)S(1)}) custom-call(f32[320,1024]{1,0:T(8,128)S(1)} %get-tuple-element.47.normed_ref, f32[320,128]{1,0:T(8,128)S(1)} %copy-done.15, bf16[320,1024]{1,0:T(8,128)(2,1)S(1)} %copy-done.9, bf16[1024,1024]{1,0:T(8,128)(2,1)S(1)} %copy-done.2, f32[1,1024]{1,0:T(1,128)S(1)} %get-tuple-element.70.gain_ref), custom_call_target="tpu_custom_call" | custom-call | flops 671088640 | bytes 4231168 | tf_op jit(solution)/shard_map/pallas_call | solution.py:373
  91.4 7.9 %shard_map.132 = (bf16[256,2048]{1,0:T(8,128)(2,1)S(1)}, f32[40,1024]{1,0:T(8,128)S(1)}) custom-call(f32[2,160,1024]{2,1,0:T(8,128)S(1)} %get-tuple-element.50.grad_mix_ref, bf16[2,192,1024]{2,1,0:T(8,128)(2,1)S(1)} %bitcast.55, s32[2,192,128]{2,1,0:T(8,128)S(1)} %broadcast_in_dim.39.ids_ref, f32[8,32,128]{2,1,0:T(8,128)S(1)} %bitcast_bitcast_fusion.taps_ref, ...), custom_call_target="tpu_custom_call" | custom-call | flops 40632320 | bytes 5603328 | tf_op jit(solution)/shard_map/pallas_call | solution.py:373
  99.7 3.0 %weight_part.3 = bf16[512,1024]{1,0:T(8,128)(2,1)} custom-call(s32[1]{0:T(128)} %bitcast.19.core_ref, bf16[256,1024]{1,0:T(8,128)(2,1)} %get-tuple-element.46.left_ref, bf16[256,1024]{1,0:T(8,128)(2,1)} %collective-permute-done.10.left_other_ref, bf16[256,1024]{1,0:T(8,128)(2,1)S(1)} %bitcast.52, bf16[256,1024]{1,0:T(8,128)(2,1)S(1)} %copy-done.13), custom_call_target="tpu_custom_call" | custom-call | flops 536870912 | bytes 2097152 | tf_op jit(solution)/shard_map/weight_part/pallas_call | solution.py:282
  102.6 9.6 %all-to-all-start.2 = ((bf16[64,8,1024]{2,1,0:T(8,128)(2,1)}), bf16[64,8,1024]{2,1,0:T(8,128)(2,1)}, u32[]{:S(2)}, u32[]{:S(2)}) async-start(bf16[64,8,1024]{2,1,0:T(8,128)(2,1)} %bitcast.21), calls=%async_computation.2 | async-start | bytes 2097152 | tf_op jit(solution)/shard_map/all_to_all | solution.py:524
  112.5 1.4 collective-permute-done.9.rest_1_
  114.9 3.8 %weight_part.2 = bf16[512,2304]{1,0:T(8,128)(2,1)} custom-call(s32[1]{0:T(128)} %bitcast.19.core_ref, bf16[256,1024]{1,0:T(8,128)(2,1)S(1)} %copy-done.11, bf16[256,1024]{1,0:T(8,128)(2,1)} %collective-permute-done.7.left_other_ref, bf16[256,2048]{1,0:T(8,128)(2,1)S(1)} %get-tuple-element.54.right_ref, ...), custom_call_target="tpu_custom_call" | custom-call | flops 1073741824 | bytes 3145728 | tf_op jit(solution)/shard_map/weight_part/pallas_call | solution.py:282
  118.8 12.4 %all-to-all-done.2 = bf16[64,8,1024]{2,1,0:T(8,128)(2,1)} async-done(((bf16[64,8,1024]{2,1,0:T(8,128)(2,1)}), bf16[64,8,1024]{2,1,0:T(8,128)(2,1)}, u32[]{:S(2)}, u32[]{:S(2)}) %all-to-all-start.2) | async-done | bytes 1048608 | tf_op jit(solution)/shard_map/all_to_all | solution.py:524
  131.2 5.0 %all-to-all-start.1 = ((bf16[64,8,2304]{2,1,0:T(8,128)(2,1)}), bf16[64,8,2304]{2,1,0:T(8,128)(2,1)S(1)}, u32[]{:S(2)}, u32[]{:S(2)}) async-start(bf16[64,8,2304]{2,1,0:T(8,128)(2,1)} %bitcast.20), calls=%async_computation.1 | async-start | bytes 4718592 | tf_op jit(solution)/shard_map/all_to_all | solution.py:524
  137.3 3.9 %fusion.4 = (f32[256]{0:T(256)S(1)}, f32[256]{0:T(256)S(1)}, f32[256,1024]{1,0:T(8,128)S(1)}) fusion(bf16[256,1024]{1,0:T(8,128)(2,1)S(1)} %get-tuple-element.35.frames_ref, f32[256]{0:T(256)S(1)} %broadcast_multiply_fusion, f32[1024]{0:T(1024)S(1)} %bitcast.58, bf16[256,2048]{1,0:T(8,128)(2,1)} %copy-done.7, ...), kind=kOutput, calls=%fused_computation.10 | convolution fusion | flops 1075576320 | bytes 6822912 | tf_op jit(solution)/shard_map/dot_general | solution.py:554
  142.2 1.4 convert_reduce_fusion.out_sum_ref
  143.6 24.0 %all-to-all-done.1.parts_ref = bf16[64,8,2304]{2,1,0:T(8,128)(2,1)S(1)} async-done(((bf16[64,8,2304]{2,1,0:T(8,128)(2,1)}), bf16[64,8,2304]{2,1,0:T(8,128)(2,1)S(1)}, u32[]{:S(2)}, u32[]{:S(2)}) %all-to-all-start.1) | async-done | bytes 2359328 | tf_op jit(solution)/shard_map/all_to_all | solution.py:524
  168.9 3.9 %all-to-all-start.3 = ((bf16[16,8,3328]{2,1,0:T(8,128)(2,1)}), bf16[16,8,3328]{2,1,0:T(8,128)(2,1)S(1)}, u32[]{:S(2)}, u32[]{:S(2)}) async-start(bf16[16,8,3328]{2,1,0:T(8,128)(2,1)} %copy-done.1), calls=%async_computation.3 | async-start | bytes 1703936 | tf_op jit(solution)/shard_map/all_to_all | solution.py:576
  172.8 1.2 add_convert_fusion
  174.6 2.6 %fusion.3 = bf16[256,1024]{1,0:T(8,128)(2,1)} fusion(bf16[256,1024]{1,0:T(8,128)(2,1)} %get-tuple-element.46.left_ref, bf16[1024,1024]{1,0:T(8,128)(2,1)S(1)} %copy-done.3, bf16[256,1024]{1,0:T(8,128)(2,1)S(1)} %get-tuple-element.35.frames_ref), kind=kOutput, calls=%fused_computation.9 | convolution fusion | flops 537657344 | bytes 3670016 | tf_op jit(solution)/shard_map/dot_general | solution.py:532
  177.2 8.4 %all-to-all-done.3 = bf16[16,8,3328]{2,1,0:T(8,128)(2,1)S(1)} async-done(((bf16[16,8,3328]{2,1,0:T(8,128)(2,1)}), bf16[16,8,3328]{2,1,0:T(8,128)(2,1)S(1)}, u32[]{:S(2)}, u32[]{:S(2)}) %all-to-all-start.3) | async-done | bytes 852000 | tf_op jit(solution)/shard_map/all_to_all | solution.py:576
  185.5 1.2 shard_map.134
  (109 shorter events, 18.0 us)
Async XLA Ops:
  7.2 52.9 %all-gather.3.cloned.1.call-start = ((), (), s32[]{:S(2)}) async-start(), calls=%async_computation.4 | async-start | bytes 4718592 | tf_op jit(solution)/shard_map/all_gather | solution.py:410
  11.0 12.7 %copy-start.21 = (bf16[128,31]{0,1:T(8,128)(2,1)S(1)}, bf16[128,31]{0,1:T(8,128)(2,1)}, u32[]{:S(2)}) copy-start(bf16[128,31]{0,1:T(8,128)(2,1)} %param.13) | copy-start | bytes 23812
  11.0 12.7 %copy-start.22 = (bf16[128,2]{0,1:T(2,128)(2,1)S(1)}, bf16[128,2]{0,1:T(2,128)(2,1)}, u32[]{:S(2)}) copy-start(bf16[128,2]{0,1:T(2,128)(2,1)} %param.14) | copy-start | bytes 1540
  11.0 12.8 %copy-start = (bf16[2,128,1024]{2,1,0:T(8,128)(2,1)S(1)}, bf16[2,128,1024]{2,1,0:T(8,128)(2,1)}, u32[]{:S(2)}) copy-start(bf16[2,128,1024]{2,1,0:T(8,128)(2,1)} %upstream_ref.3) | copy-start | bytes 1572868
  11.0 13.4 %copy-start.19 = (s32[128,128]{1,0:T(8,128)S(1)}, s32[128,128]{1,0:T(8,128)}, u32[]{:S(2)}) copy-start(s32[128,128]{1,0:T(8,128)} %param.9) | copy-start | bytes 196612
  12.4 32.7 %all-to-all-start = ((bf16[128,8,512]{2,1,0:T(8,128)(2,1)}), bf16[128,8,512]{2,1,0:T(8,128)(2,1)S(1)}, u32[]{:S(2)}, u32[]{:S(2)}) async-start(bf16[128,8,512]{2,1,0:T(8,128)(2,1)} %shard_map.127), calls=%async_computation | async-start | bytes 2097152 | tf_op jit(solution)/shard_map/all_to_all | solution.py:424
  23.6 62.0 %all-gather.5.cloned.1.call-start = ((), (), s32[]{:S(2)}) async-start(), calls=%async_computation.5 | async-start | bytes 2359296 | tf_op jit(solution)/shard_map/all_gather | solution.py:411
  23.7 1.3 collective-permute-start.1
  23.8 21.3 %collective-permute-start = (bf16[256,1024]{1,0:T(8,128)(2,1)S(1)}, bf16[256,1024]{1,0:T(8,128)(2,1)S(1)}, u32[]{:S(2)}, u32[]{:S(2)}) collective-permute-start(bf16[256,1024]{1,0:T(8,128)(2,1)S(1)} %bitcast.51), channel_id=1, source_target_pairs={{0,16},{16,0},{1,17},{17,1},{2,18},{18,2},{3,19},{19,3},{4,20},{20... | collective-permute-start | bytes 1572872 | tf_op jit(solution)/shard_map/ppermute | solution.py:438
  25.1 17.0 %collective-permute-start.2 = (bf16[2,128,128]{1,2,0:T(8,128)(2,1)S(1)}, bf16[2,128,128]{1,2,0:T(8,128)(2,1)S(1)}, u32[]{:S(2)}, u32[]{:S(2)}) collective-permute-start(bf16[2,128,128]{1,2,0:T(8,128)(2,1)S(1)} %maximum_select_fusion), channel_id=1, source_target_pairs={{0,32},{32,64},{64,96},{96,0},{1,33},{33,65},{65,97},{97,1},{2,34}... | collective-permute-start | bytes 196616 | tf_op jit(solution)/shard_map/ppermute | solution.py:436
  26.2 18.9 %collective-permute-start.3 = (bf16[2,128,128]{1,2,0:T(8,128)(2,1)S(1)}, bf16[2,128,128]{1,2,0:T(8,128)(2,1)S(1)}, u32[]{:S(2)}, u32[]{:S(2)}) collective-permute-start(bf16[2,128,128]{1,2,0:T(8,128)(2,1)S(1)} %maximum_select_fusion), channel_id=1, source_target_pairs={{0,64},{32,96},{64,0},{96,32},{1,65},{33,97},{65,1},{97,33},{2,66}... | collective-permute-start | bytes 196616 | tf_op jit(solution)/shard_map/ppermute | solution.py:436
  29.4 15.7 %collective-permute-start.4 = (bf16[2,128,128]{1,2,0:T(8,128)(2,1)S(1)}, bf16[2,128,128]{1,2,0:T(8,128)(2,1)S(1)}, u32[]{:S(2)}, u32[]{:S(2)}) collective-permute-start(bf16[2,128,128]{1,2,0:T(8,128)(2,1)S(1)} %maximum_select_fusion), channel_id=1, source_target_pairs={{0,96},{32,0},{64,32},{96,64},{1,97},{33,1},{65,33},{97,65},{2,98}... | collective-permute-start | bytes 196616 | tf_op jit(solution)/shard_map/ppermute | solution.py:436
  45.9 13.9 %copy-start.20 = (s32[2,2048]{1,0:T(2,128)S(1)}, s32[2,2048]{1,0:T(2,128)}, u32[]{:S(2)}) copy-start(s32[2,2048]{1,0:T(2,128)} %param.10) | copy-start | bytes 49156
  45.9 14.0 %copy-start.23 = (pred[32]{0:T(512)(128)(4,1)S(1)}, pred[32]{0:T(512)(128)(4,1)}, u32[]{:S(2)}) copy-start(pred[32]{0:T(512)(128)(4,1)} %constant.66.clone.1) | copy-start | bytes 100
  46.9 6.8 %collective-permute-start.5 = (bf16[2,48,1024]{2,1,0:T(8,128)(2,1)S(1)}, bf16[2,48,1024]{2,1,0:T(8,128)(2,1)S(1)}, u32[]{:S(2)}, u32[]{:S(2)}) collective-permute-start(bf16[2,48,1024]{2,1,0:T(8,128)(2,1)S(1)} %get-tuple-element.36), channel_id=1, source_target_pairs={{0,1},{1,2},{2,3},{3,4},{4,5},{5,6},{6,7},{7,8},{8,9},{9,10},{10,1... | collective-permute-start | bytes 589832 | tf_op jit(solution)/shard_map/ppermute | solution.py:385
  49.7 8.1 %collective-permute-start.6 = (bf16[2,48,1024]{2,1,0:T(8,128)(2,1)S(1)}, bf16[2,48,1024]{2,1,0:T(8,128)(2,1)S(1)}, u32[]{:S(2)}, u32[]{:S(2)}) collective-permute-start(bf16[2,48,1024]{2,1,0:T(8,128)(2,1)S(1)} %get-tuple-element.37), channel_id=1, source_target_pairs={{1,0},{2,1},{3,2},{4,3},{5,4},{6,5},{7,6},{8,7},{9,8},{10,9},{11,1... | collective-permute-start | bytes 589832 | tf_op jit(solution)/shard_map/ppermute | solution.py:385
  59.9 5.5 %copy-start.10 = (bf16[256,1024]{1,0:T(8,128)(2,1)}, bf16[256,1024]{1,0:T(8,128)(2,1)S(1)}, u32[]{:S(2)}) copy-start(bf16[256,1024]{1,0:T(8,128)(2,1)S(1)} %get-tuple-element.44.left_ref) | copy-start | bytes 1572868
  59.9 6.7 %collective-permute-start.7 = (bf16[256,1024]{1,0:T(8,128)(2,1)S(1)}, bf16[256,1024]{1,0:T(8,128)(2,1)}, u32[]{:S(2)}, u32[]{:S(2)}) collective-permute-start(bf16[256,1024]{1,0:T(8,128)(2,1)S(1)} %get-tuple-element.44.left_ref), channel_id=1, source_target_pairs={{0,16},{16,0},{1,17},{17,1},{2,18},{18,2},{3,19},{19,3},{4,20},{20... | collective-permute-start | bytes 1572872 | tf_op jit(solution)/shard_map/ppermute | solution.py:490
  65.4 1.2 copy-start.4
  75.5 24.1 %collective-permute-start.10 = (bf16[256,1024]{1,0:T(8,128)(2,1)}, bf16[256,1024]{1,0:T(8,128)(2,1)}, u32[]{:S(2)}, u32[]{:S(2)}) collective-permute-start(bf16[256,1024]{1,0:T(8,128)(2,1)} %get-tuple-element.46.left_ref), channel_id=1, source_target_pairs={{0,16},{16,0},{1,17},{17,1},{2,18},{18,2},{3,19},{19,3},{4,20},{20... | collective-permute-start | bytes 1572872 | tf_op jit(solution)/shard_map/ppermute | solution.py:511
  85.6 1.6 copy-start.2
  89.2 2.1 %copy-start.5 = (f32[384,1024]{1,0:T(8,128)S(1)}, f32[384,1024]{1,0:T(8,128)}, u32[]{:S(2)}) copy-start(f32[384,1024]{1,0:T(8,128)} %copy-done.4) | copy-start | bytes 4718596
  89.2 2.1 %copy-start.6 = (f32[384,1024]{1,0:T(8,128)S(1)}, f32[384,1024]{1,0:T(8,128)}, u32[]{:S(2)}) copy-start(f32[384,1024]{1,0:T(8,128)} %get-tuple-element.52.sig_ref) | copy-start | bytes 4718596
  91.4 8.3 %copy-start.13 = (bf16[256,1024]{1,0:T(8,128)(2,1)S(1)}, bf16[256,1024]{1,0:T(8,128)(2,1)}, u32[]{:S(2)}) copy-start(bf16[256,1024]{1,0:T(8,128)(2,1)} %copy-done.12) | copy-start | bytes 1572868
  99.3 14.6 %copy-start.7 = (bf16[256,2048]{1,0:T(8,128)(2,1)}, bf16[256,2048]{1,0:T(8,128)(2,1)S(1)}, u32[]{:S(2)}) copy-start(bf16[256,2048]{1,0:T(8,128)(2,1)S(1)} %get-tuple-element.54.right_ref) | copy-start | bytes 3145732
  99.3 14.6 %collective-permute-start.8 = (bf16[256,2048]{1,0:T(8,128)(2,1)S(1)}, bf16[256,2048]{1,0:T(8,128)(2,1)S(1)}, u32[]{:S(2)}, u32[]{:S(2)}) collective-permute-start(bf16[256,2048]{1,0:T(8,128)(2,1)S(1)} %get-tuple-element.54.right_ref), channel_id=1, source_target_pairs={{0,16},{16,0},{1,17},{17,1},{2,18},{18,2},{3,19},{19,3},{4,20},{20... | collective-permute-start | bytes 3145736 | tf_op jit(solution)/shard_map/ppermute | solution.py:548
  102.6 28.6 %all-to-all-start.2 = ((bf16[64,8,1024]{2,1,0:T(8,128)(2,1)}), bf16[64,8,1024]{2,1,0:T(8,128)(2,1)}, u32[]{:S(2)}, u32[]{:S(2)}) async-start(bf16[64,8,1024]{2,1,0:T(8,128)(2,1)} %bitcast.21), calls=%async_computation.2 | async-start | bytes 2097152 | tf_op jit(solution)/shard_map/all_to_all | solution.py:524
  112.2 1.7 collective-permute-start.9
  131.2 36.3 %all-to-all-start.1 = ((bf16[64,8,2304]{2,1,0:T(8,128)(2,1)}), bf16[64,8,2304]{2,1,0:T(8,128)(2,1)S(1)}, u32[]{:S(2)}, u32[]{:S(2)}) async-start(bf16[64,8,2304]{2,1,0:T(8,128)(2,1)} %bitcast.20), calls=%async_computation.1 | async-start | bytes 4718592 | tf_op jit(solution)/shard_map/all_to_all | solution.py:524
  168.9 3.9 %copy-start.18 = (f32[256,1024]{1,0:T(8,128)S(1)}, f32[256,1024]{1,0:T(8,128)}, u32[]{:S(2)}) copy-start(f32[256,1024]{1,0:T(8,128)} %copy-done.17) | copy-start | bytes 3145732
  168.9 16.6 %all-to-all-start.3 = ((bf16[16,8,3328]{2,1,0:T(8,128)(2,1)}), bf16[16,8,3328]{2,1,0:T(8,128)(2,1)S(1)}, u32[]{:S(2)}, u32[]{:S(2)}) async-start(bf16[16,8,3328]{2,1,0:T(8,128)(2,1)} %copy-done.1), calls=%async_computation.3 | async-start | bytes 1703936 | tf_op jit(solution)/shard_map/all_to_all | solution.py:576
  172.8 1.8 copy-start.3
  (9 other events, 8.3 us)
Sparse Core Ops, SparseCore 0:
  9.7 48.8 all-gather.2
  60.3 25.2 all-gather.4

commit v7 on v6

--- a/solution.py
+++ b/solution.py
@@ -16,13 +16,13 @@
 LANES = 128
 ROWS_STEP = 32
 EPS = 1e-05
-SMALL = 2 * LANES
+SMALL = LANES
 VMEM_GRANT = 16 * 1024 * 1024
 
 
 def forward_kernel(
     gated_ref, ids_ref, taps_ref, gain_ref,
-    act_ref, normed_ref, scale_ref, pad_ref, mix_ref,
+    act_ref, normed_ref, pad_ref, mix_ref,
 ):
     slabs, padded, width = gated_ref.shape
     blocks = width // LANES
@@ -64,8 +64,8 @@
                 act_ref[pl.ds(act_row, 16), :] = (value * jax.nn.sigmoid(value)).astype(
                     act_ref.dtype
                 )
-            normed_ref[pl.ds(out_row, 16), :] = normed
-            scale_ref[pl.ds(out_row, 16), :] = jnp.broadcast_to(scale, (16, LANES))
+            normed_ref[pl.ds(out_row, 16), :width] = normed
+            normed_ref[pl.ds(out_row, 16), width:] = jnp.broadcast_to(scale, (16, LANES))
 
         steps = wide // 16
         row_step(0, False)
@@ -81,22 +81,36 @@
 
 
 def middle_kernel(
-    normed_ref, scale_ref, upstream_ref, weight_ref, gain_ref,
-    grad_mix_ref, grad_gain_ref, grad_act_ref,
+    normed_ref, upstream_ref, weight_ref, gain_ref,
+    grad_mix_ref, grad_gain_ref, grad_act_ref, up_ref, loaded_ref, arrivals,
 ):
-    slabs, frames, _ = grad_mix_ref.shape
+    slabs, frames, width = grad_mix_ref.shape
     steps = frames // 16
-    grad_act_ref[...] = lax.dot_general(
-        upstream_ref[...],
-        weight_ref[...],
-        (((1,), (1,)), ((), ())),
-        preferred_element_type=jnp.float32,
-    )
+    parts, depth, _ = loaded_ref.shape
+    up_copy = pltpu.make_async_copy(upstream_ref, up_ref, arrivals.at[parts])
+    up_copy.start()
+    copies = [
+        pltpu.make_async_copy(
+            weight_ref.at[pl.ds(h * depth, depth)], loaded_ref.at[h], arrivals.at[h]
+        )
+        for h in range(parts)
+    ]
+    for copy in copies:
+        copy.start()
+    up_copy.wait()
+    for h, copy in enumerate(copies):
+        copy.wait()
+        grad_act_ref[:, h * depth : (h + 1) * depth] = lax.dot_general(
+            up_ref[...],
+            loaded_ref[h],
+            (((1,), (1,)), ((), ())),
+            preferred_element_type=jnp.float32,
+        )
 
     def row_step(i, total):
         row = pl.multiple_of(i * 16, 16)
-        normed = normed_ref[pl.ds(row, 16), :]
-        scale = scale_ref[pl.ds(row, 16), 0:1]
+        normed = normed_ref[pl.ds(row, 16), :width]
+        scale = normed_ref[pl.ds(row, 16), width : width + 1]
         gain = gain_ref[0:1, :]
         value = normed * gain
         sig = jax.nn.sigmoid(value)
@@ -214,7 +228,9 @@
         first_ref[s, reach:, :] = upstream_ref[s, :EDGE, :]
 
 
-def total_kernel(parts_ref, out_sum_ref, weight_ref, gain_ref, total_ref, sum_ref, *, tap, scale):
+def total_kernel(
+    parts_ref, out_sum_ref, weight_ref, gain_ref, total_ref, sum_ref, tile_ref, leaving, *, tap, scale
+):
     count, share, width = parts_ref.shape
     in_width = weight_ref.shape[1]
     grad_gain = jnp.zeros((share, 1), jnp.float32)
@@ -229,9 +245,16 @@
     small = sum_ref[:, in_width:]
     column = lax.broadcasted_iota(jnp.int32, small.shape, 1)
     sum_ref[:, in_width:] = jnp.where(column == tap, grad_gain / gain_ref[...], small)
-    for i in range(total_ref.shape[0]):
-        total_ref[i, :, :width] = (sum_ref[...] * scale).astype(jnp.bfloat16)
-        total_ref[i, :, width:] = (out_sum_ref[...] * scale).astype(jnp.bfloat16)
+    tile_ref[0, :, :width] = (sum_ref[...] * scale).astype(jnp.bfloat16)
+    tile_ref[0, :, width:] = (out_sum_ref[...] * scale).astype(jnp.bfloat16)
+    copies = [
+        pltpu.make_async_copy(tile_ref, total_ref.at[pl.ds(i, 1)], leaving.at[i])
+        for i in range(total_ref.shape[0])
+    ]
+    for copy in copies:
+        copy.start()
+    for copy in copies:
+        copy.wait()
 
 
 def finish_kernel(final_ref, grad_in_ref, grad_out_ref, grad_taps_ref, grad_gains_ref):
@@ -270,7 +293,6 @@
             )
             block = slice(z * LANES, (z + 1) * LANES)
             out_ref[block, width : width + LANES] = filled.T.astype(out_ref.dtype)
-            out_ref[block, width + LANES :] = jnp.zeros((LANES, SMALL - LANES), out_ref.dtype)
 
 
 def weight_part(core, left, left_other, right, right_other, *small):
@@ -330,20 +352,43 @@
         up_wide_ref[base + EDGE + own : base + 2 * EDGE + own, :] = high_ref[s, reach:, :]
 
 
-def project_kernel(normed_ref, lin_w_ref, gate_w_ref, lin_ref, sig_ref, gated_ref):
-    lin = jnp.dot(normed_ref[...], lin_w_ref[...], preferred_element_type=jnp.float32)
-    gate = jnp.dot(normed_ref[...], gate_w_ref[...], preferred_element_type=jnp.float32)
-    sig = jax.nn.sigmoid(gate)
-    lin_ref[...] = lin
-    sig_ref[...] = sig
-    gated_ref[...] = (lin * sig).astype(jnp.bfloat16)
+def project_kernel(normed_ref, weight_ref, lin_ref, sig_ref, gated_ref, loaded_ref, arrivals):
+    parts, depth, both = loaded_ref.shape
+    width = both // 2
+    step = 256
+    copies = [
+        pltpu.make_async_copy(
+            weight_ref.at[pl.ds(h * depth, depth)], loaded_ref.at[h], arrivals.at[h]
+        )
+        for h in range(parts)
+    ]
+    for copy in copies:
+        copy.start()
+    for h, copy in enumerate(copies):
+        copy.wait()
+        rows = normed_ref[:, h * depth : (h + 1) * depth]
+        for at in range(0, width, step):
+            cols = slice(at, at + step)
+            lin = jnp.dot(rows, loaded_ref[h, :, cols], preferred_element_type=jnp.float32)
+            gate = jnp.dot(
+                rows,
+                loaded_ref[h, :, width + at : width + at + step],
+                preferred_element_type=jnp.float32,
+            )
+            if h > 0:
+                lin = lin + lin_ref[:, cols]
+                gate = gate + sig_ref[:, cols]
+            if h == parts - 1:
+                gate = jax.nn.sigmoid(gate)
+                gated_ref[:, cols] = (lin * gate).astype(jnp.bfloat16)
+            lin_ref[:, cols] = lin
+            sig_ref[:, cols] = gate
 
 
 def project(normed, weight):
     rows, width = normed.shape
-    cols = 256
-    steps = width // cols
-    out = pl.BlockSpec((rows, cols), lambda j: (0, j))
+    parts = 2
+    vmem = pl.BlockSpec(memory_space=pltpu.VMEM)
     return pl.pallas_call(
         project_kernel,
         out_shape=(
@@ -351,31 +396,44 @@
             jax.ShapeDtypeStruct((rows, width), jnp.float32),
             jax.ShapeDtypeStruct((rows, width), jnp.bfloat16),
         ),
-        grid=(steps,),
-        in_specs=[
-            pl.BlockSpec((rows, width), lambda j: (0, 0)),
-            pl.BlockSpec((width, cols), lambda j: (0, j)),
-            pl.BlockSpec((width, cols), lambda j: (0, j + steps)),
+        in_specs=[vmem, pl.BlockSpec(memory_space=pltpu.HBM)],
+        out_specs=(vmem, vmem, vmem),
+        scratch_shapes=[
+            pltpu.VMEM((parts, width // parts, 2 * width), jnp.bfloat16),
+            pltpu.SemaphoreType.DMA((parts,)),
         ],
-        out_specs=(out, out, out),
         name="project",
-        compiler_params=pltpu.CompilerParams(vmem_limit_bytes=50 * 1024 * 1024),
+        compiler_params=pltpu.CompilerParams(vmem_limit_bytes=VMEM_GRANT),
         cost_estimate=pl.CostEstimate(
             flops=4 * rows * width * width,
             bytes_accessed=4 * width * width,
             transcendentals=rows * width,
         ),
-    )(normed, weight, weight)
-
-
-def kernel_call(body, outs, scratch, flops, *args):
+    )(normed, pltpu.with_memory_space_constraint(weight, pltpu.HBM))
+
+
+def kernel_call(body, outs, scratch, flops, *args, in_hbm=(), out_hbm=False):
     moved = sum(a.size * a.dtype.itemsize for a in args)
+    specs = {}
+    if in_hbm:
+        specs["in_specs"] = [
+            pl.BlockSpec(memory_space=pltpu.HBM if i in in_hbm else pltpu.VMEM)
+            for i in range(len(args))
+        ]
+    if out_hbm:
+        specs["out_specs"] = pl.BlockSpec(memory_space=pltpu.HBM)
+        outs = pltpu.HBM(outs.shape, outs.dtype)
+    args = [
+        pltpu.with_memory_space_constraint(a, pltpu.HBM) if i in in_hbm else a
+        for i, a in enumerate(args)
+    ]
     return pl.pallas_call(
         body,
         out_shape=outs,
         scratch_shapes=scratch,
         compiler_params=pltpu.CompilerParams(vmem_limit_bytes=VMEM_GRANT),
         cost_estimate=pl.CostEstimate(flops=flops, bytes_accessed=moved, transcendentals=0),
+        **specs,
     )(*args)
 
 
@@ -433,12 +491,11 @@
         core == 0, jnp.stack([extras, extras_other]), jnp.stack([extras_other, extras])
     )
     from_z = [
-        lax.ppermute(pair, "z", [(i, (i + d) % n_z) for i in range(n_z)]) for d in range(1, n_z)
+        lax.ppermute(pair, "z", [(i, (i + d) % n_z) for i in range(n_z)])
+        for d in range(1, n_z)
     ]
     upstream_other = lax.ppermute(upstream_rows, "core", swap)
-    arrived, upstream_other, pair, *from_z = lax.optimization_barrier(
-        (arrived, upstream_other, pair, *from_z)
-    )
+    arrived, upstream_other, pair = lax.optimization_barrier((arrived, upstream_other, pair))
     by_z = jnp.stack([*from_z[::-1], pair])
     side_all = lax.dynamic_slice_in_dim(
         jnp.concatenate([by_z, by_z]), n_z - 1 - lax.axis_index("z"), n_z, 0
@@ -494,12 +551,11 @@
     elements = rows_dev * width
     wide = frames_dev + 2 * EDGE
     blocks = width // LANES
-    activated, normed_mid, scale_mid = kernel_call(
+    activated, normed_mid = kernel_call(
         forward_kernel,
         (
             jax.ShapeDtypeStruct((rows_dev, width), jnp.bfloat16),
-            jax.ShapeDtypeStruct((slabs * wide, width), jnp.float32),
-            jax.ShapeDtypeStruct((slabs * wide, LANES), jnp.float32),
+            jax.ShapeDtypeStruct((slabs * wide, width + LANES), jnp.float32),
         ),
         [
             pltpu.VMEM((blocks, padded, LANES), jnp.float32),
@@ -515,9 +571,15 @@
             jax.ShapeDtypeStruct((slabs, wide, width), jnp.float32),
             jax.ShapeDtypeStruct((8, width), jnp.float32),
         ),
-        [pltpu.VMEM((slabs * wide, width), jnp.float32)],
+        [
+            pltpu.VMEM((slabs * wide, width), jnp.float32),
+            pltpu.VMEM((slabs * wide, width), jnp.bfloat16),
+            pltpu.VMEM((4, width // 4, width), jnp.bfloat16),
+            pltpu.SemaphoreType.DMA((5,)),
+        ],
         2 * slabs * wide * width * width,
-        normed_mid, scale_mid, upstream_wide, out_full, gain_mid[None],
+        normed_mid, upstream_wide, out_full, gain_mid[None],
+        in_hbm=(1, 2),
     )
 
     def exchanged(part):
@@ -569,9 +631,14 @@
             total_kernel, tap=kernel_len, scale=1.0 / math.sqrt(devices * rows_dev)
         ),
         jax.ShapeDtypeStruct((n_seq, share, 3 * width + SMALL), jnp.bfloat16),
-        [pltpu.VMEM((share, 2 * width + SMALL), jnp.float32)],
+        [
+            pltpu.VMEM((share, 2 * width + SMALL), jnp.float32),
+            pltpu.VMEM((1, share, 3 * width + SMALL), jnp.bfloat16),
+            pltpu.SemaphoreType.DMA((n_seq,)),
+        ],
         in_parts.size,
         in_parts, out_sum, own_weight, own_gain,
+        out_hbm=True,
     )
     final = lax.all_to_all(total, SEQ, 0, 0, tiled=True).reshape(LANES, -1)
     grad_in, grad_out, grad_kernel, grad_gains = kernel_call(

time: 195 us -> 193 us (0.990)
  waiting for transfers between devices: 77.7 us -> 75.3 us
    pallas_call x8, Pallas kernels: 23.3 us -> 27 us  [kernel_call(): pl.pallas_call(body, out_shape=outs, scratch_shapes=scratch, compiler_par...]
    unnamed x56 -> x60, local copies, waits for them, and re-layouts: 10.9 us -> 12.5 us
  transfers between devices with their start and end apart: 17 -> 17, of which waited for: 9 -> 10; matrix products, arithmetic and copies ran while one was open for 7% -> 7% of each run, Pallas kernels for 17% -> 17%
where the time goes in v7:
time: 193 us; the launch traced here: 192 us
  waiting for transfers between devices  75.3 us (39%)
  starting transfers between devices  39.7 us (21%)
  Pallas kernels  36.2 us (19%)
  local copies, waits for them, and re-layouts  14.5 us (8%)
  between operations  14.5 us (8%)
  matrix products  6.48 us (3%)
  other arithmetic  5.56 us (3%)
    all_to_all x2, waiting for transfers between devices, exchanged(): lax.all_to_all(part.reshape(n_z * n_seq, LANES // n_seq, part.shape[1]),...  35 us
    pallas_call x8, Pallas kernels, kernel_call(): pl.pallas_call(body, out_shape=outs, scratch_shapes=scratch, compiler_par...  27 us
    all_to_all x2, starting transfers between devices, exchanged(): lax.all_to_all(part.reshape(n_z * n_seq, LANES // n_seq, part.shape[1]),...  14.5 us
    ppermute x3, waiting for transfers between devices, per_device(): lax.ppermute(pair, 'z', [(i, (i + d) % n_z) for i in range(n_z)])  14.1 us
    unnamed x60, local copies, waits for them, and re-layouts  12.5 us
    all_to_all x1, starting transfers between devices, per_device(): lax.all_to_all(outgoing, (*DP, *SEQ), split_axis=0, concat_axis=0, tiled=...  11.2 us
    all_gather x1, waiting for transfers between devices, per_device(): out_full = lax.all_gather(out_weight, DP, axis=0, tiled=True)  8.56 us
    all_to_all x1, waiting for transfers between devices, per_device(): final = lax.all_to_all(total, SEQ, 0, 0, tiled=True).reshape(LANES, -1)  8.1 us
  transfers between devices with their start and end apart: 17, of which 10 were waited for; matrix products, arithmetic and copies ran while one was open for 7% of the time, Pallas kernels for 17%

profile of v7, /device:TPU:0, one launch (start us, length us, event | category | flops | bytes accessed | tf_op | source)
XLA Modules:
  0.0 192.3 jit_solution(15816377159325523228)
XLA Ops:
  11.0 1.5 shard_map.127
  12.4 11.2 %all-to-all-start = ((bf16[128,8,512]{2,1,0:T(8,128)(2,1)}), bf16[128,8,512]{2,1,0:T(8,128)(2,1)S(1)}, u32[]{:S(2)}, u32[]{:S(2)}) async-start(bf16[128,8,512]{2,1,0:T(8,128)(2,1)} %shard_map.127), calls=%async_computation | async-start | bytes 2097152 | tf_op jit(solution)/shard_map/all_to_all | solution.py:482
  25.1 2.9 %collective-permute-start.4 = (bf16[2,128,128]{1,2,0:T(8,128)(2,1)S(1)}, bf16[2,128,128]{1,2,0:T(8,128)(2,1)S(1)}, u32[]{:S(2)}, u32[]{:S(2)}) collective-permute-start(bf16[2,128,128]{1,2,0:T(8,128)(2,1)S(1)} %maximum_select_fusion), channel_id=1, source_target_pairs={{0,96},{32,0},{64,32},{96,64},{1,97},{33,1},{65,33},{97,65},{2,98}... | collective-permute-start | bytes 196616 | tf_op jit(solution)/shard_map/ppermute | solution.py:494
  29.6 10.7 %collective-permute-done.4 = bf16[2,128,128]{1,2,0:T(8,128)(2,1)S(1)} collective-permute-done((bf16[2,128,128]{1,2,0:T(8,128)(2,1)S(1)}, bf16[2,128,128]{1,2,0:T(8,128)(2,1)S(1)}, u32[]{:S(2)}, u32[]{:S(2)}) %collective-permute-start.4) | collective-permute-done | bytes 65568 | tf_op jit(solution)/shard_map/ppermute | solution.py:494
  40.4 1.9 %collective-permute-done.5 = bf16[2,128,128]{1,2,0:T(8,128)(2,1)S(1)} collective-permute-done((bf16[2,128,128]{1,2,0:T(8,128)(2,1)S(1)}, bf16[2,128,128]{1,2,0:T(8,128)(2,1)S(1)}, u32[]{:S(2)}, u32[]{:S(2)}) %collective-permute-start.5) | collective-permute-done | bytes 65568 | tf_op jit(solution)/shard_map/ppermute | solution.py:494
  42.3 1.5 collective-permute-done.6
  45.6 2.8 %collective-permute-start.2 = (bf16[2,48,1024]{2,1,0:T(8,128)(2,1)S(1)}, bf16[2,48,1024]{2,1,0:T(8,128)(2,1)S(1)}, u32[]{:S(2)}, u32[]{:S(2)}) collective-permute-start(bf16[2,48,1024]{2,1,0:T(8,128)(2,1)S(1)} %get-tuple-element.32), channel_id=1, source_target_pairs={{0,1},{1,2},{2,3},{3,4},{4,5},{5,6},{6,7},{7,8},{8,9},{9,10},{10,1... | collective-permute-start | bytes 589832 | tf_op jit(solution)/shard_map/ppermute | solution.py:443
  48.3 1.3 collective-permute-start.3
  49.7 3.2 %collective-permute-done.2.low_ref = bf16[2,48,1024]{2,1,0:T(8,128)(2,1)S(1)} collective-permute-done((bf16[2,48,1024]{2,1,0:T(8,128)(2,1)S(1)}, bf16[2,48,1024]{2,1,0:T(8,128)(2,1)S(1)}, u32[]{:S(2)}, u32[]{:S(2)}) %collective-permute-start.2) | collective-permute-done | bytes 196640 | tf_op jit(solution)/shard_map/ppermute | solution.py:443
  52.9 4.1 %collective-permute-done.3.high_ref = bf16[2,48,1024]{2,1,0:T(8,128)(2,1)S(1)} collective-permute-done((bf16[2,48,1024]{2,1,0:T(8,128)(2,1)S(1)}, bf16[2,48,1024]{2,1,0:T(8,128)(2,1)S(1)}, u32[]{:S(2)}, u32[]{:S(2)}) %collective-permute-start.3) | collective-permute-done | bytes 196640 | tf_op jit(solution)/shard_map/ppermute | solution.py:443
  61.2 3.5 %project.1 = (f32[384,1024]{1,0:T(8,128)S(1)}, f32[384,1024]{1,0:T(8,128)S(1)}, bf16[384,1024]{1,0:T(8,128)(2,1)S(1)}) custom-call(bf16[384,1024]{1,0:T(8,128)(2,1)S(1)} %bitcast.58, bf16[1024,2048]{1,0:T(8,128)(2,1)} %all-gather.3.cloned.1.call-done.weight_ref), custom_call_target="tpu_custom_call" | custom-call | flops 1610612736 | bytes 4194304 | tf_op jit(solution)/shard_map/project/pallas_call | solution.py:392
  65.9 1.2 copy-done.3
  67.2 8.2 %shard_map.130 = (bf16[256,1024]{1,0:T(8,128)(2,1)}, f32[320,1152]{1,0:T(8,128)S(1)}) custom-call(bf16[2,192,1024]{2,1,0:T(8,128)(2,1)S(1)} %bitcast.54, s32[2,192,128]{2,1,0:T(8,128)S(1)} %broadcast_in_dim.39.ids_ref, f32[8,32,128]{2,1,0:T(8,128)S(1)} %bitcast_bitcast_fusion.taps_ref, f32[1,1024]{1,0:T(1,128)S(1)} %get-tuple-element.62.gain_ref), custom_call_target="tpu_custom_call" | custom-call | flops 24379392 | bytes 1118208 | tf_op jit(solution)/shard_map/pallas_call | solution.py:430
  77.0 8.6 %all-gather.5.cloned.1.call-done.weight_ref = bf16[1024,1024]{1,0:T(8,128)(2,1)} async-done(((bf16[128,1024]{1,0:T(8,128)(2,1)}), bf16[1024,1024]{1,0:T(8,128)(2,1)}) %all-gather.5.cloned.1.call-update) | async-done | bytes 2097168 | tf_op jit(solution)/shard_map/all_gather | solution.py:469
  85.6 1.4 copy-done.6
  86.9 4.8 %shard_map.131 = (f32[2,160,1024]{2,1,0:T(8,128)S(1)}, f32[8,1024]{1,0:T(8,128)S(1)}) custom-call(f32[320,1152]{1,0:T(8,128)S(1)} %copy-done.6, bf16[320,1024]{1,0:T(8,128)(2,1)} %copy-done.8, bf16[1024,1024]{1,0:T(8,128)(2,1)} %all-gather.5.cloned.1.call-done.weight_ref, f32[1,1024]{1,0:T(1,128)S(1)} %get-tuple-element.62.gain_ref), custom_call_target="tpu_custom_call" | custom-call | flops 671088640 | bytes 4231168 | tf_op jit(solution)/shard_map/pallas_call | solution.py:430
  91.8 7.9 %shard_map.132 = (bf16[256,2048]{1,0:T(8,128)(2,1)S(1)}, f32[40,1024]{1,0:T(8,128)S(1)}) custom-call(f32[2,160,1024]{2,1,0:T(8,128)S(1)} %get-tuple-element.42.grad_mix_ref, bf16[2,192,1024]{2,1,0:T(8,128)(2,1)S(1)} %bitcast.55, s32[2,192,128]{2,1,0:T(8,128)S(1)} %broadcast_in_dim.39.ids_ref, f32[8,32,128]{2,1,0:T(8,128)S(1)} %bitcast_bitcast_fusion.taps_ref, ...), custom_call_target="tpu_custom_call" | custom-call | flops 40632320 | bytes 5603328 | tf_op jit(solution)/shard_map/pallas_call | solution.py:430
  100.1 3.0 %weight_part.3 = bf16[512,1024]{1,0:T(8,128)(2,1)} custom-call(s32[1]{0:T(128)} %bitcast.19.core_ref, bf16[256,1024]{1,0:T(8,128)(2,1)} %get-tuple-element.39.left_ref, bf16[256,1024]{1,0:T(8,128)(2,1)} %collective-permute-done.10.left_other_ref, bf16[256,1024]{1,0:T(8,128)(2,1)S(1)} %bitcast.52, bf16[256,1024]{1,0:T(8,128)(2,1)S(1)} %copy-done.14), custom_call_target="tpu_custom_call" | custom-call | flops 536870912 | bytes 2097152 | tf_op jit(solution)/shard_map/weight_part/pallas_call | solution.py:304
  103.0 9.5 %all-to-all-start.2 = ((bf16[64,8,1024]{2,1,0:T(8,128)(2,1)}), bf16[64,8,1024]{2,1,0:T(8,128)(2,1)}, u32[]{:S(2)}, u32[]{:S(2)}) async-start(bf16[64,8,1024]{2,1,0:T(8,128)(2,1)} %bitcast.21), calls=%async_computation.2 | async-start | bytes 2097152 | tf_op jit(solution)/shard_map/all_to_all | solution.py:586
  112.9 1.4 collective-permute-done.9.rest_1_
  116.3 2.7 %weight_part.2 = bf16[512,2176]{1,0:T(8,128)(2,1)} custom-call(s32[1]{0:T(128)} %bitcast.19.core_ref, bf16[256,1024]{1,0:T(8,128)(2,1)S(1)} %copy-done.10, bf16[256,1024]{1,0:T(8,128)(2,1)S(1)} %copy-done.12, bf16[256,2048]{1,0:T(8,128)(2,1)S(1)} %get-tuple-element.46.right_ref, bf16[256,2048]{1,0:T(8,128)(2,1)S(1)} %collective-permute-done.8.right_other_ref, ...), custom_call_target="tpu_custom_call" | custom-call | flops 1073741824 | bytes 3145728 | tf_op jit(solution)/shard_map/weight_part/pallas_call | solution.py:304
  119.1 12.5 %all-to-all-done.2 = bf16[64,8,1024]{2,1,0:T(8,128)(2,1)} async-done(((bf16[64,8,1024]{2,1,0:T(8,128)(2,1)}), bf16[64,8,1024]{2,1,0:T(8,128)(2,1)}, u32[]{:S(2)}, u32[]{:S(2)}) %all-to-all-start.2) | async-done | bytes 1048608 | tf_op jit(solution)/shard_map/all_to_all | solution.py:586
  131.6 5.0 %all-to-all-start.1 = ((bf16[64,8,2176]{2,1,0:T(8,128)(2,1)}), bf16[64,8,2176]{2,1,0:T(8,128)(2,1)S(1)}, u32[]{:S(2)}, u32[]{:S(2)}) async-start(bf16[64,8,2176]{2,1,0:T(8,128)(2,1)} %bitcast.20), calls=%async_computation.1 | async-start | bytes 4456448 | tf_op jit(solution)/shard_map/all_to_all | solution.py:586
  137.7 3.9 %fusion.4 = (f32[256]{0:T(256)S(1)}, f32[256]{0:T(256)S(1)}, f32[256,1024]{1,0:T(8,128)S(1)}) fusion(bf16[256,1024]{1,0:T(8,128)(2,1)S(1)} %get-tuple-element.31.frames_ref, f32[256]{0:T(256)S(1)} %broadcast_multiply_fusion, f32[1024]{0:T(1024)S(1)} %bitcast.57, bf16[256,2048]{1,0:T(8,128)(2,1)} %copy-done.7, ...), kind=kOutput, calls=%fused_computation.10 | convolution fusion | flops 1075576320 | bytes 6822912 | tf_op jit(solution)/shard_map/dot_general | solution.py:616
  142.5 1.4 convert_reduce_fusion.out_sum_ref
  143.9 22.6 %all-to-all-done.1.parts_ref = bf16[64,8,2176]{2,1,0:T(8,128)(2,1)S(1)} async-done(((bf16[64,8,2176]{2,1,0:T(8,128)(2,1)}), bf16[64,8,2176]{2,1,0:T(8,128)(2,1)S(1)}, u32[]{:S(2)}, u32[]{:S(2)}) %all-to-all-start.1) | async-done | bytes 2228256 | tf_op jit(solution)/shard_map/all_to_all | solution.py:586
  166.5 1.5 shard_map.133
  168.0 3.8 %all-to-all-start.3 = ((bf16[16,8,3200]{2,1,0:T(8,128)(2,1)}), bf16[16,8,3200]{2,1,0:T(8,128)(2,1)S(1)}, u32[]{:S(2)}, u32[]{:S(2)}) async-start(bf16[16,8,3200]{2,1,0:T(8,128)(2,1)} %shard_map.133), calls=%async_computation.3 | async-start | bytes 1638400 | tf_op jit(solution)/shard_map/all_to_all | solution.py:643
  171.8 1.2 add_convert_fusion
  173.6 2.6 %fusion.3 = bf16[256,1024]{1,0:T(8,128)(2,1)} fusion(bf16[256,1024]{1,0:T(8,128)(2,1)} %get-tuple-element.39.left_ref, bf16[1024,1024]{1,0:T(8,128)(2,1)S(1)} %copy-done.20, bf16[256,1024]{1,0:T(8,128)(2,1)S(1)} %get-tuple-element.31.frames_ref), kind=kOutput, calls=%fused_computation.9 | convolution fusion | flops 537657344 | bytes 3670016 | tf_op jit(solution)/shard_map/dot_general | solution.py:594
  176.1 8.1 %all-to-all-done.3 = bf16[16,8,3200]{2,1,0:T(8,128)(2,1)S(1)} async-done(((bf16[16,8,3200]{2,1,0:T(8,128)(2,1)}), bf16[16,8,3200]{2,1,0:T(8,128)(2,1)S(1)}, u32[]{:S(2)}, u32[]{:S(2)}) %all-to-all-start.3) | async-done | bytes 819232 | tf_op jit(solution)/shard_map/all_to_all | solution.py:643
  184.2 1.2 shard_map.134
  (113 shorter events, 20.9 us)
Async XLA Ops:
  7.2 52.9 %all-gather.3.cloned.1.call-start = ((), (), s32[]{:S(2)}) async-start(), calls=%async_computation.4 | async-start | bytes 4718592 | tf_op jit(solution)/shard_map/all_gather | solution.py:468
  11.0 12.7 %copy-start.23 = (bf16[128,31]{0,1:T(8,128)(2,1)S(1)}, bf16[128,31]{0,1:T(8,128)(2,1)}, u32[]{:S(2)}) copy-start(bf16[128,31]{0,1:T(8,128)(2,1)} %param.13) | copy-start | bytes 23812
  11.0 12.7 %copy-start.24 = (bf16[128,2]{0,1:T(2,128)(2,1)S(1)}, bf16[128,2]{0,1:T(2,128)(2,1)}, u32[]{:S(2)}) copy-start(bf16[128,2]{0,1:T(2,128)(2,1)} %param.14) | copy-start | bytes 1540
  11.0 12.8 %copy-start = (bf16[2,128,1024]{2,1,0:T(8,128)(2,1)S(1)}, bf16[2,128,1024]{2,1,0:T(8,128)(2,1)}, u32[]{:S(2)}) copy-start(bf16[2,128,1024]{2,1,0:T(8,128)(2,1)} %upstream_ref.3) | copy-start | bytes 1572868
  11.0 13.4 %copy-start.21 = (s32[128,128]{1,0:T(8,128)S(1)}, s32[128,128]{1,0:T(8,128)}, u32[]{:S(2)}) copy-start(s32[128,128]{1,0:T(8,128)} %param.9) | copy-start | bytes 196612
  12.4 31.4 %all-to-all-start = ((bf16[128,8,512]{2,1,0:T(8,128)(2,1)}), bf16[128,8,512]{2,1,0:T(8,128)(2,1)S(1)}, u32[]{:S(2)}, u32[]{:S(2)}) async-start(bf16[128,8,512]{2,1,0:T(8,128)(2,1)} %shard_map.127), calls=%async_computation | async-start | bytes 2097152 | tf_op jit(solution)/shard_map/all_to_all | solution.py:482
  23.6 62.0 %all-gather.5.cloned.1.call-start = ((), (), s32[]{:S(2)}) async-start(), calls=%async_computation.5 | async-start | bytes 2359296 | tf_op jit(solution)/shard_map/all_gather | solution.py:469
  23.7 1.3 collective-permute-start.1
  23.8 20.0 %collective-permute-start = (bf16[256,1024]{1,0:T(8,128)(2,1)S(1)}, bf16[256,1024]{1,0:T(8,128)(2,1)S(1)}, u32[]{:S(2)}, u32[]{:S(2)}) collective-permute-start(bf16[256,1024]{1,0:T(8,128)(2,1)S(1)} %bitcast.51), channel_id=1, source_target_pairs={{0,16},{16,0},{1,17},{17,1},{2,18},{18,2},{3,19},{19,3},{4,20},{20... | collective-permute-start | bytes 1572872 | tf_op jit(solution)/shard_map/ppermute | solution.py:497
  25.1 15.3 %collective-permute-start.4 = (bf16[2,128,128]{1,2,0:T(8,128)(2,1)S(1)}, bf16[2,128,128]{1,2,0:T(8,128)(2,1)S(1)}, u32[]{:S(2)}, u32[]{:S(2)}) collective-permute-start(bf16[2,128,128]{1,2,0:T(8,128)(2,1)S(1)} %maximum_select_fusion), channel_id=1, source_target_pairs={{0,96},{32,0},{64,32},{96,64},{1,97},{33,1},{65,33},{97,65},{2,98}... | collective-permute-start | bytes 196616 | tf_op jit(solution)/shard_map/ppermute | solution.py:494
  28.1 14.2 %collective-permute-start.5 = (bf16[2,128,128]{1,2,0:T(8,128)(2,1)S(1)}, bf16[2,128,128]{1,2,0:T(8,128)(2,1)S(1)}, u32[]{:S(2)}, u32[]{:S(2)}) collective-permute-start(bf16[2,128,128]{1,2,0:T(8,128)(2,1)S(1)} %maximum_select_fusion), channel_id=1, source_target_pairs={{0,64},{32,96},{64,0},{96,32},{1,65},{33,97},{65,1},{97,33},{2,66}... | collective-permute-start | bytes 196616 | tf_op jit(solution)/shard_map/ppermute | solution.py:494
  28.5 15.2 %collective-permute-start.6 = (bf16[2,128,128]{1,2,0:T(8,128)(2,1)S(1)}, bf16[2,128,128]{1,2,0:T(8,128)(2,1)S(1)}, u32[]{:S(2)}, u32[]{:S(2)}) collective-permute-start(bf16[2,128,128]{1,2,0:T(8,128)(2,1)S(1)} %maximum_select_fusion), channel_id=1, source_target_pairs={{0,32},{32,64},{64,96},{96,0},{1,33},{33,65},{65,97},{97,1},{2,34}... | collective-permute-start | bytes 196616 | tf_op jit(solution)/shard_map/ppermute | solution.py:494
  44.6 15.3 %copy-start.22 = (s32[2,2048]{1,0:T(2,128)S(1)}, s32[2,2048]{1,0:T(2,128)}, u32[]{:S(2)}) copy-start(s32[2,2048]{1,0:T(2,128)} %param.10) | copy-start | bytes 49156
  44.6 15.3 %copy-start.25 = (pred[32]{0:T(512)(128)(4,1)S(1)}, pred[32]{0:T(512)(128)(4,1)}, u32[]{:S(2)}) copy-start(pred[32]{0:T(512)(128)(4,1)} %constant.66.clone.1) | copy-start | bytes 100
  45.6 7.3 %collective-permute-start.2 = (bf16[2,48,1024]{2,1,0:T(8,128)(2,1)S(1)}, bf16[2,48,1024]{2,1,0:T(8,128)(2,1)S(1)}, u32[]{:S(2)}, u32[]{:S(2)}) collective-permute-start(bf16[2,48,1024]{2,1,0:T(8,128)(2,1)S(1)} %get-tuple-element.32), channel_id=1, source_target_pairs={{0,1},{1,2},{2,3},{3,4},{4,5},{5,6},{6,7},{7,8},{8,9},{9,10},{10,1... | collective-permute-start | bytes 589832 | tf_op jit(solution)/shard_map/ppermute | solution.py:443
  48.3 8.6 %collective-permute-start.3 = (bf16[2,48,1024]{2,1,0:T(8,128)(2,1)S(1)}, bf16[2,48,1024]{2,1,0:T(8,128)(2,1)S(1)}, u32[]{:S(2)}, u32[]{:S(2)}) collective-permute-start(bf16[2,48,1024]{2,1,0:T(8,128)(2,1)S(1)} %get-tuple-element.33), channel_id=1, source_target_pairs={{1,0},{2,1},{3,2},{4,3},{5,4},{6,5},{7,6},{8,7},{9,8},{10,9},{11,1... | collective-permute-start | bytes 589832 | tf_op jit(solution)/shard_map/ppermute | solution.py:443
  59.9 4.8 %copy-start.9 = (bf16[256,1024]{1,0:T(8,128)(2,1)}, bf16[256,1024]{1,0:T(8,128)(2,1)S(1)}, u32[]{:S(2)}) copy-start(bf16[256,1024]{1,0:T(8,128)(2,1)S(1)} %get-tuple-element.37.left_ref) | copy-start | bytes 1572868
  59.9 7.2 %collective-permute-start.7 = (bf16[256,1024]{1,0:T(8,128)(2,1)S(1)}, bf16[256,1024]{1,0:T(8,128)(2,1)S(1)}, u32[]{:S(2)}, u32[]{:S(2)}) collective-permute-start(bf16[256,1024]{1,0:T(8,128)(2,1)S(1)} %get-tuple-element.37.left_ref), channel_id=1, source_target_pairs={{0,16},{16,0},{1,17},{17,1},{2,18},{18,2},{3,19},{19,3},{4,20},{20... | collective-permute-start | bytes 1572872 | tf_op jit(solution)/shard_map/ppermute | solution.py:547
  67.1 24.7 %copy-start.11 = (bf16[256,1024]{1,0:T(8,128)(2,1)}, bf16[256,1024]{1,0:T(8,128)(2,1)S(1)}, u32[]{:S(2)}) copy-start(bf16[256,1024]{1,0:T(8,128)(2,1)S(1)} %collective-permute-done.7.left_other_ref) | copy-start | bytes 1572868
  76.5 23.5 %collective-permute-start.10 = (bf16[256,1024]{1,0:T(8,128)(2,1)}, bf16[256,1024]{1,0:T(8,128)(2,1)}, u32[]{:S(2)}, u32[]{:S(2)}) collective-permute-start(bf16[256,1024]{1,0:T(8,128)(2,1)} %get-tuple-element.39.left_ref), channel_id=1, source_target_pairs={{0,16},{16,0},{1,17},{17,1},{2,18},{18,2},{3,19},{19,3},{4,20},{20... | collective-permute-start | bytes 1572872 | tf_op jit(solution)/shard_map/ppermute | solution.py:567
  85.6 1.4 copy-start.6
  86.9 4.8 %copy-start.2 = (f32[384,1024]{1,0:T(8,128)S(1)}, f32[384,1024]{1,0:T(8,128)}, u32[]{:S(2)}) copy-start(f32[384,1024]{1,0:T(8,128)} %copy-done.1) | copy-start | bytes 4718596
  86.9 4.8 %copy-start.4 = (f32[384,1024]{1,0:T(8,128)S(1)}, f32[384,1024]{1,0:T(8,128)}, u32[]{:S(2)}) copy-start(f32[384,1024]{1,0:T(8,128)} %copy-done.3) | copy-start | bytes 4718596
  91.8 8.3 %copy-start.14 = (bf16[256,1024]{1,0:T(8,128)(2,1)S(1)}, bf16[256,1024]{1,0:T(8,128)(2,1)}, u32[]{:S(2)}) copy-start(bf16[256,1024]{1,0:T(8,128)(2,1)} %copy-done.13) | copy-start | bytes 1572868
  99.7 14.5 %copy-start.7 = (bf16[256,2048]{1,0:T(8,128)(2,1)}, bf16[256,2048]{1,0:T(8,128)(2,1)S(1)}, u32[]{:S(2)}) copy-start(bf16[256,2048]{1,0:T(8,128)(2,1)S(1)} %get-tuple-element.46.right_ref) | copy-start | bytes 3145732
  99.7 14.5 %collective-permute-start.8 = (bf16[256,2048]{1,0:T(8,128)(2,1)S(1)}, bf16[256,2048]{1,0:T(8,128)(2,1)S(1)}, u32[]{:S(2)}, u32[]{:S(2)}) collective-permute-start(bf16[256,2048]{1,0:T(8,128)(2,1)S(1)} %get-tuple-element.46.right_ref), channel_id=1, source_target_pairs={{0,16},{16,0},{1,17},{17,1},{2,18},{18,2},{3,19},{19,3},{4,20},{20... | collective-permute-start | bytes 3145736 | tf_op jit(solution)/shard_map/ppermute | solution.py:610
  103.0 28.5 %all-to-all-start.2 = ((bf16[64,8,1024]{2,1,0:T(8,128)(2,1)}), bf16[64,8,1024]{2,1,0:T(8,128)(2,1)}, u32[]{:S(2)}, u32[]{:S(2)}) async-start(bf16[64,8,1024]{2,1,0:T(8,128)(2,1)} %bitcast.21), calls=%async_computation.2 | async-start | bytes 2097152 | tf_op jit(solution)/shard_map/all_to_all | solution.py:586
  112.6 1.7 collective-permute-start.9
  131.6 34.9 %all-to-all-start.1 = ((bf16[64,8,2176]{2,1,0:T(8,128)(2,1)}), bf16[64,8,2176]{2,1,0:T(8,128)(2,1)S(1)}, u32[]{:S(2)}, u32[]{:S(2)}) async-start(bf16[64,8,2176]{2,1,0:T(8,128)(2,1)} %bitcast.20), calls=%async_computation.1 | async-start | bytes 4456448 | tf_op jit(solution)/shard_map/all_to_all | solution.py:586
  168.0 3.8 %copy-start.19 = (f32[256,1024]{1,0:T(8,128)S(1)}, f32[256,1024]{1,0:T(8,128)}, u32[]{:S(2)}) copy-start(f32[256,1024]{1,0:T(8,128)} %copy-done.18) | copy-start | bytes 3145732
  168.0 16.3 %all-to-all-start.3 = ((bf16[16,8,3200]{2,1,0:T(8,128)(2,1)}), bf16[16,8,3200]{2,1,0:T(8,128)(2,1)S(1)}, u32[]{:S(2)}, u32[]{:S(2)}) async-start(bf16[16,8,3200]{2,1,0:T(8,128)(2,1)} %shard_map.133), calls=%async_computation.3 | async-start | bytes 1638400 | tf_op jit(solution)/shard_map/all_to_all | solution.py:643
  171.8 1.8 copy-start.20
  (11 other events, 11.2 us)
Sparse Core Ops, SparseCore 0:
  9.7 48.8 all-gather.2
  60.3 25.2 all-gather.4

commit v8 on v7

--- a/solution.py
+++ b/solution.py
@@ -151,7 +151,6 @@
             row = pl.multiple_of((i // (blocks // 2)) * ROWS_STEP, ROWS_STEP)
             out_row = pl.multiple_of(s * frames + row, ROWS_STEP)
             b = (i % (blocks // 2)) * 2
-            hid_row = pl.multiple_of(s * padded + 2 * EDGE + row, ROWS_STEP)
             center = ids_ref[s, pl.ds(row + 2 * EDGE, ROWS_STEP)]
             sums = [jnp.zeros((ROWS_STEP, LANES), jnp.float32) for _ in range(2)]
             cols = [pl.ds(pl.multiple_of((b + j) * LANES, LANES), LANES) for j in range(2)]
@@ -167,8 +166,8 @@
                         (part[0:8] + part[8:16]) + (part[16:24] + part[24:32])
                     )
             for j in range(2):
-                lin = lin_ref[pl.ds(hid_row, ROWS_STEP), cols[j]]
-                sig = sig_ref[pl.ds(hid_row, ROWS_STEP), cols[j]]
+                lin = lin_ref[s, pl.ds(row, ROWS_STEP), cols[j]]
+                sig = sig_ref[s, pl.ds(row, ROWS_STEP), cols[j]]
                 grad_lin = sums[j] * sig
                 grad_hidden_ref[pl.ds(out_row, ROWS_STEP), cols[j]] = grad_lin.astype(jnp.bfloat16)
                 grad_hidden_ref[
@@ -352,7 +351,11 @@
         up_wide_ref[base + EDGE + own : base + 2 * EDGE + own, :] = high_ref[s, reach:, :]
 
 
-def project_kernel(normed_ref, weight_ref, lin_ref, sig_ref, gated_ref, loaded_ref, arrivals):
+def project_kernel(
+    normed_ref, weight_ref, lin_ref, sig_ref, gated_ref,
+    loaded_ref, lin_sum_ref, gate_sum_ref, rows_ref, arrivals,
+):
+    slabs, padded = lin_ref.shape[0], normed_ref.shape[0] // lin_ref.shape[0]
     parts, depth, both = loaded_ref.shape
     width = both // 2
     step = 256
@@ -362,11 +365,14 @@
         )
         for h in range(parts)
     ]
+    rows_copy = pltpu.make_async_copy(normed_ref, rows_ref, arrivals.at[parts])
+    rows_copy.start()
     for copy in copies:
         copy.start()
+    rows_copy.wait()
     for h, copy in enumerate(copies):
         copy.wait()
-        rows = normed_ref[:, h * depth : (h + 1) * depth]
+        rows = rows_ref[:, h * depth : (h + 1) * depth]
         for at in range(0, width, step):
             cols = slice(at, at + step)
             lin = jnp.dot(rows, loaded_ref[h, :, cols], preferred_element_type=jnp.float32)
@@ -375,32 +381,40 @@
                 loaded_ref[h, :, width + at : width + at + step],
                 preferred_element_type=jnp.float32,
             )
-            if h > 0:
-                lin = lin + lin_ref[:, cols]
-                gate = gate + sig_ref[:, cols]
-            if h == parts - 1:
-                gate = jax.nn.sigmoid(gate)
-                gated_ref[:, cols] = (lin * gate).astype(jnp.bfloat16)
-            lin_ref[:, cols] = lin
-            sig_ref[:, cols] = gate
-
-
-def project(normed, weight):
+            if h < parts - 1:
+                lin_sum_ref[:, cols] = lin
+                gate_sum_ref[:, cols] = gate
+                continue
+            lin = lin + lin_sum_ref[:, cols]
+            sig = jax.nn.sigmoid(gate + gate_sum_ref[:, cols])
+            gated_ref[:, cols] = (lin * sig).astype(jnp.bfloat16)
+            for s in range(slabs):
+                inner = slice(s * padded + 2 * EDGE, (s + 1) * padded - 2 * EDGE)
+                lin_ref[s, :, cols] = lin[inner]
+                sig_ref[s, :, cols] = sig[inner]
+
+
+def project(normed, weight, slabs):
     rows, width = normed.shape
+    own = pltpu.VMEM((rows, width), jnp.float32)
+    kept = jax.ShapeDtypeStruct((slabs, rows // slabs - 4 * EDGE, width), jnp.float32)
     parts = 2
     vmem = pl.BlockSpec(memory_space=pltpu.VMEM)
     return pl.pallas_call(
         project_kernel,
         out_shape=(
-            jax.ShapeDtypeStruct((rows, width), jnp.float32),
-            jax.ShapeDtypeStruct((rows, width), jnp.float32),
+            kept,
+            kept,
             jax.ShapeDtypeStruct((rows, width), jnp.bfloat16),
         ),
-        in_specs=[vmem, pl.BlockSpec(memory_space=pltpu.HBM)],
+        in_specs=[pl.BlockSpec(memory_space=pltpu.HBM)] * 2,
         out_specs=(vmem, vmem, vmem),
         scratch_shapes=[
             pltpu.VMEM((parts, width // parts, 2 * width), jnp.bfloat16),
-            pltpu.SemaphoreType.DMA((parts,)),
+            own,
+            own,
+            pltpu.VMEM((rows, width), jnp.bfloat16),
+            pltpu.SemaphoreType.DMA((parts + 1,)),
         ],
         name="project",
         compiler_params=pltpu.CompilerParams(vmem_limit_bytes=VMEM_GRANT),
@@ -409,7 +423,7 @@
             bytes_accessed=4 * width * width,
             transcendentals=rows * width,
         ),
-    )(normed, pltpu.with_memory_space_constraint(weight, pltpu.HBM))
+    )(*(pltpu.with_memory_space_constraint(a, pltpu.HBM) for a in (normed, weight)))
 
 
 def kernel_call(body, outs, scratch, flops, *args, in_hbm=(), out_hbm=False):
@@ -545,7 +559,7 @@
         frames, low, high, upstream, gain_pre[None],
     )
     normed_other = lax.ppermute(normed, "core", swap)
-    lin, sig, gated = project(normed_wide.reshape(-1, width), in_full)
+    lin, sig, gated = project(normed_wide.reshape(-1, width), in_full, slabs)
     gated, normed_other = lax.optimization_barrier((gated, normed_other))
     gated = gated.reshape(slabs, padded, width)
     elements = rows_dev * width

time: 193 us -> 195 us (1.010)
  local copies, waits for them, and re-layouts: 14.5 us -> 11 us
  Pallas kernels: 36.2 us -> 39.5 us
  waiting for transfers between devices: 75.3 us -> 77.9 us
    unnamed x60 -> x48, local copies, waits for them, and re-layouts: 12.5 us -> 8.28 us
    all_gather x1, waiting for transfers between devices: 8.56 us -> 10.6 us  [per_device(): out_full = lax.all_gather(out_weight, DP, axis=0, tiled=True)]
  transfers between devices with their start and end apart: 17 -> 17, of which waited for: 10 -> 10; matrix products, arithmetic and copies ran while one was open for 7% -> 8% of each run, Pallas kernels for 17% -> 19%
where the time goes in v8:
time: 195 us; the launch traced here: 194 us
  waiting for transfers between devices  77.9 us (40%)
  Pallas kernels  39.5 us (20%)
  starting transfers between devices  39.2 us (20%)
  between operations  14.5 us (7%)
  local copies, waits for them, and re-layouts  11 us (6%)
  matrix products  6.48 us (3%)
  other arithmetic  5.22 us (3%)
    all_to_all x2, waiting for transfers between devices, exchanged(): lax.all_to_all(part.reshape(n_z * n_seq, LANES // n_seq, part.shape[1]),...  36.4 us
    pallas_call x8, Pallas kernels, kernel_call(): pl.pallas_call(body, out_shape=outs, scratch_shapes=scratch, compiler_par...  28.5 us
    all_to_all x2, starting transfers between devices, exchanged(): lax.all_to_all(part.reshape(n_z * n_seq, LANES // n_seq, part.shape[1]),...  14.1 us
    ppermute x3, waiting for transfers between devices, per_device(): lax.ppermute(pair, 'z', [(i, (i + d) % n_z) for i in range(n_z)])  14.1 us
    all_to_all x1, starting transfers between devices, per_device(): lax.all_to_all(outgoing, (*DP, *SEQ), split_axis=0, concat_axis=0, tiled=...  11.2 us
    all_gather x1, waiting for transfers between devices, per_device(): out_full = lax.all_gather(out_weight, DP, axis=0, tiled=True)  10.6 us
    unnamed x48, local copies, waits for them, and re-layouts  8.28 us
    all_to_all x1, waiting for transfers between devices, per_device(): final = lax.all_to_all(total, SEQ, 0, 0, tiled=True).reshape(LANES, -1)  8.12 us
  transfers between devices with their start and end apart: 17, of which 10 were waited for; matrix products, arithmetic and copies ran while one was open for 8% of the time, Pallas kernels for 19%

profile of v8, /device:TPU:0, one launch (start us, length us, event | category | flops | bytes accessed | tf_op | source)
XLA Modules:
  0.0 193.8 jit_solution(13619870820907370102)
XLA Ops:
  11.0 1.5 shard_map.127
  12.4 11.2 %all-to-all-start = ((bf16[128,8,512]{2,1,0:T(8,128)(2,1)}), bf16[128,8,512]{2,1,0:T(8,128)(2,1)S(1)}, u32[]{:S(2)}, u32[]{:S(2)}) async-start(bf16[128,8,512]{2,1,0:T(8,128)(2,1)} %shard_map.127), calls=%async_computation | async-start | bytes 2097152 | tf_op jit(solution)/shard_map/all_to_all | solution.py:496
  25.1 2.9 %collective-permute-start.4 = (bf16[2,128,128]{1,2,0:T(8,128)(2,1)S(1)}, bf16[2,128,128]{1,2,0:T(8,128)(2,1)S(1)}, u32[]{:S(2)}, u32[]{:S(2)}) collective-permute-start(bf16[2,128,128]{1,2,0:T(8,128)(2,1)S(1)} %maximum_select_fusion), channel_id=1, source_target_pairs={{0,96},{32,0},{64,32},{96,64},{1,97},{33,1},{65,33},{97,65},{2,98}... | collective-permute-start | bytes 196616 | tf_op jit(solution)/shard_map/ppermute | solution.py:508
  29.6 10.7 %collective-permute-done.4 = bf16[2,128,128]{1,2,0:T(8,128)(2,1)S(1)} collective-permute-done((bf16[2,128,128]{1,2,0:T(8,128)(2,1)S(1)}, bf16[2,128,128]{1,2,0:T(8,128)(2,1)S(1)}, u32[]{:S(2)}, u32[]{:S(2)}) %collective-permute-start.4) | collective-permute-done | bytes 65568 | tf_op jit(solution)/shard_map/ppermute | solution.py:508
  40.4 1.9 %collective-permute-done.5 = bf16[2,128,128]{1,2,0:T(8,128)(2,1)S(1)} collective-permute-done((bf16[2,128,128]{1,2,0:T(8,128)(2,1)S(1)}, bf16[2,128,128]{1,2,0:T(8,128)(2,1)S(1)}, u32[]{:S(2)}, u32[]{:S(2)}) %collective-permute-start.5) | collective-permute-done | bytes 65568 | tf_op jit(solution)/shard_map/ppermute | solution.py:508
  42.3 1.5 collective-permute-done.6
  45.9 2.8 %collective-permute-start.2 = (bf16[2,48,1024]{2,1,0:T(8,128)(2,1)S(1)}, bf16[2,48,1024]{2,1,0:T(8,128)(2,1)S(1)}, u32[]{:S(2)}, u32[]{:S(2)}) collective-permute-start(bf16[2,48,1024]{2,1,0:T(8,128)(2,1)S(1)} %get-tuple-element.32), channel_id=1, source_target_pairs={{0,1},{1,2},{2,3},{3,4},{4,5},{5,6},{6,7},{7,8},{8,9},{9,10},{10,1... | collective-permute-start | bytes 589832 | tf_op jit(solution)/shard_map/ppermute | solution.py:457
  48.7 1.3 collective-permute-start.3
  50.9 2.3 %collective-permute-done.2.low_ref = bf16[2,48,1024]{2,1,0:T(8,128)(2,1)S(1)} collective-permute-done((bf16[2,48,1024]{2,1,0:T(8,128)(2,1)S(1)}, bf16[2,48,1024]{2,1,0:T(8,128)(2,1)S(1)}, u32[]{:S(2)}, u32[]{:S(2)}) %collective-permute-start.2) | collective-permute-done | bytes 196640 | tf_op jit(solution)/shard_map/ppermute | solution.py:457
  53.2 4.1 %collective-permute-done.3.high_ref = bf16[2,48,1024]{2,1,0:T(8,128)(2,1)S(1)} collective-permute-done((bf16[2,48,1024]{2,1,0:T(8,128)(2,1)S(1)}, bf16[2,48,1024]{2,1,0:T(8,128)(2,1)S(1)}, u32[]{:S(2)}, u32[]{:S(2)}) %collective-permute-start.3) | collective-permute-done | bytes 196640 | tf_op jit(solution)/shard_map/ppermute | solution.py:457
  57.3 1.9 shard_map.129
  61.2 3.7 %project.1 = (f32[2,128,1024]{2,1,0:T(8,128)S(1)}, f32[2,128,1024]{2,1,0:T(8,128)S(1)}, bf16[384,1024]{1,0:T(8,128)(2,1)S(1)}) custom-call(bf16[384,1024]{1,0:T(8,128)(2,1)} %bitcast.58, bf16[1024,2048]{1,0:T(8,128)(2,1)} %all-gather.3.cloned.1.call-done.weight_ref), custom_call_target="tpu_custom_call" | custom-call | flops 1610612736 | bytes 4194304 | tf_op jit(solution)/shard_map/project/pallas_call | solution.py:403
  65.1 8.2 %shard_map.130 = (bf16[256,1024]{1,0:T(8,128)(2,1)}, f32[320,1152]{1,0:T(8,128)S(1)}) custom-call(bf16[2,192,1024]{2,1,0:T(8,128)(2,1)S(1)} %bitcast.54, s32[2,192,128]{2,1,0:T(8,128)S(1)} %broadcast_in_dim.39.ids_ref, f32[8,32,128]{2,1,0:T(8,128)S(1)} %bitcast_bitcast_fusion.taps_ref, f32[1,1024]{1,0:T(1,128)S(1)} %get-tuple-element.62.gain_ref), custom_call_target="tpu_custom_call" | custom-call | flops 24379392 | bytes 1118208 | tf_op jit(solution)/shard_map/pallas_call | solution.py:444
  73.3 1.1 copy-done.1
  75.0 10.6 %all-gather.5.cloned.1.call-done.weight_ref = bf16[1024,1024]{1,0:T(8,128)(2,1)} async-done(((bf16[128,1024]{1,0:T(8,128)(2,1)}), bf16[1024,1024]{1,0:T(8,128)(2,1)}) %all-gather.5.cloned.1.call-update) | async-done | bytes 2097168 | tf_op jit(solution)/shard_map/all_gather | solution.py:483
  85.6 1.4 copy-done.2
  87.0 4.7 %shard_map.131 = (f32[2,160,1024]{2,1,0:T(8,128)S(1)}, f32[8,1024]{1,0:T(8,128)S(1)}) custom-call(f32[320,1152]{1,0:T(8,128)S(1)} %copy-done.2, bf16[320,1024]{1,0:T(8,128)(2,1)} %copy-done.5, bf16[1024,1024]{1,0:T(8,128)(2,1)} %all-gather.5.cloned.1.call-done.weight_ref, f32[1,1024]{1,0:T(1,128)S(1)} %get-tuple-element.62.gain_ref), custom_call_target="tpu_custom_call" | custom-call | flops 671088640 | bytes 4231168 | tf_op jit(solution)/shard_map/pallas_call | solution.py:444
  91.7 8.7 %shard_map.132 = (bf16[256,2048]{1,0:T(8,128)(2,1)}, f32[40,1024]{1,0:T(8,128)S(1)}) custom-call(f32[2,160,1024]{2,1,0:T(8,128)S(1)} %get-tuple-element.42.grad_mix_ref, bf16[2,192,1024]{2,1,0:T(8,128)(2,1)S(1)} %bitcast.55, s32[2,192,128]{2,1,0:T(8,128)S(1)} %broadcast_in_dim.39.ids_ref, f32[8,32,128]{2,1,0:T(8,128)S(1)} %bitcast_bitcast_fusion.taps_ref, ...), custom_call_target="tpu_custom_call" | custom-call | flops 40632320 | bytes 4554752 | tf_op jit(solution)/shard_map/pallas_call | solution.py:444
  100.7 3.0 %weight_part.3 = bf16[512,1024]{1,0:T(8,128)(2,1)} custom-call(s32[1]{0:T(128)} %bitcast.19.core_ref, bf16[256,1024]{1,0:T(8,128)(2,1)} %get-tuple-element.39.left_ref, bf16[256,1024]{1,0:T(8,128)(2,1)} %collective-permute-done.10.left_other_ref, bf16[256,1024]{1,0:T(8,128)(2,1)S(1)} %bitcast.52, bf16[256,1024]{1,0:T(8,128)(2,1)S(1)} %copy-done.7), custom_call_target="tpu_custom_call" | custom-call | flops 536870912 | bytes 2097152 | tf_op jit(solution)/shard_map/weight_part/pallas_call | solution.py:303
  103.7 9.2 %all-to-all-start.2 = ((bf16[64,8,1024]{2,1,0:T(8,128)(2,1)}), bf16[64,8,1024]{2,1,0:T(8,128)(2,1)S(1)}, u32[]{:S(2)}, u32[]{:S(2)}) async-start(bf16[64,8,1024]{2,1,0:T(8,128)(2,1)} %bitcast.21), calls=%async_computation.2 | async-start | bytes 2097152 | tf_op jit(solution)/shard_map/all_to_all | solution.py:600
  113.1 1.4 collective-permute-done.9.rest_1_
  114.5 4.3 %weight_part.2 = bf16[512,2176]{1,0:T(8,128)(2,1)} custom-call(s32[1]{0:T(128)} %bitcast.19.core_ref, bf16[256,1024]{1,0:T(8,128)(2,1)} %get-tuple-element.37.left_ref, bf16[256,1024]{1,0:T(8,128)(2,1)} %collective-permute-done.7.left_other_ref, bf16[256,2048]{1,0:T(8,128)(2,1)} %get-tuple-element.46.right_ref, ...), custom_call_target="tpu_custom_call" | custom-call | flops 1073741824 | bytes 3145728 | tf_op jit(solution)/shard_map/weight_part/pallas_call | solution.py:303
  118.8 13.2 %all-to-all-done.2 = bf16[64,8,1024]{2,1,0:T(8,128)(2,1)S(1)} async-done(((bf16[64,8,1024]{2,1,0:T(8,128)(2,1)}), bf16[64,8,1024]{2,1,0:T(8,128)(2,1)S(1)}, u32[]{:S(2)}, u32[]{:S(2)}) %all-to-all-start.2) | async-done | bytes 1048608 | tf_op jit(solution)/shard_map/all_to_all | solution.py:600
  133.0 5.0 %all-to-all-start.1 = ((bf16[64,8,2176]{2,1,0:T(8,128)(2,1)}), bf16[64,8,2176]{2,1,0:T(8,128)(2,1)S(1)}, u32[]{:S(2)}, u32[]{:S(2)}) async-start(bf16[64,8,2176]{2,1,0:T(8,128)(2,1)} %bitcast.20), calls=%async_computation.1 | async-start | bytes 4456448 | tf_op jit(solution)/shard_map/all_to_all | solution.py:600
  139.1 3.9 %fusion.4 = (f32[256]{0:T(256)S(1)}, f32[256]{0:T(256)S(1)}, f32[256,1024]{1,0:T(8,128)S(1)}) fusion(bf16[256,1024]{1,0:T(8,128)(2,1)S(1)} %get-tuple-element.31.frames_ref, f32[256]{0:T(256)S(1)} %broadcast_multiply_fusion, f32[1024]{0:T(1024)S(1)} %bitcast.57, bf16[256,2048]{1,0:T(8,128)(2,1)} %get-tuple-element.46.right_ref, ...), kind=kOutput, calls=%fused_computation.10 | convolution fusion | flops 1075576320 | bytes 6822912 | tf_op jit(solution)/shard_map/dot_general | solution.py:630
  144.8 23.2 %all-to-all-done.1.parts_ref = bf16[64,8,2176]{2,1,0:T(8,128)(2,1)S(1)} async-done(((bf16[64,8,2176]{2,1,0:T(8,128)(2,1)}), bf16[64,8,2176]{2,1,0:T(8,128)(2,1)S(1)}, u32[]{:S(2)}, u32[]{:S(2)}) %all-to-all-start.1) | async-done | bytes 2228256 | tf_op jit(solution)/shard_map/all_to_all | solution.py:600
  168.0 1.5 shard_map.133
  169.5 3.8 %all-to-all-start.3 = ((bf16[16,8,3200]{2,1,0:T(8,128)(2,1)}), bf16[16,8,3200]{2,1,0:T(8,128)(2,1)S(1)}, u32[]{:S(2)}, u32[]{:S(2)}) async-start(bf16[16,8,3200]{2,1,0:T(8,128)(2,1)} %shard_map.133), calls=%async_computation.3 | async-start | bytes 1638400 | tf_op jit(solution)/shard_map/all_to_all | solution.py:657
  173.3 1.2 add_convert_fusion
  175.1 2.6 %fusion.3 = bf16[256,1024]{1,0:T(8,128)(2,1)} fusion(bf16[256,1024]{1,0:T(8,128)(2,1)} %get-tuple-element.39.left_ref, bf16[1024,1024]{1,0:T(8,128)(2,1)S(1)} %copy-done.14, bf16[256,1024]{1,0:T(8,128)(2,1)S(1)} %get-tuple-element.31.frames_ref), kind=kOutput, calls=%fused_computation.9 | convolution fusion | flops 537657344 | bytes 3670016 | tf_op jit(solution)/shard_map/dot_general | solution.py:608
  177.6 8.1 %all-to-all-done.3 = bf16[16,8,3200]{2,1,0:T(8,128)(2,1)S(1)} async-done(((bf16[16,8,3200]{2,1,0:T(8,128)(2,1)}), bf16[16,8,3200]{2,1,0:T(8,128)(2,1)S(1)}, u32[]{:S(2)}, u32[]{:S(2)}) %all-to-all-start.3) | async-done | bytes 819232 | tf_op jit(solution)/shard_map/all_to_all | solution.py:657
  185.8 1.2 shard_map.134
  (101 shorter events, 17.3 us)
Async XLA Ops:
  7.2 54.0 %all-gather.3.cloned.1.call-start = ((), (), s32[]{:S(2)}) async-start(), calls=%async_computation.4 | async-start | bytes 4718592 | tf_op jit(solution)/shard_map/all_gather | solution.py:482
  11.0 12.7 %copy-start.17 = (bf16[128,31]{0,1:T(8,128)(2,1)S(1)}, bf16[128,31]{0,1:T(8,128)(2,1)}, u32[]{:S(2)}) copy-start(bf16[128,31]{0,1:T(8,128)(2,1)} %param.13) | copy-start | bytes 23812
  11.0 12.7 %copy-start.18 = (bf16[128,2]{0,1:T(2,128)(2,1)S(1)}, bf16[128,2]{0,1:T(2,128)(2,1)}, u32[]{:S(2)}) copy-start(bf16[128,2]{0,1:T(2,128)(2,1)} %param.14) | copy-start | bytes 1540
  11.0 12.8 %copy-start = (bf16[2,128,1024]{2,1,0:T(8,128)(2,1)S(1)}, bf16[2,128,1024]{2,1,0:T(8,128)(2,1)}, u32[]{:S(2)}) copy-start(bf16[2,128,1024]{2,1,0:T(8,128)(2,1)} %upstream_ref.3) | copy-start | bytes 1572868
  11.0 13.4 %copy-start.15 = (s32[128,128]{1,0:T(8,128)S(1)}, s32[128,128]{1,0:T(8,128)}, u32[]{:S(2)}) copy-start(s32[128,128]{1,0:T(8,128)} %param.9) | copy-start | bytes 196612
  12.4 31.4 %all-to-all-start = ((bf16[128,8,512]{2,1,0:T(8,128)(2,1)}), bf16[128,8,512]{2,1,0:T(8,128)(2,1)S(1)}, u32[]{:S(2)}, u32[]{:S(2)}) async-start(bf16[128,8,512]{2,1,0:T(8,128)(2,1)} %shard_map.127), calls=%async_computation | async-start | bytes 2097152 | tf_op jit(solution)/shard_map/all_to_all | solution.py:496
  23.6 62.0 %all-gather.5.cloned.1.call-start = ((), (), s32[]{:S(2)}) async-start(), calls=%async_computation.5 | async-start | bytes 2359296 | tf_op jit(solution)/shard_map/all_gather | solution.py:483
  23.7 1.3 collective-permute-start.1
  23.8 20.0 %collective-permute-start = (bf16[256,1024]{1,0:T(8,128)(2,1)S(1)}, bf16[256,1024]{1,0:T(8,128)(2,1)S(1)}, u32[]{:S(2)}, u32[]{:S(2)}) collective-permute-start(bf16[256,1024]{1,0:T(8,128)(2,1)S(1)} %bitcast.51), channel_id=1, source_target_pairs={{0,16},{16,0},{1,17},{17,1},{2,18},{18,2},{3,19},{19,3},{4,20},{20... | collective-permute-start | bytes 1572872 | tf_op jit(solution)/shard_map/ppermute | solution.py:511
  25.1 15.3 %collective-permute-start.4 = (bf16[2,128,128]{1,2,0:T(8,128)(2,1)S(1)}, bf16[2,128,128]{1,2,0:T(8,128)(2,1)S(1)}, u32[]{:S(2)}, u32[]{:S(2)}) collective-permute-start(bf16[2,128,128]{1,2,0:T(8,128)(2,1)S(1)} %maximum_select_fusion), channel_id=1, source_target_pairs={{0,96},{32,0},{64,32},{96,64},{1,97},{33,1},{65,33},{97,65},{2,98}... | collective-permute-start | bytes 196616 | tf_op jit(solution)/shard_map/ppermute | solution.py:508
  28.1 14.2 %collective-permute-start.5 = (bf16[2,128,128]{1,2,0:T(8,128)(2,1)S(1)}, bf16[2,128,128]{1,2,0:T(8,128)(2,1)S(1)}, u32[]{:S(2)}, u32[]{:S(2)}) collective-permute-start(bf16[2,128,128]{1,2,0:T(8,128)(2,1)S(1)} %maximum_select_fusion), channel_id=1, source_target_pairs={{0,64},{32,96},{64,0},{96,32},{1,65},{33,97},{65,1},{97,33},{2,66}... | collective-permute-start | bytes 196616 | tf_op jit(solution)/shard_map/ppermute | solution.py:508
  28.5 15.2 %collective-permute-start.6 = (bf16[2,128,128]{1,2,0:T(8,128)(2,1)S(1)}, bf16[2,128,128]{1,2,0:T(8,128)(2,1)S(1)}, u32[]{:S(2)}, u32[]{:S(2)}) collective-permute-start(bf16[2,128,128]{1,2,0:T(8,128)(2,1)S(1)} %maximum_select_fusion), channel_id=1, source_target_pairs={{0,32},{32,64},{64,96},{96,0},{1,33},{33,65},{65,97},{97,1},{2,34}... | collective-permute-start | bytes 196616 | tf_op jit(solution)/shard_map/ppermute | solution.py:508
  43.8 2.1 %copy-start.6 = (bf16[256,1024]{1,0:T(8,128)(2,1)}, bf16[256,1024]{1,0:T(8,128)(2,1)S(1)}, u32[]{:S(2)}) copy-start(bf16[256,1024]{1,0:T(8,128)(2,1)S(1)} %collective-permute-done.right_other_ref) | copy-start | bytes 1572868
  44.2 16.8 %copy-start.16 = (s32[2,2048]{1,0:T(2,128)S(1)}, s32[2,2048]{1,0:T(2,128)}, u32[]{:S(2)}) copy-start(s32[2,2048]{1,0:T(2,128)} %param.10) | copy-start | bytes 49156
  44.2 16.9 %copy-start.19 = (pred[32]{0:T(512)(128)(4,1)S(1)}, pred[32]{0:T(512)(128)(4,1)}, u32[]{:S(2)}) copy-start(pred[32]{0:T(512)(128)(4,1)} %constant.66.clone.1) | copy-start | bytes 100
  45.9 7.3 %collective-permute-start.2 = (bf16[2,48,1024]{2,1,0:T(8,128)(2,1)S(1)}, bf16[2,48,1024]{2,1,0:T(8,128)(2,1)S(1)}, u32[]{:S(2)}, u32[]{:S(2)}) collective-permute-start(bf16[2,48,1024]{2,1,0:T(8,128)(2,1)S(1)} %get-tuple-element.32), channel_id=1, source_target_pairs={{0,1},{1,2},{2,3},{3,4},{4,5},{5,6},{6,7},{7,8},{8,9},{9,10},{10,1... | collective-permute-start | bytes 589832 | tf_op jit(solution)/shard_map/ppermute | solution.py:457
  48.7 8.6 %collective-permute-start.3 = (bf16[2,48,1024]{2,1,0:T(8,128)(2,1)S(1)}, bf16[2,48,1024]{2,1,0:T(8,128)(2,1)S(1)}, u32[]{:S(2)}, u32[]{:S(2)}) collective-permute-start(bf16[2,48,1024]{2,1,0:T(8,128)(2,1)S(1)} %get-tuple-element.33), channel_id=1, source_target_pairs={{1,0},{2,1},{3,2},{4,3},{5,4},{6,5},{7,6},{8,7},{9,8},{10,9},{11,1... | collective-permute-start | bytes 589832 | tf_op jit(solution)/shard_map/ppermute | solution.py:457
  61.0 4.0 %collective-permute-start.7 = (bf16[256,1024]{1,0:T(8,128)(2,1)}, bf16[256,1024]{1,0:T(8,128)(2,1)}, u32[]{:S(2)}, u32[]{:S(2)}) collective-permute-start(bf16[256,1024]{1,0:T(8,128)(2,1)} %get-tuple-element.37.left_ref), channel_id=1, source_target_pairs={{0,16},{16,0},{1,17},{17,1},{2,18},{18,2},{3,19},{19,3},{4,20},{20... | collective-permute-start | bytes 1572872 | tf_op jit(solution)/shard_map/ppermute | solution.py:561
  65.0 8.4 %copy-start.3 = (f32[2,128,1024]{2,1,0:T(8,128)}, f32[2,128,1024]{2,1,0:T(8,128)S(1)}, u32[]{:S(2)}) copy-start(f32[2,128,1024]{2,1,0:T(8,128)S(1)} %get-tuple-element.44.sig_ref) | copy-start | bytes 3145732
  73.3 1.1 copy-start.1
  74.5 26.2 %collective-permute-start.10 = (bf16[256,1024]{1,0:T(8,128)(2,1)}, bf16[256,1024]{1,0:T(8,128)(2,1)}, u32[]{:S(2)}, u32[]{:S(2)}) collective-permute-start(bf16[256,1024]{1,0:T(8,128)(2,1)} %get-tuple-element.39.left_ref), channel_id=1, source_target_pairs={{0,16},{16,0},{1,17},{17,1},{2,18},{18,2},{3,19},{19,3},{4,20},{20... | collective-permute-start | bytes 1572872 | tf_op jit(solution)/shard_map/ppermute | solution.py:581
  85.6 1.4 copy-start.2
  87.0 4.8 %copy-start.4 = (f32[2,128,1024]{2,1,0:T(8,128)S(1)}, f32[2,128,1024]{2,1,0:T(8,128)}, u32[]{:S(2)}) copy-start(f32[2,128,1024]{2,1,0:T(8,128)} %copy-done.3) | copy-start | bytes 3145732
  91.7 9.0 %copy-start.7 = (bf16[256,1024]{1,0:T(8,128)(2,1)S(1)}, bf16[256,1024]{1,0:T(8,128)(2,1)}, u32[]{:S(2)}) copy-start(bf16[256,1024]{1,0:T(8,128)(2,1)} %copy-done.6) | copy-start | bytes 1572868
  100.5 14.1 %collective-permute-start.8 = (bf16[256,2048]{1,0:T(8,128)(2,1)}, bf16[256,2048]{1,0:T(8,128)(2,1)S(1)}, u32[]{:S(2)}, u32[]{:S(2)}) collective-permute-start(bf16[256,2048]{1,0:T(8,128)(2,1)} %get-tuple-element.46.right_ref), channel_id=1, source_target_pairs={{0,16},{16,0},{1,17},{17,1},{2,18},{18,2},{3,19},{19,3},{4,20},{20... | collective-permute-start | bytes 3145736 | tf_op jit(solution)/shard_map/ppermute | solution.py:624
  103.7 28.4 %all-to-all-start.2 = ((bf16[64,8,1024]{2,1,0:T(8,128)(2,1)}), bf16[64,8,1024]{2,1,0:T(8,128)(2,1)S(1)}, u32[]{:S(2)}, u32[]{:S(2)}) async-start(bf16[64,8,1024]{2,1,0:T(8,128)(2,1)} %bitcast.21), calls=%async_computation.2 | async-start | bytes 2097152 | tf_op jit(solution)/shard_map/all_to_all | solution.py:600
  112.9 1.7 collective-permute-start.9
  133.0 35.0 %all-to-all-start.1 = ((bf16[64,8,2176]{2,1,0:T(8,128)(2,1)}), bf16[64,8,2176]{2,1,0:T(8,128)(2,1)S(1)}, u32[]{:S(2)}, u32[]{:S(2)}) async-start(bf16[64,8,2176]{2,1,0:T(8,128)(2,1)} %bitcast.20), calls=%async_computation.1 | async-start | bytes 4456448 | tf_op jit(solution)/shard_map/all_to_all | solution.py:600
  143.0 1.6 copy-start.13
  169.5 3.8 %copy-start.11 = (f32[256,1024]{1,0:T(8,128)S(1)}, f32[256,1024]{1,0:T(8,128)}, u32[]{:S(2)}) copy-start(f32[256,1024]{1,0:T(8,128)} %copy-done.10) | copy-start | bytes 3145732
  169.5 16.2 %all-to-all-start.3 = ((bf16[16,8,3200]{2,1,0:T(8,128)(2,1)}), bf16[16,8,3200]{2,1,0:T(8,128)(2,1)S(1)}, u32[]{:S(2)}, u32[]{:S(2)}) async-start(bf16[16,8,3200]{2,1,0:T(8,128)(2,1)} %shard_map.133), calls=%async_computation.3 | async-start | bytes 1638400 | tf_op jit(solution)/shard_map/all_to_all | solution.py:657
  173.3 1.8 copy-start.14
  (5 other events, 4.8 us)
Sparse Core Ops, SparseCore 0:
  9.7 48.7 all-gather.2
  60.2 25.3 all-gather.4

commit v9 on v6

--- a/solution.py
+++ b/solution.py
@@ -16,13 +16,13 @@
 LANES = 128
 ROWS_STEP = 32
 EPS = 1e-05
-SMALL = 2 * LANES
+SMALL = LANES
 VMEM_GRANT = 16 * 1024 * 1024
 
 
 def forward_kernel(
     gated_ref, ids_ref, taps_ref, gain_ref,
-    act_ref, normed_ref, scale_ref, pad_ref, mix_ref,
+    act_ref, normed_ref, pad_ref, mix_ref,
 ):
     slabs, padded, width = gated_ref.shape
     blocks = width // LANES
@@ -64,8 +64,8 @@
                 act_ref[pl.ds(act_row, 16), :] = (value * jax.nn.sigmoid(value)).astype(
                     act_ref.dtype
                 )
-            normed_ref[pl.ds(out_row, 16), :] = normed
-            scale_ref[pl.ds(out_row, 16), :] = jnp.broadcast_to(scale, (16, LANES))
+            normed_ref[pl.ds(out_row, 16), :width] = normed
+            normed_ref[pl.ds(out_row, 16), width:] = jnp.broadcast_to(scale, (16, LANES))
 
         steps = wide // 16
         row_step(0, False)
@@ -81,10 +81,10 @@
 
 
 def middle_kernel(
-    normed_ref, scale_ref, upstream_ref, weight_ref, gain_ref,
+    normed_ref, upstream_ref, weight_ref, gain_ref,
     grad_mix_ref, grad_gain_ref, grad_act_ref,
 ):
-    slabs, frames, _ = grad_mix_ref.shape
+    slabs, frames, width = grad_mix_ref.shape
     steps = frames // 16
     grad_act_ref[...] = lax.dot_general(
         upstream_ref[...],
@@ -95,8 +95,8 @@
 
     def row_step(i, total):
         row = pl.multiple_of(i * 16, 16)
-        normed = normed_ref[pl.ds(row, 16), :]
-        scale = scale_ref[pl.ds(row, 16), 0:1]
+        normed = normed_ref[pl.ds(row, 16), :width]
+        scale = normed_ref[pl.ds(row, 16), width : width + 1]
         gain = gain_ref[0:1, :]
         value = normed * gain
         sig = jax.nn.sigmoid(value)
@@ -120,7 +120,7 @@
 
 def backward_kernel(
     grad_mix_ref, gated_ref, ids_ref, taps_ref, lin_ref, sig_ref, grad_gain_ref,
-    grad_hidden_ref, grad_taps_ref, pad_ref, sum_ref,
+    grad_hidden_ref, grad_taps_ref, kept_ref, pad_ref, sum_ref, leaving,
 ):
     slabs, padded, width = gated_ref.shape
     frames = padded - 4 * EDGE
@@ -163,7 +163,13 @@
                 ] = (grad_lin * lin * (1.0 - sig)).astype(jnp.bfloat16)
             return carry
 
-        return lax.fori_loop(0, (frames // ROWS_STEP) * (blocks // 2), conv_step, carry)
+        lax.fori_loop(0, (frames // ROWS_STEP) * (blocks // 2), conv_step, 0)
+        kept_copy(s).start()
+        return carry
+
+    def kept_copy(s):
+        rows = pl.ds(pl.multiple_of(s * frames, ROWS_STEP), frames)
+        return pltpu.make_async_copy(grad_hidden_ref.at[rows], kept_ref.at[rows], leaving.at[s])
 
     lax.fori_loop(0, slabs, one_slab, 0)
     for b in range(blocks):
@@ -177,6 +183,8 @@
     grad_taps_ref[taps_count + 1 : taps_count + 2, :] = jnp.sum(
         grad_gain_ref[...], axis=0, keepdims=True
     )
+    for s in range(slabs):
+        kept_copy(s).wait()
 
 
 def send_kernel(index_ref, rows_ref, out_ref):
@@ -270,7 +278,6 @@
             )
             block = slice(z * LANES, (z + 1) * LANES)
             out_ref[block, width : width + LANES] = filled.T.astype(out_ref.dtype)
-            out_ref[block, width + LANES :] = jnp.zeros((LANES, SMALL - LANES), out_ref.dtype)
 
 
 def weight_part(core, left, left_other, right, right_other, *small):
@@ -359,7 +366,7 @@
         ],
         out_specs=(out, out, out),
         name="project",
-        compiler_params=pltpu.CompilerParams(vmem_limit_bytes=50 * 1024 * 1024),
+        compiler_params=pltpu.CompilerParams(vmem_limit_bytes=VMEM_GRANT),
         cost_estimate=pl.CostEstimate(
             flops=4 * rows * width * width,
             bytes_accessed=4 * width * width,
@@ -368,7 +375,7 @@
     )(normed, weight, weight)
 
 
-def kernel_call(body, outs, scratch, flops, *args):
+def kernel_call(body, outs, scratch, flops, *args, **specs):
     moved = sum(a.size * a.dtype.itemsize for a in args)
     return pl.pallas_call(
         body,
@@ -376,6 +383,7 @@
         scratch_shapes=scratch,
         compiler_params=pltpu.CompilerParams(vmem_limit_bytes=VMEM_GRANT),
         cost_estimate=pl.CostEstimate(flops=flops, bytes_accessed=moved, transcendentals=0),
+        **specs,
     )(*args)
 
 
@@ -433,12 +441,11 @@
         core == 0, jnp.stack([extras, extras_other]), jnp.stack([extras_other, extras])
     )
     from_z = [
-        lax.ppermute(pair, "z", [(i, (i + d) % n_z) for i in range(n_z)]) for d in range(1, n_z)
+        lax.ppermute(pair, "z", [(i, (i + d) % n_z) for i in range(n_z)])
+        for d in range(1, n_z)
     ]
     upstream_other = lax.ppermute(upstream_rows, "core", swap)
-    arrived, upstream_other, pair, *from_z = lax.optimization_barrier(
-        (arrived, upstream_other, pair, *from_z)
-    )
+    arrived, upstream_other, pair = lax.optimization_barrier((arrived, upstream_other, pair))
     by_z = jnp.stack([*from_z[::-1], pair])
     side_all = lax.dynamic_slice_in_dim(
         jnp.concatenate([by_z, by_z]), n_z - 1 - lax.axis_index("z"), n_z, 0
@@ -494,12 +501,11 @@
     elements = rows_dev * width
     wide = frames_dev + 2 * EDGE
     blocks = width // LANES
-    activated, normed_mid, scale_mid = kernel_call(
+    activated, normed_mid = kernel_call(
         forward_kernel,
         (
             jax.ShapeDtypeStruct((rows_dev, width), jnp.bfloat16),
-            jax.ShapeDtypeStruct((slabs * wide, width), jnp.float32),
-            jax.ShapeDtypeStruct((slabs * wide, LANES), jnp.float32),
+            jax.ShapeDtypeStruct((slabs * wide, width + LANES), jnp.float32),
         ),
         [
             pltpu.VMEM((blocks, padded, LANES), jnp.float32),
@@ -517,7 +523,7 @@
         ),
         [pltpu.VMEM((slabs * wide, width), jnp.float32)],
         2 * slabs * wide * width * width,
-        normed_mid, scale_mid, upstream_wide, out_full, gain_mid[None],
+        normed_mid, upstream_wide, out_full, gain_mid[None],
     )
 
     def exchanged(part):
@@ -532,18 +538,25 @@
     projected = jnp.dot(activated, out_full, preferred_element_type=jnp.float32)
     encoded = (frame_rows + projected).astype(jnp.bfloat16).reshape(slabs, frames_dev, width)
 
-    grad_hidden, grad_taps = kernel_call(
+    grad_hidden, grad_taps, grad_hidden_kept = kernel_call(
         backward_kernel,
         (
             jax.ShapeDtypeStruct((rows_dev, 2 * width), jnp.bfloat16),
             jax.ShapeDtypeStruct((kernel_len + 9, width), jnp.float32),
+            pltpu.HBM((rows_dev, 2 * width), jnp.bfloat16),
         ),
         [
             pltpu.VMEM((blocks, wide, LANES), jnp.float32),
             pltpu.VMEM((blocks, kernel_len, 8, LANES), jnp.float32),
+            pltpu.SemaphoreType.DMA((slabs,)),
         ],
         elements * 5 * kernel_len,
         grad_mixing, gated, ids, taps, lin, sig, grad_gain_mid,
+        out_specs=(
+            pl.BlockSpec(memory_space=pltpu.VMEM),
+            pl.BlockSpec(memory_space=pltpu.VMEM),
+            pl.BlockSpec(memory_space=pltpu.HBM),
+        ),
     )
     hidden_other = lax.ppermute(grad_hidden, "core", swap)
     small_other = lax.ppermute(grad_taps, "core", swap)
@@ -552,7 +565,7 @@
     )
     in_parts = exchanged(in_part)
     grad_normed = lax.dot_general(
-        grad_hidden, in_full, (((1,), (1,)), ((), ())), preferred_element_type=jnp.float32
+        grad_hidden_kept, in_full, (((1,), (1,)), ((), ())), preferred_element_type=jnp.float32
     )
     grad_rows, _ = pull_pre(grad_normed)
     grad_frames = (

time: 195 us -> 192 us (0.985)
    pallas_call x1, Pallas kernels: 5.29 us -> 3.27 us  [project(): pl.pallas_call(project_kernel, out_shape=(jax.ShapeDtypeStruct((rows, wid...]
    unnamed x56 -> x58, local copies, waits for them, and re-layouts: 10.9 us -> 11.7 us
  transfers between devices with their start and end apart: 17 -> 17, of which waited for: 9 -> 10; matrix products, arithmetic and copies ran while one was open for 7% -> 8% of each run, Pallas kernels for 17% -> 17%
where the time goes in v9:
time: 192 us
  waiting for transfers between devices  76.7 us (40%)
  starting transfers between devices  39.6 us (21%)
  Pallas kernels  34.3 us (18%)
  between operations  14.5 us (8%)
  local copies, waits for them, and re-layouts  13.7 us (7%)
  matrix products  6.48 us (3%)
  other arithmetic  6.21 us (3%)
    all_to_all x2, waiting for transfers between devices, exchanged(): lax.all_to_all(part.reshape(n_z * n_seq, LANES // n_seq, part.shape[1]),...  35.9 us
    pallas_call x8, Pallas kernels, kernel_call(): pl.pallas_call(body, out_shape=outs, scratch_shapes=scratch, compiler_par...  23.9 us
    all_to_all x2, starting transfers between devices, exchanged(): lax.all_to_all(part.reshape(n_z * n_seq, LANES // n_seq, part.shape[1]),...  14.4 us
    ppermute x3, waiting for transfers between devices, per_device(): lax.ppermute(pair, 'z', [(i, (i + d) % n_z) for i in range(n_z)])  14.1 us
    unnamed x58, local copies, waits for them, and re-layouts  11.7 us
    all_to_all x1, starting transfers between devices, per_device(): lax.all_to_all(outgoing, (*DP, *SEQ), split_axis=0, concat_axis=0, tiled=...  11.2 us
    all_gather x1, waiting for transfers between devices, per_device(): out_full = lax.all_gather(out_weight, DP, axis=0, tiled=True)  9.2 us
    all_to_all x1, waiting for transfers between devices, per_device(): final = lax.all_to_all(total, SEQ, 0, 0, tiled=True).reshape(LANES, -1)  8.12 us
  transfers between devices with their start and end apart: 17, of which 10 were waited for; matrix products, arithmetic and copies ran while one was open for 8% of the time, Pallas kernels for 17%

profile of v9, /device:TPU:0, one launch (start us, length us, event | category | flops | bytes accessed | tf_op | source)
XLA Modules:
  0.0 191.5 jit_solution(16300788424067765403)
XLA Ops:
  11.0 1.5 shard_map.127
  12.4 11.2 %all-to-all-start = ((bf16[128,8,512]{2,1,0:T(8,128)(2,1)}), bf16[128,8,512]{2,1,0:T(8,128)(2,1)S(1)}, u32[]{:S(2)}, u32[]{:S(2)}) async-start(bf16[128,8,512]{2,1,0:T(8,128)(2,1)} %shard_map.127), calls=%async_computation | async-start | bytes 2097152 | tf_op jit(solution)/shard_map/all_to_all | solution.py:432
  25.1 2.9 %collective-permute-start.4 = (bf16[2,128,128]{1,2,0:T(8,128)(2,1)S(1)}, bf16[2,128,128]{1,2,0:T(8,128)(2,1)S(1)}, u32[]{:S(2)}, u32[]{:S(2)}) collective-permute-start(bf16[2,128,128]{1,2,0:T(8,128)(2,1)S(1)} %maximum_select_fusion), channel_id=1, source_target_pairs={{0,96},{32,0},{64,32},{96,64},{1,97},{33,1},{65,33},{97,65},{2,98}... | collective-permute-start | bytes 196616 | tf_op jit(solution)/shard_map/ppermute | solution.py:444
  29.6 10.7 %collective-permute-done.4 = bf16[2,128,128]{1,2,0:T(8,128)(2,1)S(1)} collective-permute-done((bf16[2,128,128]{1,2,0:T(8,128)(2,1)S(1)}, bf16[2,128,128]{1,2,0:T(8,128)(2,1)S(1)}, u32[]{:S(2)}, u32[]{:S(2)}) %collective-permute-start.4) | collective-permute-done | bytes 65568 | tf_op jit(solution)/shard_map/ppermute | solution.py:444
  40.4 1.9 %collective-permute-done.5 = bf16[2,128,128]{1,2,0:T(8,128)(2,1)S(1)} collective-permute-done((bf16[2,128,128]{1,2,0:T(8,128)(2,1)S(1)}, bf16[2,128,128]{1,2,0:T(8,128)(2,1)S(1)}, u32[]{:S(2)}, u32[]{:S(2)}) %collective-permute-start.5) | collective-permute-done | bytes 65568 | tf_op jit(solution)/shard_map/ppermute | solution.py:444
  42.3 1.5 collective-permute-done.6
  45.6 2.8 %collective-permute-start.2 = (bf16[2,48,1024]{2,1,0:T(8,128)(2,1)S(1)}, bf16[2,48,1024]{2,1,0:T(8,128)(2,1)S(1)}, u32[]{:S(2)}, u32[]{:S(2)}) collective-permute-start(bf16[2,48,1024]{2,1,0:T(8,128)(2,1)S(1)} %get-tuple-element.33), channel_id=1, source_target_pairs={{0,1},{1,2},{2,3},{3,4},{4,5},{5,6},{6,7},{7,8},{8,9},{9,10},{10,1... | collective-permute-start | bytes 589832 | tf_op jit(solution)/shard_map/ppermute | solution.py:393
  48.3 1.3 collective-permute-start.3
  49.7 3.2 %collective-permute-done.2.low_ref = bf16[2,48,1024]{2,1,0:T(8,128)(2,1)S(1)} collective-permute-done((bf16[2,48,1024]{2,1,0:T(8,128)(2,1)S(1)}, bf16[2,48,1024]{2,1,0:T(8,128)(2,1)S(1)}, u32[]{:S(2)}, u32[]{:S(2)}) %collective-permute-start.2) | collective-permute-done | bytes 196640 | tf_op jit(solution)/shard_map/ppermute | solution.py:393
  52.8 4.1 %collective-permute-done.3.high_ref = bf16[2,48,1024]{2,1,0:T(8,128)(2,1)S(1)} collective-permute-done((bf16[2,48,1024]{2,1,0:T(8,128)(2,1)S(1)}, bf16[2,48,1024]{2,1,0:T(8,128)(2,1)S(1)}, u32[]{:S(2)}, u32[]{:S(2)}) %collective-permute-start.3) | collective-permute-done | bytes 196640 | tf_op jit(solution)/shard_map/ppermute | solution.py:393
  59.8 2.2 %copy-done = bf16[1024,2048]{1,0:T(8,128)(2,1)S(1)} copy-done((bf16[1024,2048]{1,0:T(8,128)(2,1)S(1)}, bf16[1024,2048]{1,0:T(8,128)(2,1)}, u32[]{:S(2)}) %copy-start) | copy-done | bytes 4194328
  62.0 3.3 %project.1 = (f32[384,1024]{1,0:T(8,128)S(1)}, f32[384,1024]{1,0:T(8,128)S(1)}, bf16[384,1024]{1,0:T(8,128)(2,1)S(1)}) custom-call(bf16[384,1024]{1,0:T(8,128)(2,1)S(1)} %bitcast.57, bf16[1024,2048]{1,0:T(8,128)(2,1)S(1)} %copy-done, bf16[1024,2048]{1,0:T(8,128)(2,1)S(1)} %copy-done), custom_call_target="tpu_custom_call" | custom-call | flops 1610612736 | bytes 4194304 | tf_op jit(solution)/shard_map/project/pallas_call | solution.py:354
  65.3 1.2 copy-done.5
  67.7 8.2 %shard_map.130 = (bf16[256,1024]{1,0:T(8,128)(2,1)}, f32[320,1152]{1,0:T(8,128)S(1)}) custom-call(bf16[2,192,1024]{2,1,0:T(8,128)(2,1)S(1)} %bitcast.54, s32[2,192,128]{2,1,0:T(8,128)S(1)} %broadcast_in_dim.39.ids_ref, f32[8,32,128]{2,1,0:T(8,128)S(1)} %copy-done.9, f32[1,1024]{1,0:T(1,128)S(1)} %get-tuple-element.64.gain_ref), custom_call_target="tpu_custom_call" | custom-call | flops 24379392 | bytes 1118208 | tf_op jit(solution)/shard_map/pallas_call | solution.py:380
  76.5 9.2 %all-gather.5.cloned.1.call-done.weight_ref = bf16[1024,1024]{1,0:T(8,128)(2,1)} async-done(((bf16[128,1024]{1,0:T(8,128)(2,1)}), bf16[1024,1024]{1,0:T(8,128)(2,1)}) %all-gather.5.cloned.1.call-update) | async-done | bytes 2097168 | tf_op jit(solution)/shard_map/all_gather | solution.py:419
  85.7 1.6 copy-done.3
  88.3 2.2 %shard_map.131 = (f32[2,160,1024]{2,1,0:T(8,128)S(1)}, f32[8,1024]{1,0:T(8,128)S(1)}) custom-call(f32[320,1152]{1,0:T(8,128)S(1)} %get-tuple-element.41.normed_ref, bf16[320,1024]{1,0:T(8,128)(2,1)S(1)} %copy-done.12, bf16[1024,1024]{1,0:T(8,128)(2,1)S(1)} %copy-done.3, f32[1,1024]{1,0:T(1,128)S(1)} %get-tuple-element.64.gain_ref), custom_call_target="tpu_custom_call" | custom-call | flops 671088640 | bytes 4231168 | tf_op jit(solution)/shard_map/pallas_call | solution.py:380
  90.6 8.5 %shard_map.132 = (bf16[256,2048]{1,0:T(8,128)(2,1)S(1)}, f32[40,1024]{1,0:T(8,128)S(1)}, bf16[256,2048]{1,0:T(8,128)(2,1)}) custom-call(f32[2,160,1024]{2,1,0:T(8,128)S(1)} %get-tuple-element.43.grad_mix_ref, bf16[2,192,1024]{2,1,0:T(8,128)(2,1)S(1)} %bitcast.55, s32[2,192,128]{2,1,0:T(8,128)S(1)} %broadcast_in_dim.39.ids_ref, f32[8,32,128]{2,1,0:T(8,128)S(1)} %copy-done.10, ...), custom_call_target="tpu_custom_call" | custom-call | flops 40632320 | bytes 5603328 | tf_op jit(solution)/shard_map/pallas_call | solution.py:380
  99.4 3.0 %weight_part.3 = bf16[512,1024]{1,0:T(8,128)(2,1)} custom-call(s32[1]{0:T(128)} %bitcast.19.core_ref, bf16[256,1024]{1,0:T(8,128)(2,1)} %get-tuple-element.40.left_ref, bf16[256,1024]{1,0:T(8,128)(2,1)} %collective-permute-done.10.left_other_ref, bf16[256,1024]{1,0:T(8,128)(2,1)S(1)} %bitcast.52, bf16[256,1024]{1,0:T(8,128)(2,1)S(1)} %copy-done.16), custom_call_target="tpu_custom_call" | custom-call | flops 536870912 | bytes 2097152 | tf_op jit(solution)/shard_map/weight_part/pallas_call | solution.py:289
  102.4 9.5 %all-to-all-start.2 = ((bf16[64,8,1024]{2,1,0:T(8,128)(2,1)}), bf16[64,8,1024]{2,1,0:T(8,128)(2,1)}, u32[]{:S(2)}, u32[]{:S(2)}) async-start(bf16[64,8,1024]{2,1,0:T(8,128)(2,1)} %bitcast.21), calls=%async_computation.2 | async-start | bytes 2097152 | tf_op jit(solution)/shard_map/all_to_all | solution.py:530
  112.2 1.4 collective-permute-done.9.rest_1_
  113.6 4.1 %weight_part.2 = bf16[512,2176]{1,0:T(8,128)(2,1)} custom-call(s32[1]{0:T(128)} %bitcast.19.core_ref, bf16[256,1024]{1,0:T(8,128)(2,1)S(1)} %copy-done.14, bf16[256,1024]{1,0:T(8,128)(2,1)} %collective-permute-done.7.left_other_ref, bf16[256,2048]{1,0:T(8,128)(2,1)S(1)} %get-tuple-element.49.right_ref, ...), custom_call_target="tpu_custom_call" | custom-call | flops 1073741824 | bytes 3145728 | tf_op jit(solution)/shard_map/weight_part/pallas_call | solution.py:289
  117.7 13.2 %all-to-all-done.2 = bf16[64,8,1024]{2,1,0:T(8,128)(2,1)} async-done(((bf16[64,8,1024]{2,1,0:T(8,128)(2,1)}), bf16[64,8,1024]{2,1,0:T(8,128)(2,1)}, u32[]{:S(2)}, u32[]{:S(2)}) %all-to-all-start.2) | async-done | bytes 1048608 | tf_op jit(solution)/shard_map/all_to_all | solution.py:530
  130.9 5.0 %all-to-all-start.1 = ((bf16[64,8,2176]{2,1,0:T(8,128)(2,1)}), bf16[64,8,2176]{2,1,0:T(8,128)(2,1)S(1)}, u32[]{:S(2)}, u32[]{:S(2)}) async-start(bf16[64,8,2176]{2,1,0:T(8,128)(2,1)} %bitcast.20), calls=%async_computation.1 | async-start | bytes 4456448 | tf_op jit(solution)/shard_map/all_to_all | solution.py:530
  137.0 3.9 %fusion.4 = (f32[256]{0:T(256)S(1)}, f32[256]{0:T(256)S(1)}, f32[256,1024]{1,0:T(8,128)S(1)}) fusion(bf16[256,1024]{1,0:T(8,128)(2,1)S(1)} %get-tuple-element.32.frames_ref, f32[256]{0:T(256)S(1)} %broadcast_multiply_fusion, f32[1024]{0:T(1024)S(1)} %bitcast.58, bf16[256,2048]{1,0:T(8,128)(2,1)} %get-tuple-element.47, ...), kind=kOutput, calls=%fused_computation.10 | convolution fusion | flops 1075576320 | bytes 6822912 | tf_op jit(solution)/shard_map/dot_general | solution.py:567
  141.9 1.4 convert_reduce_fusion.out_sum_ref
  143.3 22.6 %all-to-all-done.1.parts_ref = bf16[64,8,2176]{2,1,0:T(8,128)(2,1)S(1)} async-done(((bf16[64,8,2176]{2,1,0:T(8,128)(2,1)}), bf16[64,8,2176]{2,1,0:T(8,128)(2,1)S(1)}, u32[]{:S(2)}, u32[]{:S(2)}) %all-to-all-start.1) | async-done | bytes 2228256 | tf_op jit(solution)/shard_map/all_to_all | solution.py:530
  167.3 3.8 %all-to-all-start.3 = ((bf16[16,8,3200]{2,1,0:T(8,128)(2,1)}), bf16[16,8,3200]{2,1,0:T(8,128)(2,1)S(1)}, u32[]{:S(2)}, u32[]{:S(2)}) async-start(bf16[16,8,3200]{2,1,0:T(8,128)(2,1)} %copy-done.2), calls=%async_computation.3 | async-start | bytes 1638400 | tf_op jit(solution)/shard_map/all_to_all | solution.py:589
  171.0 1.2 add_convert_fusion
  172.8 2.6 %fusion.3 = bf16[256,1024]{1,0:T(8,128)(2,1)} fusion(bf16[256,1024]{1,0:T(8,128)(2,1)} %get-tuple-element.40.left_ref, bf16[1024,1024]{1,0:T(8,128)(2,1)S(1)} %copy-done.4, bf16[256,1024]{1,0:T(8,128)(2,1)S(1)} %get-tuple-element.32.frames_ref), kind=kOutput, calls=%fused_computation.9 | convolution fusion | flops 537657344 | bytes 3670016 | tf_op jit(solution)/shard_map/dot_general | solution.py:538
  175.4 8.1 %all-to-all-done.3 = bf16[16,8,3200]{2,1,0:T(8,128)(2,1)S(1)} async-done(((bf16[16,8,3200]{2,1,0:T(8,128)(2,1)}), bf16[16,8,3200]{2,1,0:T(8,128)(2,1)S(1)}, u32[]{:S(2)}, u32[]{:S(2)}) %all-to-all-start.3) | async-done | bytes 819232 | tf_op jit(solution)/shard_map/all_to_all | solution.py:589
  183.5 1.2 shard_map.134
  (111 shorter events, 18.8 us)
Async XLA Ops:
  7.2 52.6 %all-gather.3.cloned.1.call-start = ((), (), s32[]{:S(2)}) async-start(), calls=%async_computation.4 | async-start | bytes 4718592 | tf_op jit(solution)/shard_map/all_gather | solution.py:418
  11.0 12.7 %copy-start.22 = (bf16[128,31]{0,1:T(8,128)(2,1)S(1)}, bf16[128,31]{0,1:T(8,128)(2,1)}, u32[]{:S(2)}) copy-start(bf16[128,31]{0,1:T(8,128)(2,1)} %param.13) | copy-start | bytes 23812
  11.0 12.7 %copy-start.23 = (bf16[128,2]{0,1:T(2,128)(2,1)S(1)}, bf16[128,2]{0,1:T(2,128)(2,1)}, u32[]{:S(2)}) copy-start(bf16[128,2]{0,1:T(2,128)(2,1)} %param.14) | copy-start | bytes 1540
  11.0 12.8 %copy-start.1 = (bf16[2,128,1024]{2,1,0:T(8,128)(2,1)S(1)}, bf16[2,128,1024]{2,1,0:T(8,128)(2,1)}, u32[]{:S(2)}) copy-start(bf16[2,128,1024]{2,1,0:T(8,128)(2,1)} %upstream_ref.3) | copy-start | bytes 1572868
  11.0 13.4 %copy-start.20 = (s32[128,128]{1,0:T(8,128)S(1)}, s32[128,128]{1,0:T(8,128)}, u32[]{:S(2)}) copy-start(s32[128,128]{1,0:T(8,128)} %param.9) | copy-start | bytes 196612
  12.4 31.4 %all-to-all-start = ((bf16[128,8,512]{2,1,0:T(8,128)(2,1)}), bf16[128,8,512]{2,1,0:T(8,128)(2,1)S(1)}, u32[]{:S(2)}, u32[]{:S(2)}) async-start(bf16[128,8,512]{2,1,0:T(8,128)(2,1)} %shard_map.127), calls=%async_computation | async-start | bytes 2097152 | tf_op jit(solution)/shard_map/all_to_all | solution.py:432
  23.6 62.1 %all-gather.5.cloned.1.call-start = ((), (), s32[]{:S(2)}) async-start(), calls=%async_computation.5 | async-start | bytes 2359296 | tf_op jit(solution)/shard_map/all_gather | solution.py:419
  23.7 1.3 collective-permute-start.1
  23.8 20.0 %collective-permute-start = (bf16[256,1024]{1,0:T(8,128)(2,1)S(1)}, bf16[256,1024]{1,0:T(8,128)(2,1)S(1)}, u32[]{:S(2)}, u32[]{:S(2)}) collective-permute-start(bf16[256,1024]{1,0:T(8,128)(2,1)S(1)} %bitcast.51), channel_id=1, source_target_pairs={{0,16},{16,0},{1,17},{17,1},{2,18},{18,2},{3,19},{19,3},{4,20},{20... | collective-permute-start | bytes 1572872 | tf_op jit(solution)/shard_map/ppermute | solution.py:447
  25.1 15.3 %collective-permute-start.4 = (bf16[2,128,128]{1,2,0:T(8,128)(2,1)S(1)}, bf16[2,128,128]{1,2,0:T(8,128)(2,1)S(1)}, u32[]{:S(2)}, u32[]{:S(2)}) collective-permute-start(bf16[2,128,128]{1,2,0:T(8,128)(2,1)S(1)} %maximum_select_fusion), channel_id=1, source_target_pairs={{0,96},{32,0},{64,32},{96,64},{1,97},{33,1},{65,33},{97,65},{2,98}... | collective-permute-start | bytes 196616 | tf_op jit(solution)/shard_map/ppermute | solution.py:444
  28.1 14.2 %collective-permute-start.5 = (bf16[2,128,128]{1,2,0:T(8,128)(2,1)S(1)}, bf16[2,128,128]{1,2,0:T(8,128)(2,1)S(1)}, u32[]{:S(2)}, u32[]{:S(2)}) collective-permute-start(bf16[2,128,128]{1,2,0:T(8,128)(2,1)S(1)} %maximum_select_fusion), channel_id=1, source_target_pairs={{0,64},{32,96},{64,0},{96,32},{1,65},{33,97},{65,1},{97,33},{2,66}... | collective-permute-start | bytes 196616 | tf_op jit(solution)/shard_map/ppermute | solution.py:444
  28.5 15.2 %collective-permute-start.6 = (bf16[2,128,128]{1,2,0:T(8,128)(2,1)S(1)}, bf16[2,128,128]{1,2,0:T(8,128)(2,1)S(1)}, u32[]{:S(2)}, u32[]{:S(2)}) collective-permute-start(bf16[2,128,128]{1,2,0:T(8,128)(2,1)S(1)} %maximum_select_fusion), channel_id=1, source_target_pairs={{0,32},{32,64},{64,96},{96,0},{1,33},{33,65},{65,97},{97,1},{2,34}... | collective-permute-start | bytes 196616 | tf_op jit(solution)/shard_map/ppermute | solution.py:444
  44.6 14.4 %copy-start.21 = (s32[2,2048]{1,0:T(2,128)S(1)}, s32[2,2048]{1,0:T(2,128)}, u32[]{:S(2)}) copy-start(s32[2,2048]{1,0:T(2,128)} %param.10) | copy-start | bytes 49156
  44.6 14.5 %copy-start.24 = (pred[32]{0:T(512)(128)(4,1)S(1)}, pred[32]{0:T(512)(128)(4,1)}, u32[]{:S(2)}) copy-start(pred[32]{0:T(512)(128)(4,1)} %constant.66.clone.1) | copy-start | bytes 100
  45.6 7.3 %collective-permute-start.2 = (bf16[2,48,1024]{2,1,0:T(8,128)(2,1)S(1)}, bf16[2,48,1024]{2,1,0:T(8,128)(2,1)S(1)}, u32[]{:S(2)}, u32[]{:S(2)}) collective-permute-start(bf16[2,48,1024]{2,1,0:T(8,128)(2,1)S(1)} %get-tuple-element.33), channel_id=1, source_target_pairs={{0,1},{1,2},{2,3},{3,4},{4,5},{5,6},{6,7},{7,8},{8,9},{9,10},{10,1... | collective-permute-start | bytes 589832 | tf_op jit(solution)/shard_map/ppermute | solution.py:393
  48.3 8.6 %collective-permute-start.3 = (bf16[2,48,1024]{2,1,0:T(8,128)(2,1)S(1)}, bf16[2,48,1024]{2,1,0:T(8,128)(2,1)S(1)}, u32[]{:S(2)}, u32[]{:S(2)}) collective-permute-start(bf16[2,48,1024]{2,1,0:T(8,128)(2,1)S(1)} %get-tuple-element.34), channel_id=1, source_target_pairs={{1,0},{2,1},{3,2},{4,3},{5,4},{6,5},{7,6},{8,7},{9,8},{10,9},{11,1... | collective-permute-start | bytes 589832 | tf_op jit(solution)/shard_map/ppermute | solution.py:393
  59.0 6.3 %copy-start.13 = (bf16[256,1024]{1,0:T(8,128)(2,1)}, bf16[256,1024]{1,0:T(8,128)(2,1)S(1)}, u32[]{:S(2)}) copy-start(bf16[256,1024]{1,0:T(8,128)(2,1)S(1)} %get-tuple-element.38.left_ref) | copy-start | bytes 1572868
  59.0 8.7 %collective-permute-start.7 = (bf16[256,1024]{1,0:T(8,128)(2,1)S(1)}, bf16[256,1024]{1,0:T(8,128)(2,1)}, u32[]{:S(2)}, u32[]{:S(2)}) collective-permute-start(bf16[256,1024]{1,0:T(8,128)(2,1)S(1)} %get-tuple-element.38.left_ref), channel_id=1, source_target_pairs={{0,16},{16,0},{1,17},{17,1},{2,18},{18,2},{3,19},{19,3},{4,20},{20... | collective-permute-start | bytes 1572872 | tf_op jit(solution)/shard_map/ppermute | solution.py:497
  59.8 2.2 %copy-start = (bf16[1024,2048]{1,0:T(8,128)(2,1)S(1)}, bf16[1024,2048]{1,0:T(8,128)(2,1)}, u32[]{:S(2)}) copy-start(bf16[1024,2048]{1,0:T(8,128)(2,1)} %all-gather.3.cloned.1.call-done.lin_w_ref.gate_w_ref) | copy-start | bytes 12582916
  62.0 5.8 %copy-start.9 = (f32[8,32,128]{2,1,0:T(8,128)S(1)}, f32[8,32,128]{2,1,0:T(8,128)}, u32[]{:S(2)}) copy-start(f32[8,32,128]{2,1,0:T(8,128)} %bitcast_bitcast_fusion.taps_ref) | copy-start | bytes 393220
  76.0 23.5 %collective-permute-start.10 = (bf16[256,1024]{1,0:T(8,128)(2,1)}, bf16[256,1024]{1,0:T(8,128)(2,1)}, u32[]{:S(2)}, u32[]{:S(2)}) collective-permute-start(bf16[256,1024]{1,0:T(8,128)(2,1)} %get-tuple-element.40.left_ref), channel_id=1, source_target_pairs={{0,16},{16,0},{1,17},{17,1},{2,18},{18,2},{3,19},{19,3},{4,20},{20... | collective-permute-start | bytes 1572872 | tf_op jit(solution)/shard_map/ppermute | solution.py:517
  88.3 2.2 %copy-start.6 = (f32[384,1024]{1,0:T(8,128)S(1)}, f32[384,1024]{1,0:T(8,128)}, u32[]{:S(2)}) copy-start(f32[384,1024]{1,0:T(8,128)} %copy-done.5) | copy-start | bytes 4718596
  88.3 2.2 %copy-start.8 = (f32[384,1024]{1,0:T(8,128)S(1)}, f32[384,1024]{1,0:T(8,128)}, u32[]{:S(2)}) copy-start(f32[384,1024]{1,0:T(8,128)} %copy-done.7) | copy-start | bytes 4718596
  88.3 2.2 %copy-start.10 = (f32[8,32,128]{2,1,0:T(8,128)S(1)}, f32[8,32,128]{2,1,0:T(8,128)}, u32[]{:S(2)}) copy-start(f32[8,32,128]{2,1,0:T(8,128)} %bitcast_bitcast_fusion.taps_ref) | copy-start | bytes 393220
  90.6 8.9 %copy-start.16 = (bf16[256,1024]{1,0:T(8,128)(2,1)S(1)}, bf16[256,1024]{1,0:T(8,128)(2,1)}, u32[]{:S(2)}) copy-start(bf16[256,1024]{1,0:T(8,128)(2,1)} %copy-done.15) | copy-start | bytes 1572868
  99.1 14.5 %collective-permute-start.8 = (bf16[256,2048]{1,0:T(8,128)(2,1)S(1)}, bf16[256,2048]{1,0:T(8,128)(2,1)}, u32[]{:S(2)}, u32[]{:S(2)}) collective-permute-start(bf16[256,2048]{1,0:T(8,128)(2,1)S(1)} %get-tuple-element.49.right_ref), channel_id=1, source_target_pairs={{0,16},{16,0},{1,17},{17,1},{2,18},{18,2},{3,19},{19,3},{4,20},{20... | collective-permute-start | bytes 3145736 | tf_op jit(solution)/shard_map/ppermute | solution.py:561
  99.4 14.1 %copy-start.14 = (bf16[256,1024]{1,0:T(8,128)(2,1)S(1)}, bf16[256,1024]{1,0:T(8,128)(2,1)}, u32[]{:S(2)}) copy-start(bf16[256,1024]{1,0:T(8,128)(2,1)} %copy-done.13) | copy-start | bytes 1572868
  102.4 28.5 %all-to-all-start.2 = ((bf16[64,8,1024]{2,1,0:T(8,128)(2,1)}), bf16[64,8,1024]{2,1,0:T(8,128)(2,1)}, u32[]{:S(2)}, u32[]{:S(2)}) async-start(bf16[64,8,1024]{2,1,0:T(8,128)(2,1)} %bitcast.21), calls=%async_computation.2 | async-start | bytes 2097152 | tf_op jit(solution)/shard_map/all_to_all | solution.py:530
  111.9 1.7 collective-permute-start.9
  130.9 35.0 %all-to-all-start.1 = ((bf16[64,8,2176]{2,1,0:T(8,128)(2,1)}), bf16[64,8,2176]{2,1,0:T(8,128)(2,1)S(1)}, u32[]{:S(2)}, u32[]{:S(2)}) async-start(bf16[64,8,2176]{2,1,0:T(8,128)(2,1)} %bitcast.20), calls=%async_computation.1 | async-start | bytes 4456448 | tf_op jit(solution)/shard_map/all_to_all | solution.py:530
  167.3 3.8 %copy-start.19 = (f32[256,1024]{1,0:T(8,128)S(1)}, f32[256,1024]{1,0:T(8,128)}, u32[]{:S(2)}) copy-start(f32[256,1024]{1,0:T(8,128)} %copy-done.18) | copy-start | bytes 3145732
  167.3 16.2 %all-to-all-start.3 = ((bf16[16,8,3200]{2,1,0:T(8,128)(2,1)}), bf16[16,8,3200]{2,1,0:T(8,128)(2,1)S(1)}, u32[]{:S(2)}, u32[]{:S(2)}) async-start(bf16[16,8,3200]{2,1,0:T(8,128)(2,1)} %copy-done.2), calls=%async_computation.3 | async-start | bytes 1638400 | tf_op jit(solution)/shard_map/all_to_all | solution.py:589
  (10 other events, 11.4 us)
Sparse Core Ops, SparseCore 0:
  9.7 48.8 all-gather.2
  60.3 25.3 all-gather.4

commit v10 on v9

--- a/solution.py
+++ b/solution.py
@@ -114,13 +114,13 @@
         return total
 
     grad_gain_ref[...] = lax.fori_loop(
-        0, slabs * steps, row_step, jnp.zeros(grad_gain_ref.shape, jnp.float32), unroll=4
+        0, slabs * steps, row_step, jnp.zeros(grad_gain_ref.shape, jnp.float32), unroll=10
     )
 
 
 def backward_kernel(
     grad_mix_ref, gated_ref, ids_ref, taps_ref, lin_ref, sig_ref, grad_gain_ref,
-    grad_hidden_ref, grad_taps_ref, kept_ref, pad_ref, sum_ref, leaving,
+    grad_hidden_ref, grad_taps_ref, pad_ref, sum_ref,
 ):
     slabs, padded, width = gated_ref.shape
     frames = padded - 4 * EDGE
@@ -163,13 +163,7 @@
                 ] = (grad_lin * lin * (1.0 - sig)).astype(jnp.bfloat16)
             return carry
 
-        lax.fori_loop(0, (frames // ROWS_STEP) * (blocks // 2), conv_step, 0)
-        kept_copy(s).start()
-        return carry
-
-    def kept_copy(s):
-        rows = pl.ds(pl.multiple_of(s * frames, ROWS_STEP), frames)
-        return pltpu.make_async_copy(grad_hidden_ref.at[rows], kept_ref.at[rows], leaving.at[s])
+        return lax.fori_loop(0, (frames // ROWS_STEP) * (blocks // 2), conv_step, carry)
 
     lax.fori_loop(0, slabs, one_slab, 0)
     for b in range(blocks):
@@ -183,8 +177,6 @@
     grad_taps_ref[taps_count + 1 : taps_count + 2, :] = jnp.sum(
         grad_gain_ref[...], axis=0, keepdims=True
     )
-    for s in range(slabs):
-        kept_copy(s).wait()
 
 
 def send_kernel(index_ref, rows_ref, out_ref):
@@ -255,7 +247,7 @@
     small_refs, out_ref, turned_ref = rest[:-2], rest[-2], rest[-1]
     rows, channels = left_ref.shape
     width = right_ref.shape[1]
-    step = 512
+    step = 1024
     picks = [
         pl.ds(pl.multiple_of((2 * z + core_ref[0]) * LANES, LANES), LANES)
         for z in range(channels // LANES // 2)
@@ -375,7 +367,7 @@
     )(normed, weight, weight)
 
 
-def kernel_call(body, outs, scratch, flops, *args, **specs):
+def kernel_call(body, outs, scratch, flops, *args):
     moved = sum(a.size * a.dtype.itemsize for a in args)
     return pl.pallas_call(
         body,
@@ -383,7 +375,6 @@
         scratch_shapes=scratch,
         compiler_params=pltpu.CompilerParams(vmem_limit_bytes=VMEM_GRANT),
         cost_estimate=pl.CostEstimate(flops=flops, bytes_accessed=moved, transcendentals=0),
-        **specs,
     )(*args)
 
 
@@ -538,25 +529,18 @@
     projected = jnp.dot(activated, out_full, preferred_element_type=jnp.float32)
     encoded = (frame_rows + projected).astype(jnp.bfloat16).reshape(slabs, frames_dev, width)
 
-    grad_hidden, grad_taps, grad_hidden_kept = kernel_call(
+    grad_hidden, grad_taps = kernel_call(
         backward_kernel,
         (
             jax.ShapeDtypeStruct((rows_dev, 2 * width), jnp.bfloat16),
             jax.ShapeDtypeStruct((kernel_len + 9, width), jnp.float32),
-            pltpu.HBM((rows_dev, 2 * width), jnp.bfloat16),
         ),
         [
             pltpu.VMEM((blocks, wide, LANES), jnp.float32),
             pltpu.VMEM((blocks, kernel_len, 8, LANES), jnp.float32),
-            pltpu.SemaphoreType.DMA((slabs,)),
         ],
         elements * 5 * kernel_len,
         grad_mixing, gated, ids, taps, lin, sig, grad_gain_mid,
-        out_specs=(
-            pl.BlockSpec(memory_space=pltpu.VMEM),
-            pl.BlockSpec(memory_space=pltpu.VMEM),
-            pl.BlockSpec(memory_space=pltpu.HBM),
-        ),
     )
     hidden_other = lax.ppermute(grad_hidden, "core", swap)
     small_other = lax.ppermute(grad_taps, "core", swap)
@@ -565,7 +549,7 @@
     )
     in_parts = exchanged(in_part)
     grad_normed = lax.dot_general(
-        grad_hidden_kept, in_full, (((1,), (1,)), ((), ())), preferred_element_type=jnp.float32
+        grad_hidden, in_full, (((1,), (1,)), ((), ())), preferred_element_type=jnp.float32
     )
     grad_rows, _ = pull_pre(grad_normed)
     grad_frames = (

time: 192 us -> 192 us (level)
    unnamed x58 -> x60, local copies, waits for them, and re-layouts: 11.7 us -> 11.7 us
where the time goes in v10:
time: 192 us; the launch traced here: 191 us
  waiting for transfers between devices  76.7 us (40%)
  starting transfers between devices  39.6 us (21%)
  Pallas kernels  33.5 us (17%)
  between operations  14.5 us (8%)
  local copies, waits for them, and re-layouts  13.7 us (7%)
  matrix products  6.48 us (3%)
  other arithmetic  6.21 us (3%)
    all_to_all x2, waiting for transfers between devices, exchanged(): lax.all_to_all(part.reshape(n_z * n_seq, LANES // n_seq, part.shape[1]),...  35.8 us
    pallas_call x8, Pallas kernels, kernel_call(): pl.pallas_call(body, out_shape=outs, scratch_shapes=scratch, compiler_par...  23.1 us
    all_to_all x2, starting transfers between devices, exchanged(): lax.all_to_all(part.reshape(n_z * n_seq, LANES // n_seq, part.shape[1]),...  14.5 us
    ppermute x3, waiting for transfers between devices, per_device(): lax.ppermute(pair, 'z', [(i, (i + d) % n_z) for i in range(n_z)])  14.1 us
    unnamed x60, local copies, waits for them, and re-layouts  11.7 us
    all_to_all x1, starting transfers between devices, per_device(): lax.all_to_all(outgoing, (*DP, *SEQ), split_axis=0, concat_axis=0, tiled=...  11.2 us
    all_gather x1, waiting for transfers between devices, per_device(): out_full = lax.all_gather(out_weight, DP, axis=0, tiled=True)  9.2 us
    all_to_all x1, waiting for transfers between devices, per_device(): final = lax.all_to_all(total, SEQ, 0, 0, tiled=True).reshape(LANES, -1)  8.11 us
  transfers between devices with their start and end apart: 17, of which 10 were waited for; matrix products, arithmetic and copies ran while one was open for 8% of the time, Pallas kernels for 17%

profile of v10, /device:TPU:0, one launch (start us, length us, event | category | flops | bytes accessed | tf_op | source)
XLA Modules:
  0.0 190.7 jit_solution(7004156682141514282)
XLA Ops:
  11.0 1.5 shard_map.127
  12.4 11.2 %all-to-all-start = ((bf16[128,8,512]{2,1,0:T(8,128)(2,1)}), bf16[128,8,512]{2,1,0:T(8,128)(2,1)S(1)}, u32[]{:S(2)}, u32[]{:S(2)}) async-start(bf16[128,8,512]{2,1,0:T(8,128)(2,1)} %shard_map.127), calls=%async_computation | async-start | bytes 2097152 | tf_op jit(solution)/shard_map/all_to_all | solution.py:423
  25.1 2.9 %collective-permute-start.4 = (bf16[2,128,128]{1,2,0:T(8,128)(2,1)S(1)}, bf16[2,128,128]{1,2,0:T(8,128)(2,1)S(1)}, u32[]{:S(2)}, u32[]{:S(2)}) collective-permute-start(bf16[2,128,128]{1,2,0:T(8,128)(2,1)S(1)} %maximum_select_fusion), channel_id=1, source_target_pairs={{0,96},{32,0},{64,32},{96,64},{1,97},{33,1},{65,33},{97,65},{2,98}... | collective-permute-start | bytes 196616 | tf_op jit(solution)/shard_map/ppermute | solution.py:435
  29.6 10.7 %collective-permute-done.4 = bf16[2,128,128]{1,2,0:T(8,128)(2,1)S(1)} collective-permute-done((bf16[2,128,128]{1,2,0:T(8,128)(2,1)S(1)}, bf16[2,128,128]{1,2,0:T(8,128)(2,1)S(1)}, u32[]{:S(2)}, u32[]{:S(2)}) %collective-permute-start.4) | collective-permute-done | bytes 65568 | tf_op jit(solution)/shard_map/ppermute | solution.py:435
  40.4 1.9 %collective-permute-done.5 = bf16[2,128,128]{1,2,0:T(8,128)(2,1)S(1)} collective-permute-done((bf16[2,128,128]{1,2,0:T(8,128)(2,1)S(1)}, bf16[2,128,128]{1,2,0:T(8,128)(2,1)S(1)}, u32[]{:S(2)}, u32[]{:S(2)}) %collective-permute-start.5) | collective-permute-done | bytes 65568 | tf_op jit(solution)/shard_map/ppermute | solution.py:435
  42.3 1.5 collective-permute-done.6
  45.6 2.8 %collective-permute-start.2 = (bf16[2,48,1024]{2,1,0:T(8,128)(2,1)S(1)}, bf16[2,48,1024]{2,1,0:T(8,128)(2,1)S(1)}, u32[]{:S(2)}, u32[]{:S(2)}) collective-permute-start(bf16[2,48,1024]{2,1,0:T(8,128)(2,1)S(1)} %get-tuple-element.32), channel_id=1, source_target_pairs={{0,1},{1,2},{2,3},{3,4},{4,5},{5,6},{6,7},{7,8},{8,9},{9,10},{10,1... | collective-permute-start | bytes 589832 | tf_op jit(solution)/shard_map/ppermute | solution.py:384
  48.3 1.3 collective-permute-start.3
  49.7 3.2 %collective-permute-done.2.low_ref = bf16[2,48,1024]{2,1,0:T(8,128)(2,1)S(1)} collective-permute-done((bf16[2,48,1024]{2,1,0:T(8,128)(2,1)S(1)}, bf16[2,48,1024]{2,1,0:T(8,128)(2,1)S(1)}, u32[]{:S(2)}, u32[]{:S(2)}) %collective-permute-start.2) | collective-permute-done | bytes 196640 | tf_op jit(solution)/shard_map/ppermute | solution.py:384
  52.8 4.1 %collective-permute-done.3.high_ref = bf16[2,48,1024]{2,1,0:T(8,128)(2,1)S(1)} collective-permute-done((bf16[2,48,1024]{2,1,0:T(8,128)(2,1)S(1)}, bf16[2,48,1024]{2,1,0:T(8,128)(2,1)S(1)}, u32[]{:S(2)}, u32[]{:S(2)}) %collective-permute-start.3) | collective-permute-done | bytes 196640 | tf_op jit(solution)/shard_map/ppermute | solution.py:384
  59.8 2.2 %copy-done = bf16[1024,2048]{1,0:T(8,128)(2,1)S(1)} copy-done((bf16[1024,2048]{1,0:T(8,128)(2,1)S(1)}, bf16[1024,2048]{1,0:T(8,128)(2,1)}, u32[]{:S(2)}) %copy-start) | copy-done | bytes 4194328
  62.0 3.3 %project.1 = (f32[384,1024]{1,0:T(8,128)S(1)}, f32[384,1024]{1,0:T(8,128)S(1)}, bf16[384,1024]{1,0:T(8,128)(2,1)S(1)}) custom-call(bf16[384,1024]{1,0:T(8,128)(2,1)S(1)} %bitcast.57, bf16[1024,2048]{1,0:T(8,128)(2,1)S(1)} %copy-done, bf16[1024,2048]{1,0:T(8,128)(2,1)S(1)} %copy-done), custom_call_target="tpu_custom_call" | custom-call | flops 1610612736 | bytes 4194304 | tf_op jit(solution)/shard_map/project/pallas_call | solution.py:346
  66.4 1.2 copy-done.7
  67.7 8.2 %shard_map.130 = (bf16[256,1024]{1,0:T(8,128)(2,1)}, f32[320,1152]{1,0:T(8,128)S(1)}) custom-call(bf16[2,192,1024]{2,1,0:T(8,128)(2,1)S(1)} %bitcast.54, s32[2,192,128]{2,1,0:T(8,128)S(1)} %broadcast_in_dim.39.ids_ref, f32[8,32,128]{2,1,0:T(8,128)S(1)} %copy-done.9, f32[1,1024]{1,0:T(1,128)S(1)} %get-tuple-element.62.gain_ref), custom_call_target="tpu_custom_call" | custom-call | flops 24379392 | bytes 1118208 | tf_op jit(solution)/shard_map/pallas_call | solution.py:372
  76.5 9.2 %all-gather.5.cloned.1.call-done.weight_ref = bf16[1024,1024]{1,0:T(8,128)(2,1)} async-done(((bf16[128,1024]{1,0:T(8,128)(2,1)}), bf16[1024,1024]{1,0:T(8,128)(2,1)}) %all-gather.5.cloned.1.call-update) | async-done | bytes 2097168 | tf_op jit(solution)/shard_map/all_gather | solution.py:410
  85.7 1.6 copy-done.3
  88.4 1.9 %shard_map.131 = (f32[2,160,1024]{2,1,0:T(8,128)S(1)}, f32[8,1024]{1,0:T(8,128)S(1)}) custom-call(f32[320,1152]{1,0:T(8,128)S(1)} %get-tuple-element.40.normed_ref, bf16[320,1024]{1,0:T(8,128)(2,1)S(1)} %copy-done.13, bf16[1024,1024]{1,0:T(8,128)(2,1)S(1)} %copy-done.3, f32[1,1024]{1,0:T(1,128)S(1)} %get-tuple-element.62.gain_ref), custom_call_target="tpu_custom_call" | custom-call | flops 671088640 | bytes 4231168 | tf_op jit(solution)/shard_map/pallas_call | solution.py:372
  90.3 7.9 %shard_map.132 = (bf16[256,2048]{1,0:T(8,128)(2,1)S(1)}, f32[40,1024]{1,0:T(8,128)S(1)}) custom-call(f32[2,160,1024]{2,1,0:T(8,128)S(1)} %get-tuple-element.42.grad_mix_ref, bf16[2,192,1024]{2,1,0:T(8,128)(2,1)S(1)} %bitcast.55, s32[2,192,128]{2,1,0:T(8,128)S(1)} %broadcast_in_dim.39.ids_ref, f32[8,32,128]{2,1,0:T(8,128)S(1)} %copy-done.10, ...), custom_call_target="tpu_custom_call" | custom-call | flops 40632320 | bytes 5603328 | tf_op jit(solution)/shard_map/pallas_call | solution.py:372
  98.6 3.0 %weight_part.3 = bf16[512,1024]{1,0:T(8,128)(2,1)} custom-call(s32[1]{0:T(128)} %bitcast.19.core_ref, bf16[256,1024]{1,0:T(8,128)(2,1)} %get-tuple-element.39.left_ref, bf16[256,1024]{1,0:T(8,128)(2,1)} %collective-permute-done.10.left_other_ref, bf16[256,1024]{1,0:T(8,128)(2,1)S(1)} %bitcast.52, bf16[256,1024]{1,0:T(8,128)(2,1)S(1)} %copy-done.17), custom_call_target="tpu_custom_call" | custom-call | flops 536870912 | bytes 2097152 | tf_op jit(solution)/shard_map/weight_part/pallas_call | solution.py:281
  101.6 9.5 %all-to-all-start.2 = ((bf16[64,8,1024]{2,1,0:T(8,128)(2,1)}), bf16[64,8,1024]{2,1,0:T(8,128)(2,1)}, u32[]{:S(2)}, u32[]{:S(2)}) async-start(bf16[64,8,1024]{2,1,0:T(8,128)(2,1)} %bitcast.21), calls=%async_computation.2 | async-start | bytes 2097152 | tf_op jit(solution)/shard_map/all_to_all | solution.py:521
  111.4 1.4 collective-permute-done.9.rest_1_
  112.8 4.1 %weight_part.2 = bf16[512,2176]{1,0:T(8,128)(2,1)} custom-call(s32[1]{0:T(128)} %bitcast.19.core_ref, bf16[256,1024]{1,0:T(8,128)(2,1)S(1)} %copy-done.15, bf16[256,1024]{1,0:T(8,128)(2,1)} %collective-permute-done.7.left_other_ref, bf16[256,2048]{1,0:T(8,128)(2,1)S(1)} %get-tuple-element.46.right_ref, ...), custom_call_target="tpu_custom_call" | custom-call | flops 1073741824 | bytes 3145728 | tf_op jit(solution)/shard_map/weight_part/pallas_call | solution.py:281
  116.9 13.2 %all-to-all-done.2 = bf16[64,8,1024]{2,1,0:T(8,128)(2,1)} async-done(((bf16[64,8,1024]{2,1,0:T(8,128)(2,1)}), bf16[64,8,1024]{2,1,0:T(8,128)(2,1)}, u32[]{:S(2)}, u32[]{:S(2)}) %all-to-all-start.2) | async-done | bytes 1048608 | tf_op jit(solution)/shard_map/all_to_all | solution.py:521
  130.1 5.0 %all-to-all-start.1 = ((bf16[64,8,2176]{2,1,0:T(8,128)(2,1)}), bf16[64,8,2176]{2,1,0:T(8,128)(2,1)S(1)}, u32[]{:S(2)}, u32[]{:S(2)}) async-start(bf16[64,8,2176]{2,1,0:T(8,128)(2,1)} %bitcast.20), calls=%async_computation.1 | async-start | bytes 4456448 | tf_op jit(solution)/shard_map/all_to_all | solution.py:521
  136.2 3.9 %fusion.4 = (f32[256]{0:T(256)S(1)}, f32[256]{0:T(256)S(1)}, f32[256,1024]{1,0:T(8,128)S(1)}) fusion(bf16[256,1024]{1,0:T(8,128)(2,1)S(1)} %get-tuple-element.31.frames_ref, f32[256]{0:T(256)S(1)} %broadcast_multiply_fusion, f32[1024]{0:T(1024)S(1)} %bitcast.58, bf16[256,2048]{1,0:T(8,128)(2,1)} %copy-done.11, ...), kind=kOutput, calls=%fused_computation.10 | convolution fusion | flops 1075576320 | bytes 6822912 | tf_op jit(solution)/shard_map/dot_general | solution.py:551
  141.0 1.4 convert_reduce_fusion.out_sum_ref
  142.4 22.6 %all-to-all-done.1.parts_ref = bf16[64,8,2176]{2,1,0:T(8,128)(2,1)S(1)} async-done(((bf16[64,8,2176]{2,1,0:T(8,128)(2,1)}), bf16[64,8,2176]{2,1,0:T(8,128)(2,1)S(1)}, u32[]{:S(2)}, u32[]{:S(2)}) %all-to-all-start.1) | async-done | bytes 2228256 | tf_op jit(solution)/shard_map/all_to_all | solution.py:521
  166.4 3.8 %all-to-all-start.3 = ((bf16[16,8,3200]{2,1,0:T(8,128)(2,1)}), bf16[16,8,3200]{2,1,0:T(8,128)(2,1)S(1)}, u32[]{:S(2)}, u32[]{:S(2)}) async-start(bf16[16,8,3200]{2,1,0:T(8,128)(2,1)} %copy-done.2), calls=%async_computation.3 | async-start | bytes 1638400 | tf_op jit(solution)/shard_map/all_to_all | solution.py:573
  170.2 1.2 add_convert_fusion
  172.0 2.6 %fusion.3 = bf16[256,1024]{1,0:T(8,128)(2,1)} fusion(bf16[256,1024]{1,0:T(8,128)(2,1)} %get-tuple-element.39.left_ref, bf16[1024,1024]{1,0:T(8,128)(2,1)S(1)} %copy-done.4, bf16[256,1024]{1,0:T(8,128)(2,1)S(1)} %get-tuple-element.31.frames_ref), kind=kOutput, calls=%fused_computation.9 | convolution fusion | flops 537657344 | bytes 3670016 | tf_op jit(solution)/shard_map/dot_general | solution.py:529
  174.5 8.1 %all-to-all-done.3 = bf16[16,8,3200]{2,1,0:T(8,128)(2,1)S(1)} async-done(((bf16[16,8,3200]{2,1,0:T(8,128)(2,1)}), bf16[16,8,3200]{2,1,0:T(8,128)(2,1)S(1)}, u32[]{:S(2)}, u32[]{:S(2)}) %all-to-all-start.3) | async-done | bytes 819232 | tf_op jit(solution)/shard_map/all_to_all | solution.py:573
  182.6 1.2 shard_map.134
  (113 shorter events, 18.8 us)
Async XLA Ops:
  7.2 52.6 %all-gather.3.cloned.1.call-start = ((), (), s32[]{:S(2)}) async-start(), calls=%async_computation.4 | async-start | bytes 4718592 | tf_op jit(solution)/shard_map/all_gather | solution.py:409
  11.0 12.7 %copy-start.23 = (bf16[128,31]{0,1:T(8,128)(2,1)S(1)}, bf16[128,31]{0,1:T(8,128)(2,1)}, u32[]{:S(2)}) copy-start(bf16[128,31]{0,1:T(8,128)(2,1)} %param.13) | copy-start | bytes 23812
  11.0 12.7 %copy-start.24 = (bf16[128,2]{0,1:T(2,128)(2,1)S(1)}, bf16[128,2]{0,1:T(2,128)(2,1)}, u32[]{:S(2)}) copy-start(bf16[128,2]{0,1:T(2,128)(2,1)} %param.14) | copy-start | bytes 1540
  11.0 12.8 %copy-start.1 = (bf16[2,128,1024]{2,1,0:T(8,128)(2,1)S(1)}, bf16[2,128,1024]{2,1,0:T(8,128)(2,1)}, u32[]{:S(2)}) copy-start(bf16[2,128,1024]{2,1,0:T(8,128)(2,1)} %upstream_ref.3) | copy-start | bytes 1572868
  11.0 13.4 %copy-start.21 = (s32[128,128]{1,0:T(8,128)S(1)}, s32[128,128]{1,0:T(8,128)}, u32[]{:S(2)}) copy-start(s32[128,128]{1,0:T(8,128)} %param.9) | copy-start | bytes 196612
  12.4 31.4 %all-to-all-start = ((bf16[128,8,512]{2,1,0:T(8,128)(2,1)}), bf16[128,8,512]{2,1,0:T(8,128)(2,1)S(1)}, u32[]{:S(2)}, u32[]{:S(2)}) async-start(bf16[128,8,512]{2,1,0:T(8,128)(2,1)} %shard_map.127), calls=%async_computation | async-start | bytes 2097152 | tf_op jit(solution)/shard_map/all_to_all | solution.py:423
  23.6 62.1 %all-gather.5.cloned.1.call-start = ((), (), s32[]{:S(2)}) async-start(), calls=%async_computation.5 | async-start | bytes 2359296 | tf_op jit(solution)/shard_map/all_gather | solution.py:410
  23.7 1.3 collective-permute-start.1
  23.8 20.0 %collective-permute-start = (bf16[256,1024]{1,0:T(8,128)(2,1)S(1)}, bf16[256,1024]{1,0:T(8,128)(2,1)S(1)}, u32[]{:S(2)}, u32[]{:S(2)}) collective-permute-start(bf16[256,1024]{1,0:T(8,128)(2,1)S(1)} %bitcast.51), channel_id=1, source_target_pairs={{0,16},{16,0},{1,17},{17,1},{2,18},{18,2},{3,19},{19,3},{4,20},{20... | collective-permute-start | bytes 1572872 | tf_op jit(solution)/shard_map/ppermute | solution.py:438
  25.1 15.3 %collective-permute-start.4 = (bf16[2,128,128]{1,2,0:T(8,128)(2,1)S(1)}, bf16[2,128,128]{1,2,0:T(8,128)(2,1)S(1)}, u32[]{:S(2)}, u32[]{:S(2)}) collective-permute-start(bf16[2,128,128]{1,2,0:T(8,128)(2,1)S(1)} %maximum_select_fusion), channel_id=1, source_target_pairs={{0,96},{32,0},{64,32},{96,64},{1,97},{33,1},{65,33},{97,65},{2,98}... | collective-permute-start | bytes 196616 | tf_op jit(solution)/shard_map/ppermute | solution.py:435
  28.1 14.2 %collective-permute-start.5 = (bf16[2,128,128]{1,2,0:T(8,128)(2,1)S(1)}, bf16[2,128,128]{1,2,0:T(8,128)(2,1)S(1)}, u32[]{:S(2)}, u32[]{:S(2)}) collective-permute-start(bf16[2,128,128]{1,2,0:T(8,128)(2,1)S(1)} %maximum_select_fusion), channel_id=1, source_target_pairs={{0,64},{32,96},{64,0},{96,32},{1,65},{33,97},{65,1},{97,33},{2,66}... | collective-permute-start | bytes 196616 | tf_op jit(solution)/shard_map/ppermute | solution.py:435
  28.5 15.2 %collective-permute-start.6 = (bf16[2,128,128]{1,2,0:T(8,128)(2,1)S(1)}, bf16[2,128,128]{1,2,0:T(8,128)(2,1)S(1)}, u32[]{:S(2)}, u32[]{:S(2)}) collective-permute-start(bf16[2,128,128]{1,2,0:T(8,128)(2,1)S(1)} %maximum_select_fusion), channel_id=1, source_target_pairs={{0,32},{32,64},{64,96},{96,0},{1,33},{33,65},{65,97},{97,1},{2,34}... | collective-permute-start | bytes 196616 | tf_op jit(solution)/shard_map/ppermute | solution.py:435
  44.6 14.4 %copy-start.22 = (s32[2,2048]{1,0:T(2,128)S(1)}, s32[2,2048]{1,0:T(2,128)}, u32[]{:S(2)}) copy-start(s32[2,2048]{1,0:T(2,128)} %param.10) | copy-start | bytes 49156
  44.6 14.5 %copy-start.25 = (pred[32]{0:T(512)(128)(4,1)S(1)}, pred[32]{0:T(512)(128)(4,1)}, u32[]{:S(2)}) copy-start(pred[32]{0:T(512)(128)(4,1)} %constant.66.clone.1) | copy-start | bytes 100
  45.6 7.3 %collective-permute-start.2 = (bf16[2,48,1024]{2,1,0:T(8,128)(2,1)S(1)}, bf16[2,48,1024]{2,1,0:T(8,128)(2,1)S(1)}, u32[]{:S(2)}, u32[]{:S(2)}) collective-permute-start(bf16[2,48,1024]{2,1,0:T(8,128)(2,1)S(1)} %get-tuple-element.32), channel_id=1, source_target_pairs={{0,1},{1,2},{2,3},{3,4},{4,5},{5,6},{6,7},{7,8},{8,9},{9,10},{10,1... | collective-permute-start | bytes 589832 | tf_op jit(solution)/shard_map/ppermute | solution.py:384
  48.3 8.6 %collective-permute-start.3 = (bf16[2,48,1024]{2,1,0:T(8,128)(2,1)S(1)}, bf16[2,48,1024]{2,1,0:T(8,128)(2,1)S(1)}, u32[]{:S(2)}, u32[]{:S(2)}) collective-permute-start(bf16[2,48,1024]{2,1,0:T(8,128)(2,1)S(1)} %get-tuple-element.33), channel_id=1, source_target_pairs={{1,0},{2,1},{3,2},{4,3},{5,4},{6,5},{7,6},{8,7},{9,8},{10,9},{11,1... | collective-permute-start | bytes 589832 | tf_op jit(solution)/shard_map/ppermute | solution.py:384
  59.0 6.3 %copy-start.14 = (bf16[256,1024]{1,0:T(8,128)(2,1)}, bf16[256,1024]{1,0:T(8,128)(2,1)S(1)}, u32[]{:S(2)}) copy-start(bf16[256,1024]{1,0:T(8,128)(2,1)S(1)} %get-tuple-element.37.left_ref) | copy-start | bytes 1572868
  59.0 8.7 %collective-permute-start.7 = (bf16[256,1024]{1,0:T(8,128)(2,1)S(1)}, bf16[256,1024]{1,0:T(8,128)(2,1)}, u32[]{:S(2)}, u32[]{:S(2)}) collective-permute-start(bf16[256,1024]{1,0:T(8,128)(2,1)S(1)} %get-tuple-element.37.left_ref), channel_id=1, source_target_pairs={{0,16},{16,0},{1,17},{17,1},{2,18},{18,2},{3,19},{19,3},{4,20},{20... | collective-permute-start | bytes 1572872 | tf_op jit(solution)/shard_map/ppermute | solution.py:488
  59.8 2.2 %copy-start = (bf16[1024,2048]{1,0:T(8,128)(2,1)S(1)}, bf16[1024,2048]{1,0:T(8,128)(2,1)}, u32[]{:S(2)}) copy-start(bf16[1024,2048]{1,0:T(8,128)(2,1)} %all-gather.3.cloned.1.call-done.lin_w_ref.gate_w_ref) | copy-start | bytes 12582916
  62.0 5.8 %copy-start.9 = (f32[8,32,128]{2,1,0:T(8,128)S(1)}, f32[8,32,128]{2,1,0:T(8,128)}, u32[]{:S(2)}) copy-start(f32[8,32,128]{2,1,0:T(8,128)} %bitcast_bitcast_fusion.taps_ref) | copy-start | bytes 393220
  76.0 22.6 %collective-permute-start.10 = (bf16[256,1024]{1,0:T(8,128)(2,1)}, bf16[256,1024]{1,0:T(8,128)(2,1)}, u32[]{:S(2)}, u32[]{:S(2)}) collective-permute-start(bf16[256,1024]{1,0:T(8,128)(2,1)} %get-tuple-element.39.left_ref), channel_id=1, source_target_pairs={{0,16},{16,0},{1,17},{17,1},{2,18},{18,2},{3,19},{19,3},{4,20},{20... | collective-permute-start | bytes 1572872 | tf_op jit(solution)/shard_map/ppermute | solution.py:508
  88.3 2.0 %copy-start.8 = (f32[384,1024]{1,0:T(8,128)S(1)}, f32[384,1024]{1,0:T(8,128)}, u32[]{:S(2)}) copy-start(f32[384,1024]{1,0:T(8,128)} %copy-done.7) | copy-start | bytes 4718596
  88.3 2.0 %copy-start.10 = (f32[8,32,128]{2,1,0:T(8,128)S(1)}, f32[8,32,128]{2,1,0:T(8,128)}, u32[]{:S(2)}) copy-start(f32[8,32,128]{2,1,0:T(8,128)} %bitcast_bitcast_fusion.taps_ref) | copy-start | bytes 393220
  90.3 8.3 %copy-start.17 = (bf16[256,1024]{1,0:T(8,128)(2,1)S(1)}, bf16[256,1024]{1,0:T(8,128)(2,1)}, u32[]{:S(2)}) copy-start(bf16[256,1024]{1,0:T(8,128)(2,1)} %copy-done.16) | copy-start | bytes 1572868
  98.3 14.5 %copy-start.11 = (bf16[256,2048]{1,0:T(8,128)(2,1)}, bf16[256,2048]{1,0:T(8,128)(2,1)S(1)}, u32[]{:S(2)}) copy-start(bf16[256,2048]{1,0:T(8,128)(2,1)S(1)} %get-tuple-element.46.right_ref) | copy-start | bytes 3145732
  98.3 14.5 %collective-permute-start.8 = (bf16[256,2048]{1,0:T(8,128)(2,1)S(1)}, bf16[256,2048]{1,0:T(8,128)(2,1)}, u32[]{:S(2)}, u32[]{:S(2)}) collective-permute-start(bf16[256,2048]{1,0:T(8,128)(2,1)S(1)} %get-tuple-element.46.right_ref), channel_id=1, source_target_pairs={{0,16},{16,0},{1,17},{17,1},{2,18},{18,2},{3,19},{19,3},{4,20},{20... | collective-permute-start | bytes 3145736 | tf_op jit(solution)/shard_map/ppermute | solution.py:545
  98.6 14.2 %copy-start.15 = (bf16[256,1024]{1,0:T(8,128)(2,1)S(1)}, bf16[256,1024]{1,0:T(8,128)(2,1)}, u32[]{:S(2)}) copy-start(bf16[256,1024]{1,0:T(8,128)(2,1)} %copy-done.14) | copy-start | bytes 1572868
  101.6 28.5 %all-to-all-start.2 = ((bf16[64,8,1024]{2,1,0:T(8,128)(2,1)}), bf16[64,8,1024]{2,1,0:T(8,128)(2,1)}, u32[]{:S(2)}, u32[]{:S(2)}) async-start(bf16[64,8,1024]{2,1,0:T(8,128)(2,1)} %bitcast.21), calls=%async_computation.2 | async-start | bytes 2097152 | tf_op jit(solution)/shard_map/all_to_all | solution.py:521
  111.1 1.7 collective-permute-start.9
  130.1 35.0 %all-to-all-start.1 = ((bf16[64,8,2176]{2,1,0:T(8,128)(2,1)}), bf16[64,8,2176]{2,1,0:T(8,128)(2,1)S(1)}, u32[]{:S(2)}, u32[]{:S(2)}) async-start(bf16[64,8,2176]{2,1,0:T(8,128)(2,1)} %bitcast.20), calls=%async_computation.1 | async-start | bytes 4456448 | tf_op jit(solution)/shard_map/all_to_all | solution.py:521
  166.4 3.8 %copy-start.20 = (f32[256,1024]{1,0:T(8,128)S(1)}, f32[256,1024]{1,0:T(8,128)}, u32[]{:S(2)}) copy-start(f32[256,1024]{1,0:T(8,128)} %copy-done.19) | copy-start | bytes 3145732
  166.4 16.2 %all-to-all-start.3 = ((bf16[16,8,3200]{2,1,0:T(8,128)(2,1)}), bf16[16,8,3200]{2,1,0:T(8,128)(2,1)S(1)}, u32[]{:S(2)}, u32[]{:S(2)}) async-start(bf16[16,8,3200]{2,1,0:T(8,128)(2,1)} %copy-done.2), calls=%async_computation.3 | async-start | bytes 1638400 | tf_op jit(solution)/shard_map/all_to_all | solution.py:573
  (11 other events, 13.3 us)
Sparse Core Ops, SparseCore 0:
  9.7 48.8 all-gather.2
  60.3 25.3 all-gather.4
